TPU v7x, 32 devices: a whole 2x2x4 slice. The times are simulated.
32 devices in a mesh: dp: 8 (over z, x), mp: 4 (over y, core).
Axes of the slice: x: 2, y: 2, z: 4, core: 2. Of those that a mesh axis runs over, the one named last changes fastest.
Arguments:
- tokens: bfloat16 [16384, 1024], P('dp'), may hold values from -6 to 6
- cotangent: bfloat16 [16384, 1024], P('dp'), may hold values from -15 to 15
- item_lengths: int32 [8, 8], P('dp'), may hold values from 1 to 1024, 2048 in all within a row
- w_qkv: bfloat16 [3, 1024, 1024], P(None, None, 'mp'), may hold values from -0.1875 to 0.1875
- b_qv: float32 [2, 1024], P(None, 'mp'), may hold values from -3 to 3
- w_out: bfloat16 [1024, 1024], P('mp'), may hold values from -0.75 to 0.75
- b_out: float32 [1024], replicated, may hold values from -1.75 to 1.75
- w_fc1: bfloat16 [1024, 4096], P(None, 'mp'), may hold values from -0.1875 to 0.1875
- b_fc1: float32 [4096], P('mp'), may hold values from -3 to 3
- w_fc2: bfloat16 [4096, 1024], P('mp'), may hold values from -0.09375 to 0.09375
- b_fc2: float32 [1024], replicated, may hold values from -1.75 to 1.75
- ln1_gain: float32 [1024], replicated, may hold values from 0.5 to 1.5
- ln1_bias: float32 [1024], replicated, may hold values from -1.75 to 1.75
- ln2_gain: float32 [1024], replicated, may hold values from 0.5 to 1.5
- ln2_bias: float32 [1024], replicated, may hold values from -1.75 to 1.75
Outputs:
- output: bfloat16 [16384, 1024], P('dp')
- grad_tokens: float32 [16384, 1024], P('dp')
- grad_w_qkv: float32 [3, 1024, 1024], P(None, 'dp', 'mp')
- grad_b_qv: float32 [2, 1024], P(None, 'mp')
- grad_w_out: float32 [1024, 1024], P('mp', 'dp')
- grad_b_out: float32 [1024], replicated
- grad_w_fc1: float32 [1024, 4096], P('dp', 'mp')
- grad_b_fc1: float32 [4096], P('mp')
- grad_w_fc2: float32 [4096, 1024], P('mp', 'dp')
- grad_b_fc2: float32 [1024], replicated
- grad_ln1_gain: float32 [1024], replicated
- grad_ln1_bias: float32 [1024], replicated
- grad_ln2_gain: float32 [1024], replicated
- grad_ln2_bias: float32 [1024], replicated
Inputs may be any that keep to these rules, and one draw needn't show every extreme that they name: `item_lengths`: each row sums to 2048, and each row's longest item has exactly 1024 patches.
All inputs are finite; a program needn't handle non-finite values.
Results may differ from a plain program's by a relative error of at most 0.019.
Values may be sent and summed in bfloat16 or wider, within the bound.
A program may use at most 192 MiB of HBM per device.

v0:
```python
from functools import partial

import jax
import jax.numpy as jnp
from jax import lax
from jax.experimental import pallas as pl
from jax.experimental.pallas import tpu as pltpu
from jax.sharding import PartitionSpec as P

HEAD = 64
QBLOCK = 512
TQ = 256
TK = 256
NEG = -1e30


def _fwd_kernel(lo_ref, hi_ref, segc_ref, segr_ref, qt_ref, k_ref, vt_ref, ot_ref, o32t_ref, lse_ref):
    rows = qt_ref.shape[2]
    scale = HEAD ** (-0.5)

    def q_body(i, carry):
        r0 = pl.multiple_of(i * TQ, TQ)
        qt = qt_ref[0, :, pl.ds(r0, TQ)]
        sq = segr_ref[:, pl.ds(r0, TQ)]

        def kv_body(j, state):
            m, l, acc = state
            c0 = pl.multiple_of(j * TK, TK)
            s = jnp.dot(k_ref[0, pl.ds(c0, TK), :], qt, preferred_element_type=jnp.float32) * scale
            same = segc_ref[pl.ds(c0, TK), :] == sq
            s = jnp.where(same, s, NEG)
            m_new = jnp.maximum(m, jnp.max(s, axis=0, keepdims=True))
            p = jnp.exp(s - m_new)
            alpha = jnp.exp(m - m_new)
            l = alpha * l + jnp.sum(p, axis=0, keepdims=True)
            pv = jnp.dot(vt_ref[0, :, pl.ds(c0, TK)], p.astype(jnp.bfloat16),
                         preferred_element_type=jnp.float32)
            return m_new, l, alpha * acc + pv

        m0 = jnp.full((1, TQ), NEG, jnp.float32)
        l0 = jnp.zeros((1, TQ), jnp.float32)
        acc0 = jnp.zeros((HEAD, TQ), jnp.float32)
        m, l, acc = lax.fori_loop(lo_ref[i], hi_ref[i], kv_body, (m0, l0, acc0))
        out = acc / l
        ot_ref[0, :, pl.ds(r0, TQ)] = out.astype(ot_ref.dtype)
        o32t_ref[0, :, pl.ds(r0, TQ)] = out
        lse_ref[0, :, pl.ds(r0, TQ)] = m + jnp.log(l)
        return carry

    lax.fori_loop(0, rows // TQ, q_body, 0)


def _bwd_kernel(lo_ref, hi_ref, segc_ref, segr_ref, q_ref, qt_ref, k_ref, kt_ref, v_ref, do_ref, dot_ref,
                o32t_ref, lse_ref, dqt_ref, dk_ref, dv_ref, dvec_ref):
    rows = q_ref.shape[1]
    scale = HEAD ** (-0.5)
    dqt_ref[...] = jnp.zeros_like(dqt_ref)

    def d_body(i, carry):
        r0 = pl.multiple_of(i * TQ, TQ)
        prod = dot_ref[0, :, pl.ds(r0, TQ)].astype(jnp.float32) * o32t_ref[0, :, pl.ds(r0, TQ)]
        dvec_ref[:, pl.ds(r0, TQ)] = jnp.sum(prod, axis=0, keepdims=True)
        return carry

    lax.fori_loop(0, rows // TQ, d_body, 0)

    def kv_body(j, carry):
        c0 = pl.multiple_of(j * TK, TK)
        k = k_ref[0, pl.ds(c0, TK), :]
        v = v_ref[0, pl.ds(c0, TK), :]
        kt = kt_ref[0, :, pl.ds(c0, TK)]
        sk = segc_ref[pl.ds(c0, TK), :]

        def q_body(i, grads):
            dk, dv = grads
            r0 = pl.multiple_of(i * TQ, TQ)
            s = jnp.dot(k, qt_ref[0, :, pl.ds(r0, TQ)], preferred_element_type=jnp.float32) * scale
            same = sk == segr_ref[:, pl.ds(r0, TQ)]
            s = jnp.where(same, s, NEG)
            p = jnp.exp(s - lse_ref[0, :, pl.ds(r0, TQ)])
            dp = jnp.dot(v, dot_ref[0, :, pl.ds(r0, TQ)], preferred_element_type=jnp.float32)
            ds = (p * (dp - dvec_ref[:, pl.ds(r0, TQ)])).astype(jnp.bfloat16)
            dv = dv + jnp.dot(p.astype(jnp.bfloat16), do_ref[0, pl.ds(r0, TQ), :],
                              preferred_element_type=jnp.float32)
            dk = dk + jnp.dot(ds, q_ref[0, pl.ds(r0, TQ), :], preferred_element_type=jnp.float32)
            dqt_ref[0, :, pl.ds(r0, TQ)] += jnp.dot(kt, ds, preferred_element_type=jnp.float32)
            return dk, dv

        zeros = jnp.zeros((TK, HEAD), jnp.float32)
        dk, dv = lax.fori_loop(lo_ref[j], hi_ref[j], q_body, (zeros, zeros))
        dk_ref[0, pl.ds(c0, TK), :] = dk * scale
        dv_ref[0, pl.ds(c0, TK), :] = dv
        return carry

    lax.fori_loop(0, rows // TK, kv_body, 0)
    dqt_ref[...] = dqt_ref[...] * scale


def block_ranges(segments, item_lengths_row):
    rows = segments.shape[0]
    ends = jnp.cumsum(item_lengths_row.astype(jnp.int32))
    starts = ends - item_lengths_row.astype(jnp.int32)
    first = segments[0::TQ]
    last = segments[TQ - 1::TQ]
    n_items = item_lengths_row.shape[0]
    key_lo = jnp.take(starts, jnp.clip(first, 0, n_items - 1))
    key_hi = jnp.take(ends, jnp.clip(last, 0, n_items - 1))
    lo = jnp.clip(key_lo // TK, 0, rows // TK)
    hi = jnp.clip((key_hi + TK - 1) // TK, 0, rows // TK)
    return lo.astype(jnp.int32), hi.astype(jnp.int32)


def _head_specs(rows):
    plain = pl.BlockSpec((1, rows, HEAD), lambda h, lo, hi: (h, 0, 0))
    flipped = pl.BlockSpec((1, HEAD, rows), lambda h, lo, hi: (h, 0, 0))
    stat = pl.BlockSpec((1, 1, rows), lambda h, lo, hi: (h, 0, 0))
    col = pl.BlockSpec((rows, 1), lambda h, lo, hi: (0, 0))
    row = pl.BlockSpec((1, rows), lambda h, lo, hi: (0, 0))
    return plain, flipped, stat, col, row


def flash_forward(q, k, v, segments, lo, hi):
    heads, rows, _ = q.shape
    plain, flipped, stat, col, row = _head_specs(rows)
    flops = int(heads * rows * rows * HEAD * 2 * 2 * 0.6)
    return pl.pallas_call(
        _fwd_kernel,
        out_shape=(
            jax.ShapeDtypeStruct((heads, HEAD, rows), jnp.bfloat16),
            jax.ShapeDtypeStruct((heads, HEAD, rows), jnp.float32),
            jax.ShapeDtypeStruct((heads, 1, rows), jnp.float32),
        ),
        grid_spec=pltpu.PrefetchScalarGridSpec(
            num_scalar_prefetch=2,
            grid=(heads,),
            in_specs=[col, row, flipped, plain, flipped],
            out_specs=[flipped, flipped, stat],
        ),
        compiler_params=pltpu.CompilerParams(
            dimension_semantics=("arbitrary",), vmem_limit_bytes=48 * 1024 * 1024),
        cost_estimate=pl.CostEstimate(
            flops=flops, transcendentals=int(heads * rows * rows * 0.6),
            bytes_accessed=int(heads * rows * HEAD * (2 * 4 + 4) + heads * rows * 4)),
        name="segment_flash_fwd",
    )(lo, hi, segments.reshape(rows, 1), segments.reshape(1, rows),
      q.transpose(0, 2, 1), k, v.transpose(0, 2, 1))


def flash_backward(q, k, v, do, o32t, lse, segments, lo, hi):
    heads, rows, _ = q.shape
    plain, flipped, stat, col, row = _head_specs(rows)
    flops = int(heads * rows * rows * HEAD * 2 * 4 * 0.6)
    return pl.pallas_call(
        _bwd_kernel,
        out_shape=(
            jax.ShapeDtypeStruct((heads, HEAD, rows), jnp.float32),
            jax.ShapeDtypeStruct((heads, rows, HEAD), jnp.float32),
            jax.ShapeDtypeStruct((heads, rows, HEAD), jnp.float32),
        ),
        grid_spec=pltpu.PrefetchScalarGridSpec(
            num_scalar_prefetch=2,
            grid=(heads,),
            in_specs=[col, row, plain, flipped, plain, flipped, plain, plain, flipped, flipped, stat],
            out_specs=[flipped, plain, plain],
            scratch_shapes=[pltpu.VMEM((1, rows), jnp.float32)],
        ),
        compiler_params=pltpu.CompilerParams(
            dimension_semantics=("arbitrary",), vmem_limit_bytes=48 * 1024 * 1024),
        cost_estimate=pl.CostEstimate(
            flops=flops, transcendentals=int(heads * rows * rows * 0.6),
            bytes_accessed=int(heads * rows * HEAD * (2 * 7 + 4 * 4) + heads * rows * 4)),
        name="segment_flash_bwd",
    )(lo, hi, segments.reshape(rows, 1), segments.reshape(1, rows),
      q, q.transpose(0, 2, 1), k, k.transpose(0, 2, 1), v, do, do.transpose(0, 2, 1), o32t, lse)

def normalize(values, gain, shift):
    center = jnp.mean(values, axis=-1, keepdims=True)
    centered = values - center
    spread = jnp.mean(centered * centered, axis=-1, keepdims=True)
    return centered * lax.rsqrt(spread + 1e-06) * gain + shift


def exact_gelu(values):
    return jax.nn.gelu(values, approximate=False)


def segment_ids(lengths_row, row_count):
    ends = jnp.cumsum(lengths_row)
    positions = jnp.arange(row_count, dtype=jnp.int32)
    return jnp.sum((positions[:, None] >= ends[None, :]).astype(jnp.int32), axis=1)


def mp_allreduce(partial, n_mp):
    if n_mp != 4:
        return lax.psum(partial, "mp").astype(jnp.float32)
    idx = lax.axis_index("mp")
    low_bit = idx % 2
    half = partial.shape[0] // 2
    mine = lax.dynamic_slice_in_dim(partial, low_bit * half, half, 0)
    other = lax.dynamic_slice_in_dim(partial, (1 - low_bit) * half, half, 0)
    got = lax.ppermute(other, "mp", [(k, k ^ 1) for k in range(4)])
    first = (mine.astype(jnp.float32) + got.astype(jnp.float32)).astype(jnp.bfloat16)
    got_far = lax.ppermute(first, "mp", [(k, k ^ 2) for k in range(4)])
    second = (first.astype(jnp.float32) + got_far.astype(jnp.float32)).astype(jnp.bfloat16)
    got_back = lax.ppermute(second, "mp", [(k, k ^ 1) for k in range(4)])
    top = jnp.where(low_bit == 0, second, got_back)
    bottom = jnp.where(low_bit == 0, got_back, second)
    return jnp.concatenate([top, bottom], axis=0).astype(jnp.float32)


def dp_allreduce(values, n_dp):
    if n_dp & (n_dp - 1):
        return lax.psum(values, "dp")
    total = values
    step = 1
    while step < n_dp:
        total = total + lax.ppermute(total, "dp", [(k, k ^ step) for k in range(n_dp)])
        step *= 2
    return total


def per_device(n_mp, n_dp,

    tokens,
    cotangent,
    item_lengths,
    w_qkv,
    b_qv,
    w_out,
    b_out,
    w_fc1,
    b_fc1,
    w_fc2,
    b_fc2,
    ln1_gain,
    ln1_bias,
    ln2_gain,
    ln2_bias,
):
    row_count = tokens.shape[0]
    local_cols = w_qkv.shape[2]
    heads_here = local_cols // HEAD
    segments = segment_ids(item_lengths[0], row_count)
    inputs = tokens.astype(jnp.float32)
    norm_one, norm_one_back = jax.vjp(normalize, inputs, ln1_gain, ln1_bias)
    normed_one = norm_one.astype(jnp.bfloat16)
    queries = (jnp.dot(normed_one, w_qkv[0], preferred_element_type=jnp.float32) + b_qv[0]).astype(
        jnp.bfloat16
    )
    key_rows = jnp.dot(normed_one, w_qkv[1], preferred_element_type=jnp.float32).astype(
        jnp.bfloat16
    )
    value_rows = (
        jnp.dot(normed_one, w_qkv[2], preferred_element_type=jnp.float32) + b_qv[1]
    ).astype(jnp.bfloat16)
    def to_heads(values):
        return values.reshape(row_count, heads_here, HEAD).transpose(1, 0, 2)

    def from_heads(values):
        return values.transpose(1, 0, 2).reshape(row_count, local_cols)

    lo_blocks, hi_blocks = block_ranges(segments, item_lengths[0])
    query_heads = to_heads(queries)
    key_heads = to_heads(key_rows)
    value_heads = to_heads(value_rows)
    out_heads, out_f32, log_norms = flash_forward(
        query_heads, key_heads, value_heads, segments, lo_blocks, hi_blocks
    )
    attended = out_heads.transpose(2, 0, 1).reshape(row_count, local_cols)
    attention_sum = mp_allreduce(
        jnp.dot(attended, w_out, preferred_element_type=jnp.float32).astype(jnp.bfloat16), n_mp
    )
    middle = inputs + attention_sum + b_out
    norm_two, norm_two_back = jax.vjp(normalize, middle, ln2_gain, ln2_bias)
    normed_two = norm_two.astype(jnp.bfloat16)
    hidden_pre = jnp.dot(normed_two, w_fc1, preferred_element_type=jnp.float32) + b_fc1
    activated_full, gelu_back = jax.vjp(exact_gelu, hidden_pre)
    activated = activated_full.astype(jnp.bfloat16)
    mlp_partial = jnp.dot(activated, w_fc2, preferred_element_type=jnp.float32).astype(jnp.bfloat16)
    upstream = cotangent.astype(jnp.float32)
    grad_b_fc2 = jnp.sum(upstream, axis=0)
    grad_w_fc2 = jnp.einsum("tf,td->fd", activated, cotangent, preferred_element_type=jnp.float32)
    d_act = jnp.einsum("td,fd->tf", cotangent, w_fc2, preferred_element_type=jnp.float32)
    d_pre = gelu_back(d_act)[0]
    grad_b_fc1 = jnp.sum(d_pre, axis=0)
    d_pre_low = d_pre.astype(jnp.bfloat16)
    grad_w_fc1 = jnp.einsum("td,tf->df", normed_two, d_pre_low, preferred_element_type=jnp.float32)
    d_normed_two = mp_allreduce(
        jnp.einsum("tf,df->td", d_pre_low, w_fc1, preferred_element_type=jnp.float32).astype(
            jnp.bfloat16
        ),
        n_mp,
    )
    d_middle_norm, grad_ln2_gain, grad_ln2_bias = norm_two_back(d_normed_two)
    d_middle = upstream + d_middle_norm
    mlp_partial, d_middle = lax.optimization_barrier((mlp_partial, d_middle))
    mlp_sum = mp_allreduce(mlp_partial, n_mp)
    output = (middle + mlp_sum + b_fc2).astype(jnp.bfloat16)
    grad_b_out = jnp.sum(d_middle, axis=0)
    d_middle_low = d_middle.astype(jnp.bfloat16)
    grad_w_out = jnp.einsum("tc,td->cd", attended, d_middle_low, preferred_element_type=jnp.float32)
    d_attended = jnp.einsum(
        "td,cd->tc", d_middle_low, w_out, preferred_element_type=jnp.float32
    ).astype(jnp.bfloat16)
    d_q_heads, d_k_heads, d_v_heads = flash_backward(
        query_heads, key_heads, value_heads, to_heads(d_attended), out_f32, log_norms,
        segments, lo_blocks, hi_blocks,
    )
    d_queries = d_q_heads.transpose(2, 0, 1).reshape(row_count, local_cols)
    d_keys = from_heads(d_k_heads)
    d_values = from_heads(d_v_heads)
    grad_b_qv = jnp.stack([jnp.sum(d_queries, axis=0), jnp.sum(d_values, axis=0)])
    stacked = jnp.stack([d_queries, d_keys, d_values]).astype(jnp.bfloat16)
    grad_w_qkv = jnp.einsum("td,stc->sdc", normed_one, stacked, preferred_element_type=jnp.float32)
    d_normed_one = mp_allreduce(
        jnp.einsum("stc,sdc->td", stacked, w_qkv, preferred_element_type=jnp.float32).astype(
            jnp.bfloat16
        ),
        n_mp,
    )
    d_input_norm, grad_ln1_gain, grad_ln1_bias = norm_one_back(d_normed_one)
    grad_tokens = d_middle + d_input_norm
    def scatter(grad, dim):
        return lax.psum_scatter(
            grad.astype(jnp.bfloat16), "dp", scatter_dimension=dim, tiled=True
        ).astype(jnp.float32)

    summed_qkv = scatter(grad_w_qkv, 1)
    summed_out = scatter(grad_w_out, 1)
    summed_fc1 = scatter(grad_w_fc1, 0)
    summed_fc2 = scatter(grad_w_fc2, 1)
    early = dp_allreduce(
        jnp.concatenate([grad_ln2_gain, grad_ln2_bias, grad_b_out, grad_b_fc2, grad_b_fc1]), n_dp
    )
    late = dp_allreduce(jnp.concatenate([grad_ln1_gain, grad_ln1_bias, grad_b_qv.reshape(-1)]), n_dp)
    width = grad_ln1_gain.shape[0]
    pieces = [late[0:width], late[width : 2 * width]] + [
        early[k * width : (k + 1) * width] for k in range(4)
    ]
    summed_b_qv = late[2 * width :].reshape(grad_b_qv.shape)
    summed_b_fc1 = early[4 * width :]
    return (
        output,
        grad_tokens,
        summed_qkv,
        summed_b_qv,
        summed_out,
        pieces[4],
        summed_fc1,
        summed_b_fc1,
        summed_fc2,
        pieces[5],
        pieces[0],
        pieces[1],
        pieces[2],
        pieces[3],
    )


def solution(mesh):
    in_specs = (
        P("dp", None),
        P("dp", None),
        P("dp", None),
        P(None, None, "mp"),
        P(None, "mp"),
        P("mp", None),
        P(),
        P(None, "mp"),
        P("mp"),
        P("mp", None),
        P(),
        P(),
        P(),
        P(),
        P(),
    )
    out_specs = (
        P("dp", None),
        P("dp", None),
        P(None, "dp", "mp"),
        P(None, "mp"),
        P("mp", "dp"),
        P(),
        P("dp", "mp"),
        P("mp"),
        P("mp", "dp"),
        P(),
        P(),
        P(),
        P(),
        P(),
    )
    return jax.shard_map(
        partial(per_device, mesh.shape["mp"], mesh.shape["dp"]), mesh=mesh, in_specs=in_specs, out_specs=out_specs, check_vma=False
    )
```

profile of v0, /device:TPU:0, one launch (start us, length us, event | category | flops | bytes accessed | tf_op | source)
XLA Modules:
  0.0 644.1 jit_solution(14818714995603244315)
XLA Ops:
  11.3 3.0 convert_reduce_fusion.2
  18.1 3.4 fusion.9
  22.9 2.3 fusion.28
  25.1 2.3 fusion.27
  27.4 1.9 copy.80.k_ref
  33.0 44.7 %segment_flash_fwd.1 = (bf16[4,64,2048]{2,1,0:T(8,128)(2,1)S(1)}, f32[4,64,2048]{2,1,0:T(8,128)}, f32[4,1,2048]{2,1,0:T(1,128)S(1)}) custom-call(s32[8]{0:T(128)S(1)} %fusion.56.lo_ref, s32[8]{0:T(128)S(1)} %fusion.55.hi_ref, s32[2048,1]{1,0:T(8,128)S(1)} %copy-done.9, s32[1,2048]{1,0:T(1,128)S(1)} %bitcast.104, bf16[4,64,2048]{2,1,0:T(8,128)(2,1)S(1)} %bitcast.98, ...), custom_call_target="tpu_custom_call" | custom-call | flops 2576980480 | bytes 6324224 | tf_op jit(solution)/shard_map/segment_flash_fwd/pallas_call | solution.py:126
  82.1 4.1 collective-permute-done
  86.3 3.2 add_convert_fusion.9
  89.4 2.9 collective-permute-start.1
  92.4 45.9 %collective-permute-done.1 = bf16[1024,1024]{1,0:T(8,128)(2,1)S(1)} collective-permute-done((bf16[1024,1024]{1,0:T(8,128)(2,1)S(1)}, bf16[1024,1024]{1,0:T(8,128)(2,1)S(1)}, u32[]{:S(2)}, u32[]{:S(2)}) %collective-permute-start.1) | collective-permute-done | bytes 2097184 | tf_op jit(solution)/shard_map/ppermute | solution.py:203
  138.3 2.3 add_convert_fusion.8
  140.6 4.5 collective-permute-done.2
  145.1 2.5 broadcast_select_fusion.7
  149.2 3.6 multiply_reduce_fusion
  152.9 5.8 fusion.61
  158.7 24.8 %fusion.64 = (f32[1024]{0:T(1024)S(1)}, bf16[2048,1024]{1,0:T(8,128)(2,1)S(1)}, f32[2048,1024]{1,0:T(8,128)}) fusion(f32[2048,1024]{1,0:T(8,128)S(1)} %fusion.61, f32[1024]{0:T(1024)S(1)} %copy-done.49, bf16[2048,1024]{1,0:T(8,128)(2,1)S(1)} %copy-done.28, bf16[1024,1024]{1,0:T(8,128)(2,1)S(1)} %copy-done), kind=kOutput, calls=%fused_computation.154 | convolution fusion | flops 4450155520 | bytes 27271168 | tf_op jit(solution)/shard_map/td,fd->tf/dot_general | solution.py:283
  183.5 5.4 convolution_convert_fusion.1
  189.4 4.0 collective-permute-done.3
  193.4 2.3 add_convert_fusion.7
  195.7 1.7 collective-permute-start.4
  197.4 1.8 copy.83.q_ref
  199.2 2.7 copy.81
  202.0 41.7 %collective-permute-done.4 = bf16[1024,1024]{1,0:T(8,128)(2,1)} collective-permute-done((bf16[1024,1024]{1,0:T(8,128)(2,1)}, bf16[1024,1024]{1,0:T(8,128)(2,1)}, u32[]{:S(2)}, u32[]{:S(2)}) %collective-permute-start.4) | collective-permute-done | bytes 2097184 | tf_op jit(solution)/shard_map/ppermute | solution.py:203
  243.7 4.6 add_convert_fusion.6
  248.3 10.1 %multiply_convert_fusion = bf16[2048,1024]{1,0:T(8,128)(2,1)} fusion(f32[2048,1024]{1,0:T(8,128)} %get-tuple-element.109, f32[2048,1024]{1,0:T(8,128)} %copy-done.27, f32[1024]{0:T(1024)S(1)} %copy-done.49), kind=kLoop, calls=%fused_computation.37 | loop fusion | flops 8388608 | bytes 20975616 | tf_op jit(solution)/shard_map/convert_element_type | solution.py:278
  258.4 9.4 %convolution_convert_fusion.5 = bf16[1024,1024]{1,0:T(8,128)(2,1)} fusion(bf16[2048,1024]{1,0:T(8,128)(2,1)} %multiply_convert_fusion, bf16[2048,1024]{1,0:T(8,128)(2,1)} %param.18), kind=kOutput, calls=%fused_computation.99 | convolution fusion | flops 4296015872 | bytes 10485760 | tf_op jit(solution)/shard_map/tf,td->fd/dot_general | solution.py:282
  267.7 3.9 copy.98
  271.8 8.6 %convolution_convert_fusion.2 = bf16[2048,1024]{1,0:T(8,128)(2,1)} fusion(bf16[2048,1024]{1,0:T(8,128)(2,1)} %multiply_convert_fusion, bf16[1024,1024]{1,0:T(8,128)(2,1)S(1)} %copy-done), kind=kOutput, calls=%fused_computation.73 | convolution fusion | flops 4297064448 | bytes 10485760 | tf_op jit(solution)/shard_map/dot_general | solution.py:279
  280.3 2.6 broadcast_select_fusion.5
  285.1 6.4 fusion.10
  291.5 9.0 %fusion.15 = (f32[1024]{0:T(1024)S(1)}, f32[2048]{0:T(1024)S(1)}, f32[1024]{0:T(1024)S(1)}) fusion(f32[2048]{0:T(1024)S(1)} %fusion.54, bf16[1024,1024]{1,0:T(8,128)(2,1)S(1)} %get-tuple-element.120, bf16[1024,1024]{1,0:T(8,128)(2,1)S(1)} %get-tuple-element.119, f32[2048]{0:T(1024)S(1)} %broadcast_multiply_fusion, f32[1024]{0:T(1024)S(1)} %copy-done.39, ...), kind=kLoop, calls=%fused_computation.31 | loop fusion | flops 46133248 | bytes 12632064 | tf_op jit(solution)/shard_map/transpose(jvp())/reduce_sum | solution.py:180
  300.5 8.1 %convert_reduce_fusion.3 = (f32[1024]{0:T(1024)S(1)}, f32[2048,1024]{1,0:T(8,128)S(1)}) fusion(bf16[2048,1024]{1,0:T(8,128)(2,1)S(1)} %copy-done.29, f32[2048]{0:T(1024)S(1)} %negate_multiply_fusion.2, f32[2048]{0:T(1024)S(1)} %multiply_multiply_fusion.6, f32[2048]{0:T(1024)S(1)} %broadcast_multiply_fusion, f32[1024]{0:T(1024)S(1)} %copy-done.39, ...), kind=kLoop, calls=%fused_computation.18 | loop fusion | flops 44039168 | bytes 25210880 | tf_op jit(solution)/shard_map/reduce_sum | solution.py:281
  309.9 2.1 copy-done.16
  312.0 1.8 copy.85.do_ref
  317.5 47.9 %segment_flash_bwd.1 = (f32[4,64,2048]{2,1,0:T(8,128)}, f32[4,2048,64]{2,1,0:T(8,128)}, f32[4,2048,64]{2,1,0:T(8,128)}) custom-call(s32[8]{0:T(128)S(1)} %fusion.56.lo_ref, s32[8]{0:T(128)S(1)} %fusion.55.hi_ref, s32[2048,1]{1,0:T(8,128)S(1)} %copy-done.10, s32[1,2048]{1,0:T(1,128)S(1)} %bitcast.105, bf16[4,2048,64]{2,1,0:T(8,128)(2,1)} %copy.83.q_ref, ...), custom_call_target="tpu_custom_call" | custom-call | flops 5153960960 | bytes 15761408 | tf_op jit(solution)/shard_map/segment_flash_bwd/pallas_call | solution.py:153
  365.4 3.9 convert_bitcast_fusion
  369.3 1.9 copy.86
  372.5 1.7 bitcast_convert_fusion.2
  375.6 3.8 bitcast_convert_fusion.1
  379.3 1.9 copy.87
  383.0 6.0 bitcast_convert_fusion
  389.0 2.0 copy-done.32
  393.9 7.4 %fusion.35 = bf16[1024,1024]{1,0:T(8,128)(2,1)} fusion(bf16[2048,1024]{1,0:T(8,128)(2,1)S(1)} %copy-done.55, f32[1024]{0:T(1024)S(1)} %copy-done.53, f32[1024]{0:T(1024)S(1)} %copy-done.46, f32[2048]{0:T(1024)S(1)} %fusion.54, bf16[2048,1024]{1,0:T(8,128)(2,1)S(1)} %copy-done.14, f32[2048]{0:T(1024)S(1)} %broadcast_multiply_fusion, ...), kind=kOutput, calls=%fused_computation.98 | convolution fusion | flops 4321181696 | bytes 14708736 | tf_op jit(solution)/shard_map/td,tf->df/dot_general | solution.py:287
  401.4 1.9 constant_dynamic-slice_fusion.1
  404.2 2.9 add_convert_fusion.3
  407.1 1.8 collective-permute-start.10
  408.9 2.3 add_convert_fusion.5
  411.8 43.9 %collective-permute-done.10 = bf16[1024,1024]{1,0:T(8,128)(2,1)S(1)} collective-permute-done((bf16[1024,1024]{1,0:T(8,128)(2,1)S(1)}, bf16[1024,1024]{1,0:T(8,128)(2,1)S(1)}, u32[]{:S(2)}, u32[]{:S(2)}) %collective-permute-start.10) | collective-permute-done | bytes 2097184 | tf_op jit(solution)/shard_map/ppermute | solution.py:203
  455.7 2.3 add_convert_fusion.2
  460.5 2.7 bitcast_reduce_fusion
  463.9 7.5 %fusion.41 = bf16[3,1024,256]{1,2,0:T(8,128)(2,1)} fusion(bf16[2048,1024]{1,0:T(8,128)(2,1)} %copy-done.30, bf16[1,2048,256]{2,1,0:T(8,128)(2,1)} %copy.90, bf16[1,2048,256]{2,1,0:T(8,128)(2,1)S(1)} %copy-done.36, bf16[1,2048,256]{2,1,0:T(8,128)(2,1)} %copy.88), kind=kOutput, calls=%fused_computation.101 | convolution fusion | flops 3225157632 | bytes 8912896 | tf_op jit(solution)/shard_map/td,stc->sdc/dot_general | solution.py:314
  471.4 4.2 copy.94
  475.6 3.1 copy.100
  478.7 21.6 %collective-permute-done.7 = bf16[1024,1024]{1,0:T(8,128)(2,1)} collective-permute-done((bf16[1024,1024]{1,0:T(8,128)(2,1)}, bf16[1024,1024]{1,0:T(8,128)(2,1)}, u32[]{:S(2)}, u32[]{:S(2)}) %collective-permute-start.7) | collective-permute-done | bytes 2097184 | tf_op jit(solution)/shard_map/ppermute | solution.py:203
  500.3 3.2 add_convert_fusion.4
  503.6 2.6 broadcast_select_fusion.1
  506.9 3.2 fusion.12
  510.2 7.0 %fusion.16 = (f32[1024]{0:T(1024)S(1)}, f32[2048]{0:T(1024)S(1)}, f32[1024]{0:T(1024)S(1)}) fusion(bf16[2048,1024]{1,0:T(8,128)(2,1)S(1)} %copy-done.15, f32[2048]{0:T(1024)S(1)} %copy-done.41, f32[2048]{0:T(1024)S(1)} %copy-done.38, bf16[1024,1024]{1,0:T(8,128)(2,1)S(1)} %get-tuple-element.116, bf16[1024,1024]{1,0:T(8,128)(2,1)S(1)} %get-tuple-element.115, ...), kind=kLoop, calls=%fused_computation.32 | loop fusion | flops 33550336 | bytes 8433664 | tf_op jit(solution)/shard_map/transpose(jvp())/reduce_sum | solution.py:180
  517.2 27.1 %collective-permute-start.12 = (f32[2560]{0:T(1024)S(1)}, f32[2560]{0:T(1024)S(1)}, u32[]{:S(2)}, u32[]{:S(2)}) collective-permute-start(f32[2560]{0:T(1024)S(1)} %pad_maximum_fusion.6), channel_id=1, source_target_pairs={{0,4},{4,0},{8,12},{12,8},{16,20},{20,16},{24,28},{28,24},{1,5},{5... | collective-permute-start | bytes 30728 | tf_op jit(solution)/shard_map/ppermute | solution.py:217
  546.5 11.0 %fusion.66 = (f32[1024]{0:T(1024)S(1)}, f32[2048,1024]{1,0:T(8,128)}, bf16[2048,1024]{1,0:T(8,128)(2,1)}) fusion(f32[2048,1024]{1,0:T(8,128)S(1)} %bitcast.111, f32[2048]{0:T(1024)S(1)} %negate_multiply_fusion.1, f32[2048]{0:T(1024)S(1)} %multiply_multiply_fusion.5, f32[2048]{0:T(1024)S(1)} %copy-done.38, bf16[2048,1024]{1,0:T(8,128)(2,1)S(1)} %copy-done.15, ...), kind=kLoop, calls=%fused_computation.155 | loop fusion | flops 56622080 | bytes 37797888 | tf_op jit(solution)/shard_map/reduce_sum | solution.py:299
  562.9 2.6 collective-permute-start.14
  567.5 1.8 convert_element_type.214
  570.9 58.9 %reduce-scatter.13.cloned.1.call-done = bf16[128,768]{1,0:T(8,128)(2,1)} async-done(((bf16[1024,768]{1,0:T(8,128)(2,1)}), bf16[128,768]{1,0:T(8,128)(2,1)}) %reduce-scatter.13.cloned.1.call-update) | async-done | bytes 196624
  634.4 2.3 collective-permute-done.17
  (218 shorter events, 55.6 us)
Async XLA Ops:
  7.2 151.5 %copy-start = (bf16[1024,1024]{1,0:T(8,128)(2,1)S(1)}, bf16[1024,1024]{1,0:T(8,128)(2,1)}, u32[]{:S(2)}) copy-start(bf16[1024,1024]{1,0:T(8,128)(2,1)} %param.26) | copy-start | bytes 6291460
  7.2 558.3 %reduce-scatter.17.cloned.1.call-start = ((), (), s32[]{:S(2)}) async-start(), calls=%async_computation.7 | async-start | bytes 2359296
  11.3 3.5 copy-start.11
  11.3 6.8 %copy-start.44 = (f32[1024]{0:T(1024)S(1)}, f32[1024]{0:T(1024)}, u32[]{:S(2)}) copy-start(f32[1024]{0:T(1024)} %param.28) | copy-start | bytes 12292
  11.3 6.8 %copy-start.47 = (f32[1024]{0:T(1024)S(1)}, f32[1024]{0:T(1024)}, u32[]{:S(2)}) copy-start(f32[1024]{0:T(1024)} %param.29) | copy-start | bytes 12292
  14.7 3.4 copy-start.37
  18.1 3.4 copy-start.51
  21.5 3.6 copy-start.30
  22.8 4.6 copy-start.3
  32.9 44.7 %copy-start.34 = (bf16[256,1024]{1,0:T(8,128)(2,1)S(1)}, bf16[256,1024]{1,0:T(8,128)(2,1)}, u32[]{:S(2)}) copy-start(bf16[256,1024]{1,0:T(8,128)(2,1)} %param.22) | copy-start | bytes 1572868
  81.6 4.6 collective-permute-start
  89.4 48.9 %collective-permute-start.1 = (bf16[1024,1024]{1,0:T(8,128)(2,1)S(1)}, bf16[1024,1024]{1,0:T(8,128)(2,1)S(1)}, u32[]{:S(2)}, u32[]{:S(2)}) collective-permute-start(bf16[1024,1024]{1,0:T(8,128)(2,1)S(1)} %add_convert_fusion.9), channel_id=1, source_target_pairs={{0,2},{1,3},{2,0},{3,1},{4,6},{5,7},{6,4},{7,5},{8,10},{9,11},{10,... | collective-permute-start | bytes 6291464 | tf_op jit(solution)/shard_map/ppermute | solution.py:203
  140.6 4.5 collective-permute-start.2
  140.6 7.0 %copy-start.12 = (bf16[2048,1024]{1,0:T(8,128)(2,1)S(1)}, bf16[2048,1024]{1,0:T(8,128)(2,1)}, u32[]{:S(2)}) copy-start(bf16[2048,1024]{1,0:T(8,128)(2,1)} %param.17) | copy-start | bytes 12582916
  140.6 7.0 %copy-start.39 = (f32[1024]{0:T(1024)S(1)}, f32[1024]{0:T(1024)}, u32[]{:S(2)}) copy-start(f32[1024]{0:T(1024)} %param.23) | copy-start | bytes 12292
  147.6 5.2 copy-start.17
  147.6 5.2 copy-start.21
  149.2 3.6 copy-start.46
  149.2 3.6 copy-start.50
  149.2 3.6 copy-start.52
  152.9 5.8 copy-start.28
  152.9 5.8 copy-start.49
  158.7 24.8 %copy-start.27 = (f32[2048,1024]{1,0:T(8,128)}, f32[2048,1024]{1,0:T(8,128)S(1)}, u32[]{:S(2)}) copy-start(f32[2048,1024]{1,0:T(8,128)S(1)} %fusion.61) | copy-start | bytes 25165828
  183.5 5.4 copy-start.54
  189.2 8.3 %copy-start.6 = (bf16[2048,256]{0,1:T(8,128)(2,1)S(1)}, bf16[2048,256]{0,1:T(8,128)(2,1)}, u32[]{:S(2)}) copy-start(bf16[2048,256]{0,1:T(8,128)(2,1)} %fusion.27) | copy-start | bytes 3145732
  189.2 4.2 collective-permute-start.3
  195.7 48.0 %collective-permute-start.4 = (bf16[1024,1024]{1,0:T(8,128)(2,1)}, bf16[1024,1024]{1,0:T(8,128)(2,1)}, u32[]{:S(2)}, u32[]{:S(2)}) collective-permute-start(bf16[1024,1024]{1,0:T(8,128)(2,1)} %add_convert_fusion.7), channel_id=1, source_target_pairs={{0,2},{1,3},{2,0},{3,1},{4,6},{5,7},{6,4},{7,5},{8,10},{9,11},{10,... | collective-permute-start | bytes 6291464 | tf_op jit(solution)/shard_map/ppermute | solution.py:203
  248.3 32.1 %collective-permute-start.5 = (bf16[1024,1024]{1,0:T(8,128)(2,1)}, bf16[1024,1024]{1,0:T(8,128)(2,1)}, u32[]{:S(2)}, u32[]{:S(2)}) collective-permute-start(bf16[1024,1024]{1,0:T(8,128)(2,1)} %add_convert_fusion.6), channel_id=1, source_target_pairs={{0,1},{1,0},{2,3},{3,2},{4,5},{5,4},{6,7},{7,6},{8,9},{9,8},{10,11... | collective-permute-start | bytes 6291464 | tf_op jit(solution)/shard_map/ppermute | solution.py:205
  271.7 295.8 %reduce-scatter.11.cloned.1.call-start = ((), (), s32[]{:S(2)}) async-start(), calls=%async_computation.4 | async-start | bytes 2359296 | tf_op jit(solution)/shard_map/reduce_scatter | solution.py:324
  280.3 3.4 copy-start.13
  280.3 4.1 copy-start.18
  280.3 4.7 copy-start.22
  291.5 9.0 %copy-start.29 = (bf16[2048,1024]{1,0:T(8,128)(2,1)S(1)}, bf16[2048,1024]{1,0:T(8,128)(2,1)}, u32[]{:S(2)}) copy-start(bf16[2048,1024]{1,0:T(8,128)(2,1)} %param.18) | copy-start | bytes 12582916
  300.5 8.2 %copy-start.35 = (bf16[256,1024]{1,0:T(8,128)(2,1)S(1)}, bf16[256,1024]{1,0:T(8,128)(2,1)}, u32[]{:S(2)}) copy-start(bf16[256,1024]{1,0:T(8,128)(2,1)} %param.22) | copy-start | bytes 1572868
  308.6 3.4 copy-start.16
  382.9 10.1 %copy-start.19 = (bf16[1024,1024]{1,0:T(8,128)(2,1)S(1)}, bf16[1024,1024]{1,0:T(8,128)(2,1)}, u32[]{:S(2)}) copy-start(bf16[1024,1024]{1,0:T(8,128)(2,1)} %copy-done.17) | copy-start | bytes 6291460
  383.0 10.1 %copy-start.23 = (bf16[1024,1024]{1,0:T(8,128)(2,1)S(1)}, bf16[1024,1024]{1,0:T(8,128)(2,1)}, u32[]{:S(2)}) copy-start(bf16[1024,1024]{1,0:T(8,128)(2,1)} %copy-done.21) | copy-start | bytes 6291460
  383.0 10.1 %copy-start.53 = (f32[1024]{0:T(1024)S(1)}, f32[1024]{0:T(1024)}, u32[]{:S(2)}) copy-start(f32[1024]{0:T(1024)} %param.31) | copy-start | bytes 12292
  383.0 10.1 %copy-start.55 = (bf16[2048,1024]{1,0:T(8,128)(2,1)S(1)}, bf16[2048,1024]{1,0:T(8,128)(2,1)}, u32[]{:S(2)}) copy-start(bf16[2048,1024]{1,0:T(8,128)(2,1)} %copy-done.54) | copy-start | bytes 12582916
  392.6 11.3 %collective-permute-start.9 = (bf16[1024,1024]{1,0:T(8,128)(2,1)}, bf16[1024,1024]{1,0:T(8,128)(2,1)}, u32[]{:S(2)}, u32[]{:S(2)}) collective-permute-start(bf16[1024,1024]{1,0:T(8,128)(2,1)} %constant_dynamic-slice_fusion), channel_id=1, source_target_pairs={{0,1},{1,0},{2,3},{3,2},{4,5},{5,4},{6,7},{7,6},{8,9},{9,8},{10,11... | collective-permute-start | bytes 6291464 | tf_op jit(solution)/shard_map/ppermute | solution.py:201
  401.3 167.9 %reduce-scatter.15.cloned.1.call-start = ((), (), s32[]{:S(2)}) async-start(), calls=%async_computation.6 | async-start | bytes 589824
  403.3 5.6 copy-start.31
  403.3 5.6 collective-permute-start.6
  404.2 53.8 %slice-start = ((s8[8388608]{0:T(1024)(128)(4,1)}), s8[4194304]{0:T(1024)(128)(4,1)S(1)}, s32[]{:S(2)}) async-start(s8[8388608]{0:T(1024)(128)(4,1)} %bitcast.108), calls=%async_computation.8 | async-start | bytes 8388608
  407.1 50.9 %slice-start.1 = ((s8[8388608]{0:T(1024)(128)(4,1)}), s8[4194304]{0:T(1024)(128)(4,1)S(1)}, s32[]{:S(2)}) async-start(s8[8388608]{0:T(1024)(128)(4,1)} %bitcast.108), calls=%async_computation.9 | async-start | bytes 8388608
  407.1 48.6 %collective-permute-start.10 = (bf16[1024,1024]{1,0:T(8,128)(2,1)S(1)}, bf16[1024,1024]{1,0:T(8,128)(2,1)S(1)}, u32[]{:S(2)}, u32[]{:S(2)}) collective-permute-start(bf16[1024,1024]{1,0:T(8,128)(2,1)S(1)} %add_convert_fusion.3), channel_id=1, source_target_pairs={{0,2},{1,3},{2,0},{3,1},{4,6},{5,7},{6,4},{7,5},{8,10},{9,11},{10,... | collective-permute-start | bytes 6291464 | tf_op jit(solution)/shard_map/ppermute | solution.py:203
  411.3 46.7 %copy-start.2 = (bf16[4,64,2048]{2,1,0:T(8,128)(2,1)S(1)}, bf16[4,64,2048]{2,1,0:T(8,128)(2,1)}, u32[]{:S(2)}) copy-start(bf16[4,64,2048]{2,1,0:T(8,128)(2,1)} %copy-done.1) | copy-start | bytes 3145732
  411.3 89.0 %collective-permute-start.7 = (bf16[1024,1024]{1,0:T(8,128)(2,1)}, bf16[1024,1024]{1,0:T(8,128)(2,1)}, u32[]{:S(2)}, u32[]{:S(2)}) collective-permute-start(bf16[1024,1024]{1,0:T(8,128)(2,1)} %add_convert_fusion.5), channel_id=1, source_target_pairs={{0,2},{1,3},{2,0},{3,1},{4,6},{5,7},{6,4},{7,5},{8,10},{9,11},{10,... | collective-permute-start | bytes 6291464 | tf_op jit(solution)/shard_map/ppermute | solution.py:203
  458.0 45.6 %collective-permute-start.11 = (bf16[1024,1024]{1,0:T(8,128)(2,1)}, bf16[1024,1024]{1,0:T(8,128)(2,1)}, u32[]{:S(2)}, u32[]{:S(2)}) collective-permute-start(bf16[1024,1024]{1,0:T(8,128)(2,1)} %add_convert_fusion.2), channel_id=1, source_target_pairs={{0,1},{1,0},{2,3},{3,2},{4,5},{5,4},{6,7},{7,6},{8,9},{9,8},{10,11... | collective-permute-start | bytes 6291464 | tf_op jit(solution)/shard_map/ppermute | solution.py:205
  460.3 3.6 copy-start.36
  460.3 169.6 %reduce-scatter.13.cloned.1.call-start = ((), (), s32[]{:S(2)}) async-start(), calls=%async_computation.5 | async-start | bytes 1769472
  503.4 3.5 copy-start.15
  503.4 3.5 copy-start.38
  503.5 3.5 copy-start.45
  503.5 40.8 %collective-permute-start.8 = (bf16[1024,1024]{1,0:T(8,128)(2,1)S(1)}, bf16[1024,1024]{1,0:T(8,128)(2,1)S(1)}, u32[]{:S(2)}, u32[]{:S(2)}) collective-permute-start(bf16[1024,1024]{1,0:T(8,128)(2,1)S(1)} %add_convert_fusion.4), channel_id=1, source_target_pairs={{0,1},{1,0},{2,3},{3,2},{4,5},{5,4},{6,7},{7,6},{8,9},{9,8},{10,11... | collective-permute-start | bytes 6291464 | tf_op jit(solution)/shard_map/ppermute | solution.py:205
  506.9 3.2 copy-start.41
  510.2 34.4 %slice-start.2 = ((s8[8388608]{0:T(1024)(128)(4,1)}), s8[4194304]{0:T(1024)(128)(4,1)S(1)}, s32[]{:S(2)}) async-start(s8[8388608]{0:T(1024)(128)(4,1)} %bitcast.110), calls=%async_computation.10 | async-start | bytes 8388608
  517.1 27.4 %slice-start.3 = ((s8[8388608]{0:T(1024)(128)(4,1)}), s8[4194304]{0:T(1024)(128)(4,1)S(1)}, s32[]{:S(2)}) async-start(s8[8388608]{0:T(1024)(128)(4,1)} %bitcast.110), calls=%async_computation.11 | async-start | bytes 8388608
  517.2 41.6 %collective-permute-start.12 = (f32[2560]{0:T(1024)S(1)}, f32[2560]{0:T(1024)S(1)}, u32[]{:S(2)}, u32[]{:S(2)}) collective-permute-start(f32[2560]{0:T(1024)S(1)} %pad_maximum_fusion.6), channel_id=1, source_target_pairs={{0,4},{4,0},{8,12},{12,8},{16,20},{20,16},{24,28},{28,24},{1,5},{5... | collective-permute-start | bytes 30728 | tf_op jit(solution)/shard_map/ppermute | solution.py:217
  557.5 3.8 collective-permute-start.15
  558.8 4.2 collective-permute-start.13
  561.4 70.7 %collective-permute-start.16 = (f32[5120]{0:T(1024)S(1)}, f32[5120]{0:T(1024)S(1)}, u32[]{:S(2)}, u32[]{:S(2)}) collective-permute-start(f32[5120]{0:T(1024)S(1)} %add.206), channel_id=1, source_target_pairs={{0,8},{4,12},{8,0},{12,4},{16,24},{20,28},{24,16},{28,20},{1,9},{5... | collective-permute-start | bytes 61448 | tf_op jit(solution)/shard_map/ppermute | solution.py:217
  562.9 69.1 %collective-permute-start.14 = (f32[2560]{0:T(1024)S(1)}, f32[2560]{0:T(1024)S(1)}, u32[]{:S(2)}, u32[]{:S(2)}) collective-permute-start(f32[2560]{0:T(1024)S(1)} %add.204), channel_id=1, source_target_pairs={{0,16},{4,20},{8,24},{12,28},{16,0},{20,4},{24,8},{28,12},{1,17},{... | collective-permute-start | bytes 30728 | tf_op jit(solution)/shard_map/ppermute | solution.py:217
  632.0 4.7 collective-permute-start.17
  (18 other events, 33.3 us)
Sparse Core Ops, SparseCore 0:
  271.8 82.5 reduce-scatter.16
  401.5 95.4 reduce-scatter.10
  500.3 61.7 reduce-scatter.14
  565.3 64.4 reduce-scatter.12
where the time goes:
time: 656 us; the launch traced here: 644 us
  waiting for transfers between devices  228 us (35%)
  other arithmetic  116 us (18%)
  Pallas kernels  92.6 us (14%)
  matrix products  84.5 us (13%)
  local copies, waits for them, and re-layouts  63.5 us (10%)
  starting transfers between devices  44.5 us (7%)
  between operations  14.9 us (2%)
    ppermute x4, waiting for transfers between devices, mp_allreduce(): got_far = lax.ppermute(first, 'mp', [(k, k ^ 2) for k in range(4)])  153 us
    unnamed x7, waiting for transfers between devices  59 us
    pallas_call x1, Pallas kernels, flash_backward(): pl.pallas_call(_bwd_kernel, out_shape=(jax.ShapeDtypeStruct((heads, HEAD,...  47.9 us
    pallas_call x1, Pallas kernels, flash_forward(): pl.pallas_call(_fwd_kernel, out_shape=(jax.ShapeDtypeStruct((heads, HEAD,...  44.7 us
    unnamed x134, local copies, waits for them, and re-layouts  36.3 us
    ppermute x6, starting transfers between devices, dp_allreduce(): lax.ppermute(total, 'dp', [(k, k ^ step) for k in range(n_dp)])  35.4 us
    reduce_sum x4, other arithmetic, normalize(): return centered * lax.rsqrt(spread + 1e-06) * gain + shift  25.5 us
    dot_general x1, matrix products, per_device(): jnp.einsum('td,fd->tf', cotangent, w_fc2, preferred_element_type=jnp.floa...  24.8 us
  transfers between devices with their start and end apart: 22, of which 10 were waited for; matrix products, arithmetic and copies ran while one was open for 25% of the time, Pallas kernels for 7%

commit v1 on v0

--- a/solution.py
+++ b/solution.py
@@ -1,5 +1,3 @@
-from functools import partial
-
 import jax
 import jax.numpy as jnp
 from jax import lax
@@ -7,8 +5,8 @@
 from jax.experimental.pallas import tpu as pltpu
 from jax.sharding import PartitionSpec as P
 
+
 HEAD = 64
-QBLOCK = 512
 TQ = 256
 TK = 256
 NEG = -1e30
@@ -172,6 +170,7 @@
         name="segment_flash_bwd",
     )(lo, hi, segments.reshape(rows, 1), segments.reshape(1, rows),
       q, q.transpose(0, 2, 1), k, k.transpose(0, 2, 1), v, do, do.transpose(0, 2, 1), o32t, lse)
+
 
 def normalize(values, gain, shift):
     center = jnp.mean(values, axis=-1, keepdims=True)
@@ -220,7 +219,6 @@
 
 
 def per_device(n_mp, n_dp,
-
     tokens,
     cotangent,
     item_lengths,
@@ -253,6 +251,7 @@
     value_rows = (
         jnp.dot(normed_one, w_qkv[2], preferred_element_type=jnp.float32) + b_qv[1]
     ).astype(jnp.bfloat16)
+
     def to_heads(values):
         return values.reshape(row_count, heads_here, HEAD).transpose(1, 0, 2)
 
@@ -268,7 +267,7 @@
     )
     attended = out_heads.transpose(2, 0, 1).reshape(row_count, local_cols)
     attention_sum = mp_allreduce(
-        jnp.dot(attended, w_out, preferred_element_type=jnp.float32).astype(jnp.bfloat16), n_mp
+        jnp.dot(attended, w_out, preferred_element_type=jnp.float32).astype(jnp.bfloat16), n_mp,
     )
     middle = inputs + attention_sum + b_out
     norm_two, norm_two_back = jax.vjp(normalize, middle, ln2_gain, ln2_bias)
@@ -302,8 +301,9 @@
     d_attended = jnp.einsum(
         "td,cd->tc", d_middle_low, w_out, preferred_element_type=jnp.float32
     ).astype(jnp.bfloat16)
+    d_att_heads = to_heads(d_attended)
     d_q_heads, d_k_heads, d_v_heads = flash_backward(
-        query_heads, key_heads, value_heads, to_heads(d_attended), out_f32, log_norms,
+        query_heads, key_heads, value_heads, d_att_heads, out_f32, log_norms,
         segments, lo_blocks, hi_blocks,
     )
     d_queries = d_q_heads.transpose(2, 0, 1).reshape(row_count, local_cols)
@@ -320,6 +320,7 @@
     )
     d_input_norm, grad_ln1_gain, grad_ln1_bias = norm_one_back(d_normed_one)
     grad_tokens = d_middle + d_input_norm
+
     def scatter(grad, dim):
         return lax.psum_scatter(
             grad.astype(jnp.bfloat16), "dp", scatter_dimension=dim, tiled=True
@@ -391,6 +392,10 @@
         P(),
         P(),
     )
+
+    def body(*args):
+        return per_device(mesh.shape["mp"], mesh.shape["dp"], *args)
+
     return jax.shard_map(
-        partial(per_device, mesh.shape["mp"], mesh.shape["dp"]), mesh=mesh, in_specs=in_specs, out_specs=out_specs, check_vma=False
-    )
+        body, mesh=mesh, in_specs=in_specs, out_specs=out_specs, check_vma=False
+    )

time: 656 us -> 652 us (level)
  transfers between devices with their start and end apart: 22 -> 22, of which waited for: 10 -> 10; matrix products, arithmetic and copies ran while one was open for 25% -> 25% of each run, Pallas kernels for 7% -> 8%
where the time goes in v1:
time: 652 us; the launch traced here: 643 us
  waiting for transfers between devices  227 us (35%)
  other arithmetic  116 us (18%)
  Pallas kernels  98.9 us (15%)
  matrix products  84.5 us (13%)
  local copies, waits for them, and re-layouts  63.1 us (10%)
  starting transfers between devices  38.2 us (6%)
  between operations  15.1 us (2%)
    ppermute x4, waiting for transfers between devices, mp_allreduce(): got_far = lax.ppermute(first, 'mp', [(k, k ^ 2) for k in range(4)])  153 us
    unnamed x7, waiting for transfers between devices  58.3 us
    pallas_call x1, Pallas kernels, flash_backward(): pl.pallas_call(_bwd_kernel, out_shape=(jax.ShapeDtypeStruct((heads, HEAD,...  51 us
    pallas_call x1, Pallas kernels, flash_forward(): pl.pallas_call(_fwd_kernel, out_shape=(jax.ShapeDtypeStruct((heads, HEAD,...  47.9 us
    unnamed x134, local copies, waits for them, and re-layouts  36.1 us
    ppermute x6, starting transfers between devices, dp_allreduce(): lax.ppermute(total, 'dp', [(k, k ^ step) for k in range(n_dp)])  28.9 us
    reduce_sum x4, other arithmetic, normalize(): return centered * lax.rsqrt(spread + 1e-06) * gain + shift  25.5 us
    dot_general x1, matrix products, per_device(): jnp.einsum('td,fd->tf', cotangent, w_fc2, preferred_element_type=jnp.floa...  24.8 us
  transfers between devices with their start and end apart: 22, of which 10 were waited for; matrix products, arithmetic and copies ran while one was open for 25% of the time, Pallas kernels for 8%

profile of v1, /device:TPU:0, one launch (start us, length us, event | category | flops | bytes accessed | tf_op | source)
XLA Modules:
  0.0 643.0 jit_solution(14818714995603244315)
XLA Ops:
  11.3 3.0 convert_reduce_fusion.2
  18.1 3.4 fusion.9
  22.9 2.3 fusion.28
  25.1 2.3 fusion.27
  27.4 1.9 copy.80.k_ref
  33.0 47.9 %segment_flash_fwd.1 = (bf16[4,64,2048]{2,1,0:T(8,128)(2,1)S(1)}, f32[4,64,2048]{2,1,0:T(8,128)}, f32[4,1,2048]{2,1,0:T(1,128)S(1)}) custom-call(s32[8]{0:T(128)S(1)} %fusion.56.lo_ref, s32[8]{0:T(128)S(1)} %fusion.55.hi_ref, s32[2048,1]{1,0:T(8,128)S(1)} %copy-done.9, s32[1,2048]{1,0:T(1,128)S(1)} %bitcast.104, bf16[4,64,2048]{2,1,0:T(8,128)(2,1)S(1)} %bitcast.98, ...), custom_call_target="tpu_custom_call" | custom-call | flops 2576980480 | bytes 6324224 | tf_op jit(solution)/shard_map/segment_flash_fwd/pallas_call | solution.py:124
  85.3 4.1 collective-permute-done
  89.4 3.2 add_convert_fusion.9
  92.6 2.9 collective-permute-start.1
  95.6 45.9 %collective-permute-done.1 = bf16[1024,1024]{1,0:T(8,128)(2,1)S(1)} collective-permute-done((bf16[1024,1024]{1,0:T(8,128)(2,1)S(1)}, bf16[1024,1024]{1,0:T(8,128)(2,1)S(1)}, u32[]{:S(2)}, u32[]{:S(2)}) %collective-permute-start.1) | collective-permute-done | bytes 2097184 | tf_op jit(solution)/shard_map/ppermute | solution.py:202
  141.5 2.3 add_convert_fusion.8
  143.8 4.5 collective-permute-done.2
  148.3 2.5 broadcast_select_fusion.7
  152.4 3.5 multiply_reduce_fusion
  156.0 5.8 fusion.61
  161.9 24.8 %fusion.64 = (f32[1024]{0:T(1024)S(1)}, bf16[2048,1024]{1,0:T(8,128)(2,1)S(1)}, f32[2048,1024]{1,0:T(8,128)}) fusion(f32[2048,1024]{1,0:T(8,128)S(1)} %fusion.61, f32[1024]{0:T(1024)S(1)} %copy-done.49, bf16[2048,1024]{1,0:T(8,128)(2,1)S(1)} %copy-done.28, bf16[1024,1024]{1,0:T(8,128)(2,1)S(1)} %copy-done), kind=kOutput, calls=%fused_computation.154 | convolution fusion | flops 4450155520 | bytes 27271168 | tf_op jit(solution)/shard_map/td,fd->tf/dot_general | solution.py:282
  186.7 5.2 convolution_convert_fusion.1
  192.3 4.0 collective-permute-done.3
  196.3 2.3 add_convert_fusion.7
  198.6 1.7 collective-permute-start.4
  200.4 1.8 copy.83.q_ref
  202.2 2.7 copy.81
  204.9 41.7 %collective-permute-done.4 = bf16[1024,1024]{1,0:T(8,128)(2,1)} collective-permute-done((bf16[1024,1024]{1,0:T(8,128)(2,1)}, bf16[1024,1024]{1,0:T(8,128)(2,1)}, u32[]{:S(2)}, u32[]{:S(2)}) %collective-permute-start.4) | collective-permute-done | bytes 2097184 | tf_op jit(solution)/shard_map/ppermute | solution.py:202
  246.6 4.6 add_convert_fusion.6
  251.2 10.1 %multiply_convert_fusion = bf16[2048,1024]{1,0:T(8,128)(2,1)} fusion(f32[2048,1024]{1,0:T(8,128)} %get-tuple-element.109, f32[2048,1024]{1,0:T(8,128)} %copy-done.27, f32[1024]{0:T(1024)S(1)} %copy-done.49), kind=kLoop, calls=%fused_computation.37 | loop fusion | flops 8388608 | bytes 20975616 | tf_op jit(solution)/shard_map/convert_element_type | solution.py:277
  261.3 9.4 %convolution_convert_fusion.5 = bf16[1024,1024]{1,0:T(8,128)(2,1)} fusion(bf16[2048,1024]{1,0:T(8,128)(2,1)} %multiply_convert_fusion, bf16[2048,1024]{1,0:T(8,128)(2,1)} %param.18), kind=kOutput, calls=%fused_computation.99 | convolution fusion | flops 4296015872 | bytes 10485760 | tf_op jit(solution)/shard_map/tf,td->fd/dot_general | solution.py:281
  270.7 3.9 copy.98
  274.7 8.8 %convolution_convert_fusion.2 = bf16[2048,1024]{1,0:T(8,128)(2,1)} fusion(bf16[2048,1024]{1,0:T(8,128)(2,1)} %multiply_convert_fusion, bf16[1024,1024]{1,0:T(8,128)(2,1)S(1)} %copy-done), kind=kOutput, calls=%fused_computation.73 | convolution fusion | flops 4297064448 | bytes 10485760 | tf_op jit(solution)/shard_map/dot_general | solution.py:278
  283.5 2.6 broadcast_select_fusion.5
  288.2 6.4 fusion.10
  294.6 9.0 %fusion.15 = (f32[1024]{0:T(1024)S(1)}, f32[2048]{0:T(1024)S(1)}, f32[1024]{0:T(1024)S(1)}) fusion(f32[2048]{0:T(1024)S(1)} %fusion.54, bf16[1024,1024]{1,0:T(8,128)(2,1)S(1)} %get-tuple-element.120, bf16[1024,1024]{1,0:T(8,128)(2,1)S(1)} %get-tuple-element.119, f32[2048]{0:T(1024)S(1)} %broadcast_multiply_fusion, f32[1024]{0:T(1024)S(1)} %copy-done.39, ...), kind=kLoop, calls=%fused_computation.31 | loop fusion | flops 46133248 | bytes 12632064 | tf_op jit(solution)/shard_map/transpose(jvp())/reduce_sum | solution.py:179
  303.6 8.1 %convert_reduce_fusion.3 = (f32[1024]{0:T(1024)S(1)}, f32[2048,1024]{1,0:T(8,128)S(1)}) fusion(bf16[2048,1024]{1,0:T(8,128)(2,1)S(1)} %copy-done.29, f32[2048]{0:T(1024)S(1)} %negate_multiply_fusion.2, f32[2048]{0:T(1024)S(1)} %multiply_multiply_fusion.6, f32[2048]{0:T(1024)S(1)} %broadcast_multiply_fusion, f32[1024]{0:T(1024)S(1)} %copy-done.39, ...), kind=kLoop, calls=%fused_computation.18 | loop fusion | flops 44039168 | bytes 25210880 | tf_op jit(solution)/shard_map/reduce_sum | solution.py:280
  313.1 2.1 copy-done.16
  315.2 1.8 copy.85.do_ref
  320.7 51.0 %segment_flash_bwd.1 = (f32[4,64,2048]{2,1,0:T(8,128)}, f32[4,2048,64]{2,1,0:T(8,128)}, f32[4,2048,64]{2,1,0:T(8,128)}) custom-call(s32[8]{0:T(128)S(1)} %fusion.56.lo_ref, s32[8]{0:T(128)S(1)} %fusion.55.hi_ref, s32[2048,1]{1,0:T(8,128)S(1)} %copy-done.10, s32[1,2048]{1,0:T(1,128)S(1)} %bitcast.105, bf16[4,2048,64]{2,1,0:T(8,128)(2,1)} %copy.83.q_ref, ...), custom_call_target="tpu_custom_call" | custom-call | flops 5153960960 | bytes 15761408 | tf_op jit(solution)/shard_map/segment_flash_bwd/pallas_call | solution.py:151
  371.7 3.9 convert_bitcast_fusion
  375.6 1.9 copy.86
  381.8 3.8 bitcast_convert_fusion.1
  385.6 1.9 copy.87
  389.0 6.0 bitcast_convert_fusion
  395.0 2.0 copy-done.32
  400.0 7.4 %fusion.35 = bf16[1024,1024]{1,0:T(8,128)(2,1)} fusion(bf16[2048,1024]{1,0:T(8,128)(2,1)S(1)} %copy-done.55, f32[1024]{0:T(1024)S(1)} %copy-done.53, f32[1024]{0:T(1024)S(1)} %copy-done.46, f32[2048]{0:T(1024)S(1)} %fusion.54, bf16[2048,1024]{1,0:T(8,128)(2,1)S(1)} %copy-done.14, f32[2048]{0:T(1024)S(1)} %broadcast_multiply_fusion, ...), kind=kOutput, calls=%fused_computation.98 | convolution fusion | flops 4321181696 | bytes 14708736 | tf_op jit(solution)/shard_map/td,tf->df/dot_general | solution.py:286
  407.5 1.9 constant_dynamic-slice_fusion.1
  410.3 2.9 add_convert_fusion.3
  413.2 1.8 collective-permute-start.10
  415.0 2.3 add_convert_fusion.5
  417.9 43.8 %collective-permute-done.10 = bf16[1024,1024]{1,0:T(8,128)(2,1)S(1)} collective-permute-done((bf16[1024,1024]{1,0:T(8,128)(2,1)S(1)}, bf16[1024,1024]{1,0:T(8,128)(2,1)S(1)}, u32[]{:S(2)}, u32[]{:S(2)}) %collective-permute-start.10) | collective-permute-done | bytes 2097184 | tf_op jit(solution)/shard_map/ppermute | solution.py:202
  461.7 2.3 add_convert_fusion.2
  466.6 2.7 bitcast_reduce_fusion
  469.9 7.5 %fusion.41 = bf16[3,1024,256]{1,2,0:T(8,128)(2,1)} fusion(bf16[2048,1024]{1,0:T(8,128)(2,1)} %copy-done.30, bf16[1,2048,256]{2,1,0:T(8,128)(2,1)} %copy.90, bf16[1,2048,256]{2,1,0:T(8,128)(2,1)S(1)} %copy-done.36, bf16[1,2048,256]{2,1,0:T(8,128)(2,1)} %copy.88), kind=kOutput, calls=%fused_computation.101 | convolution fusion | flops 3225157632 | bytes 8912896 | tf_op jit(solution)/shard_map/td,stc->sdc/dot_general | solution.py:314
  477.4 4.2 copy.94
  481.6 3.1 copy.100
  484.7 21.6 %collective-permute-done.7 = bf16[1024,1024]{1,0:T(8,128)(2,1)} collective-permute-done((bf16[1024,1024]{1,0:T(8,128)(2,1)}, bf16[1024,1024]{1,0:T(8,128)(2,1)}, u32[]{:S(2)}, u32[]{:S(2)}) %collective-permute-start.7) | collective-permute-done | bytes 2097184 | tf_op jit(solution)/shard_map/ppermute | solution.py:202
  506.4 3.2 add_convert_fusion.4
  509.7 2.7 broadcast_select_fusion.1
  513.0 3.2 fusion.12
  516.3 7.0 %fusion.16 = (f32[1024]{0:T(1024)S(1)}, f32[2048]{0:T(1024)S(1)}, f32[1024]{0:T(1024)S(1)}) fusion(bf16[2048,1024]{1,0:T(8,128)(2,1)S(1)} %copy-done.15, f32[2048]{0:T(1024)S(1)} %copy-done.41, f32[2048]{0:T(1024)S(1)} %copy-done.38, bf16[1024,1024]{1,0:T(8,128)(2,1)S(1)} %get-tuple-element.116, bf16[1024,1024]{1,0:T(8,128)(2,1)S(1)} %get-tuple-element.115, ...), kind=kLoop, calls=%fused_computation.32 | loop fusion | flops 33550336 | bytes 8433664 | tf_op jit(solution)/shard_map/transpose(jvp())/reduce_sum | solution.py:179
  523.3 20.7 %collective-permute-start.12 = (f32[2560]{0:T(1024)S(1)}, f32[2560]{0:T(1024)S(1)}, u32[]{:S(2)}, u32[]{:S(2)}) collective-permute-start(f32[2560]{0:T(1024)S(1)} %pad_maximum_fusion.6), channel_id=1, source_target_pairs={{0,4},{4,0},{8,12},{12,8},{16,20},{20,16},{24,28},{28,24},{1,5},{5... | collective-permute-start | bytes 30728 | tf_op jit(solution)/shard_map/ppermute | solution.py:216
  546.2 11.0 %fusion.66 = (f32[1024]{0:T(1024)S(1)}, f32[2048,1024]{1,0:T(8,128)}, bf16[2048,1024]{1,0:T(8,128)(2,1)}) fusion(f32[2048,1024]{1,0:T(8,128)S(1)} %bitcast.111, f32[2048]{0:T(1024)S(1)} %negate_multiply_fusion.1, f32[2048]{0:T(1024)S(1)} %multiply_multiply_fusion.5, f32[2048]{0:T(1024)S(1)} %copy-done.38, bf16[2048,1024]{1,0:T(8,128)(2,1)S(1)} %copy-done.15, ...), kind=kLoop, calls=%fused_computation.155 | loop fusion | flops 56622080 | bytes 37797888 | tf_op jit(solution)/shard_map/reduce_sum | solution.py:298
  558.5 1.8 collective-permute-start.13
  562.8 2.2 collective-permute-start.14
  566.9 1.8 convert_element_type.214
  570.3 58.2 %reduce-scatter.13.cloned.1.call-done = bf16[128,768]{1,0:T(8,128)(2,1)} async-done(((bf16[1024,768]{1,0:T(8,128)(2,1)}), bf16[128,768]{1,0:T(8,128)(2,1)}) %reduce-scatter.13.cloned.1.call-update) | async-done | bytes 196624
  633.2 2.3 collective-permute-done.17
  (218 shorter events, 55.5 us)
Async XLA Ops:
  7.2 154.7 %copy-start = (bf16[1024,1024]{1,0:T(8,128)(2,1)S(1)}, bf16[1024,1024]{1,0:T(8,128)(2,1)}, u32[]{:S(2)}) copy-start(bf16[1024,1024]{1,0:T(8,128)(2,1)} %param.26) | copy-start | bytes 6291460
  7.2 557.8 %reduce-scatter.17.cloned.1.call-start = ((), (), s32[]{:S(2)}) async-start(), calls=%async_computation.7 | async-start | bytes 2359296
  11.3 3.5 copy-start.11
  11.3 6.8 %copy-start.44 = (f32[1024]{0:T(1024)S(1)}, f32[1024]{0:T(1024)}, u32[]{:S(2)}) copy-start(f32[1024]{0:T(1024)} %param.28) | copy-start | bytes 12292
  11.3 6.8 %copy-start.47 = (f32[1024]{0:T(1024)S(1)}, f32[1024]{0:T(1024)}, u32[]{:S(2)}) copy-start(f32[1024]{0:T(1024)} %param.29) | copy-start | bytes 12292
  14.7 3.4 copy-start.37
  18.1 3.4 copy-start.51
  21.5 3.6 copy-start.30
  22.9 4.6 copy-start.3
  33.0 47.9 %copy-start.34 = (bf16[256,1024]{1,0:T(8,128)(2,1)S(1)}, bf16[256,1024]{1,0:T(8,128)(2,1)}, u32[]{:S(2)}) copy-start(bf16[256,1024]{1,0:T(8,128)(2,1)} %param.22) | copy-start | bytes 1572868
  84.8 4.6 collective-permute-start
  92.6 48.9 %collective-permute-start.1 = (bf16[1024,1024]{1,0:T(8,128)(2,1)S(1)}, bf16[1024,1024]{1,0:T(8,128)(2,1)S(1)}, u32[]{:S(2)}, u32[]{:S(2)}) collective-permute-start(bf16[1024,1024]{1,0:T(8,128)(2,1)S(1)} %add_convert_fusion.9), channel_id=1, source_target_pairs={{0,2},{1,3},{2,0},{3,1},{4,6},{5,7},{6,4},{7,5},{8,10},{9,11},{10,... | collective-permute-start | bytes 6291464 | tf_op jit(solution)/shard_map/ppermute | solution.py:202
  143.8 4.5 collective-permute-start.2
  143.8 7.0 %copy-start.12 = (bf16[2048,1024]{1,0:T(8,128)(2,1)S(1)}, bf16[2048,1024]{1,0:T(8,128)(2,1)}, u32[]{:S(2)}) copy-start(bf16[2048,1024]{1,0:T(8,128)(2,1)} %param.17) | copy-start | bytes 12582916
  143.8 7.0 %copy-start.39 = (f32[1024]{0:T(1024)S(1)}, f32[1024]{0:T(1024)}, u32[]{:S(2)}) copy-start(f32[1024]{0:T(1024)} %param.23) | copy-start | bytes 12292
  150.8 5.2 copy-start.17
  150.8 5.2 copy-start.21
  152.4 3.6 copy-start.46
  152.4 3.6 copy-start.50
  152.4 3.6 copy-start.52
  156.0 5.9 copy-start.28
  156.0 5.9 copy-start.49
  161.9 24.8 %copy-start.27 = (f32[2048,1024]{1,0:T(8,128)}, f32[2048,1024]{1,0:T(8,128)S(1)}, u32[]{:S(2)}) copy-start(f32[2048,1024]{1,0:T(8,128)S(1)} %fusion.61) | copy-start | bytes 25165828
  186.7 5.3 copy-start.54
  192.1 8.3 %copy-start.6 = (bf16[2048,256]{0,1:T(8,128)(2,1)S(1)}, bf16[2048,256]{0,1:T(8,128)(2,1)}, u32[]{:S(2)}) copy-start(bf16[2048,256]{0,1:T(8,128)(2,1)} %fusion.27) | copy-start | bytes 3145732
  192.1 4.2 collective-permute-start.3
  198.6 48.0 %collective-permute-start.4 = (bf16[1024,1024]{1,0:T(8,128)(2,1)}, bf16[1024,1024]{1,0:T(8,128)(2,1)}, u32[]{:S(2)}, u32[]{:S(2)}) collective-permute-start(bf16[1024,1024]{1,0:T(8,128)(2,1)} %add_convert_fusion.7), channel_id=1, source_target_pairs={{0,2},{1,3},{2,0},{3,1},{4,6},{5,7},{6,4},{7,5},{8,10},{9,11},{10,... | collective-permute-start | bytes 6291464 | tf_op jit(solution)/shard_map/ppermute | solution.py:202
  251.2 32.3 %collective-permute-start.5 = (bf16[1024,1024]{1,0:T(8,128)(2,1)}, bf16[1024,1024]{1,0:T(8,128)(2,1)}, u32[]{:S(2)}, u32[]{:S(2)}) collective-permute-start(bf16[1024,1024]{1,0:T(8,128)(2,1)} %add_convert_fusion.6), channel_id=1, source_target_pairs={{0,1},{1,0},{2,3},{3,2},{4,5},{5,4},{6,7},{7,6},{8,9},{9,8},{10,11... | collective-permute-start | bytes 6291464 | tf_op jit(solution)/shard_map/ppermute | solution.py:204
  274.6 292.3 %reduce-scatter.11.cloned.1.call-start = ((), (), s32[]{:S(2)}) async-start(), calls=%async_computation.4 | async-start | bytes 2359296 | tf_op jit(solution)/shard_map/reduce_scatter | solution.py:325
  283.5 3.4 copy-start.13
  283.5 4.1 copy-start.18
  283.5 4.7 copy-start.22
  294.6 9.0 %copy-start.29 = (bf16[2048,1024]{1,0:T(8,128)(2,1)S(1)}, bf16[2048,1024]{1,0:T(8,128)(2,1)}, u32[]{:S(2)}) copy-start(bf16[2048,1024]{1,0:T(8,128)(2,1)} %param.18) | copy-start | bytes 12582916
  303.6 8.2 %copy-start.35 = (bf16[256,1024]{1,0:T(8,128)(2,1)S(1)}, bf16[256,1024]{1,0:T(8,128)(2,1)}, u32[]{:S(2)}) copy-start(bf16[256,1024]{1,0:T(8,128)(2,1)} %param.22) | copy-start | bytes 1572868
  311.8 3.4 copy-start.16
  389.0 10.2 %copy-start.19 = (bf16[1024,1024]{1,0:T(8,128)(2,1)S(1)}, bf16[1024,1024]{1,0:T(8,128)(2,1)}, u32[]{:S(2)}) copy-start(bf16[1024,1024]{1,0:T(8,128)(2,1)} %copy-done.17) | copy-start | bytes 6291460
  389.0 10.2 %copy-start.23 = (bf16[1024,1024]{1,0:T(8,128)(2,1)S(1)}, bf16[1024,1024]{1,0:T(8,128)(2,1)}, u32[]{:S(2)}) copy-start(bf16[1024,1024]{1,0:T(8,128)(2,1)} %copy-done.21) | copy-start | bytes 6291460
  389.0 10.1 %copy-start.53 = (f32[1024]{0:T(1024)S(1)}, f32[1024]{0:T(1024)}, u32[]{:S(2)}) copy-start(f32[1024]{0:T(1024)} %param.31) | copy-start | bytes 12292
  389.0 10.1 %copy-start.55 = (bf16[2048,1024]{1,0:T(8,128)(2,1)S(1)}, bf16[2048,1024]{1,0:T(8,128)(2,1)}, u32[]{:S(2)}) copy-start(bf16[2048,1024]{1,0:T(8,128)(2,1)} %copy-done.54) | copy-start | bytes 12582916
  398.6 11.4 %collective-permute-start.9 = (bf16[1024,1024]{1,0:T(8,128)(2,1)}, bf16[1024,1024]{1,0:T(8,128)(2,1)}, u32[]{:S(2)}, u32[]{:S(2)}) collective-permute-start(bf16[1024,1024]{1,0:T(8,128)(2,1)} %constant_dynamic-slice_fusion), channel_id=1, source_target_pairs={{0,1},{1,0},{2,3},{3,2},{4,5},{5,4},{6,7},{7,6},{8,9},{9,8},{10,11... | collective-permute-start | bytes 6291464 | tf_op jit(solution)/shard_map/ppermute | solution.py:200
  407.4 161.3 %reduce-scatter.15.cloned.1.call-start = ((), (), s32[]{:S(2)}) async-start(), calls=%async_computation.6 | async-start | bytes 589824
  409.4 5.6 copy-start.31
  409.4 5.6 collective-permute-start.6
  410.3 53.8 %slice-start = ((s8[8388608]{0:T(1024)(128)(4,1)}), s8[4194304]{0:T(1024)(128)(4,1)S(1)}, s32[]{:S(2)}) async-start(s8[8388608]{0:T(1024)(128)(4,1)} %bitcast.108), calls=%async_computation.8 | async-start | bytes 8388608
  413.2 50.9 %slice-start.1 = ((s8[8388608]{0:T(1024)(128)(4,1)}), s8[4194304]{0:T(1024)(128)(4,1)S(1)}, s32[]{:S(2)}) async-start(s8[8388608]{0:T(1024)(128)(4,1)} %bitcast.108), calls=%async_computation.9 | async-start | bytes 8388608
  413.2 48.6 %collective-permute-start.10 = (bf16[1024,1024]{1,0:T(8,128)(2,1)S(1)}, bf16[1024,1024]{1,0:T(8,128)(2,1)S(1)}, u32[]{:S(2)}, u32[]{:S(2)}) collective-permute-start(bf16[1024,1024]{1,0:T(8,128)(2,1)S(1)} %add_convert_fusion.3), channel_id=1, source_target_pairs={{0,2},{1,3},{2,0},{3,1},{4,6},{5,7},{6,4},{7,5},{8,10},{9,11},{10,... | collective-permute-start | bytes 6291464 | tf_op jit(solution)/shard_map/ppermute | solution.py:202
  417.3 46.7 %copy-start.2 = (bf16[4,64,2048]{2,1,0:T(8,128)(2,1)S(1)}, bf16[4,64,2048]{2,1,0:T(8,128)(2,1)}, u32[]{:S(2)}) copy-start(bf16[4,64,2048]{2,1,0:T(8,128)(2,1)} %copy-done.1) | copy-start | bytes 3145732
  417.3 89.0 %collective-permute-start.7 = (bf16[1024,1024]{1,0:T(8,128)(2,1)}, bf16[1024,1024]{1,0:T(8,128)(2,1)}, u32[]{:S(2)}, u32[]{:S(2)}) collective-permute-start(bf16[1024,1024]{1,0:T(8,128)(2,1)} %add_convert_fusion.5), channel_id=1, source_target_pairs={{0,2},{1,3},{2,0},{3,1},{4,6},{5,7},{6,4},{7,5},{8,10},{9,11},{10,... | collective-permute-start | bytes 6291464 | tf_op jit(solution)/shard_map/ppermute | solution.py:202
  464.0 45.6 %collective-permute-start.11 = (bf16[1024,1024]{1,0:T(8,128)(2,1)}, bf16[1024,1024]{1,0:T(8,128)(2,1)}, u32[]{:S(2)}, u32[]{:S(2)}) collective-permute-start(bf16[1024,1024]{1,0:T(8,128)(2,1)} %add_convert_fusion.2), channel_id=1, source_target_pairs={{0,1},{1,0},{2,3},{3,2},{4,5},{5,4},{6,7},{7,6},{8,9},{9,8},{10,11... | collective-permute-start | bytes 6291464 | tf_op jit(solution)/shard_map/ppermute | solution.py:204
  466.3 3.6 copy-start.36
  466.3 162.2 %reduce-scatter.13.cloned.1.call-start = ((), (), s32[]{:S(2)}) async-start(), calls=%async_computation.5 | async-start | bytes 1769472
  509.5 3.5 copy-start.15
  509.6 3.5 copy-start.38
  509.6 3.5 copy-start.45
  509.6 34.4 %collective-permute-start.8 = (bf16[1024,1024]{1,0:T(8,128)(2,1)S(1)}, bf16[1024,1024]{1,0:T(8,128)(2,1)S(1)}, u32[]{:S(2)}, u32[]{:S(2)}) collective-permute-start(bf16[1024,1024]{1,0:T(8,128)(2,1)S(1)} %add_convert_fusion.4), channel_id=1, source_target_pairs={{0,1},{1,0},{2,3},{3,2},{4,5},{5,4},{6,7},{7,6},{8,9},{9,8},{10,11... | collective-permute-start | bytes 6291464 | tf_op jit(solution)/shard_map/ppermute | solution.py:204
  513.0 3.2 copy-start.41
  516.3 28.0 %slice-start.2 = ((s8[8388608]{0:T(1024)(128)(4,1)}), s8[4194304]{0:T(1024)(128)(4,1)S(1)}, s32[]{:S(2)}) async-start(s8[8388608]{0:T(1024)(128)(4,1)} %bitcast.110), calls=%async_computation.10 | async-start | bytes 8388608
  523.3 21.0 %slice-start.3 = ((s8[8388608]{0:T(1024)(128)(4,1)}), s8[4194304]{0:T(1024)(128)(4,1)S(1)}, s32[]{:S(2)}) async-start(s8[8388608]{0:T(1024)(128)(4,1)} %bitcast.110), calls=%async_computation.11 | async-start | bytes 8388608
  523.3 35.2 %collective-permute-start.12 = (f32[2560]{0:T(1024)S(1)}, f32[2560]{0:T(1024)S(1)}, u32[]{:S(2)}, u32[]{:S(2)}) collective-permute-start(f32[2560]{0:T(1024)S(1)} %pad_maximum_fusion.6), channel_id=1, source_target_pairs={{0,4},{4,0},{8,12},{12,8},{16,20},{20,16},{24,28},{28,24},{1,5},{5... | collective-permute-start | bytes 30728 | tf_op jit(solution)/shard_map/ppermute | solution.py:216
  557.2 3.8 collective-permute-start.15
  558.5 4.3 collective-permute-start.13
  561.1 69.7 %collective-permute-start.16 = (f32[5120]{0:T(1024)S(1)}, f32[5120]{0:T(1024)S(1)}, u32[]{:S(2)}, u32[]{:S(2)}) collective-permute-start(f32[5120]{0:T(1024)S(1)} %add.206), channel_id=1, source_target_pairs={{0,8},{4,12},{8,0},{12,4},{16,24},{20,28},{24,16},{28,20},{1,9},{5... | collective-permute-start | bytes 61448 | tf_op jit(solution)/shard_map/ppermute | solution.py:216
  562.8 67.9 %collective-permute-start.14 = (f32[2560]{0:T(1024)S(1)}, f32[2560]{0:T(1024)S(1)}, u32[]{:S(2)}, u32[]{:S(2)}) collective-permute-start(f32[2560]{0:T(1024)S(1)} %add.204), channel_id=1, source_target_pairs={{0,16},{4,20},{8,24},{12,28},{16,0},{20,4},{24,8},{28,12},{1,17},{... | collective-permute-start | bytes 30728 | tf_op jit(solution)/shard_map/ppermute | solution.py:216
  630.7 4.7 collective-permute-start.17
  (18 other events, 33.3 us)
Sparse Core Ops, SparseCore 0:
  274.8 78.6 reduce-scatter.16
  407.5 88.1 reduce-scatter.10
  499.1 61.6 reduce-scatter.14
  564.1 64.4 reduce-scatter.12

commit v2 on v1

--- a/solution.py
+++ b/solution.py
@@ -283,13 +283,14 @@
     d_pre = gelu_back(d_act)[0]
     grad_b_fc1 = jnp.sum(d_pre, axis=0)
     d_pre_low = d_pre.astype(jnp.bfloat16)
-    grad_w_fc1 = jnp.einsum("td,tf->df", normed_two, d_pre_low, preferred_element_type=jnp.float32)
-    d_normed_two = mp_allreduce(
-        jnp.einsum("tf,df->td", d_pre_low, w_fc1, preferred_element_type=jnp.float32).astype(
-            jnp.bfloat16
-        ),
-        n_mp,
-    )
+    grad_w_fc1_t = jnp.einsum("tf,td->fd", d_pre_low, normed_two, preferred_element_type=jnp.float32)
+    dn_two_partial = jnp.einsum(
+        "tf,df->td", d_pre_low, w_fc1, preferred_element_type=jnp.float32
+    ).astype(jnp.bfloat16)
+    mlp_weight_grads = jnp.concatenate([grad_w_fc2, grad_w_fc1_t], axis=0).astype(jnp.bfloat16)
+    mlp_weight_grads, dn_two_partial = lax.optimization_barrier((mlp_weight_grads, dn_two_partial))
+    summed_mlp = lax.psum_scatter(mlp_weight_grads, "dp", scatter_dimension=1, tiled=True)
+    d_normed_two = mp_allreduce(dn_two_partial, n_mp)
     d_middle_norm, grad_ln2_gain, grad_ln2_bias = norm_two_back(d_normed_two)
     d_middle = upstream + d_middle_norm
     mlp_partial, d_middle = lax.optimization_barrier((mlp_partial, d_middle))
@@ -306,12 +307,13 @@
         query_heads, key_heads, value_heads, d_att_heads, out_f32, log_norms,
         segments, lo_blocks, hi_blocks,
     )
+    summed_mlp, d_q_heads = lax.optimization_barrier((summed_mlp, d_q_heads))
     d_queries = d_q_heads.transpose(2, 0, 1).reshape(row_count, local_cols)
     d_keys = from_heads(d_k_heads)
     d_values = from_heads(d_v_heads)
     grad_b_qv = jnp.stack([jnp.sum(d_queries, axis=0), jnp.sum(d_values, axis=0)])
     stacked = jnp.stack([d_queries, d_keys, d_values]).astype(jnp.bfloat16)
-    grad_w_qkv = jnp.einsum("td,stc->sdc", normed_one, stacked, preferred_element_type=jnp.float32)
+    grad_w_qkv_t = jnp.einsum("stc,td->scd", stacked, normed_one, preferred_element_type=jnp.float32)
     d_normed_one = mp_allreduce(
         jnp.einsum("stc,sdc->td", stacked, w_qkv, preferred_element_type=jnp.float32).astype(
             jnp.bfloat16
@@ -322,14 +324,19 @@
     grad_tokens = d_middle + d_input_norm
 
     def scatter(grad, dim):
-        return lax.psum_scatter(
-            grad.astype(jnp.bfloat16), "dp", scatter_dimension=dim, tiled=True
-        ).astype(jnp.float32)
-
-    summed_qkv = scatter(grad_w_qkv, 1)
-    summed_out = scatter(grad_w_out, 1)
-    summed_fc1 = scatter(grad_w_fc1, 0)
-    summed_fc2 = scatter(grad_w_fc2, 1)
+        return lax.psum_scatter(grad.astype(jnp.bfloat16), "dp", scatter_dimension=dim, tiled=True).astype(jnp.float32)
+
+    tail_grads = jnp.concatenate(
+        [grad_w_qkv_t.reshape(3 * local_cols, -1), grad_w_out], axis=0
+    )
+    summed_tail = scatter(tail_grads, 1)
+    share = summed_tail.shape[1]
+    summed_qkv = summed_tail[: 3 * local_cols].reshape(3, local_cols, share).transpose(0, 2, 1)
+    summed_out = summed_tail[3 * local_cols :]
+    summed_mlp = summed_mlp.astype(jnp.float32)
+    units = grad_w_fc2.shape[0]
+    summed_fc2 = summed_mlp[:units]
+    summed_fc1 = summed_mlp[units:].T
     early = dp_allreduce(
         jnp.concatenate([grad_ln2_gain, grad_ln2_bias, grad_b_out, grad_b_fc2, grad_b_fc1]), n_dp
     )

time: 652 us -> 654 us (level)
    unnamed x7 -> x4, waiting for transfers between devices: 58.3 us -> 29.5 us
    ppermute x4, waiting for transfers between devices: 153 us -> 175 us  [mp_allreduce(): got_far = lax.ppermute(first, 'mp', [(k, k ^ 2) for k in range(4)])]
    unnamed x134 -> x120, local copies, waits for them, and re-layouts: 36.1 us -> 31.5 us
  transfers between devices with their start and end apart: 22 -> 20, of which waited for: 10 -> 10; matrix products, arithmetic and copies ran while one was open for 25% -> 22% of each run, Pallas kernels for 8% -> 8%
where the time goes in v2:
time: 654 us; the launch traced here: 644 us
  waiting for transfers between devices  221 us (34%)
  other arithmetic  119 us (18%)
  Pallas kernels  98.9 us (15%)
  matrix products  87.9 us (13%)
  local copies, waits for them, and re-layouts  64.5 us (10%)
  starting transfers between devices  37.3 us (6%)
  between operations  15.2 us (2%)
    ppermute x4, waiting for transfers between devices, mp_allreduce(): got_far = lax.ppermute(first, 'mp', [(k, k ^ 2) for k in range(4)])  175 us
    pallas_call x1, Pallas kernels, flash_backward(): pl.pallas_call(_bwd_kernel, out_shape=(jax.ShapeDtypeStruct((heads, HEAD,...  51 us
    pallas_call x1, Pallas kernels, flash_forward(): pl.pallas_call(_fwd_kernel, out_shape=(jax.ShapeDtypeStruct((heads, HEAD,...  47.9 us
    unnamed x120, local copies, waits for them, and re-layouts  31.5 us
    unnamed x4, waiting for transfers between devices  29.5 us
    ppermute x6, starting transfers between devices, dp_allreduce(): lax.ppermute(total, 'dp', [(k, k ^ step) for k in range(n_dp)])  29.2 us
    reduce_sum x4, other arithmetic, normalize(): return centered * lax.rsqrt(spread + 1e-06) * gain + shift  25.5 us
    dot_general x1, matrix products, per_device(): jnp.einsum('td,fd->tf', cotangent, w_fc2, preferred_element_type=jnp.floa...  25.1 us
  transfers between devices with their start and end apart: 20, of which 10 were waited for; matrix products, arithmetic and copies ran while one was open for 22% of the time, Pallas kernels for 8%

profile of v2, /device:TPU:0, one launch (start us, length us, event | category | flops | bytes accessed | tf_op | source)
XLA Modules:
  0.0 644.1 jit_solution(17305830871728654602)
XLA Ops:
  11.3 3.0 convert_reduce_fusion.2
  18.1 3.4 fusion.9
  22.8 2.3 fusion.28
  25.1 2.3 fusion.27
  27.4 1.9 copy.84.k_ref
  33.0 47.9 %segment_flash_fwd.1 = (bf16[4,64,2048]{2,1,0:T(8,128)(2,1)S(1)}, f32[4,64,2048]{2,1,0:T(8,128)}, f32[4,1,2048]{2,1,0:T(1,128)S(1)}) custom-call(s32[8]{0:T(128)S(1)} %fusion.53.lo_ref, s32[8]{0:T(128)S(1)} %fusion.52.hi_ref, s32[2048,1]{1,0:T(8,128)S(1)} %copy-done.9, s32[1,2048]{1,0:T(1,128)S(1)} %bitcast.100, bf16[4,64,2048]{2,1,0:T(8,128)(2,1)S(1)} %bitcast.94, ...), custom_call_target="tpu_custom_call" | custom-call | flops 2576980480 | bytes 6324224 | tf_op jit(solution)/shard_map/segment_flash_fwd/pallas_call | solution.py:124
  85.3 4.1 collective-permute-done
  89.4 3.2 add_convert_fusion.9
  92.6 2.9 collective-permute-start.1
  95.6 45.9 %collective-permute-done.1 = bf16[1024,1024]{1,0:T(8,128)(2,1)S(1)} collective-permute-done((bf16[1024,1024]{1,0:T(8,128)(2,1)S(1)}, bf16[1024,1024]{1,0:T(8,128)(2,1)S(1)}, u32[]{:S(2)}, u32[]{:S(2)}) %collective-permute-start.1) | collective-permute-done | bytes 2097184 | tf_op jit(solution)/shard_map/ppermute | solution.py:202
  141.5 2.3 add_convert_fusion.8
  143.8 4.5 collective-permute-done.2
  148.3 2.5 broadcast_select_fusion.7
  152.4 3.8 multiply_reduce_fusion
  156.3 5.8 fusion.58
  162.2 25.1 %fusion.61 = (f32[1024]{0:T(1024)S(1)}, bf16[2048,1024]{1,0:T(8,128)(2,1)}, f32[2048,1024]{1,0:T(8,128)}) fusion(f32[2048,1024]{1,0:T(8,128)S(1)} %fusion.58, f32[1024]{0:T(1024)S(1)} %copy-done.47, bf16[2048,1024]{1,0:T(8,128)(2,1)S(1)} %copy-done.26, bf16[1024,1024]{1,0:T(8,128)(2,1)S(1)} %copy-done), kind=kOutput, calls=%fused_computation.156 | convolution fusion | flops 4450155520 | bytes 27271168 | tf_op jit(solution)/shard_map/td,fd->tf/dot_general | solution.py:282
  187.3 8.2 %fusion.35 = bf16[1024,1024]{1,0:T(8,128)(2,1)S(1)} fusion(bf16[2048,1024]{1,0:T(8,128)(2,1)} %get-tuple-element.116, f32[1024]{0:T(1024)S(1)} %copy-done.51, f32[1024]{0:T(1024)S(1)} %copy-done.44, f32[2048]{0:T(1024)S(1)} %fusion.51, bf16[2048,1024]{1,0:T(8,128)(2,1)S(1)} %copy-done.12, f32[2048]{0:T(1024)S(1)} %broadcast_multiply_fusion, ...), kind=kOutput, calls=%fused_computation.100 | convolution fusion | flops 4321181696 | bytes 14708736 | tf_op jit(solution)/shard_map/tf,td->fd/dot_general | solution.py:286
  195.6 6.4 convolution_convert_fusion.1
  202.0 10.0 %multiply_convert_fusion = bf16[2048,1024]{1,0:T(8,128)(2,1)} fusion(f32[2048,1024]{1,0:T(8,128)} %get-tuple-element.117, f32[2048,1024]{1,0:T(8,128)} %copy-done.25, f32[1024]{0:T(1024)S(1)} %copy-done.47), kind=kLoop, calls=%fused_computation.37 | loop fusion | flops 8388608 | bytes 20975616 | tf_op jit(solution)/shard_map/convert_element_type | solution.py:277
  212.1 8.0 %convolution_convert_fusion.5 = bf16[1024,1024]{1,0:T(8,128)(2,1)S(1)} fusion(bf16[2048,1024]{1,0:T(8,128)(2,1)} %multiply_convert_fusion, bf16[2048,1024]{1,0:T(8,128)(2,1)} %param.18), kind=kOutput, calls=%fused_computation.101 | convolution fusion | flops 4296015872 | bytes 10485760 | tf_op jit(solution)/shard_map/tf,td->fd/dot_general | solution.py:281
  220.1 2.6 pad_maximum_fusion.1
  224.2 4.0 collective-permute-done.3
  229.2 1.8 collective-permute-start.4
  231.0 45.9 %collective-permute-done.4 = bf16[1024,1024]{1,0:T(8,128)(2,1)S(1)} collective-permute-done((bf16[1024,1024]{1,0:T(8,128)(2,1)S(1)}, bf16[1024,1024]{1,0:T(8,128)(2,1)S(1)}, u32[]{:S(2)}, u32[]{:S(2)}) %collective-permute-start.4) | collective-permute-done | bytes 2097184 | tf_op jit(solution)/shard_map/ppermute | solution.py:202
  276.9 2.3 add_convert_fusion.6
  279.2 6.6 %copy.99 = bf16[2048,1024]{0,1:T(8,128)(2,1)} copy(bf16[2048,1024]{1,0:T(8,128)(2,1)} %pad_maximum_fusion.1) | data formatting | bytes 8388608
  287.0 2.2 copy.87.q_ref
  289.2 2.7 copy.85
  291.9 8.3 %convolution_convert_fusion.2 = bf16[2048,1024]{1,0:T(8,128)(2,1)} fusion(bf16[2048,1024]{1,0:T(8,128)(2,1)} %multiply_convert_fusion, bf16[1024,1024]{1,0:T(8,128)(2,1)S(1)} %copy-done), kind=kOutput, calls=%fused_computation.74 | convolution fusion | flops 4297064448 | bytes 10485760 | tf_op jit(solution)/shard_map/dot_general | solution.py:278
  300.2 2.6 broadcast_select_fusion.5
  305.3 6.4 fusion.10
  311.7 9.0 %fusion.15 = (f32[1024]{0:T(1024)S(1)}, f32[2048]{0:T(1024)S(1)}, f32[1024]{0:T(1024)S(1)}) fusion(f32[2048]{0:T(1024)S(1)} %fusion.51, bf16[1024,1024]{1,0:T(8,128)(2,1)S(1)} %get-tuple-element.128, bf16[1024,1024]{1,0:T(8,128)(2,1)S(1)} %get-tuple-element.127, f32[2048]{0:T(1024)S(1)} %broadcast_multiply_fusion, f32[1024]{0:T(1024)S(1)} %copy-done.35, ...), kind=kLoop, calls=%fused_computation.31 | loop fusion | flops 46133248 | bytes 12632064 | tf_op jit(solution)/shard_map/transpose(jvp())/reduce_sum | solution.py:179
  320.7 8.1 %convert_reduce_fusion.3 = (f32[1024]{0:T(1024)S(1)}, f32[2048,1024]{1,0:T(8,128)S(1)}) fusion(bf16[2048,1024]{1,0:T(8,128)(2,1)S(1)} %copy-done.27, f32[2048]{0:T(1024)S(1)} %negate_multiply_fusion.2, f32[2048]{0:T(1024)S(1)} %multiply_multiply_fusion.6, f32[2048]{0:T(1024)S(1)} %broadcast_multiply_fusion, f32[1024]{0:T(1024)S(1)} %copy-done.35, ...), kind=kLoop, calls=%fused_computation.18 | loop fusion | flops 44039168 | bytes 25210880 | tf_op jit(solution)/shard_map/reduce_sum | solution.py:280
  330.2 2.1 copy-done.15
  337.8 51.0 %segment_flash_bwd.1 = (f32[4,64,2048]{2,1,0:T(8,128)}, f32[4,2048,64]{2,1,0:T(8,128)}, f32[4,2048,64]{2,1,0:T(8,128)}) custom-call(s32[8]{0:T(128)S(1)} %fusion.53.lo_ref, s32[8]{0:T(128)S(1)} %fusion.52.hi_ref, s32[2048,1]{1,0:T(8,128)S(1)} %copy-done.10, s32[1,2048]{1,0:T(1,128)S(1)} %bitcast.101, bf16[4,2048,64]{2,1,0:T(8,128)(2,1)} %copy.87.q_ref, ...), custom_call_target="tpu_custom_call" | custom-call | flops 5153960960 | bytes 15761408 | tf_op jit(solution)/shard_map/segment_flash_bwd/pallas_call | solution.py:151
  388.8 3.9 bitcast_convert_fusion.1
  392.7 1.9 copy.91
  395.9 3.9 convert_bitcast_fusion
  399.8 1.9 copy.90
  403.0 3.1 constant_dynamic-slice_fusion.1
  407.9 2.8 bitcast_convert_fusion.2
  410.8 2.4 copy.92
  413.2 5.8 bitcast_convert_fusion
  419.3 1.9 copy-done.29
  421.2 3.9 add_convert_fusion.5
  426.8 2.3 add_convert_fusion.3
  429.8 44.1 %collective-permute-done.7 = bf16[1024,1024]{1,0:T(8,128)(2,1)} collective-permute-done((bf16[1024,1024]{1,0:T(8,128)(2,1)}, bf16[1024,1024]{1,0:T(8,128)(2,1)}, u32[]{:S(2)}, u32[]{:S(2)}) %collective-permute-start.7) | collective-permute-done | bytes 2097184 | tf_op jit(solution)/shard_map/ppermute | solution.py:202
  473.9 4.5 add_convert_fusion.4
  478.4 39.5 %collective-permute-done.10 = bf16[1024,1024]{1,0:T(8,128)(2,1)} collective-permute-done((bf16[1024,1024]{1,0:T(8,128)(2,1)}, bf16[1024,1024]{1,0:T(8,128)(2,1)}, u32[]{:S(2)}, u32[]{:S(2)}) %collective-permute-start.10) | collective-permute-done | bytes 2097184 | tf_op jit(solution)/shard_map/ppermute | solution.py:202
  517.9 4.5 add_convert_fusion.2
  522.4 4.8 fusion.41
  527.5 6.9 %fusion.38 = bf16[3,256,1024]{2,1,0:T(8,128)(2,1)S(1)} fusion(bf16[2048,1024]{1,0:T(8,128)(2,1)} %copy-done.28, bf16[1,2048,256]{2,1,0:T(8,128)(2,1)} %copy.94, bf16[1,2048,256]{2,1,0:T(8,128)(2,1)} %copy.93, bf16[1,2048,256]{2,1,0:T(8,128)(2,1)} %copy.92), kind=kOutput, calls=%fused_computation.102 | convolution fusion | flops 3225157632 | bytes 8912896 | tf_op jit(solution)/shard_map/stc,td->scd/dot_general | solution.py:316
  535.9 3.9 copy.101
  539.9 2.5 broadcast_select_fusion.3
  542.4 2.6 broadcast_select_fusion.1
  545.9 3.2 fusion.12
  549.1 7.0 %fusion.16 = (f32[1024]{0:T(1024)S(1)}, f32[2048]{0:T(1024)S(1)}, f32[1024]{0:T(1024)S(1)}) fusion(bf16[2048,1024]{1,0:T(8,128)(2,1)S(1)} %copy-done.14, f32[2048]{0:T(1024)S(1)} %copy-done.37, f32[2048]{0:T(1024)S(1)} %copy-done.34, bf16[1024,1024]{1,0:T(8,128)(2,1)S(1)} %get-tuple-element.124, bf16[1024,1024]{1,0:T(8,128)(2,1)S(1)} %get-tuple-element.123, ...), kind=kLoop, calls=%fused_computation.32 | loop fusion | flops 33550336 | bytes 8433664 | tf_op jit(solution)/shard_map/transpose(jvp())/reduce_sum | solution.py:179
  556.1 20.8 %collective-permute-start.12 = (f32[2560]{0:T(1024)S(1)}, f32[2560]{0:T(1024)S(1)}, u32[]{:S(2)}, u32[]{:S(2)}) collective-permute-start(f32[2560]{0:T(1024)S(1)} %pad_maximum_fusion.8), channel_id=1, source_target_pairs={{0,4},{4,0},{8,12},{12,8},{16,20},{20,16},{24,28},{28,24},{1,5},{5... | collective-permute-start | bytes 30728 | tf_op jit(solution)/shard_map/ppermute | solution.py:216
  576.9 11.0 %fusion.63 = (f32[1024]{0:T(1024)S(1)}, f32[2048,1024]{1,0:T(8,128)}, bf16[2048,1024]{1,0:T(8,128)(2,1)}) fusion(f32[2048,1024]{1,0:T(8,128)S(1)} %bitcast.105, f32[2048]{0:T(1024)S(1)} %negate_multiply_fusion.1, f32[2048]{0:T(1024)S(1)} %multiply_multiply_fusion.5, f32[2048]{0:T(1024)S(1)} %copy-done.34, bf16[2048,1024]{1,0:T(8,128)(2,1)S(1)} %copy-done.14, ...), kind=kLoop, calls=%fused_computation.157 | loop fusion | flops 56622080 | bytes 37797888 | tf_op jit(solution)/shard_map/reduce_sum | solution.py:299
  588.1 2.1 collective-permute-start.13
  591.9 2.6 collective-permute-start.14
  594.6 2.1 collective-permute-start.16
  598.5 29.4 %reduce-scatter.9.cloned.1.call-done = bf16[128,1024]{1,0:T(8,128)(2,1)} async-done(((bf16[1024,1024]{1,0:T(8,128)(2,1)}), bf16[128,1024]{1,0:T(8,128)(2,1)}) %reduce-scatter.9.cloned.1.call-update) | async-done | bytes 262160
  634.3 2.1 collective-permute-done.17
  (203 shorter events, 52.2 us)
Async XLA Ops:
  7.2 154.9 %copy-start = (bf16[1024,1024]{1,0:T(8,128)(2,1)S(1)}, bf16[1024,1024]{1,0:T(8,128)(2,1)}, u32[]{:S(2)}) copy-start(bf16[1024,1024]{1,0:T(8,128)(2,1)} %param.26) | copy-start | bytes 6291460
  7.2 399.4 %reduce-scatter.7.cloned.1.call-start = ((), (), s32[]{:S(2)}) async-start(), calls=%async_computation.2 | async-start | bytes 4718592
  11.3 3.5 copy-start.11
  11.3 6.8 %copy-start.42 = (f32[1024]{0:T(1024)S(1)}, f32[1024]{0:T(1024)}, u32[]{:S(2)}) copy-start(f32[1024]{0:T(1024)} %param.28) | copy-start | bytes 12292
  11.3 6.8 %copy-start.45 = (f32[1024]{0:T(1024)S(1)}, f32[1024]{0:T(1024)}, u32[]{:S(2)}) copy-start(f32[1024]{0:T(1024)} %param.29) | copy-start | bytes 12292
  14.7 3.4 copy-start.33
  18.1 3.4 copy-start.50
  21.5 3.6 copy-start.28
  22.8 4.6 copy-start.3
  33.0 47.9 %copy-start.31 = (bf16[256,1024]{1,0:T(8,128)(2,1)S(1)}, bf16[256,1024]{1,0:T(8,128)(2,1)}, u32[]{:S(2)}) copy-start(bf16[256,1024]{1,0:T(8,128)(2,1)} %param.22) | copy-start | bytes 1572868
  82.2 2.6 copy-start.22
  84.8 4.6 collective-permute-start
  92.6 48.9 %collective-permute-start.1 = (bf16[1024,1024]{1,0:T(8,128)(2,1)S(1)}, bf16[1024,1024]{1,0:T(8,128)(2,1)S(1)}, u32[]{:S(2)}, u32[]{:S(2)}) collective-permute-start(bf16[1024,1024]{1,0:T(8,128)(2,1)S(1)} %add_convert_fusion.9), channel_id=1, source_target_pairs={{0,2},{1,3},{2,0},{3,1},{4,6},{5,7},{6,4},{7,5},{8,10},{9,11},{10,... | collective-permute-start | bytes 6291464 | tf_op jit(solution)/shard_map/ppermute | solution.py:202
  143.8 4.5 collective-permute-start.2
  143.8 7.0 %copy-start.12 = (bf16[2048,1024]{1,0:T(8,128)(2,1)S(1)}, bf16[2048,1024]{1,0:T(8,128)(2,1)}, u32[]{:S(2)}) copy-start(bf16[2048,1024]{1,0:T(8,128)(2,1)} %param.17) | copy-start | bytes 12582916
  143.8 7.0 %copy-start.35 = (f32[1024]{0:T(1024)S(1)}, f32[1024]{0:T(1024)}, u32[]{:S(2)}) copy-start(f32[1024]{0:T(1024)} %param.23) | copy-start | bytes 12292
  150.8 36.5 %copy-start.16 = (bf16[1024,1024]{1,0:T(8,128)(2,1)}, bf16[1024,1024]{1,0:T(8,128)(2,1)S(1)}, u32[]{:S(2)}) copy-start(bf16[1024,1024]{1,0:T(8,128)(2,1)S(1)} %get-tuple-element.129) | copy-start | bytes 6291460
  150.8 36.5 %copy-start.19 = (bf16[1024,1024]{1,0:T(8,128)(2,1)}, bf16[1024,1024]{1,0:T(8,128)(2,1)S(1)}, u32[]{:S(2)}) copy-start(bf16[1024,1024]{1,0:T(8,128)(2,1)S(1)} %get-tuple-element.130) | copy-start | bytes 6291460
  152.4 3.9 copy-start.44
  152.4 3.9 copy-start.48
  152.4 3.9 copy-start.51
  156.2 5.9 copy-start.40
  156.3 5.9 copy-start.26
  156.3 5.9 copy-start.47
  162.1 25.1 %copy-start.25 = (f32[2048,1024]{1,0:T(8,128)}, f32[2048,1024]{1,0:T(8,128)S(1)}, u32[]{:S(2)}) copy-start(f32[2048,1024]{1,0:T(8,128)S(1)} %fusion.58) | copy-start | bytes 25165828
  187.3 8.3 %copy-start.49 = (bf16[1024,1024]{1,0:T(8,128)(2,1)S(1)}, bf16[1024,1024]{1,0:T(8,128)(2,1)}, u32[]{:S(2)}) copy-start(bf16[1024,1024]{1,0:T(8,128)(2,1)} %param.24) | copy-start | bytes 6291460
  187.3 8.3 %copy-start.52 = (bf16[2048,1024]{1,0:T(8,128)(2,1)S(1)}, bf16[2048,1024]{1,0:T(8,128)(2,1)}, u32[]{:S(2)}) copy-start(bf16[2048,1024]{1,0:T(8,128)(2,1)} %get-tuple-element.116) | copy-start | bytes 12582916
  220.1 3.7 copy-start.30
  224.0 4.2 collective-permute-start.3
  229.2 47.7 %collective-permute-start.4 = (bf16[1024,1024]{1,0:T(8,128)(2,1)S(1)}, bf16[1024,1024]{1,0:T(8,128)(2,1)S(1)}, u32[]{:S(2)}, u32[]{:S(2)}) collective-permute-start(bf16[1024,1024]{1,0:T(8,128)(2,1)S(1)} %add_convert_fusion.7), channel_id=1, source_target_pairs={{0,2},{1,3},{2,0},{3,1},{4,6},{5,7},{6,4},{7,5},{8,10},{9,11},{10,... | collective-permute-start | bytes 6291464 | tf_op jit(solution)/shard_map/ppermute | solution.py:202
  279.2 21.0 %collective-permute-start.5 = (bf16[1024,1024]{1,0:T(8,128)(2,1)}, bf16[1024,1024]{1,0:T(8,128)(2,1)}, u32[]{:S(2)}, u32[]{:S(2)}) collective-permute-start(bf16[1024,1024]{1,0:T(8,128)(2,1)} %add_convert_fusion.6), channel_id=1, source_target_pairs={{0,1},{1,0},{2,3},{3,2},{4,5},{5,4},{6,7},{7,6},{8,9},{9,8},{10,11... | collective-permute-start | bytes 6291464 | tf_op jit(solution)/shard_map/ppermute | solution.py:204
  285.8 342.2 %reduce-scatter.9.cloned.1.call-start = ((), (), s32[]{:S(2)}) async-start(), calls=%async_computation.3 | async-start | bytes 2359296
  300.2 3.7 copy-start.13
  300.2 4.5 copy-start.17
  300.2 5.1 copy-start.20
  305.3 6.4 copy-start.41
  311.7 9.0 %copy-start.27 = (bf16[2048,1024]{1,0:T(8,128)(2,1)S(1)}, bf16[2048,1024]{1,0:T(8,128)(2,1)}, u32[]{:S(2)}) copy-start(bf16[2048,1024]{1,0:T(8,128)(2,1)} %param.18) | copy-start | bytes 12582916
  320.7 8.2 %copy-start.32 = (bf16[256,1024]{1,0:T(8,128)(2,1)S(1)}, bf16[256,1024]{1,0:T(8,128)(2,1)}, u32[]{:S(2)}) copy-start(bf16[256,1024]{1,0:T(8,128)(2,1)} %param.22) | copy-start | bytes 1572868
  328.9 3.4 copy-start.15
  406.1 13.2 %collective-permute-start.6 = (bf16[1024,1024]{1,0:T(8,128)(2,1)}, bf16[1024,1024]{1,0:T(8,128)(2,1)}, u32[]{:S(2)}, u32[]{:S(2)}) collective-permute-start(bf16[1024,1024]{1,0:T(8,128)(2,1)} %constant_dynamic-slice_fusion.1), channel_id=1, source_target_pairs={{0,1},{1,0},{2,3},{3,2},{4,5},{5,4},{6,7},{7,6},{8,9},{9,8},{10,11... | collective-permute-start | bytes 6291464 | tf_op jit(solution)/shard_map/ppermute | solution.py:200
  419.2 7.6 %collective-permute-start.9 = (bf16[1024,1024]{1,0:T(8,128)(2,1)S(1)}, bf16[1024,1024]{1,0:T(8,128)(2,1)S(1)}, u32[]{:S(2)}, u32[]{:S(2)}) collective-permute-start(bf16[1024,1024]{1,0:T(8,128)(2,1)S(1)} %constant_dynamic-slice_fusion), channel_id=1, source_target_pairs={{0,1},{1,0},{2,3},{3,2},{4,5},{5,4},{6,7},{7,6},{8,9},{9,8},{10,11... | collective-permute-start | bytes 6291464 | tf_op jit(solution)/shard_map/ppermute | solution.py:200
  425.1 4.3 copy-start.23
  425.1 48.8 %collective-permute-start.7 = (bf16[1024,1024]{1,0:T(8,128)(2,1)}, bf16[1024,1024]{1,0:T(8,128)(2,1)}, u32[]{:S(2)}, u32[]{:S(2)}) collective-permute-start(bf16[1024,1024]{1,0:T(8,128)(2,1)} %add_convert_fusion.5), channel_id=1, source_target_pairs={{0,2},{1,3},{2,0},{3,1},{4,6},{5,7},{6,4},{7,5},{8,10},{9,11},{10,... | collective-permute-start | bytes 6291464 | tf_op jit(solution)/shard_map/ppermute | solution.py:202
  429.1 88.7 %collective-permute-start.10 = (bf16[1024,1024]{1,0:T(8,128)(2,1)}, bf16[1024,1024]{1,0:T(8,128)(2,1)}, u32[]{:S(2)}, u32[]{:S(2)}) collective-permute-start(bf16[1024,1024]{1,0:T(8,128)(2,1)} %add_convert_fusion.3), channel_id=1, source_target_pairs={{0,2},{1,3},{2,0},{3,1},{4,6},{5,7},{6,4},{7,5},{8,10},{9,11},{10,... | collective-permute-start | bytes 6291464 | tf_op jit(solution)/shard_map/ppermute | solution.py:202
  478.4 44.0 %copy-start.2 = (bf16[4,64,2048]{2,1,0:T(8,128)(2,1)S(1)}, bf16[4,64,2048]{2,1,0:T(8,128)(2,1)}, u32[]{:S(2)}) copy-start(bf16[4,64,2048]{2,1,0:T(8,128)(2,1)} %copy-done.1) | copy-start | bytes 3145732
  478.4 61.5 %collective-permute-start.8 = (bf16[1024,1024]{1,0:T(8,128)(2,1)}, bf16[1024,1024]{1,0:T(8,128)(2,1)}, u32[]{:S(2)}, u32[]{:S(2)}) collective-permute-start(bf16[1024,1024]{1,0:T(8,128)(2,1)} %add_convert_fusion.4), channel_id=1, source_target_pairs={{0,1},{1,0},{2,3},{3,2},{4,5},{5,4},{6,7},{7,6},{8,9},{9,8},{10,11... | collective-permute-start | bytes 6291464 | tf_op jit(solution)/shard_map/ppermute | solution.py:204
  522.4 4.8 copy-start.24
  522.4 20.0 %collective-permute-start.11 = (bf16[1024,1024]{1,0:T(8,128)(2,1)}, bf16[1024,1024]{1,0:T(8,128)(2,1)}, u32[]{:S(2)}, u32[]{:S(2)}) collective-permute-start(bf16[1024,1024]{1,0:T(8,128)(2,1)} %add_convert_fusion.2), channel_id=1, source_target_pairs={{0,1},{1,0},{2,3},{3,2},{4,5},{5,4},{6,7},{7,6},{8,9},{9,8},{10,11... | collective-permute-start | bytes 6291464 | tf_op jit(solution)/shard_map/ppermute | solution.py:204
  542.4 3.5 copy-start.14
  542.4 3.4 copy-start.34
  542.4 3.4 copy-start.43
  545.8 3.2 copy-start.39
  545.8 3.2 copy-start.37
  545.8 31.1 %slice-start = ((s8[8388608]{0:T(1024)(128)(4,1)}), s8[4194304]{0:T(1024)(128)(4,1)S(1)}, s32[]{:S(2)}) async-start(s8[8388608]{0:T(1024)(128)(4,1)} %bitcast.104), calls=%async_computation.4 | async-start | bytes 8388608
  549.1 27.8 %slice-start.1 = ((s8[8388608]{0:T(1024)(128)(4,1)}), s8[4194304]{0:T(1024)(128)(4,1)S(1)}, s32[]{:S(2)}) async-start(s8[8388608]{0:T(1024)(128)(4,1)} %bitcast.104), calls=%async_computation.5 | async-start | bytes 8388608
  549.1 27.8 %copy-start.18 = (bf16[1024,1024]{1,0:T(8,128)(2,1)S(1)}, bf16[1024,1024]{1,0:T(8,128)(2,1)}, u32[]{:S(2)}) copy-start(bf16[1024,1024]{1,0:T(8,128)(2,1)} %copy-done.16) | copy-start | bytes 6291460
  549.1 27.8 %copy-start.21 = (bf16[1024,1024]{1,0:T(8,128)(2,1)S(1)}, bf16[1024,1024]{1,0:T(8,128)(2,1)}, u32[]{:S(2)}) copy-start(bf16[1024,1024]{1,0:T(8,128)(2,1)} %copy-done.19) | copy-start | bytes 6291460
  549.1 27.8 %copy-start.46 = (f32[1024]{0:T(1024)S(1)}, f32[1024]{0:T(1024)}, u32[]{:S(2)}) copy-start(f32[1024]{0:T(1024)} %param.27) | copy-start | bytes 12292
  556.1 32.0 %collective-permute-start.12 = (f32[2560]{0:T(1024)S(1)}, f32[2560]{0:T(1024)S(1)}, u32[]{:S(2)}, u32[]{:S(2)}) collective-permute-start(f32[2560]{0:T(1024)S(1)} %pad_maximum_fusion.8), channel_id=1, source_target_pairs={{0,4},{4,0},{8,12},{12,8},{16,20},{20,16},{24,28},{28,24},{1,5},{5... | collective-permute-start | bytes 30728 | tf_op jit(solution)/shard_map/ppermute | solution.py:216
  588.0 6.6 %collective-permute-start.15 = (f32[5120]{0:T(1024)S(1)}, f32[5120]{0:T(1024)S(1)}, u32[]{:S(2)}, u32[]{:S(2)}) collective-permute-start(f32[5120]{0:T(1024)S(1)} %constant_dynamic-update-slice_fusion), channel_id=1, source_target_pairs={{0,4},{4,0},{8,12},{12,8},{16,20},{20,16},{24,28},{28,24},{1,5},{5... | collective-permute-start | bytes 61448 | tf_op jit(solution)/shard_map/ppermute | solution.py:216
  588.1 3.8 collective-permute-start.13
  591.9 39.7 %collective-permute-start.14 = (f32[2560]{0:T(1024)S(1)}, f32[2560]{0:T(1024)S(1)}, u32[]{:S(2)}, u32[]{:S(2)}) collective-permute-start(f32[2560]{0:T(1024)S(1)} %add.200), channel_id=1, source_target_pairs={{0,16},{4,20},{8,24},{12,28},{16,0},{20,4},{24,8},{28,12},{1,17},{... | collective-permute-start | bytes 30728 | tf_op jit(solution)/shard_map/ppermute | solution.py:216
  594.6 37.0 %collective-permute-start.16 = (f32[5120]{0:T(1024)S(1)}, f32[5120]{0:T(1024)S(1)}, u32[]{:S(2)}, u32[]{:S(2)}) collective-permute-start(f32[5120]{0:T(1024)S(1)} %add.202), channel_id=1, source_target_pairs={{0,8},{4,12},{8,0},{12,4},{16,24},{20,28},{24,16},{28,20},{1,9},{5... | collective-permute-start | bytes 61448 | tf_op jit(solution)/shard_map/ppermute | solution.py:216
  631.6 4.7 collective-permute-start.17
  (11 other events, 14.1 us)
Sparse Core Ops, SparseCore 0:
  285.9 98.5 reduce-scatter.6
  540.0 87.9 reduce-scatter.8

commit v3 on v2

--- a/solution.py
+++ b/solution.py
@@ -117,31 +117,36 @@
     return plain, flipped, stat, col, row
 
 
-def flash_forward(q, k, v, segments, lo, hi):
-    heads, rows, _ = q.shape
-    plain, flipped, stat, col, row = _head_specs(rows)
-    flops = int(heads * rows * rows * HEAD * 2 * 2 * 0.6)
+def flash_forward(qt, k, vt, seg_q, seg_k, lo, hi):
+    heads, _, rows_q = qt.shape
+    rows_k = k.shape[1]
+    flipped_q = pl.BlockSpec((1, HEAD, rows_q), lambda h, lo, hi: (h, 0, 0))
+    flipped_k = pl.BlockSpec((1, HEAD, rows_k), lambda h, lo, hi: (h, 0, 0))
+    plain_k = pl.BlockSpec((1, rows_k, HEAD), lambda h, lo, hi: (h, 0, 0))
+    stat = pl.BlockSpec((1, 1, rows_q), lambda h, lo, hi: (h, 0, 0))
+    col = pl.BlockSpec((rows_k, 1), lambda h, lo, hi: (0, 0))
+    row = pl.BlockSpec((1, rows_q), lambda h, lo, hi: (0, 0))
+    flops = int(heads * rows_q * rows_k * HEAD * 2 * 2 * 0.6)
     return pl.pallas_call(
         _fwd_kernel,
         out_shape=(
-            jax.ShapeDtypeStruct((heads, HEAD, rows), jnp.bfloat16),
-            jax.ShapeDtypeStruct((heads, HEAD, rows), jnp.float32),
-            jax.ShapeDtypeStruct((heads, 1, rows), jnp.float32),
+            jax.ShapeDtypeStruct((heads, HEAD, rows_q), jnp.bfloat16),
+            jax.ShapeDtypeStruct((heads, HEAD, rows_q), jnp.float32),
+            jax.ShapeDtypeStruct((heads, 1, rows_q), jnp.float32),
         ),
         grid_spec=pltpu.PrefetchScalarGridSpec(
             num_scalar_prefetch=2,
             grid=(heads,),
-            in_specs=[col, row, flipped, plain, flipped],
-            out_specs=[flipped, flipped, stat],
+            in_specs=[col, row, flipped_q, plain_k, flipped_k],
+            out_specs=[flipped_q, flipped_q, stat],
         ),
         compiler_params=pltpu.CompilerParams(
             dimension_semantics=("arbitrary",), vmem_limit_bytes=48 * 1024 * 1024),
         cost_estimate=pl.CostEstimate(
-            flops=flops, transcendentals=int(heads * rows * rows * 0.6),
-            bytes_accessed=int(heads * rows * HEAD * (2 * 4 + 4) + heads * rows * 4)),
+            flops=flops, transcendentals=int(heads * rows_q * rows_k * 0.6),
+            bytes_accessed=int(heads * HEAD * (rows_q * 8 + rows_k * 4))),
         name="segment_flash_fwd",
-    )(lo, hi, segments.reshape(rows, 1), segments.reshape(1, rows),
-      q.transpose(0, 2, 1), k, v.transpose(0, 2, 1))
+    )(lo, hi, seg_k.reshape(rows_k, 1), seg_q.reshape(1, rows_q), qt, k, vt)
 
 
 def flash_backward(q, k, v, do, o32t, lse, segments, lo, hi):
@@ -253,7 +258,7 @@
     ).astype(jnp.bfloat16)
 
     def to_heads(values):
-        return values.reshape(row_count, heads_here, HEAD).transpose(1, 0, 2)
+        return values.reshape(values.shape[0], heads_here, HEAD).transpose(1, 0, 2)
 
     def from_heads(values):
         return values.transpose(1, 0, 2).reshape(row_count, local_cols)
@@ -262,47 +267,89 @@
     query_heads = to_heads(queries)
     key_heads = to_heads(key_rows)
     value_heads = to_heads(value_rows)
-    out_heads, out_f32, log_norms = flash_forward(
-        query_heads, key_heads, value_heads, segments, lo_blocks, hi_blocks
-    )
-    attended = out_heads.transpose(2, 0, 1).reshape(row_count, local_cols)
-    attention_sum = mp_allreduce(
-        jnp.dot(attended, w_out, preferred_element_type=jnp.float32).astype(jnp.bfloat16), n_mp,
-    )
-    middle = inputs + attention_sum + b_out
-    norm_two, norm_two_back = jax.vjp(normalize, middle, ln2_gain, ln2_bias)
-    normed_two = norm_two.astype(jnp.bfloat16)
-    hidden_pre = jnp.dot(normed_two, w_fc1, preferred_element_type=jnp.float32) + b_fc1
-    activated_full, gelu_back = jax.vjp(exact_gelu, hidden_pre)
-    activated = activated_full.astype(jnp.bfloat16)
-    mlp_partial = jnp.dot(activated, w_fc2, preferred_element_type=jnp.float32).astype(jnp.bfloat16)
+    query_t = queries.reshape(row_count, heads_here, HEAD).transpose(1, 2, 0)
+    value_t = value_rows.reshape(row_count, heads_here, HEAD).transpose(1, 2, 0)
     upstream = cotangent.astype(jnp.float32)
+    q_blocks = row_count // TQ
+    first_blocks = (q_blocks * 3) // 8
+    bounds = [(0, first_blocks), (first_blocks, q_blocks)]
+    pieces_fwd = []
+    for b0, b1 in bounds:
+        rows = slice(b0 * TQ, b1 * TQ)
+        out_t, out32_t, lse_h = flash_forward(
+            query_t[:, :, rows], key_heads, value_t, segments[rows], segments,
+            lo_blocks[b0:b1], hi_blocks[b0:b1],
+        )
+        attended_h = out_t.transpose(2, 0, 1).reshape((b1 - b0) * TQ, local_cols)
+        att_sum_h = mp_allreduce(
+            jnp.dot(attended_h, w_out, preferred_element_type=jnp.float32).astype(jnp.bfloat16),
+            n_mp,
+        )
+        middle_h = inputs[rows] + att_sum_h + b_out
+        norm_two_h, back_two_h = jax.vjp(normalize, middle_h, ln2_gain, ln2_bias)
+        normed_two_h = norm_two_h.astype(jnp.bfloat16)
+        hidden_pre_h = jnp.dot(normed_two_h, w_fc1, preferred_element_type=jnp.float32) + b_fc1
+        act_h, gelu_back_h = jax.vjp(exact_gelu, hidden_pre_h)
+        activated_h = act_h.astype(jnp.bfloat16)
+        mlp_partial_h = jnp.dot(
+            activated_h, w_fc2, preferred_element_type=jnp.float32
+        ).astype(jnp.bfloat16)
+        pieces_fwd.append(dict(
+            rows=rows, out32_t=out32_t, lse=lse_h, attended=attended_h, middle=middle_h,
+            back_two=back_two_h, normed_two=normed_two_h, gelu_back=gelu_back_h,
+            activated=activated_h, mlp_partial=mlp_partial_h,
+        ))
     grad_b_fc2 = jnp.sum(upstream, axis=0)
+    for piece in pieces_fwd:
+        d_act_h = jnp.einsum(
+            "td,fd->tf", cotangent[piece["rows"]], w_fc2, preferred_element_type=jnp.float32
+        )
+        d_pre_h = piece["gelu_back"](d_act_h)[0]
+        piece["b_fc1"] = jnp.sum(d_pre_h, axis=0)
+        piece["d_pre_low"] = d_pre_h.astype(jnp.bfloat16)
+        piece["dn_two_partial"] = jnp.einsum(
+            "tf,df->td", piece["d_pre_low"], w_fc1, preferred_element_type=jnp.float32
+        ).astype(jnp.bfloat16)
+    activated = jnp.concatenate([p["activated"] for p in pieces_fwd], axis=0)
+    normed_two = jnp.concatenate([p["normed_two"] for p in pieces_fwd], axis=0)
+    d_pre_low = jnp.concatenate([p["d_pre_low"] for p in pieces_fwd], axis=0)
+    grad_b_fc1 = sum(p["b_fc1"] for p in pieces_fwd)
     grad_w_fc2 = jnp.einsum("tf,td->fd", activated, cotangent, preferred_element_type=jnp.float32)
-    d_act = jnp.einsum("td,fd->tf", cotangent, w_fc2, preferred_element_type=jnp.float32)
-    d_pre = gelu_back(d_act)[0]
-    grad_b_fc1 = jnp.sum(d_pre, axis=0)
-    d_pre_low = d_pre.astype(jnp.bfloat16)
     grad_w_fc1_t = jnp.einsum("tf,td->fd", d_pre_low, normed_two, preferred_element_type=jnp.float32)
-    dn_two_partial = jnp.einsum(
-        "tf,df->td", d_pre_low, w_fc1, preferred_element_type=jnp.float32
-    ).astype(jnp.bfloat16)
     mlp_weight_grads = jnp.concatenate([grad_w_fc2, grad_w_fc1_t], axis=0).astype(jnp.bfloat16)
-    mlp_weight_grads, dn_two_partial = lax.optimization_barrier((mlp_weight_grads, dn_two_partial))
+    mlp_weight_grads, pieces_fwd[-1]["dn_two_partial"] = lax.optimization_barrier(
+        (mlp_weight_grads, pieces_fwd[-1]["dn_two_partial"])
+    )
     summed_mlp = lax.psum_scatter(mlp_weight_grads, "dp", scatter_dimension=1, tiled=True)
-    d_normed_two = mp_allreduce(dn_two_partial, n_mp)
-    d_middle_norm, grad_ln2_gain, grad_ln2_bias = norm_two_back(d_normed_two)
-    d_middle = upstream + d_middle_norm
-    mlp_partial, d_middle = lax.optimization_barrier((mlp_partial, d_middle))
-    mlp_sum = mp_allreduce(mlp_partial, n_mp)
-    output = (middle + mlp_sum + b_fc2).astype(jnp.bfloat16)
+    for piece in pieces_fwd:
+        d_normed_two_h = mp_allreduce(piece["dn_two_partial"], n_mp)
+        d_mid_norm_h, gain_h, shift_h = piece["back_two"](d_normed_two_h)
+        piece["ln2_gain"] = gain_h
+        piece["ln2_bias"] = shift_h
+        piece["d_middle"] = upstream[piece["rows"]] + d_mid_norm_h
+        d_middle_low_h = piece["d_middle"].astype(jnp.bfloat16)
+        piece["d_middle_low"] = d_middle_low_h
+        piece["d_attended"] = jnp.einsum(
+            "td,cd->tc", d_middle_low_h, w_out, preferred_element_type=jnp.float32
+        ).astype(jnp.bfloat16)
+    grad_ln2_gain = sum(p["ln2_gain"] for p in pieces_fwd)
+    grad_ln2_bias = sum(p["ln2_bias"] for p in pieces_fwd)
+    d_middle = jnp.concatenate([p["d_middle"] for p in pieces_fwd], axis=0)
     grad_b_out = jnp.sum(d_middle, axis=0)
-    d_middle_low = d_middle.astype(jnp.bfloat16)
+    d_middle_low = jnp.concatenate([p["d_middle_low"] for p in pieces_fwd], axis=0)
+    attended = jnp.concatenate([p["attended"] for p in pieces_fwd], axis=0)
     grad_w_out = jnp.einsum("tc,td->cd", attended, d_middle_low, preferred_element_type=jnp.float32)
-    d_attended = jnp.einsum(
-        "td,cd->tc", d_middle_low, w_out, preferred_element_type=jnp.float32
-    ).astype(jnp.bfloat16)
+    d_attended = jnp.concatenate([p["d_attended"] for p in pieces_fwd], axis=0)
+    out_f32 = jnp.concatenate([p["out32_t"] for p in pieces_fwd], axis=2)
+    log_norms = jnp.concatenate([p["lse"] for p in pieces_fwd], axis=2)
     d_att_heads = to_heads(d_attended)
+    partials = lax.optimization_barrier(tuple(p["mlp_partial"] for p in pieces_fwd) + (d_att_heads,))
+    d_att_heads = partials[-1]
+    outputs = []
+    for h, piece in enumerate(pieces_fwd):
+        mlp_sum_h = mp_allreduce(partials[h], n_mp)
+        outputs.append((piece["middle"] + mlp_sum_h + b_fc2).astype(jnp.bfloat16))
+    output = jnp.concatenate(outputs, axis=0)
     d_q_heads, d_k_heads, d_v_heads = flash_backward(
         query_heads, key_heads, value_heads, d_att_heads, out_f32, log_norms,
         segments, lo_blocks, hi_blocks,
@@ -324,7 +371,9 @@
     grad_tokens = d_middle + d_input_norm
 
     def scatter(grad, dim):
-        return lax.psum_scatter(grad.astype(jnp.bfloat16), "dp", scatter_dimension=dim, tiled=True).astype(jnp.float32)
+        return lax.psum_scatter(
+            grad.astype(jnp.bfloat16), "dp", scatter_dimension=dim, tiled=True
+        ).astype(jnp.float32)
 
     tail_grads = jnp.concatenate(
         [grad_w_qkv_t.reshape(3 * local_cols, -1), grad_w_out], axis=0

time: 654 us -> 629 us (0.962)
  waiting for transfers between devices: 221 us -> 150 us
  matrix products: 87.9 us -> 106 us
  starting transfers between devices: 37.3 us -> 51 us
  local copies, waits for them, and re-layouts: 64.5 us -> 73 us
    ppermute x4 -> x7, waiting for transfers between devices: 175 us -> 99 us  [mp_allreduce(): got_far = lax.ppermute(first, 'mp', [(k, k ^ 2) for k in range(4)])]
    dot_general x6 -> x12, matrix products: 48.2 us -> 76.7 us  [the longest x2 45.1 us: per_device(): jnp.dot(normed_two_h, w_fc1, preferred_element_type=jnp.float32) + b_fc1]
    unnamed x4, waiting for transfers between devices: 29.5 us -> 43.7 us
    add x0 -> x1, other arithmetic: none -> 10.8 us  [per_device(): grad_tokens = d_middle + d_input_norm]
    convert_element_type x1 -> x8, other arithmetic: 10 us -> 20.6 us  [the longest x2 7.2 us: per_device(): outputs.append((piece['middle'] + mlp_sum_h + b_fc2).astype(jnp.bfloat16))]
    reduce_sum x1, other arithmetic: 8.14 us -> 0.68 us  [per_device(): grad_b_fc2 = jnp.sum(upstream, axis=0)]
    ppermute x4 -> x7, waiting for transfers between devices: 8.16 us -> 1.28 us  [mp_allreduce(): got = lax.ppermute(other, 'mp', [(k, k ^ 1) for k in range(4)])]
    ppermute x6, starting transfers between devices: 29.2 us -> 36 us  [dp_allreduce(): lax.ppermute(total, 'dp', [(k, k ^ step) for k in range(n_dp)])]
  transfers between devices with their start and end apart: 20 -> 29, of which waited for: 10 -> 10; matrix products, arithmetic and copies ran while one was open for 22% -> 38% of each run, Pallas kernels for 8% -> 14%
where the time goes in v3:
time: 629 us; the launch traced here: 618 us
  waiting for transfers between devices  150 us (24%)
  other arithmetic  123 us (20%)
  matrix products  106 us (17%)
  Pallas kernels  98.7 us (16%)
  local copies, waits for them, and re-layouts  73 us (12%)
  starting transfers between devices  51 us (8%)
  between operations  15.7 us (2%)
    ppermute x7, waiting for transfers between devices, mp_allreduce(): got_far = lax.ppermute(first, 'mp', [(k, k ^ 2) for k in range(4)])  99 us
    pallas_call x1, Pallas kernels, flash_backward(): pl.pallas_call(_bwd_kernel, out_shape=(jax.ShapeDtypeStruct((heads, HEAD,...  51.1 us
    pallas_call x2, Pallas kernels, flash_forward(): pl.pallas_call(_fwd_kernel, out_shape=(jax.ShapeDtypeStruct((heads, HEAD,...  47.6 us
    dot_general x2, matrix products, per_device(): jnp.dot(normed_two_h, w_fc1, preferred_element_type=jnp.float32) + b_fc1  45.1 us
    unnamed x4, waiting for transfers between devices  43.7 us
    unnamed x185, local copies, waits for them, and re-layouts  38.2 us
    ppermute x6, starting transfers between devices, dp_allreduce(): lax.ppermute(total, 'dp', [(k, k ^ step) for k in range(n_dp)])  36 us
    reduce_sum x6, other arithmetic, normalize(): return centered * lax.rsqrt(spread + 1e-06) * gain + shift  20 us
  transfers between devices with their start and end apart: 29, of which 10 were waited for; matrix products, arithmetic and copies ran while one was open for 38% of the time, Pallas kernels for 14%

profile of v3, /device:TPU:0, one launch (start us, length us, event | category | flops | bytes accessed | tf_op | source)
XLA Modules:
  0.0 618.2 jit_solution(3880629396130925676)
XLA Ops:
  12.4 3.0 convert_reduce_fusion.2
  20.1 2.4 convolution_convert_fusion.4
  23.8 2.8 copy.96.k_ref
  26.5 4.6 fusion.49
  35.9 15.2 %segment_flash_fwd.2 = (bf16[4,64,768]{2,1,0:T(8,128)(2,1)S(1)}, f32[4,64,768]{2,1,0:T(8,128)S(1)}, f32[4,1,768]{2,1,0:T(1,128)S(1)}) custom-call(s32[3]{0:T(128)S(1)} %bitcast.118, s32[3]{0:T(128)S(1)} %bitcast.119, s32[2048,1]{1,0:T(8,128)S(1)} %copy-done.10, s32[1,768]{1,0:T(1,128)S(1)} %reshape.216.segr_ref, bf16[4,64,768]{2,1,0:T(8,128)(2,1)S(1)} %slice.149.qt_ref, ...), custom_call_target="tpu_custom_call" | custom-call | flops 966367616 | bytes 3670016 | tf_op jit(solution)/shard_map/segment_flash_fwd/pallas_call | solution.py:130
  55.1 2.1 constant_dynamic-slice_fusion.6
  62.3 32.4 %segment_flash_fwd.3 = (bf16[4,64,1280]{2,1,0:T(8,128)(2,1)S(1)}, f32[4,64,1280]{2,1,0:T(8,128)S(1)}, f32[4,1,1280]{2,1,0:T(1,128)S(1)}) custom-call(s32[5]{0:T(128)S(1)} %slice.122.lo_ref, s32[5]{0:T(128)S(1)} %slice.123.hi_ref, s32[2048,1]{1,0:T(8,128)S(1)} %copy-done.11, s32[1,1280]{1,0:T(1,128)S(1)} %reshape.221.segr_ref, ...), custom_call_target="tpu_custom_call" | custom-call | flops 1610612736 | bytes 4718592 | tf_op jit(solution)/shard_map/segment_flash_fwd/pallas_call | solution.py:130
  95.8 2.6 add_convert_fusion.18
  98.4 2.5 collective-permute-start.1
  100.9 2.3 convolution_convert_fusion
  103.2 2.5 constant_dynamic-slice_fusion.5
  106.0 13.5 %collective-permute-done.1 = bf16[384,1024]{1,0:T(8,128)(2,1)} collective-permute-done((bf16[384,1024]{1,0:T(8,128)(2,1)}, bf16[384,1024]{1,0:T(8,128)(2,1)}, u32[]{:S(2)}, u32[]{:S(2)}) %collective-permute-start.1) | collective-permute-done | bytes 786464 | tf_op jit(solution)/shard_map/ppermute | solution.py:207
  119.4 2.6 add_convert_fusion.17
  122.0 6.6 %convert_element_type.234 = f32[2048,1024]{1,0:T(8,128)} convert(bf16[2048,1024]{1,0:T(8,128)(2,1)} %param.17) | non-fusion elementwise | flops 2097152 | bytes 12582912 | tf_op jit(solution)/shard_map/convert_element_type | solution.py:247
  128.6 2.2 add_convert_fusion.12
  134.2 2.4 fusion.96
  138.3 17.9 %multiply_convert_fusion.1 = (bf16[768,1024]{1,0:T(8,128)(2,1)S(1)}, f32[768,1024]{1,0:T(8,128)S(1)}, f32[768,1024]{1,0:T(8,128)S(1)}) fusion(f32[1024]{0:T(1024)S(1)} %copy-done.79, bf16[768,1024]{1,0:T(8,128)(2,1)S(1)} %add_convert_fusion.6, bf16[1024,1024]{1,0:T(8,128)(2,1)S(1)} %copy-done), kind=kOutput, calls=%fused_computation.90 | convolution fusion | flops 1662517248 | bytes 11538432 | tf_op jit(solution)/shard_map/dot_general | solution.py:291
  156.1 6.0 collective-permute-done.4
  162.8 3.4 fusion.99
  172.5 27.3 %multiply_convert_fusion = (bf16[1280,1024]{1,0:T(8,128)(2,1)S(1)}, f32[1280,1024]{1,0:T(8,128)}, f32[1280,1024]{1,0:T(8,128)}) fusion(f32[1024]{0:T(1024)S(1)} %copy-done.79, bf16[1280,1024]{1,0:T(8,128)(2,1)S(1)} %add_convert_fusion.2, bf16[1024,1024]{1,0:T(8,128)(2,1)S(1)} %copy-done), kind=kOutput, calls=%fused_computation.31 | convolution fusion | flops 2770862080 | bytes 17829888 | tf_op jit(solution)/shard_map/dot_general | solution.py:291
  199.8 8.3 %fusion.98 = (f32[1024]{0:T(1024)S(1)}, bf16[1280,1024]{1,0:T(8,128)(2,1)S(1)}) fusion(f32[1280,1024]{1,0:T(8,128)} %get-tuple-element.131, bf16[1024,1024]{1,0:T(8,128)(2,1)S(1)} %copy-done.75, bf16[2048,1024]{1,0:T(8,128)(2,1)S(1)} %copy-done.31, f32[1280,1024]{1,0:T(8,128)} %get-tuple-element.166, f32[1024]{0:T(1024)S(1)} %copy-done.79), kind=kOutput, calls=%fused_computation.230 | convolution fusion | flops 2705325056 | bytes 17833984 | tf_op jit(solution)/shard_map/td,fd->tf/dot_general | solution.py:304
  208.1 4.6 fusion.50
  212.7 4.8 fusion.55
  217.5 2.5 pad_maximum_fusion
  220.0 3.1 convolution_convert_fusion.1
  227.9 4.4 convert_element_type.262
  234.2 2.7 copy.100
  239.7 2.9 convolution_convert_fusion.6
  242.6 3.3 collective-permute-done.7
  247.7 6.7 %copy.114 = bf16[2048,1024]{0,1:T(8,128)(2,1)} copy(bf16[2048,1024]{1,0:T(8,128)(2,1)} %pad_maximum_fusion) | data formatting | bytes 8388608
  254.5 2.4 add_convert_fusion.10
  258.7 6.3 %convolution_convert_fusion.2 = bf16[1280,1024]{1,0:T(8,128)(2,1)} fusion(bf16[1280,1024]{1,0:T(8,128)(2,1)} %copy-done.80, bf16[1024,1024]{1,0:T(8,128)(2,1)S(1)} %copy-done.77), kind=kOutput, calls=%fused_computation.78 | convolution fusion | flops 2685665280 | bytes 7340032 | tf_op jit(solution)/shard_map/dot_general | solution.py:294
  267.9 20.0 %collective-permute-done.10 = bf16[640,1024]{1,0:T(8,128)(2,1)S(1)} collective-permute-done((bf16[640,1024]{1,0:T(8,128)(2,1)S(1)}, bf16[640,1024]{1,0:T(8,128)(2,1)S(1)}, u32[]{:S(2)}, u32[]{:S(2)}) %collective-permute-start.10) | collective-permute-done | bytes 1310752 | tf_op jit(solution)/shard_map/ppermute | solution.py:207
  288.6 2.5 fusion.37
  297.9 2.4 fusion.7
  300.3 4.3 fusion.9
  304.6 3.3 fusion.90
  317.4 51.1 %segment_flash_bwd.1 = (f32[4,64,2048]{2,1,0:T(8,128)}, f32[4,2048,64]{2,1,0:T(8,128)}, f32[4,2048,64]{2,1,0:T(8,128)}) custom-call(s32[8]{0:T(128)S(1)} %fusion.81.lo_ref, s32[8]{0:T(128)S(1)} %copy-done.21, s32[2048,1]{1,0:T(8,128)S(1)} %copy-done.12, s32[1,2048]{1,0:T(1,128)S(1)} %bitcast.117, bf16[4,2048,64]{2,1,0:T(8,128)(2,1)} %copy.102.q_ref, ...), custom_call_target="tpu_custom_call" | custom-call | flops 5153960960 | bytes 15761408 | tf_op jit(solution)/shard_map/segment_flash_bwd/pallas_call | solution.py:156
  368.5 2.5 bitcast_convert_fusion.1
  373.2 2.5 convert_bitcast_fusion
  377.8 2.0 copy.115
  380.7 5.9 bitcast_convert_fusion
  388.9 2.2 copy-done.32
  395.9 20.6 %collective-permute-start.24 = (f32[5120]{0:T(1024)S(1)}, f32[5120]{0:T(1024)S(1)}, u32[]{:S(2)}, u32[]{:S(2)}) collective-permute-start(f32[5120]{0:T(1024)S(1)} %constant_dynamic-update-slice_fusion), channel_id=1, source_target_pairs={{0,4},{4,0},{8,12},{12,8},{16,20},{20,16},{24,28},{28,24},{1,5},{5... | collective-permute-start | bytes 61448 | tf_op jit(solution)/shard_map/ppermute | solution.py:221
  418.2 2.1 collective-permute-start.25
  420.4 4.5 add_convert_fusion.4
  425.5 2.6 add_convert_fusion.13
  431.3 2.0 fusion.65
  433.3 2.6 collective-permute-start.26
  440.2 3.6 add_convert_fusion.5
  443.8 56.1 %collective-permute-done.16 = bf16[640,1024]{1,0:T(8,128)(2,1)} collective-permute-done((bf16[640,1024]{1,0:T(8,128)(2,1)S(1)}, bf16[640,1024]{1,0:T(8,128)(2,1)}, u32[]{:S(2)}, u32[]{:S(2)}) %collective-permute-start.16) | collective-permute-done | bytes 1310752 | tf_op jit(solution)/shard_map/ppermute | solution.py:207
  500.0 3.0 add_convert_fusion.7
  503.0 4.7 add_convert_fusion.3
  508.0 3.7 fusion.58
  512.0 2.6 copy.116
  516.1 3.6 add_convert_fusion.1
  519.7 2.5 pad_maximum_fusion.1
  522.6 2.6 broadcast_select_fusion.1
  526.0 3.2 fusion.2
  529.2 7.0 %fusion.3 = (f32[1024]{0:T(1024)S(1)}, f32[2048]{0:T(1024)S(1)}, f32[1024]{0:T(1024)S(1)}) fusion(bf16[2048,1024]{1,0:T(8,128)(2,1)S(1)} %copy-done.24, f32[2048]{0:T(1024)S(1)} %copy-done.64, f32[2048]{0:T(1024)S(1)} %copy-done.61, bf16[1024,1024]{1,0:T(8,128)(2,1)S(1)} %get-tuple-element.141, bf16[1024,1024]{1,0:T(8,128)(2,1)S(1)} %get-tuple-element.140, ...), kind=kLoop, calls=%fused_computation.9 | loop fusion | flops 33550336 | bytes 8433664 | tf_op jit(solution)/shard_map/transpose(jvp())/reduce_sum | solution.py:184
  536.2 8.4 %collective-permute-start.21 = (f32[2560]{0:T(1024)S(1)}, f32[2560]{0:T(1024)S(1)}, u32[]{:S(2)}, u32[]{:S(2)}) collective-permute-start(f32[2560]{0:T(1024)S(1)} %pad_maximum_fusion.12), channel_id=1, source_target_pairs={{0,4},{4,0},{8,12},{12,8},{16,20},{20,16},{24,28},{28,24},{1,5},{5... | collective-permute-start | bytes 30728 | tf_op jit(solution)/shard_map/ppermute | solution.py:221
  546.5 43.7 %reduce-scatter.9.cloned.1.call-done = bf16[128,1024]{1,0:T(8,128)(2,1)} async-done(((bf16[1024,1024]{1,0:T(8,128)(2,1)}), bf16[128,1024]{1,0:T(8,128)(2,1)}) %reduce-scatter.9.cloned.1.call-update) | async-done | bytes 262160
  594.8 2.8 collective-permute-done.22
  598.9 10.8 %maximum_add_fusion = f32[2048,1024]{1,0:T(8,128)} fusion(f32[1280,1024]{1,0:T(8,128)} %copy-done.27, f32[768,1024]{1,0:T(8,128)} %copy-done.30, bf16[2048,1024]{1,0:T(8,128)(2,1)} %param.17, f32[2048]{0:T(1024)S(1)} %negate_multiply_fusion.2, f32[2048]{0:T(1024)S(1)} %multiply_multiply_fusion.10, f32[1024]{0:T(1024)S(1)} %copy-done.68, ...), kind=kLoop, calls=%fused_computation.10 | loop fusion | flops 29360128 | bytes 25202688 | tf_op jit(solution)/shard_map/add | solution.py:371
  (340 shorter events, 104.8 us)
Async XLA Ops:
  7.2 131.1 %copy-start = (bf16[1024,1024]{1,0:T(8,128)(2,1)S(1)}, bf16[1024,1024]{1,0:T(8,128)(2,1)}, u32[]{:S(2)}) copy-start(bf16[1024,1024]{1,0:T(8,128)(2,1)} %param.24) | copy-start | bytes 6291460
  7.2 370.6 %reduce-scatter.7.cloned.1.call-start = ((), (), s32[]{:S(2)}) async-start(), calls=%async_computation.2 | async-start | bytes 4718592
  35.9 17.4 %copy-start.49 = (bf16[256,1024]{1,0:T(8,128)(2,1)S(1)}, bf16[256,1024]{1,0:T(8,128)(2,1)}, u32[]{:S(2)}) copy-start(bf16[256,1024]{1,0:T(8,128)(2,1)} %param.22) | copy-start | bytes 1572868
  52.6 5.2 copy-start.21
  57.2 38.6 %collective-permute-start = (bf16[384,1024]{1,0:T(8,128)(2,1)}, bf16[384,1024]{1,0:T(8,128)(2,1)}, u32[]{:S(2)}, u32[]{:S(2)}) collective-permute-start(bf16[384,1024]{1,0:T(8,128)(2,1)} %constant_dynamic-slice_fusion.6), channel_id=1, source_target_pairs={{0,1},{1,0},{2,3},{3,2},{4,5},{5,4},{6,7},{7,6},{8,9},{9,8},{10,11... | collective-permute-start | bytes 2359304 | tf_op jit(solution)/shard_map/ppermute | solution.py:205
  62.3 33.6 %copy-start.37 = (bf16[768,1024]{1,0:T(8,128)(2,1)S(1)}, bf16[768,1024]{1,0:T(8,128)(2,1)}, u32[]{:S(2)}) copy-start(bf16[768,1024]{1,0:T(8,128)(2,1)} %convolution_convert_fusion.7) | copy-start | bytes 4718596
  62.3 38.6 %copy-start.50 = (bf16[256,1024]{1,0:T(8,128)(2,1)S(1)}, bf16[256,1024]{1,0:T(8,128)(2,1)}, u32[]{:S(2)}) copy-start(bf16[256,1024]{1,0:T(8,128)(2,1)} %param.22) | copy-start | bytes 1572868
  95.8 5.1 copy-start.2
  98.4 21.0 %collective-permute-start.1 = (bf16[384,1024]{1,0:T(8,128)(2,1)}, bf16[384,1024]{1,0:T(8,128)(2,1)}, u32[]{:S(2)}, u32[]{:S(2)}) collective-permute-start(bf16[384,1024]{1,0:T(8,128)(2,1)} %add_convert_fusion.18), channel_id=1, source_target_pairs={{0,2},{1,3},{2,0},{3,1},{4,6},{5,7},{6,4},{7,5},{8,10},{9,11},{10,... | collective-permute-start | bytes 2359304 | tf_op jit(solution)/shard_map/ppermute | solution.py:207
  105.7 22.9 %collective-permute-start.3 = (bf16[640,1024]{1,0:T(8,128)(2,1)}, bf16[640,1024]{1,0:T(8,128)(2,1)}, u32[]{:S(2)}, u32[]{:S(2)}) collective-permute-start(bf16[640,1024]{1,0:T(8,128)(2,1)} %constant_dynamic-slice_fusion.5), channel_id=1, source_target_pairs={{0,1},{1,0},{2,3},{3,2},{4,5},{5,4},{6,7},{7,6},{8,9},{9,8},{10,11... | collective-permute-start | bytes 3932168 | tf_op jit(solution)/shard_map/ppermute | solution.py:205
  122.0 10.7 %collective-permute-start.2 = (bf16[384,1024]{1,0:T(8,128)(2,1)}, bf16[384,1024]{1,0:T(8,128)(2,1)}, u32[]{:S(2)}, u32[]{:S(2)}) collective-permute-start(bf16[384,1024]{1,0:T(8,128)(2,1)} %add_convert_fusion.17), channel_id=1, source_target_pairs={{0,1},{1,0},{2,3},{3,2},{4,5},{5,4},{6,7},{7,6},{8,9},{9,8},{10,11... | collective-permute-start | bytes 2359304 | tf_op jit(solution)/shard_map/ppermute | solution.py:209
  128.6 5.6 copy-start.69
  130.9 31.3 %collective-permute-start.4 = (bf16[640,1024]{1,0:T(8,128)(2,1)S(1)}, bf16[640,1024]{1,0:T(8,128)(2,1)S(1)}, u32[]{:S(2)}, u32[]{:S(2)}) collective-permute-start(bf16[640,1024]{1,0:T(8,128)(2,1)S(1)} %add_convert_fusion.12), channel_id=1, source_target_pairs={{0,2},{1,3},{2,0},{3,1},{4,6},{5,7},{6,4},{7,5},{8,10},{9,11},{10,... | collective-permute-start | bytes 3932168 | tf_op jit(solution)/shard_map/ppermute | solution.py:207
  138.3 24.5 %copy-start.31 = (bf16[2048,1024]{1,0:T(8,128)(2,1)S(1)}, bf16[2048,1024]{1,0:T(8,128)(2,1)}, u32[]{:S(2)}) copy-start(bf16[2048,1024]{1,0:T(8,128)(2,1)} %param.18) | copy-start | bytes 12582916
  156.1 56.6 %copy-start.81 = (bf16[768,1024]{1,0:T(8,128)(2,1)}, bf16[768,1024]{1,0:T(8,128)(2,1)S(1)}, u32[]{:S(2)}) copy-start(bf16[768,1024]{1,0:T(8,128)(2,1)S(1)} %get-tuple-element.134) | copy-start | bytes 4718596
  156.1 6.6 %copy-start.75 = (bf16[1024,1024]{1,0:T(8,128)(2,1)S(1)}, bf16[1024,1024]{1,0:T(8,128)(2,1)}, u32[]{:S(2)}) copy-start(bf16[1024,1024]{1,0:T(8,128)(2,1)} %param.26) | copy-start | bytes 6291460
  162.7 6.0 collective-permute-start.5
  168.1 56.8 %collective-permute-start.6 = (bf16[384,1024]{1,0:T(8,128)(2,1)S(1)}, bf16[384,1024]{1,0:T(8,128)(2,1)S(1)}, u32[]{:S(2)}, u32[]{:S(2)}) collective-permute-start(bf16[384,1024]{1,0:T(8,128)(2,1)S(1)} %constant_dynamic-slice_fusion.4), channel_id=1, source_target_pairs={{0,1},{1,0},{2,3},{3,2},{4,5},{5,4},{6,7},{7,6},{8,9},{9,8},{10,11... | collective-permute-start | bytes 2359304 | tf_op jit(solution)/shard_map/ppermute | solution.py:205
  170.6 29.1 %copy-start.22 = (f32[1280,1024]{1,0:T(8,128)}, f32[1280,1024]{1,0:T(8,128)S(1)}, u32[]{:S(2)}) copy-start(f32[1280,1024]{1,0:T(8,128)S(1)} %get-tuple-element.133) | copy-start | bytes 15728644
  199.8 13.0 %copy-start.80 = (bf16[1280,1024]{1,0:T(8,128)(2,1)}, bf16[1280,1024]{1,0:T(8,128)(2,1)S(1)}, u32[]{:S(2)}) copy-start(bf16[1280,1024]{1,0:T(8,128)(2,1)S(1)} %get-tuple-element.130) | copy-start | bytes 7864324
  223.1 4.8 copy-start.46
  223.1 4.7 copy-start.19
  224.4 30.0 %collective-permute-start.9 = (bf16[640,1024]{1,0:T(8,128)(2,1)}, bf16[640,1024]{1,0:T(8,128)(2,1)}, u32[]{:S(2)}, u32[]{:S(2)}) collective-permute-start(bf16[640,1024]{1,0:T(8,128)(2,1)} %constant_dynamic-slice_fusion.3), channel_id=1, source_target_pairs={{0,1},{1,0},{2,3},{3,2},{4,5},{5,4},{6,7},{7,6},{8,9},{9,8},{10,11... | collective-permute-start | bytes 3932168 | tf_op jit(solution)/shard_map/ppermute | solution.py:205
  226.1 19.8 %collective-permute-start.7 = (bf16[384,1024]{1,0:T(8,128)(2,1)}, bf16[384,1024]{1,0:T(8,128)(2,1)}, u32[]{:S(2)}, u32[]{:S(2)}) collective-permute-start(bf16[384,1024]{1,0:T(8,128)(2,1)} %add_convert_fusion.16), channel_id=1, source_target_pairs={{0,2},{1,3},{2,0},{3,1},{4,6},{5,7},{6,4},{7,5},{8,10},{9,11},{10,... | collective-permute-start | bytes 2359304 | tf_op jit(solution)/shard_map/ppermute | solution.py:207
  232.4 4.5 copy-start.6
  232.4 4.5 copy-start.14
  247.6 6.8 %copy-start.42 = (bf16[384,1024]{1,0:T(8,128)(2,1)}, bf16[384,1024]{1,0:T(8,128)(2,1)S(1)}, u32[]{:S(2)}) copy-start(bf16[384,1024]{1,0:T(8,128)(2,1)S(1)} %add_convert_fusion.15) | copy-start | bytes 2359300
  247.6 17.4 %collective-permute-start.8 = (bf16[384,1024]{1,0:T(8,128)(2,1)S(1)}, bf16[384,1024]{1,0:T(8,128)(2,1)}, u32[]{:S(2)}, u32[]{:S(2)}) collective-permute-start(bf16[384,1024]{1,0:T(8,128)(2,1)S(1)} %add_convert_fusion.15), channel_id=1, source_target_pairs={{0,1},{1,0},{2,3},{3,2},{4,5},{5,4},{6,7},{7,6},{8,9},{9,8},{10,11... | collective-permute-start | bytes 2359304 | tf_op jit(solution)/shard_map/ppermute | solution.py:209
  254.4 335.8 %reduce-scatter.9.cloned.1.call-start = ((), (), s32[]{:S(2)}) async-start(), calls=%async_computation.3 | async-start | bytes 2359296
  254.5 36.6 %slice-start.4 = ((s8[8388608]{0:T(1024)(128)(4,1)}), s8[4194304]{0:T(1024)(128)(4,1)S(1)}, s32[]{:S(2)}) async-start(s8[8388608]{0:T(1024)(128)(4,1)} %bitcast.126), calls=%async_computation.8 | async-start | bytes 8388608
  256.9 8.2 %copy-start.43 = (bf16[384,1024]{1,0:T(8,128)(2,1)S(1)}, bf16[384,1024]{1,0:T(8,128)(2,1)}, u32[]{:S(2)}) copy-start(bf16[384,1024]{1,0:T(8,128)(2,1)} %copy-done.42) | copy-start | bytes 2359300
  256.9 34.2 %slice-start.5 = ((s8[8388608]{0:T(1024)(128)(4,1)}), s8[4194304]{0:T(1024)(128)(4,1)S(1)}, s32[]{:S(2)}) async-start(s8[8388608]{0:T(1024)(128)(4,1)} %bitcast.126), calls=%async_computation.9 | async-start | bytes 8388608
  256.9 31.0 %collective-permute-start.10 = (bf16[640,1024]{1,0:T(8,128)(2,1)S(1)}, bf16[640,1024]{1,0:T(8,128)(2,1)S(1)}, u32[]{:S(2)}, u32[]{:S(2)}) collective-permute-start(bf16[640,1024]{1,0:T(8,128)(2,1)S(1)} %add_convert_fusion.10), channel_id=1, source_target_pairs={{0,2},{1,3},{2,0},{3,1},{4,6},{5,7},{6,4},{7,5},{8,10},{9,11},{10,... | collective-permute-start | bytes 3932168 | tf_op jit(solution)/shard_map/ppermute | solution.py:207
  288.5 7.7 %collective-permute-start.11 = (bf16[640,1024]{1,0:T(8,128)(2,1)S(1)}, bf16[640,1024]{1,0:T(8,128)(2,1)S(1)}, u32[]{:S(2)}, u32[]{:S(2)}) collective-permute-start(bf16[640,1024]{1,0:T(8,128)(2,1)S(1)} %add_convert_fusion.9), channel_id=1, source_target_pairs={{0,1},{1,0},{2,3},{3,2},{4,5},{5,4},{6,7},{7,6},{8,9},{9,8},{10,11... | collective-permute-start | bytes 3932168 | tf_op jit(solution)/shard_map/ppermute | solution.py:209
  380.7 5.9 copy-start.57
  380.7 8.0 %copy-start.52 = (bf16[768,1024]{1,0:T(8,128)(2,1)S(1)}, bf16[768,1024]{1,0:T(8,128)(2,1)}, u32[]{:S(2)}) copy-start(bf16[768,1024]{1,0:T(8,128)(2,1)} %convolution_convert_fusion.6) | copy-start | bytes 4718596
  386.7 5.1 copy-start.41
  388.2 32.1 %collective-permute-start.18 = (bf16[1024,1024]{1,0:T(8,128)(2,1)}, bf16[1024,1024]{1,0:T(8,128)(2,1)}, u32[]{:S(2)}, u32[]{:S(2)}) collective-permute-start(bf16[1024,1024]{1,0:T(8,128)(2,1)} %constant_dynamic-slice_fusion), channel_id=1, source_target_pairs={{0,1},{1,0},{2,3},{3,2},{4,5},{5,4},{6,7},{7,6},{8,9},{9,8},{10,11... | collective-permute-start | bytes 6291464 | tf_op jit(solution)/shard_map/ppermute | solution.py:205
  388.7 5.1 collective-permute-start.12
  392.0 36.1 %collective-permute-start.15 = (bf16[640,1024]{1,0:T(8,128)(2,1)S(1)}, bf16[640,1024]{1,0:T(8,128)(2,1)}, u32[]{:S(2)}, u32[]{:S(2)}) collective-permute-start(bf16[640,1024]{1,0:T(8,128)(2,1)S(1)} %constant_dynamic-slice_fusion.1), channel_id=1, source_target_pairs={{0,1},{1,0},{2,3},{3,2},{4,5},{5,4},{6,7},{7,6},{8,9},{9,8},{10,11... | collective-permute-start | bytes 3932168 | tf_op jit(solution)/shard_map/ppermute | solution.py:205
  394.1 31.4 %collective-permute-start.13 = (bf16[384,1024]{1,0:T(8,128)(2,1)S(1)}, bf16[384,1024]{1,0:T(8,128)(2,1)}, u32[]{:S(2)}, u32[]{:S(2)}) collective-permute-start(bf16[384,1024]{1,0:T(8,128)(2,1)S(1)} %add_convert_fusion.14), channel_id=1, source_target_pairs={{0,2},{1,3},{2,0},{3,1},{4,6},{5,7},{6,4},{7,5},{8,10},{9,11},{10,... | collective-permute-start | bytes 2359304 | tf_op jit(solution)/shard_map/ppermute | solution.py:207
  395.9 22.3 %collective-permute-start.24 = (f32[5120]{0:T(1024)S(1)}, f32[5120]{0:T(1024)S(1)}, u32[]{:S(2)}, u32[]{:S(2)}) collective-permute-start(f32[5120]{0:T(1024)S(1)} %constant_dynamic-update-slice_fusion), channel_id=1, source_target_pairs={{0,4},{4,0},{8,12},{12,8},{16,20},{20,16},{24,28},{28,24},{1,5},{5... | collective-permute-start | bytes 61448 | tf_op jit(solution)/shard_map/ppermute | solution.py:221
  418.2 9.8 %copy-start.45 = (bf16[1280,1024]{1,0:T(8,128)(2,1)S(1)}, bf16[1280,1024]{1,0:T(8,128)(2,1)}, u32[]{:S(2)}) copy-start(bf16[1280,1024]{1,0:T(8,128)(2,1)} %convolution_convert_fusion.2) | copy-start | bytes 7864324
  418.2 15.1 %collective-permute-start.25 = (f32[5120]{0:T(1024)S(1)}, f32[5120]{0:T(1024)S(1)}, u32[]{:S(2)}, u32[]{:S(2)}) collective-permute-start(f32[5120]{0:T(1024)S(1)} %add.334), channel_id=1, source_target_pairs={{0,8},{4,12},{8,0},{12,4},{16,24},{20,28},{24,16},{28,20},{1,9},{5... | collective-permute-start | bytes 61448 | tf_op jit(solution)/shard_map/ppermute | solution.py:221
  424.9 6.4 %copy-start.3 = (bf16[4,64,1280]{2,1,0:T(8,128)(2,1)S(1)}, bf16[4,64,1280]{2,1,0:T(8,128)(2,1)}, u32[]{:S(2)}) copy-start(bf16[4,64,1280]{2,1,0:T(8,128)(2,1)} %copy-done.2) | copy-start | bytes 1966084
  424.9 6.4 %copy-start.17 = (bf16[4,64,768]{2,1,0:T(8,128)(2,1)S(1)}, bf16[4,64,768]{2,1,0:T(8,128)(2,1)}, u32[]{:S(2)}) copy-start(bf16[4,64,768]{2,1,0:T(8,128)(2,1)} %copy-done.16) | copy-start | bytes 1179652
  424.9 6.4 %copy-start.48 = (bf16[1280,1024]{1,0:T(8,128)(2,1)S(1)}, bf16[1280,1024]{1,0:T(8,128)(2,1)}, u32[]{:S(2)}) copy-start(bf16[1280,1024]{1,0:T(8,128)(2,1)} %copy-done.47) | copy-start | bytes 7864324
  424.9 6.4 %copy-start.54 = (bf16[768,1024]{1,0:T(8,128)(2,1)S(1)}, bf16[768,1024]{1,0:T(8,128)(2,1)}, u32[]{:S(2)}) copy-start(bf16[768,1024]{1,0:T(8,128)(2,1)} %copy-done.53) | copy-start | bytes 4718596
  424.9 78.1 %collective-permute-start.19 = (bf16[1024,1024]{1,0:T(8,128)(2,1)}, bf16[1024,1024]{1,0:T(8,128)(2,1)}, u32[]{:S(2)}, u32[]{:S(2)}) collective-permute-start(bf16[1024,1024]{1,0:T(8,128)(2,1)} %add_convert_fusion.4), channel_id=1, source_target_pairs={{0,2},{1,3},{2,0},{3,1},{4,6},{5,7},{6,4},{7,5},{8,10},{9,11},{10,... | collective-permute-start | bytes 6291464 | tf_op jit(solution)/shard_map/ppermute | solution.py:207
  428.1 10.6 %collective-permute-start.14 = (bf16[384,1024]{1,0:T(8,128)(2,1)}, bf16[384,1024]{1,0:T(8,128)(2,1)}, u32[]{:S(2)}, u32[]{:S(2)}) collective-permute-start(bf16[384,1024]{1,0:T(8,128)(2,1)} %add_convert_fusion.13), channel_id=1, source_target_pairs={{0,1},{1,0},{2,3},{3,2},{4,5},{5,4},{6,7},{7,6},{8,9},{9,8},{10,11... | collective-permute-start | bytes 2359304 | tf_op jit(solution)/shard_map/ppermute | solution.py:209
  429.9 6.0 copy-start.33
  430.0 70.0 %collective-permute-start.16 = (bf16[640,1024]{1,0:T(8,128)(2,1)S(1)}, bf16[640,1024]{1,0:T(8,128)(2,1)}, u32[]{:S(2)}, u32[]{:S(2)}) collective-permute-start(bf16[640,1024]{1,0:T(8,128)(2,1)S(1)} %add_convert_fusion.8), channel_id=1, source_target_pairs={{0,2},{1,3},{2,0},{3,1},{4,6},{5,7},{6,4},{7,5},{8,10},{9,11},{10,... | collective-permute-start | bytes 3932168 | tf_op jit(solution)/shard_map/ppermute | solution.py:207
  433.3 6.9 %copy-start.71 = (f32[1024]{0:T(1024)S(1)}, f32[1024]{0:T(1024)}, u32[]{:S(2)}) copy-start(f32[1024]{0:T(1024)} %param.27) | copy-start | bytes 12292
  433.3 4.7 collective-permute-start.26
  500.0 8.0 %copy-start.58 = (bf16[1,2048,256]{2,1,0:T(8,128)(2,1)S(1)}, bf16[1,2048,256]{2,1,0:T(8,128)(2,1)}, u32[]{:S(2)}) copy-start(bf16[1,2048,256]{2,1,0:T(8,128)(2,1)} %copy-done.57) | copy-start | bytes 3145732
  503.0 5.0 copy-start.40
  503.0 5.0 copy-start.55
  503.0 5.0 copy-start.56
  503.0 11.6 %collective-permute-start.17 = (bf16[640,1024]{1,0:T(8,128)(2,1)}, bf16[640,1024]{1,0:T(8,128)(2,1)S(1)}, u32[]{:S(2)}, u32[]{:S(2)}) collective-permute-start(bf16[640,1024]{1,0:T(8,128)(2,1)} %add_convert_fusion.7), channel_id=1, source_target_pairs={{0,1},{1,0},{2,3},{3,2},{4,5},{5,4},{6,7},{7,6},{8,9},{9,8},{10,11... | collective-permute-start | bytes 3932168 | tf_op jit(solution)/shard_map/ppermute | solution.py:209
  507.7 14.9 %collective-permute-start.20 = (bf16[1024,1024]{1,0:T(8,128)(2,1)}, bf16[1024,1024]{1,0:T(8,128)(2,1)}, u32[]{:S(2)}, u32[]{:S(2)}) collective-permute-start(bf16[1024,1024]{1,0:T(8,128)(2,1)} %add_convert_fusion.3), channel_id=1, source_target_pairs={{0,1},{1,0},{2,3},{3,2},{4,5},{5,4},{6,7},{7,6},{8,9},{9,8},{10,11... | collective-permute-start | bytes 6291464 | tf_op jit(solution)/shard_map/ppermute | solution.py:209
  536.2 57.6 %collective-permute-start.21 = (f32[2560]{0:T(1024)S(1)}, f32[2560]{0:T(1024)S(1)}, u32[]{:S(2)}, u32[]{:S(2)}) collective-permute-start(f32[2560]{0:T(1024)S(1)} %pad_maximum_fusion.12), channel_id=1, source_target_pairs={{0,4},{4,0},{8,12},{12,8},{16,20},{20,16},{24,28},{28,24},{1,5},{5... | collective-permute-start | bytes 30728 | tf_op jit(solution)/shard_map/ppermute | solution.py:221
  593.9 3.8 collective-permute-start.22
  597.6 12.1 %collective-permute-start.23 = (f32[2560]{0:T(1024)S(1)}, f32[2560]{0:T(1024)S(1)}, u32[]{:S(2)}, u32[]{:S(2)}) collective-permute-start(f32[2560]{0:T(1024)S(1)} %add.329), channel_id=1, source_target_pairs={{0,16},{4,20},{8,24},{12,28},{16,0},{20,4},{24,8},{28,12},{1,17},{... | collective-permute-start | bytes 30728 | tf_op jit(solution)/shard_map/ppermute | solution.py:221
  598.9 12.1 %copy-start.1 = (bf16[1024,1024]{1,0:T(8,128)(2,1)S(1)}, bf16[1024,1024]{1,0:T(8,128)(2,1)}, u32[]{:S(2)}) copy-start(bf16[1024,1024]{1,0:T(8,128)(2,1)} %param.24) | copy-start | bytes 6291460
  (54 other events, 125.2 us)
Sparse Core Ops, SparseCore 0:
  254.5 98.3 reduce-scatter.6
  514.7 75.4 reduce-scatter.8

commit v4 on v3

--- a/solution.py
+++ b/solution.py
@@ -12,37 +12,47 @@
 NEG = -1e30
 
 
+HPS = 4
+
+
 def _fwd_kernel(lo_ref, hi_ref, segc_ref, segr_ref, qt_ref, k_ref, vt_ref, ot_ref, o32t_ref, lse_ref):
     rows = qt_ref.shape[2]
     scale = HEAD ** (-0.5)
 
     def q_body(i, carry):
         r0 = pl.multiple_of(i * TQ, TQ)
-        qt = qt_ref[0, :, pl.ds(r0, TQ)]
+        qts = [qt_ref[hh, :, pl.ds(r0, TQ)] for hh in range(HPS)]
         sq = segr_ref[:, pl.ds(r0, TQ)]
 
         def kv_body(j, state):
-            m, l, acc = state
             c0 = pl.multiple_of(j * TK, TK)
-            s = jnp.dot(k_ref[0, pl.ds(c0, TK), :], qt, preferred_element_type=jnp.float32) * scale
             same = segc_ref[pl.ds(c0, TK), :] == sq
-            s = jnp.where(same, s, NEG)
-            m_new = jnp.maximum(m, jnp.max(s, axis=0, keepdims=True))
-            p = jnp.exp(s - m_new)
-            alpha = jnp.exp(m - m_new)
-            l = alpha * l + jnp.sum(p, axis=0, keepdims=True)
-            pv = jnp.dot(vt_ref[0, :, pl.ds(c0, TK)], p.astype(jnp.bfloat16),
-                         preferred_element_type=jnp.float32)
-            return m_new, l, alpha * acc + pv
-
-        m0 = jnp.full((1, TQ), NEG, jnp.float32)
-        l0 = jnp.zeros((1, TQ), jnp.float32)
-        acc0 = jnp.zeros((HEAD, TQ), jnp.float32)
-        m, l, acc = lax.fori_loop(lo_ref[i], hi_ref[i], kv_body, (m0, l0, acc0))
-        out = acc / l
-        ot_ref[0, :, pl.ds(r0, TQ)] = out.astype(ot_ref.dtype)
-        o32t_ref[0, :, pl.ds(r0, TQ)] = out
-        lse_ref[0, :, pl.ds(r0, TQ)] = m + jnp.log(l)
+            new_state = []
+            for hh in range(HPS):
+                m, l, acc = state[hh]
+                s = jnp.dot(k_ref[hh, pl.ds(c0, TK), :], qts[hh], preferred_element_type=jnp.float32) * scale
+                s = jnp.where(same, s, NEG)
+                m_new = jnp.maximum(m, jnp.max(s, axis=0, keepdims=True))
+                p = jnp.exp(s - m_new)
+                alpha = jnp.exp(m - m_new)
+                l = alpha * l + jnp.sum(p, axis=0, keepdims=True)
+                pv = jnp.dot(vt_ref[hh, :, pl.ds(c0, TK)], p.astype(jnp.bfloat16),
+                             preferred_element_type=jnp.float32)
+                new_state.append((m_new, l, alpha * acc + pv))
+            return tuple(new_state)
+
+        init = tuple(
+            (jnp.full((1, TQ), NEG, jnp.float32), jnp.zeros((1, TQ), jnp.float32),
+             jnp.zeros((HEAD, TQ), jnp.float32))
+            for _ in range(HPS)
+        )
+        final = lax.fori_loop(lo_ref[i], hi_ref[i], kv_body, init)
+        for hh in range(HPS):
+            m, l, acc = final[hh]
+            out = acc / l
+            ot_ref[hh, :, pl.ds(r0, TQ)] = out.astype(ot_ref.dtype)
+            o32t_ref[hh, :, pl.ds(r0, TQ)] = out
+            lse_ref[hh, :, pl.ds(r0, TQ)] = m + jnp.log(l)
         return carry
 
     lax.fori_loop(0, rows // TQ, q_body, 0)
@@ -56,38 +66,44 @@
 
     def d_body(i, carry):
         r0 = pl.multiple_of(i * TQ, TQ)
-        prod = dot_ref[0, :, pl.ds(r0, TQ)].astype(jnp.float32) * o32t_ref[0, :, pl.ds(r0, TQ)]
-        dvec_ref[:, pl.ds(r0, TQ)] = jnp.sum(prod, axis=0, keepdims=True)
+        for hh in range(HPS):
+            prod = dot_ref[hh, :, pl.ds(r0, TQ)].astype(jnp.float32) * o32t_ref[hh, :, pl.ds(r0, TQ)]
+            dvec_ref[hh, :, pl.ds(r0, TQ)] = jnp.sum(prod, axis=0, keepdims=True)
         return carry
 
     lax.fori_loop(0, rows // TQ, d_body, 0)
 
     def kv_body(j, carry):
         c0 = pl.multiple_of(j * TK, TK)
-        k = k_ref[0, pl.ds(c0, TK), :]
-        v = v_ref[0, pl.ds(c0, TK), :]
-        kt = kt_ref[0, :, pl.ds(c0, TK)]
+        ks = [k_ref[hh, pl.ds(c0, TK), :] for hh in range(HPS)]
+        vs = [v_ref[hh, pl.ds(c0, TK), :] for hh in range(HPS)]
+        kts = [kt_ref[hh, :, pl.ds(c0, TK)] for hh in range(HPS)]
         sk = segc_ref[pl.ds(c0, TK), :]
 
         def q_body(i, grads):
-            dk, dv = grads
             r0 = pl.multiple_of(i * TQ, TQ)
-            s = jnp.dot(k, qt_ref[0, :, pl.ds(r0, TQ)], preferred_element_type=jnp.float32) * scale
             same = sk == segr_ref[:, pl.ds(r0, TQ)]
-            s = jnp.where(same, s, NEG)
-            p = jnp.exp(s - lse_ref[0, :, pl.ds(r0, TQ)])
-            dp = jnp.dot(v, dot_ref[0, :, pl.ds(r0, TQ)], preferred_element_type=jnp.float32)
-            ds = (p * (dp - dvec_ref[:, pl.ds(r0, TQ)])).astype(jnp.bfloat16)
-            dv = dv + jnp.dot(p.astype(jnp.bfloat16), do_ref[0, pl.ds(r0, TQ), :],
-                              preferred_element_type=jnp.float32)
-            dk = dk + jnp.dot(ds, q_ref[0, pl.ds(r0, TQ), :], preferred_element_type=jnp.float32)
-            dqt_ref[0, :, pl.ds(r0, TQ)] += jnp.dot(kt, ds, preferred_element_type=jnp.float32)
-            return dk, dv
+            new_grads = []
+            for hh in range(HPS):
+                dk, dv = grads[hh]
+                s = jnp.dot(ks[hh], qt_ref[hh, :, pl.ds(r0, TQ)], preferred_element_type=jnp.float32) * scale
+                s = jnp.where(same, s, NEG)
+                p = jnp.exp(s - lse_ref[hh, :, pl.ds(r0, TQ)])
+                dp = jnp.dot(vs[hh], dot_ref[hh, :, pl.ds(r0, TQ)], preferred_element_type=jnp.float32)
+                ds = (p * (dp - dvec_ref[hh, :, pl.ds(r0, TQ)])).astype(jnp.bfloat16)
+                dv = dv + jnp.dot(p.astype(jnp.bfloat16), do_ref[hh, pl.ds(r0, TQ), :],
+                                  preferred_element_type=jnp.float32)
+                dk = dk + jnp.dot(ds, q_ref[hh, pl.ds(r0, TQ), :], preferred_element_type=jnp.float32)
+                dqt_ref[hh, :, pl.ds(r0, TQ)] += jnp.dot(kts[hh], ds, preferred_element_type=jnp.float32)
+                new_grads.append((dk, dv))
+            return tuple(new_grads)
 
         zeros = jnp.zeros((TK, HEAD), jnp.float32)
-        dk, dv = lax.fori_loop(lo_ref[j], hi_ref[j], q_body, (zeros, zeros))
-        dk_ref[0, pl.ds(c0, TK), :] = dk * scale
-        dv_ref[0, pl.ds(c0, TK), :] = dv
+        final = lax.fori_loop(lo_ref[j], hi_ref[j], q_body, tuple((zeros, zeros) for _ in range(HPS)))
+        for hh in range(HPS):
+            dk, dv = final[hh]
+            dk_ref[hh, pl.ds(c0, TK), :] = dk * scale
+            dv_ref[hh, pl.ds(c0, TK), :] = dv
         return carry
 
     lax.fori_loop(0, rows // TK, kv_body, 0)
@@ -109,9 +125,9 @@
 
 
 def _head_specs(rows):
-    plain = pl.BlockSpec((1, rows, HEAD), lambda h, lo, hi: (h, 0, 0))
-    flipped = pl.BlockSpec((1, HEAD, rows), lambda h, lo, hi: (h, 0, 0))
-    stat = pl.BlockSpec((1, 1, rows), lambda h, lo, hi: (h, 0, 0))
+    plain = pl.BlockSpec((HPS, rows, HEAD), lambda h, lo, hi: (h, 0, 0))
+    flipped = pl.BlockSpec((HPS, HEAD, rows), lambda h, lo, hi: (h, 0, 0))
+    stat = pl.BlockSpec((HPS, 1, rows), lambda h, lo, hi: (h, 0, 0))
     col = pl.BlockSpec((rows, 1), lambda h, lo, hi: (0, 0))
     row = pl.BlockSpec((1, rows), lambda h, lo, hi: (0, 0))
     return plain, flipped, stat, col, row
@@ -120,10 +136,10 @@
 def flash_forward(qt, k, vt, seg_q, seg_k, lo, hi):
     heads, _, rows_q = qt.shape
     rows_k = k.shape[1]
-    flipped_q = pl.BlockSpec((1, HEAD, rows_q), lambda h, lo, hi: (h, 0, 0))
-    flipped_k = pl.BlockSpec((1, HEAD, rows_k), lambda h, lo, hi: (h, 0, 0))
-    plain_k = pl.BlockSpec((1, rows_k, HEAD), lambda h, lo, hi: (h, 0, 0))
-    stat = pl.BlockSpec((1, 1, rows_q), lambda h, lo, hi: (h, 0, 0))
+    flipped_q = pl.BlockSpec((HPS, HEAD, rows_q), lambda h, lo, hi: (h, 0, 0))
+    flipped_k = pl.BlockSpec((HPS, HEAD, rows_k), lambda h, lo, hi: (h, 0, 0))
+    plain_k = pl.BlockSpec((HPS, rows_k, HEAD), lambda h, lo, hi: (h, 0, 0))
+    stat = pl.BlockSpec((HPS, 1, rows_q), lambda h, lo, hi: (h, 0, 0))
     col = pl.BlockSpec((rows_k, 1), lambda h, lo, hi: (0, 0))
     row = pl.BlockSpec((1, rows_q), lambda h, lo, hi: (0, 0))
     flops = int(heads * rows_q * rows_k * HEAD * 2 * 2 * 0.6)
@@ -136,7 +152,7 @@
         ),
         grid_spec=pltpu.PrefetchScalarGridSpec(
             num_scalar_prefetch=2,
-            grid=(heads,),
+            grid=(heads // HPS,),
             in_specs=[col, row, flipped_q, plain_k, flipped_k],
             out_specs=[flipped_q, flipped_q, stat],
         ),
@@ -162,10 +178,10 @@
         ),
         grid_spec=pltpu.PrefetchScalarGridSpec(
             num_scalar_prefetch=2,
-            grid=(heads,),
+            grid=(heads // HPS,),
             in_specs=[col, row, plain, flipped, plain, flipped, plain, plain, flipped, flipped, stat],
             out_specs=[flipped, plain, plain],
-            scratch_shapes=[pltpu.VMEM((1, rows), jnp.float32)],
+            scratch_shapes=[pltpu.VMEM((HPS, 1, rows), jnp.float32)],
         ),
         compiler_params=pltpu.CompilerParams(
             dimension_semantics=("arbitrary",), vmem_limit_bytes=48 * 1024 * 1024),
@@ -282,8 +298,7 @@
         )
         attended_h = out_t.transpose(2, 0, 1).reshape((b1 - b0) * TQ, local_cols)
         att_sum_h = mp_allreduce(
-            jnp.dot(attended_h, w_out, preferred_element_type=jnp.float32).astype(jnp.bfloat16),
-            n_mp,
+            jnp.dot(attended_h, w_out, preferred_element_type=jnp.float32).astype(jnp.bfloat16), n_mp
         )
         middle_h = inputs[rows] + att_sum_h + b_out
         norm_two_h, back_two_h = jax.vjp(normalize, middle_h, ln2_gain, ln2_bias)
@@ -371,9 +386,7 @@
     grad_tokens = d_middle + d_input_norm
 
     def scatter(grad, dim):
-        return lax.psum_scatter(
-            grad.astype(jnp.bfloat16), "dp", scatter_dimension=dim, tiled=True
-        ).astype(jnp.float32)
+        return lax.psum_scatter(grad.astype(jnp.bfloat16), "dp", scatter_dimension=dim, tiled=True).astype(jnp.float32)
 
     tail_grads = jnp.concatenate(
         [grad_w_qkv_t.reshape(3 * local_cols, -1), grad_w_out], axis=0

time: 629 us -> 595 us (0.946)
  Pallas kernels: 98.7 us -> 83.6 us
  matrix products: 106 us -> 94.6 us
    dot_general x2, matrix products: 45.1 us -> 33.5 us  [per_device(): jnp.dot(normed_two_h, w_fc1, preferred_element_type=jnp.float32) + b_fc1]
    pallas_call x2, Pallas kernels: 47.6 us -> 38.3 us  [flash_forward(): pl.pallas_call(_fwd_kernel, out_shape=(jax.ShapeDtypeStruct((heads, HEAD,...]
  transfers between devices with their start and end apart: 29 -> 29, of which waited for: 10 -> 10; matrix products, arithmetic and copies ran while one was open for 38% -> 38% of each run, Pallas kernels for 14% -> 12%
where the time goes in v4:
time: 595 us; the launch traced here: 587 us
  waiting for transfers between devices  150 us (25%)
  other arithmetic  123 us (21%)
  matrix products  94.6 us (16%)
  Pallas kernels  83.6 us (14%)
  local copies, waits for them, and re-layouts  72.9 us (12%)
  starting transfers between devices  46.5 us (8%)
  between operations  15.7 us (3%)
    ppermute x7, waiting for transfers between devices, mp_allreduce(): got_far = lax.ppermute(first, 'mp', [(k, k ^ 2) for k in range(4)])  98.8 us
    pallas_call x1, Pallas kernels, flash_backward(): pl.pallas_call(_bwd_kernel, out_shape=(jax.ShapeDtypeStruct((heads, HEAD,...  45.3 us
    unnamed x4, waiting for transfers between devices  43.6 us
    pallas_call x2, Pallas kernels, flash_forward(): pl.pallas_call(_fwd_kernel, out_shape=(jax.ShapeDtypeStruct((heads, HEAD,...  38.3 us
    unnamed x185, local copies, waits for them, and re-layouts  38.2 us
    dot_general x2, matrix products, per_device(): jnp.dot(normed_two_h, w_fc1, preferred_element_type=jnp.float32) + b_fc1  33.5 us
    ppermute x6, starting transfers between devices, dp_allreduce(): lax.ppermute(total, 'dp', [(k, k ^ step) for k in range(n_dp)])  31.4 us
    reduce_sum x6, other arithmetic, normalize(): return centered * lax.rsqrt(spread + 1e-06) * gain + shift  20 us
  transfers between devices with their start and end apart: 29, of which 10 were waited for; matrix products, arithmetic and copies ran while one was open for 38% of the time, Pallas kernels for 12%

profile of v4, /device:TPU:0, one launch (start us, length us, event | category | flops | bytes accessed | tf_op | source)
XLA Modules:
  0.0 586.9 jit_solution(2995044969380004935)
XLA Ops:
  12.4 3.0 convert_reduce_fusion.2
  20.1 2.4 convolution_convert_fusion.4
  23.8 2.8 copy.96.k_ref
  26.5 4.6 fusion.49
  35.9 11.9 %segment_flash_fwd.2 = (bf16[4,64,768]{2,1,0:T(8,128)(2,1)S(1)}, f32[4,64,768]{2,1,0:T(8,128)S(1)}, f32[4,1,768]{2,1,0:T(1,128)S(1)}) custom-call(s32[3]{0:T(128)S(1)} %bitcast.118, s32[3]{0:T(128)S(1)} %bitcast.119, s32[2048,1]{1,0:T(8,128)S(1)} %copy-done.10, s32[1,768]{1,0:T(1,128)S(1)} %reshape.216.segr_ref, bf16[4,64,768]{2,1,0:T(8,128)(2,1)S(1)} %slice.149.qt_ref, ...), custom_call_target="tpu_custom_call" | custom-call | flops 966367616 | bytes 3670016 | tf_op jit(solution)/shard_map/segment_flash_fwd/pallas_call | solution.py:146
  51.8 2.1 constant_dynamic-slice_fusion.6
  59.0 26.4 %segment_flash_fwd.3 = (bf16[4,64,1280]{2,1,0:T(8,128)(2,1)S(1)}, f32[4,64,1280]{2,1,0:T(8,128)S(1)}, f32[4,1,1280]{2,1,0:T(1,128)S(1)}) custom-call(s32[5]{0:T(128)S(1)} %slice.122.lo_ref, s32[5]{0:T(128)S(1)} %slice.123.hi_ref, s32[2048,1]{1,0:T(8,128)S(1)} %copy-done.11, s32[1,1280]{1,0:T(1,128)S(1)} %reshape.221.segr_ref, ...), custom_call_target="tpu_custom_call" | custom-call | flops 1610612736 | bytes 4718592 | tf_op jit(solution)/shard_map/segment_flash_fwd/pallas_call | solution.py:146
  86.5 2.6 add_convert_fusion.18
  89.1 2.5 collective-permute-start.1
  91.6 2.3 convolution_convert_fusion
  93.9 2.5 constant_dynamic-slice_fusion.5
  96.6 13.5 %collective-permute-done.1 = bf16[384,1024]{1,0:T(8,128)(2,1)} collective-permute-done((bf16[384,1024]{1,0:T(8,128)(2,1)}, bf16[384,1024]{1,0:T(8,128)(2,1)}, u32[]{:S(2)}, u32[]{:S(2)}) %collective-permute-start.1) | collective-permute-done | bytes 786464 | tf_op jit(solution)/shard_map/ppermute | solution.py:223
  110.1 2.6 add_convert_fusion.17
  112.7 6.6 %convert_element_type.234 = f32[2048,1024]{1,0:T(8,128)} convert(bf16[2048,1024]{1,0:T(8,128)(2,1)} %param.17) | non-fusion elementwise | flops 2097152 | bytes 12582912 | tf_op jit(solution)/shard_map/convert_element_type | solution.py:263
  119.3 2.2 add_convert_fusion.12
  124.9 2.4 fusion.96
  128.9 18.0 %multiply_convert_fusion.1 = (bf16[768,1024]{1,0:T(8,128)(2,1)S(1)}, f32[768,1024]{1,0:T(8,128)S(1)}, f32[768,1024]{1,0:T(8,128)S(1)}) fusion(f32[1024]{0:T(1024)S(1)} %copy-done.79, bf16[768,1024]{1,0:T(8,128)(2,1)S(1)} %add_convert_fusion.6, bf16[1024,1024]{1,0:T(8,128)(2,1)S(1)} %copy-done), kind=kOutput, calls=%fused_computation.90 | convolution fusion | flops 1662517248 | bytes 11538432 | tf_op jit(solution)/shard_map/dot_general | solution.py:306
  147.0 5.8 collective-permute-done.4
  153.4 3.4 fusion.99
  163.2 15.5 %multiply_convert_fusion = (bf16[1280,1024]{1,0:T(8,128)(2,1)S(1)}, f32[1280,1024]{1,0:T(8,128)}, f32[1280,1024]{1,0:T(8,128)}) fusion(f32[1024]{0:T(1024)S(1)} %copy-done.79, bf16[1280,1024]{1,0:T(8,128)(2,1)S(1)} %add_convert_fusion.2, bf16[1024,1024]{1,0:T(8,128)(2,1)S(1)} %copy-done), kind=kOutput, calls=%fused_computation.31 | convolution fusion | flops 2770862080 | bytes 17829888 | tf_op jit(solution)/shard_map/dot_general | solution.py:306
  178.6 8.5 %fusion.98 = (f32[1024]{0:T(1024)S(1)}, bf16[1280,1024]{1,0:T(8,128)(2,1)S(1)}) fusion(f32[1280,1024]{1,0:T(8,128)} %get-tuple-element.131, bf16[1024,1024]{1,0:T(8,128)(2,1)S(1)} %copy-done.75, bf16[2048,1024]{1,0:T(8,128)(2,1)S(1)} %copy-done.31, f32[1280,1024]{1,0:T(8,128)} %get-tuple-element.166, f32[1024]{0:T(1024)S(1)} %copy-done.79), kind=kOutput, calls=%fused_computation.230 | convolution fusion | flops 2705325056 | bytes 17833984 | tf_op jit(solution)/shard_map/td,fd->tf/dot_general | solution.py:319
  187.2 4.6 fusion.50
  191.8 4.8 fusion.55
  196.6 2.5 pad_maximum_fusion
  199.0 3.1 convolution_convert_fusion.1
  207.0 4.4 convert_element_type.262
  213.2 2.7 copy.100
  218.7 2.9 convolution_convert_fusion.6
  221.6 3.3 collective-permute-done.7
  226.7 6.7 %copy.114 = bf16[2048,1024]{0,1:T(8,128)(2,1)} copy(bf16[2048,1024]{1,0:T(8,128)(2,1)} %pad_maximum_fusion) | data formatting | bytes 8388608
  233.5 2.4 add_convert_fusion.10
  237.8 6.3 %convolution_convert_fusion.2 = bf16[1280,1024]{1,0:T(8,128)(2,1)} fusion(bf16[1280,1024]{1,0:T(8,128)(2,1)} %copy-done.80, bf16[1024,1024]{1,0:T(8,128)(2,1)S(1)} %copy-done.77), kind=kOutput, calls=%fused_computation.78 | convolution fusion | flops 2685665280 | bytes 7340032 | tf_op jit(solution)/shard_map/dot_general | solution.py:309
  247.0 20.0 %collective-permute-done.10 = bf16[640,1024]{1,0:T(8,128)(2,1)S(1)} collective-permute-done((bf16[640,1024]{1,0:T(8,128)(2,1)S(1)}, bf16[640,1024]{1,0:T(8,128)(2,1)S(1)}, u32[]{:S(2)}, u32[]{:S(2)}) %collective-permute-start.10) | collective-permute-done | bytes 1310752 | tf_op jit(solution)/shard_map/ppermute | solution.py:223
  267.6 2.5 fusion.37
  276.9 2.4 fusion.7
  279.3 4.3 fusion.9
  283.6 3.3 fusion.90
  296.7 45.3 %segment_flash_bwd.1 = (f32[4,64,2048]{2,1,0:T(8,128)}, f32[4,2048,64]{2,1,0:T(8,128)}, f32[4,2048,64]{2,1,0:T(8,128)}) custom-call(s32[8]{0:T(128)S(1)} %fusion.81.lo_ref, s32[8]{0:T(128)S(1)} %copy-done.21, s32[2048,1]{1,0:T(8,128)S(1)} %copy-done.12, s32[1,2048]{1,0:T(1,128)S(1)} %bitcast.117, bf16[4,2048,64]{2,1,0:T(8,128)(2,1)} %copy.102.q_ref, ...), custom_call_target="tpu_custom_call" | custom-call | flops 5153960960 | bytes 15761408 | tf_op jit(solution)/shard_map/segment_flash_bwd/pallas_call | solution.py:172
  341.9 2.5 bitcast_convert_fusion.1
  346.6 2.5 convert_bitcast_fusion
  351.3 2.0 copy.115
  354.0 5.9 %bitcast_convert_fusion = bf16[2048,1024]{1,0:T(8,128)(2,1)S(1)} fusion(bf16[3,1024,256]{2,1,0:T(8,128)(2,1)} %param.20, bf16[1,2048,256]{2,1,0:T(8,128)(2,1)} %copy.109, bf16[1,2048,256]{2,1,0:T(8,128)(2,1)} %copy.108, bf16[1,2048,256]{2,1,0:T(8,128)(2,1)S(1)} %copy.107), kind=kOutput, calls=%fused_computation.11 | convolution fusion | flops 3226468352 | bytes 8912896 | tf_op jit(solution)/shard_map/stc,sdc->td/dot_general | solution.py:380
  362.2 2.2 copy-done.32
  369.3 16.0 %collective-permute-start.24 = (f32[5120]{0:T(1024)S(1)}, f32[5120]{0:T(1024)S(1)}, u32[]{:S(2)}, u32[]{:S(2)}) collective-permute-start(f32[5120]{0:T(1024)S(1)} %constant_dynamic-update-slice_fusion), channel_id=1, source_target_pairs={{0,4},{4,0},{8,12},{12,8},{16,20},{20,16},{24,28},{28,24},{1,5},{5... | collective-permute-start | bytes 61448 | tf_op jit(solution)/shard_map/ppermute | solution.py:237
  387.0 2.1 collective-permute-start.25
  389.1 4.5 add_convert_fusion.4
  394.2 2.6 add_convert_fusion.13
  400.0 2.0 fusion.65
  402.1 2.6 collective-permute-start.26
  409.0 3.6 add_convert_fusion.5
  412.6 56.1 %collective-permute-done.16 = bf16[640,1024]{1,0:T(8,128)(2,1)} collective-permute-done((bf16[640,1024]{1,0:T(8,128)(2,1)S(1)}, bf16[640,1024]{1,0:T(8,128)(2,1)}, u32[]{:S(2)}, u32[]{:S(2)}) %collective-permute-start.16) | collective-permute-done | bytes 1310752 | tf_op jit(solution)/shard_map/ppermute | solution.py:223
  468.7 3.0 add_convert_fusion.7
  471.8 4.7 add_convert_fusion.3
  476.8 3.7 fusion.58
  480.7 2.6 copy.116
  484.8 3.6 add_convert_fusion.1
  488.5 2.5 pad_maximum_fusion.1
  491.3 2.6 broadcast_select_fusion.1
  494.8 3.2 fusion.2
  498.0 7.0 %fusion.3 = (f32[1024]{0:T(1024)S(1)}, f32[2048]{0:T(1024)S(1)}, f32[1024]{0:T(1024)S(1)}) fusion(bf16[2048,1024]{1,0:T(8,128)(2,1)S(1)} %copy-done.24, f32[2048]{0:T(1024)S(1)} %copy-done.64, f32[2048]{0:T(1024)S(1)} %copy-done.61, bf16[1024,1024]{1,0:T(8,128)(2,1)S(1)} %get-tuple-element.141, bf16[1024,1024]{1,0:T(8,128)(2,1)S(1)} %get-tuple-element.140, ...), kind=kLoop, calls=%fused_computation.9 | loop fusion | flops 33550336 | bytes 8433664 | tf_op jit(solution)/shard_map/transpose(jvp())/reduce_sum | solution.py:200
  505.0 8.4 %collective-permute-start.21 = (f32[2560]{0:T(1024)S(1)}, f32[2560]{0:T(1024)S(1)}, u32[]{:S(2)}, u32[]{:S(2)}) collective-permute-start(f32[2560]{0:T(1024)S(1)} %pad_maximum_fusion.12), channel_id=1, source_target_pairs={{0,4},{4,0},{8,12},{12,8},{16,20},{20,16},{24,28},{28,24},{1,5},{5... | collective-permute-start | bytes 30728 | tf_op jit(solution)/shard_map/ppermute | solution.py:237
  515.3 43.6 %reduce-scatter.9.cloned.1.call-done = bf16[128,1024]{1,0:T(8,128)(2,1)} async-done(((bf16[1024,1024]{1,0:T(8,128)(2,1)}), bf16[128,1024]{1,0:T(8,128)(2,1)}) %reduce-scatter.9.cloned.1.call-update) | async-done | bytes 262160
  563.5 2.8 collective-permute-done.22
  567.6 10.8 %maximum_add_fusion = f32[2048,1024]{1,0:T(8,128)} fusion(f32[1280,1024]{1,0:T(8,128)} %copy-done.27, f32[768,1024]{1,0:T(8,128)} %copy-done.30, bf16[2048,1024]{1,0:T(8,128)(2,1)} %param.17, f32[2048]{0:T(1024)S(1)} %negate_multiply_fusion.2, f32[2048]{0:T(1024)S(1)} %multiply_multiply_fusion.10, f32[1024]{0:T(1024)S(1)} %copy-done.68, ...), kind=kLoop, calls=%fused_computation.10 | loop fusion | flops 29360128 | bytes 25202688 | tf_op jit(solution)/shard_map/add | solution.py:386
  (340 shorter events, 105.0 us)
Async XLA Ops:
  7.2 121.7 %copy-start = (bf16[1024,1024]{1,0:T(8,128)(2,1)S(1)}, bf16[1024,1024]{1,0:T(8,128)(2,1)}, u32[]{:S(2)}) copy-start(bf16[1024,1024]{1,0:T(8,128)(2,1)} %param.24) | copy-start | bytes 6291460
  7.2 344.1 %reduce-scatter.7.cloned.1.call-start = ((), (), s32[]{:S(2)}) async-start(), calls=%async_computation.2 | async-start | bytes 4718592
  35.9 14.1 %copy-start.49 = (bf16[256,1024]{1,0:T(8,128)(2,1)S(1)}, bf16[256,1024]{1,0:T(8,128)(2,1)}, u32[]{:S(2)}) copy-start(bf16[256,1024]{1,0:T(8,128)(2,1)} %param.22) | copy-start | bytes 1572868
  49.3 5.2 copy-start.21
  53.9 32.6 %collective-permute-start = (bf16[384,1024]{1,0:T(8,128)(2,1)}, bf16[384,1024]{1,0:T(8,128)(2,1)}, u32[]{:S(2)}, u32[]{:S(2)}) collective-permute-start(bf16[384,1024]{1,0:T(8,128)(2,1)} %constant_dynamic-slice_fusion.6), channel_id=1, source_target_pairs={{0,1},{1,0},{2,3},{3,2},{4,5},{5,4},{6,7},{7,6},{8,9},{9,8},{10,11... | collective-permute-start | bytes 2359304 | tf_op jit(solution)/shard_map/ppermute | solution.py:221
  59.0 27.5 %copy-start.37 = (bf16[768,1024]{1,0:T(8,128)(2,1)S(1)}, bf16[768,1024]{1,0:T(8,128)(2,1)}, u32[]{:S(2)}) copy-start(bf16[768,1024]{1,0:T(8,128)(2,1)} %convolution_convert_fusion.7) | copy-start | bytes 4718596
  59.0 32.6 %copy-start.50 = (bf16[256,1024]{1,0:T(8,128)(2,1)S(1)}, bf16[256,1024]{1,0:T(8,128)(2,1)}, u32[]{:S(2)}) copy-start(bf16[256,1024]{1,0:T(8,128)(2,1)} %param.22) | copy-start | bytes 1572868
  86.5 5.1 copy-start.2
  89.1 21.0 %collective-permute-start.1 = (bf16[384,1024]{1,0:T(8,128)(2,1)}, bf16[384,1024]{1,0:T(8,128)(2,1)}, u32[]{:S(2)}, u32[]{:S(2)}) collective-permute-start(bf16[384,1024]{1,0:T(8,128)(2,1)} %add_convert_fusion.18), channel_id=1, source_target_pairs={{0,2},{1,3},{2,0},{3,1},{4,6},{5,7},{6,4},{7,5},{8,10},{9,11},{10,... | collective-permute-start | bytes 2359304 | tf_op jit(solution)/shard_map/ppermute | solution.py:223
  96.4 22.9 %collective-permute-start.3 = (bf16[640,1024]{1,0:T(8,128)(2,1)}, bf16[640,1024]{1,0:T(8,128)(2,1)}, u32[]{:S(2)}, u32[]{:S(2)}) collective-permute-start(bf16[640,1024]{1,0:T(8,128)(2,1)} %constant_dynamic-slice_fusion.5), channel_id=1, source_target_pairs={{0,1},{1,0},{2,3},{3,2},{4,5},{5,4},{6,7},{7,6},{8,9},{9,8},{10,11... | collective-permute-start | bytes 3932168 | tf_op jit(solution)/shard_map/ppermute | solution.py:221
  112.7 10.7 %collective-permute-start.2 = (bf16[384,1024]{1,0:T(8,128)(2,1)}, bf16[384,1024]{1,0:T(8,128)(2,1)}, u32[]{:S(2)}, u32[]{:S(2)}) collective-permute-start(bf16[384,1024]{1,0:T(8,128)(2,1)} %add_convert_fusion.17), channel_id=1, source_target_pairs={{0,1},{1,0},{2,3},{3,2},{4,5},{5,4},{6,7},{7,6},{8,9},{9,8},{10,11... | collective-permute-start | bytes 2359304 | tf_op jit(solution)/shard_map/ppermute | solution.py:225
  119.3 5.6 copy-start.69
  121.6 31.3 %collective-permute-start.4 = (bf16[640,1024]{1,0:T(8,128)(2,1)S(1)}, bf16[640,1024]{1,0:T(8,128)(2,1)S(1)}, u32[]{:S(2)}, u32[]{:S(2)}) collective-permute-start(bf16[640,1024]{1,0:T(8,128)(2,1)S(1)} %add_convert_fusion.12), channel_id=1, source_target_pairs={{0,2},{1,3},{2,0},{3,1},{4,6},{5,7},{6,4},{7,5},{8,10},{9,11},{10,... | collective-permute-start | bytes 3932168 | tf_op jit(solution)/shard_map/ppermute | solution.py:223
  128.9 24.5 %copy-start.31 = (bf16[2048,1024]{1,0:T(8,128)(2,1)S(1)}, bf16[2048,1024]{1,0:T(8,128)(2,1)}, u32[]{:S(2)}) copy-start(bf16[2048,1024]{1,0:T(8,128)(2,1)} %param.18) | copy-start | bytes 12582916
  147.0 44.8 %copy-start.81 = (bf16[768,1024]{1,0:T(8,128)(2,1)}, bf16[768,1024]{1,0:T(8,128)(2,1)S(1)}, u32[]{:S(2)}) copy-start(bf16[768,1024]{1,0:T(8,128)(2,1)S(1)} %get-tuple-element.134) | copy-start | bytes 4718596
  147.0 6.5 %copy-start.75 = (bf16[1024,1024]{1,0:T(8,128)(2,1)S(1)}, bf16[1024,1024]{1,0:T(8,128)(2,1)}, u32[]{:S(2)}) copy-start(bf16[1024,1024]{1,0:T(8,128)(2,1)} %param.26) | copy-start | bytes 6291460
  153.3 6.0 %collective-permute-start.5 = (bf16[640,1024]{1,0:T(8,128)(2,1)S(1)}, bf16[640,1024]{1,0:T(8,128)(2,1)S(1)}, u32[]{:S(2)}, u32[]{:S(2)}) collective-permute-start(bf16[640,1024]{1,0:T(8,128)(2,1)S(1)} %add_convert_fusion.11), channel_id=1, source_target_pairs={{0,1},{1,0},{2,3},{3,2},{4,5},{5,4},{6,7},{7,6},{8,9},{9,8},{10,11... | collective-permute-start | bytes 3932168 | tf_op jit(solution)/shard_map/ppermute | solution.py:225
  158.8 45.1 %collective-permute-start.6 = (bf16[384,1024]{1,0:T(8,128)(2,1)S(1)}, bf16[384,1024]{1,0:T(8,128)(2,1)S(1)}, u32[]{:S(2)}, u32[]{:S(2)}) collective-permute-start(bf16[384,1024]{1,0:T(8,128)(2,1)S(1)} %constant_dynamic-slice_fusion.4), channel_id=1, source_target_pairs={{0,1},{1,0},{2,3},{3,2},{4,5},{5,4},{6,7},{7,6},{8,9},{9,8},{10,11... | collective-permute-start | bytes 2359304 | tf_op jit(solution)/shard_map/ppermute | solution.py:221
  161.3 17.3 %copy-start.22 = (f32[1280,1024]{1,0:T(8,128)}, f32[1280,1024]{1,0:T(8,128)S(1)}, u32[]{:S(2)}) copy-start(f32[1280,1024]{1,0:T(8,128)S(1)} %get-tuple-element.133) | copy-start | bytes 15728644
  178.6 13.1 %copy-start.80 = (bf16[1280,1024]{1,0:T(8,128)(2,1)}, bf16[1280,1024]{1,0:T(8,128)(2,1)S(1)}, u32[]{:S(2)}) copy-start(bf16[1280,1024]{1,0:T(8,128)(2,1)S(1)} %get-tuple-element.130) | copy-start | bytes 7864324
  202.2 4.8 copy-start.46
  202.2 4.8 copy-start.19
  203.5 30.0 %collective-permute-start.9 = (bf16[640,1024]{1,0:T(8,128)(2,1)}, bf16[640,1024]{1,0:T(8,128)(2,1)}, u32[]{:S(2)}, u32[]{:S(2)}) collective-permute-start(bf16[640,1024]{1,0:T(8,128)(2,1)} %constant_dynamic-slice_fusion.3), channel_id=1, source_target_pairs={{0,1},{1,0},{2,3},{3,2},{4,5},{5,4},{6,7},{7,6},{8,9},{9,8},{10,11... | collective-permute-start | bytes 3932168 | tf_op jit(solution)/shard_map/ppermute | solution.py:221
  205.2 19.8 %collective-permute-start.7 = (bf16[384,1024]{1,0:T(8,128)(2,1)}, bf16[384,1024]{1,0:T(8,128)(2,1)}, u32[]{:S(2)}, u32[]{:S(2)}) collective-permute-start(bf16[384,1024]{1,0:T(8,128)(2,1)} %add_convert_fusion.16), channel_id=1, source_target_pairs={{0,2},{1,3},{2,0},{3,1},{4,6},{5,7},{6,4},{7,5},{8,10},{9,11},{10,... | collective-permute-start | bytes 2359304 | tf_op jit(solution)/shard_map/ppermute | solution.py:223
  211.4 4.5 copy-start.6
  211.4 4.5 copy-start.14
  226.6 6.8 %copy-start.42 = (bf16[384,1024]{1,0:T(8,128)(2,1)}, bf16[384,1024]{1,0:T(8,128)(2,1)S(1)}, u32[]{:S(2)}) copy-start(bf16[384,1024]{1,0:T(8,128)(2,1)S(1)} %add_convert_fusion.15) | copy-start | bytes 2359300
  226.7 17.4 %collective-permute-start.8 = (bf16[384,1024]{1,0:T(8,128)(2,1)S(1)}, bf16[384,1024]{1,0:T(8,128)(2,1)}, u32[]{:S(2)}, u32[]{:S(2)}) collective-permute-start(bf16[384,1024]{1,0:T(8,128)(2,1)S(1)} %add_convert_fusion.15), channel_id=1, source_target_pairs={{0,1},{1,0},{2,3},{3,2},{4,5},{5,4},{6,7},{7,6},{8,9},{9,8},{10,11... | collective-permute-start | bytes 2359304 | tf_op jit(solution)/shard_map/ppermute | solution.py:225
  233.4 325.5 %reduce-scatter.9.cloned.1.call-start = ((), (), s32[]{:S(2)}) async-start(), calls=%async_computation.3 | async-start | bytes 2359296
  233.5 36.6 %slice-start.4 = ((s8[8388608]{0:T(1024)(128)(4,1)}), s8[4194304]{0:T(1024)(128)(4,1)S(1)}, s32[]{:S(2)}) async-start(s8[8388608]{0:T(1024)(128)(4,1)} %bitcast.126), calls=%async_computation.8 | async-start | bytes 8388608
  235.9 8.2 %copy-start.43 = (bf16[384,1024]{1,0:T(8,128)(2,1)S(1)}, bf16[384,1024]{1,0:T(8,128)(2,1)}, u32[]{:S(2)}) copy-start(bf16[384,1024]{1,0:T(8,128)(2,1)} %copy-done.42) | copy-start | bytes 2359300
  235.9 34.2 %slice-start.5 = ((s8[8388608]{0:T(1024)(128)(4,1)}), s8[4194304]{0:T(1024)(128)(4,1)S(1)}, s32[]{:S(2)}) async-start(s8[8388608]{0:T(1024)(128)(4,1)} %bitcast.126), calls=%async_computation.9 | async-start | bytes 8388608
  235.9 31.0 %collective-permute-start.10 = (bf16[640,1024]{1,0:T(8,128)(2,1)S(1)}, bf16[640,1024]{1,0:T(8,128)(2,1)S(1)}, u32[]{:S(2)}, u32[]{:S(2)}) collective-permute-start(bf16[640,1024]{1,0:T(8,128)(2,1)S(1)} %add_convert_fusion.10), channel_id=1, source_target_pairs={{0,2},{1,3},{2,0},{3,1},{4,6},{5,7},{6,4},{7,5},{8,10},{9,11},{10,... | collective-permute-start | bytes 3932168 | tf_op jit(solution)/shard_map/ppermute | solution.py:223
  267.5 7.7 %collective-permute-start.11 = (bf16[640,1024]{1,0:T(8,128)(2,1)S(1)}, bf16[640,1024]{1,0:T(8,128)(2,1)S(1)}, u32[]{:S(2)}, u32[]{:S(2)}) collective-permute-start(bf16[640,1024]{1,0:T(8,128)(2,1)S(1)} %add_convert_fusion.9), channel_id=1, source_target_pairs={{0,1},{1,0},{2,3},{3,2},{4,5},{5,4},{6,7},{7,6},{8,9},{9,8},{10,11... | collective-permute-start | bytes 3932168 | tf_op jit(solution)/shard_map/ppermute | solution.py:225
  354.0 5.9 %copy-start.57 = (bf16[1,2048,256]{2,1,0:T(8,128)(2,1)}, bf16[1,2048,256]{2,1,0:T(8,128)(2,1)S(1)}, u32[]{:S(2)}) copy-start(bf16[1,2048,256]{2,1,0:T(8,128)(2,1)S(1)} %copy.107) | copy-start | bytes 3145732
  354.0 8.0 %copy-start.52 = (bf16[768,1024]{1,0:T(8,128)(2,1)S(1)}, bf16[768,1024]{1,0:T(8,128)(2,1)}, u32[]{:S(2)}) copy-start(bf16[768,1024]{1,0:T(8,128)(2,1)} %convolution_convert_fusion.6) | copy-start | bytes 4718596
  359.9 5.1 copy-start.41
  361.5 27.7 %collective-permute-start.18 = (bf16[1024,1024]{1,0:T(8,128)(2,1)}, bf16[1024,1024]{1,0:T(8,128)(2,1)}, u32[]{:S(2)}, u32[]{:S(2)}) collective-permute-start(bf16[1024,1024]{1,0:T(8,128)(2,1)} %constant_dynamic-slice_fusion), channel_id=1, source_target_pairs={{0,1},{1,0},{2,3},{3,2},{4,5},{5,4},{6,7},{7,6},{8,9},{9,8},{10,11... | collective-permute-start | bytes 6291464 | tf_op jit(solution)/shard_map/ppermute | solution.py:221
  362.1 5.1 collective-permute-start.12
  365.3 31.6 %collective-permute-start.15 = (bf16[640,1024]{1,0:T(8,128)(2,1)S(1)}, bf16[640,1024]{1,0:T(8,128)(2,1)}, u32[]{:S(2)}, u32[]{:S(2)}) collective-permute-start(bf16[640,1024]{1,0:T(8,128)(2,1)S(1)} %constant_dynamic-slice_fusion.1), channel_id=1, source_target_pairs={{0,1},{1,0},{2,3},{3,2},{4,5},{5,4},{6,7},{7,6},{8,9},{9,8},{10,11... | collective-permute-start | bytes 3932168 | tf_op jit(solution)/shard_map/ppermute | solution.py:221
  367.5 26.8 %collective-permute-start.13 = (bf16[384,1024]{1,0:T(8,128)(2,1)S(1)}, bf16[384,1024]{1,0:T(8,128)(2,1)}, u32[]{:S(2)}, u32[]{:S(2)}) collective-permute-start(bf16[384,1024]{1,0:T(8,128)(2,1)S(1)} %add_convert_fusion.14), channel_id=1, source_target_pairs={{0,2},{1,3},{2,0},{3,1},{4,6},{5,7},{6,4},{7,5},{8,10},{9,11},{10,... | collective-permute-start | bytes 2359304 | tf_op jit(solution)/shard_map/ppermute | solution.py:223
  369.3 17.8 %collective-permute-start.24 = (f32[5120]{0:T(1024)S(1)}, f32[5120]{0:T(1024)S(1)}, u32[]{:S(2)}, u32[]{:S(2)}) collective-permute-start(f32[5120]{0:T(1024)S(1)} %constant_dynamic-update-slice_fusion), channel_id=1, source_target_pairs={{0,4},{4,0},{8,12},{12,8},{16,20},{20,16},{24,28},{28,24},{1,5},{5... | collective-permute-start | bytes 61448 | tf_op jit(solution)/shard_map/ppermute | solution.py:237
  387.0 9.8 %copy-start.45 = (bf16[1280,1024]{1,0:T(8,128)(2,1)S(1)}, bf16[1280,1024]{1,0:T(8,128)(2,1)}, u32[]{:S(2)}) copy-start(bf16[1280,1024]{1,0:T(8,128)(2,1)} %convolution_convert_fusion.2) | copy-start | bytes 7864324
  387.0 15.0 %collective-permute-start.25 = (f32[5120]{0:T(1024)S(1)}, f32[5120]{0:T(1024)S(1)}, u32[]{:S(2)}, u32[]{:S(2)}) collective-permute-start(f32[5120]{0:T(1024)S(1)} %add.334), channel_id=1, source_target_pairs={{0,8},{4,12},{8,0},{12,4},{16,24},{20,28},{24,16},{28,20},{1,9},{5... | collective-permute-start | bytes 61448 | tf_op jit(solution)/shard_map/ppermute | solution.py:237
  393.7 6.4 %copy-start.3 = (bf16[4,64,1280]{2,1,0:T(8,128)(2,1)S(1)}, bf16[4,64,1280]{2,1,0:T(8,128)(2,1)}, u32[]{:S(2)}) copy-start(bf16[4,64,1280]{2,1,0:T(8,128)(2,1)} %copy-done.2) | copy-start | bytes 1966084
  393.7 6.4 %copy-start.17 = (bf16[4,64,768]{2,1,0:T(8,128)(2,1)S(1)}, bf16[4,64,768]{2,1,0:T(8,128)(2,1)}, u32[]{:S(2)}) copy-start(bf16[4,64,768]{2,1,0:T(8,128)(2,1)} %copy-done.16) | copy-start | bytes 1179652
  393.7 6.4 %copy-start.48 = (bf16[1280,1024]{1,0:T(8,128)(2,1)S(1)}, bf16[1280,1024]{1,0:T(8,128)(2,1)}, u32[]{:S(2)}) copy-start(bf16[1280,1024]{1,0:T(8,128)(2,1)} %copy-done.47) | copy-start | bytes 7864324
  393.7 6.4 %copy-start.54 = (bf16[768,1024]{1,0:T(8,128)(2,1)S(1)}, bf16[768,1024]{1,0:T(8,128)(2,1)}, u32[]{:S(2)}) copy-start(bf16[768,1024]{1,0:T(8,128)(2,1)} %copy-done.53) | copy-start | bytes 4718596
  393.7 78.1 %collective-permute-start.19 = (bf16[1024,1024]{1,0:T(8,128)(2,1)}, bf16[1024,1024]{1,0:T(8,128)(2,1)}, u32[]{:S(2)}, u32[]{:S(2)}) collective-permute-start(bf16[1024,1024]{1,0:T(8,128)(2,1)} %add_convert_fusion.4), channel_id=1, source_target_pairs={{0,2},{1,3},{2,0},{3,1},{4,6},{5,7},{6,4},{7,5},{8,10},{9,11},{10,... | collective-permute-start | bytes 6291464 | tf_op jit(solution)/shard_map/ppermute | solution.py:223
  396.9 10.6 %collective-permute-start.14 = (bf16[384,1024]{1,0:T(8,128)(2,1)}, bf16[384,1024]{1,0:T(8,128)(2,1)}, u32[]{:S(2)}, u32[]{:S(2)}) collective-permute-start(bf16[384,1024]{1,0:T(8,128)(2,1)} %add_convert_fusion.13), channel_id=1, source_target_pairs={{0,1},{1,0},{2,3},{3,2},{4,5},{5,4},{6,7},{7,6},{8,9},{9,8},{10,11... | collective-permute-start | bytes 2359304 | tf_op jit(solution)/shard_map/ppermute | solution.py:225
  398.7 6.0 %copy-start.33 = (f32[4,2048,64]{2,1,0:T(8,128)S(1)}, f32[4,2048,64]{2,1,0:T(8,128)}, u32[]{:S(2)}) copy-start(f32[4,2048,64]{2,1,0:T(8,128)} %get-tuple-element.45) | copy-start | bytes 6291460
  398.7 70.0 %collective-permute-start.16 = (bf16[640,1024]{1,0:T(8,128)(2,1)S(1)}, bf16[640,1024]{1,0:T(8,128)(2,1)}, u32[]{:S(2)}, u32[]{:S(2)}) collective-permute-start(bf16[640,1024]{1,0:T(8,128)(2,1)S(1)} %add_convert_fusion.8), channel_id=1, source_target_pairs={{0,2},{1,3},{2,0},{3,1},{4,6},{5,7},{6,4},{7,5},{8,10},{9,11},{10,... | collective-permute-start | bytes 3932168 | tf_op jit(solution)/shard_map/ppermute | solution.py:223
  402.1 6.9 %copy-start.71 = (f32[1024]{0:T(1024)S(1)}, f32[1024]{0:T(1024)}, u32[]{:S(2)}) copy-start(f32[1024]{0:T(1024)} %param.27) | copy-start | bytes 12292
  402.1 4.7 collective-permute-start.26
  468.7 8.0 %copy-start.58 = (bf16[1,2048,256]{2,1,0:T(8,128)(2,1)S(1)}, bf16[1,2048,256]{2,1,0:T(8,128)(2,1)}, u32[]{:S(2)}) copy-start(bf16[1,2048,256]{2,1,0:T(8,128)(2,1)} %copy-done.57) | copy-start | bytes 3145732
  471.8 5.0 copy-start.40
  471.8 5.0 copy-start.55
  471.8 5.0 copy-start.56
  471.8 11.6 %collective-permute-start.17 = (bf16[640,1024]{1,0:T(8,128)(2,1)}, bf16[640,1024]{1,0:T(8,128)(2,1)S(1)}, u32[]{:S(2)}, u32[]{:S(2)}) collective-permute-start(bf16[640,1024]{1,0:T(8,128)(2,1)} %add_convert_fusion.7), channel_id=1, source_target_pairs={{0,1},{1,0},{2,3},{3,2},{4,5},{5,4},{6,7},{7,6},{8,9},{9,8},{10,11... | collective-permute-start | bytes 3932168 | tf_op jit(solution)/shard_map/ppermute | solution.py:225
  476.5 14.9 %collective-permute-start.20 = (bf16[1024,1024]{1,0:T(8,128)(2,1)}, bf16[1024,1024]{1,0:T(8,128)(2,1)}, u32[]{:S(2)}, u32[]{:S(2)}) collective-permute-start(bf16[1024,1024]{1,0:T(8,128)(2,1)} %add_convert_fusion.3), channel_id=1, source_target_pairs={{0,1},{1,0},{2,3},{3,2},{4,5},{5,4},{6,7},{7,6},{8,9},{9,8},{10,11... | collective-permute-start | bytes 6291464 | tf_op jit(solution)/shard_map/ppermute | solution.py:225
  505.0 57.5 %collective-permute-start.21 = (f32[2560]{0:T(1024)S(1)}, f32[2560]{0:T(1024)S(1)}, u32[]{:S(2)}, u32[]{:S(2)}) collective-permute-start(f32[2560]{0:T(1024)S(1)} %pad_maximum_fusion.12), channel_id=1, source_target_pairs={{0,4},{4,0},{8,12},{12,8},{16,20},{20,16},{24,28},{28,24},{1,5},{5... | collective-permute-start | bytes 30728 | tf_op jit(solution)/shard_map/ppermute | solution.py:237
  562.5 3.8 collective-permute-start.22
  566.3 12.2 %collective-permute-start.23 = (f32[2560]{0:T(1024)S(1)}, f32[2560]{0:T(1024)S(1)}, u32[]{:S(2)}, u32[]{:S(2)}) collective-permute-start(f32[2560]{0:T(1024)S(1)} %add.329), channel_id=1, source_target_pairs={{0,16},{4,20},{8,24},{12,28},{16,0},{20,4},{24,8},{28,12},{1,17},{... | collective-permute-start | bytes 30728 | tf_op jit(solution)/shard_map/ppermute | solution.py:237
  567.6 12.1 %copy-start.1 = (bf16[1024,1024]{1,0:T(8,128)(2,1)S(1)}, bf16[1024,1024]{1,0:T(8,128)(2,1)}, u32[]{:S(2)}) copy-start(bf16[1024,1024]{1,0:T(8,128)(2,1)} %param.24) | copy-start | bytes 6291460
  (54 other events, 125.5 us)
Sparse Core Ops, SparseCore 0:
  233.5 96.2 reduce-scatter.6
  483.5 75.3 reduce-scatter.8

commit v5 on v4

--- a/solution.py
+++ b/solution.py
@@ -261,7 +261,7 @@
     heads_here = local_cols // HEAD
     segments = segment_ids(item_lengths[0], row_count)
     inputs = tokens.astype(jnp.float32)
-    norm_one, norm_one_back = jax.vjp(normalize, inputs, ln1_gain, ln1_bias)
+    norm_one = normalize(inputs, ln1_gain, ln1_bias)
     normed_one = norm_one.astype(jnp.bfloat16)
     queries = (jnp.dot(normed_one, w_qkv[0], preferred_element_type=jnp.float32) + b_qv[0]).astype(
         jnp.bfloat16
@@ -330,11 +330,10 @@
     d_pre_low = jnp.concatenate([p["d_pre_low"] for p in pieces_fwd], axis=0)
     grad_b_fc1 = sum(p["b_fc1"] for p in pieces_fwd)
     grad_w_fc2 = jnp.einsum("tf,td->fd", activated, cotangent, preferred_element_type=jnp.float32)
-    grad_w_fc1_t = jnp.einsum("tf,td->fd", d_pre_low, normed_two, preferred_element_type=jnp.float32)
+    grad_w_fc1_t = jnp.einsum(
+        "tf,td->fd", d_pre_low, normed_two, preferred_element_type=jnp.float32
+    )
     mlp_weight_grads = jnp.concatenate([grad_w_fc2, grad_w_fc1_t], axis=0).astype(jnp.bfloat16)
-    mlp_weight_grads, pieces_fwd[-1]["dn_two_partial"] = lax.optimization_barrier(
-        (mlp_weight_grads, pieces_fwd[-1]["dn_two_partial"])
-    )
     summed_mlp = lax.psum_scatter(mlp_weight_grads, "dp", scatter_dimension=1, tiled=True)
     for piece in pieces_fwd:
         d_normed_two_h = mp_allreduce(piece["dn_two_partial"], n_mp)
@@ -375,15 +374,27 @@
     d_values = from_heads(d_v_heads)
     grad_b_qv = jnp.stack([jnp.sum(d_queries, axis=0), jnp.sum(d_values, axis=0)])
     stacked = jnp.stack([d_queries, d_keys, d_values]).astype(jnp.bfloat16)
-    grad_w_qkv_t = jnp.einsum("stc,td->scd", stacked, normed_one, preferred_element_type=jnp.float32)
-    d_normed_one = mp_allreduce(
-        jnp.einsum("stc,sdc->td", stacked, w_qkv, preferred_element_type=jnp.float32).astype(
-            jnp.bfloat16
-        ),
-        n_mp,
-    )
-    d_input_norm, grad_ln1_gain, grad_ln1_bias = norm_one_back(d_normed_one)
-    grad_tokens = d_middle + d_input_norm
+    tail_parts = []
+    for b0, b1 in bounds:
+        rows = slice(b0 * TQ, b1 * TQ)
+        dn_one_partial_h = jnp.einsum(
+            "stc,sdc->td", stacked[:, rows], w_qkv, preferred_element_type=jnp.float32
+        ).astype(jnp.bfloat16)
+        tail_parts.append((rows, dn_one_partial_h))
+    grad_w_qkv_t = jnp.einsum(
+        "stc,td->scd", stacked, normed_one, preferred_element_type=jnp.float32
+    )
+    grad_pieces = []
+    grad_ln1_gain = 0.0
+    grad_ln1_bias = 0.0
+    for rows, dn_one_partial_h in tail_parts:
+        d_normed_one_h = mp_allreduce(dn_one_partial_h, n_mp)
+        _, back_one_h = jax.vjp(normalize, inputs[rows], ln1_gain, ln1_bias)
+        d_input_h, gain_h, shift_h = back_one_h(d_normed_one_h)
+        grad_ln1_gain = grad_ln1_gain + gain_h
+        grad_ln1_bias = grad_ln1_bias + shift_h
+        grad_pieces.append(d_middle[rows] + d_input_h)
+    grad_tokens = jnp.concatenate(grad_pieces, axis=0)
 
     def scatter(grad, dim):
         return lax.psum_scatter(grad.astype(jnp.bfloat16), "dp", scatter_dimension=dim, tiled=True).astype(jnp.float32)

time: 595 us -> 561 us (0.943)
  waiting for transfers between devices: 150 us -> 115 us
  other arithmetic: 123 us -> 117 us
    unnamed x4, waiting for transfers between devices: 43.6 us -> 17 us
    add x1 -> x4, other arithmetic: 10.8 us -> 0.95 us  [the longest x2 0.94 us: per_device(): grad_pieces.append(d_middle[rows] + d_input_h)]
    convert_element_type x7 -> x8, other arithmetic: 15.6 us -> 7.62 us  [mp_allreduce(): (first.astype(jnp.float32) + got_far.astype(jnp.float32)).astype(jnp.bflo...]
    reduce_sum x3 -> x5, other arithmetic: 6.26 us -> 13.9 us  [normalize(): center = jnp.mean(values, axis=-1, keepdims=True)]
    reduce_sum x0 -> x2, other arithmetic: none -> 6.92 us  [normalize(): centered = values - center]
    convert_element_type x7 -> x8, other arithmetic: 15.1 us -> 11 us  [mp_allreduce(): (mine.astype(jnp.float32) + got.astype(jnp.float32)).astype(jnp.bfloat16)]
    unnamed x185 -> x211, local copies, waits for them, and re-layouts: 38.2 us -> 35.5 us
    ppermute x7 -> x8, waiting for transfers between devices: 98.8 us -> 96.5 us  [mp_allreduce(): got_far = lax.ppermute(first, 'mp', [(k, k ^ 2) for k in range(4)])]
  transfers between devices with their start and end apart: 29 -> 32, of which waited for: 10 -> 9; matrix products, arithmetic and copies ran while one was open for 38% -> 42% of each run, Pallas kernels for 12% -> 13%
where the time goes in v5:
time: 561 us; the launch traced here: 552 us
  other arithmetic  117 us (21%)
  waiting for transfers between devices  115 us (20%)
  matrix products  97.1 us (17%)
  Pallas kernels  84.1 us (15%)
  local copies, waits for them, and re-layouts  78.5 us (14%)
  starting transfers between devices  45.1 us (8%)
  between operations  15.9 us (3%)
    ppermute x8, waiting for transfers between devices, mp_allreduce(): got_far = lax.ppermute(first, 'mp', [(k, k ^ 2) for k in range(4)])  96.5 us
    pallas_call x1, Pallas kernels, flash_backward(): pl.pallas_call(_bwd_kernel, out_shape=(jax.ShapeDtypeStruct((heads, HEAD,...  45.9 us
    pallas_call x2, Pallas kernels, flash_forward(): pl.pallas_call(_fwd_kernel, out_shape=(jax.ShapeDtypeStruct((heads, HEAD,...  38.2 us
    unnamed x211, local copies, waits for them, and re-layouts  35.5 us
    dot_general x2, matrix products, per_device(): jnp.dot(normed_two_h, w_fc1, preferred_element_type=jnp.float32) + b_fc1  34.3 us
    ppermute x6, starting transfers between devices, dp_allreduce(): lax.ppermute(total, 'dp', [(k, k ^ step) for k in range(n_dp)])  30.6 us
    reduce_sum x6, other arithmetic, normalize(): return centered * lax.rsqrt(spread + 1e-06) * gain + shift  17.1 us
    unnamed x4, waiting for transfers between devices  17 us
  transfers between devices with their start and end apart: 32, of which 9 were waited for; matrix products, arithmetic and copies ran while one was open for 42% of the time, Pallas kernels for 13%

profile of v5, /device:TPU:0, one launch (start us, length us, event | category | flops | bytes accessed | tf_op | source)
XLA Modules:
  0.0 552.3 jit_solution(11331186951248908378)
XLA Ops:
  11.6 3.1 convert_reduce_fusion.2
  17.9 2.3 convolution_convert_fusion.4
  23.0 2.7 copy.96.k_ref
  25.7 4.6 fusion.55
  35.1 11.9 %segment_flash_fwd.2 = (bf16[4,64,768]{2,1,0:T(8,128)(2,1)S(1)}, f32[4,64,768]{2,1,0:T(8,128)S(1)}, f32[4,1,768]{2,1,0:T(1,128)S(1)}) custom-call(s32[3]{0:T(128)S(1)} %bitcast.122, s32[3]{0:T(128)S(1)} %bitcast.121, s32[2048,1]{1,0:T(8,128)S(1)} %copy-done.10, s32[1,768]{1,0:T(1,128)S(1)} %reshape.258.segr_ref, bf16[4,64,768]{2,1,0:T(8,128)(2,1)S(1)} %slice.159.qt_ref, ...), custom_call_target="tpu_custom_call" | custom-call | flops 966367616 | bytes 3670016 | tf_op jit(solution)/shard_map/segment_flash_fwd/pallas_call | solution.py:146
  55.4 26.3 %segment_flash_fwd.3 = (bf16[4,64,1280]{2,1,0:T(8,128)(2,1)S(1)}, f32[4,64,1280]{2,1,0:T(8,128)S(1)}, f32[4,1,1280]{2,1,0:T(1,128)S(1)}) custom-call(s32[5]{0:T(128)S(1)} %slice.130.lo_ref, s32[5]{0:T(128)S(1)} %slice.131.hi_ref, s32[2048,1]{1,0:T(8,128)S(1)} %copy-done.11, s32[1,1280]{1,0:T(1,128)S(1)} %reshape.263.segr_ref, ...), custom_call_target="tpu_custom_call" | custom-call | flops 1610612736 | bytes 4718592 | tf_op jit(solution)/shard_map/segment_flash_fwd/pallas_call | solution.py:146
  85.1 6.6 %convert_element_type.258 = f32[2048,1024]{1,0:T(8,128)} convert(bf16[2048,1024]{1,0:T(8,128)(2,1)} %param.17) | non-fusion elementwise | flops 2097152 | bytes 12582912 | tf_op jit(solution)/shard_map/convert_element_type | solution.py:263
  91.8 2.3 slice_reduce_fusion.1
  95.7 2.9 collective-permute-start.1
  100.2 2.9 slice_reduce_fusion
  103.2 13.3 %collective-permute-done.1 = bf16[384,1024]{1,0:T(8,128)(2,1)S(1)} collective-permute-done((bf16[384,1024]{1,0:T(8,128)(2,1)S(1)}, bf16[384,1024]{1,0:T(8,128)(2,1)S(1)}, u32[]{:S(2)}, u32[]{:S(2)}) %collective-permute-start.1) | collective-permute-done | bytes 786464 | tf_op jit(solution)/shard_map/ppermute | solution.py:223
  122.1 2.8 fusion.117
  126.6 18.6 %multiply_convert_fusion.1 = (bf16[768,1024]{1,0:T(8,128)(2,1)}, f32[768,1024]{1,0:T(8,128)S(1)}, f32[768,1024]{1,0:T(8,128)S(1)}) fusion(f32[1024]{0:T(1024)S(1)} %copy-done.84, bf16[768,1024]{1,0:T(8,128)(2,1)S(1)} %add_convert_fusion.4, bf16[1024,1024]{1,0:T(8,128)(2,1)S(1)} %copy-done), kind=kOutput, calls=%fused_computation.102 | convolution fusion | flops 1662517248 | bytes 11538432 | tf_op jit(solution)/shard_map/dot_general | solution.py:306
  145.2 2.9 fusion.119
  148.1 1.9 convolution_convert_fusion.5
  154.5 4.2 convert_element_type.286
  158.8 2.7 copy.100
  163.9 5.1 convolution_convert_fusion.6
  172.2 1.9 broadcast_select_fusion.7
  174.2 2.9 fusion.115
  179.3 15.7 %multiply_convert_fusion = (bf16[1280,1024]{1,0:T(8,128)(2,1)S(1)}, f32[1280,1024]{1,0:T(8,128)S(1)}, f32[1280,1024]{1,0:T(8,128)}) fusion(f32[1024]{0:T(1024)S(1)} %copy-done.84, bf16[1280,1024]{1,0:T(8,128)(2,1)S(1)} %add_convert_fusion.2, bf16[1024,1024]{1,0:T(8,128)(2,1)S(1)} %copy-done), kind=kOutput, calls=%fused_computation.30 | convolution fusion | flops 2770862080 | bytes 17829888 | tf_op jit(solution)/shard_map/dot_general | solution.py:306
  195.0 8.7 %fusion.118 = (f32[1024]{0:T(1024)S(1)}, bf16[1280,1024]{1,0:T(8,128)(2,1)}) fusion(f32[1280,1024]{1,0:T(8,128)S(1)} %get-tuple-element.134, bf16[1024,1024]{1,0:T(8,128)(2,1)S(1)} %copy-done.80, bf16[2048,1024]{1,0:T(8,128)(2,1)S(1)} %copy-done.32, f32[1280,1024]{1,0:T(8,128)} %get-tuple-element.173, f32[1024]{0:T(1024)S(1)} %copy-done.84), kind=kOutput, calls=%fused_computation.274 | convolution fusion | flops 2705325056 | bytes 17833984 | tf_op jit(solution)/shard_map/td,fd->tf/dot_general | solution.py:319
  203.7 6.6 %fusion.61 = bf16[1024,1024]{1,0:T(8,128)(2,1)S(1)} fusion(bf16[1280,1024]{1,0:T(8,128)(2,1)S(1)} %add_convert_fusion.2, bf16[768,1024]{1,0:T(8,128)(2,1)S(1)} %copy-done.58, bf16[1280,1024]{1,0:T(8,128)(2,1)} %get-tuple-element.144, bf16[768,1024]{1,0:T(8,128)(2,1)S(1)} %copy-done.88), kind=kOutput, calls=%fused_computation.150 | convolution fusion | flops 4312793088 | bytes 10485760 | tf_op jit(solution)/shard_map/tf,td->fd/dot_general | solution.py:333
  210.3 3.2 convolution_convert_fusion.1
  216.2 4.8 fusion.66
  221.0 2.5 pad_maximum_fusion.2
  223.4 6.4 %copy.114 = bf16[2048,1024]{0,1:T(8,128)(2,1)} copy(bf16[2048,1024]{1,0:T(8,128)(2,1)} %pad_maximum_fusion.2) | data formatting | bytes 8388608
  232.2 6.3 %convolution_convert_fusion.2 = bf16[1280,1024]{1,0:T(8,128)(2,1)} fusion(bf16[1280,1024]{1,0:T(8,128)(2,1)} %copy-done.85, bf16[1024,1024]{1,0:T(8,128)(2,1)S(1)} %copy-done.81), kind=kOutput, calls=%fused_computation.81 | convolution fusion | flops 2685665280 | bytes 7340032 | tf_op jit(solution)/shard_map/dot_general | solution.py:309
  241.3 21.7 %collective-permute-done.10 = bf16[640,1024]{1,0:T(8,128)(2,1)S(1)} collective-permute-done((bf16[640,1024]{1,0:T(8,128)(2,1)S(1)}, bf16[640,1024]{1,0:T(8,128)(2,1)S(1)}, u32[]{:S(2)}, u32[]{:S(2)}) %collective-permute-start.10) | collective-permute-done | bytes 1310752 | tf_op jit(solution)/shard_map/ppermute | solution.py:223
  263.7 2.4 fusion.38
  266.2 2.0 fusion.111
  272.9 2.4 fusion.5
  275.3 4.3 fusion.7
  279.6 3.3 fusion.110
  287.6 2.1 constant_dynamic-slice_fusion.3
  290.2 2.5 constant_dynamic-slice_fusion.2
  292.8 9.1 %collective-permute-start.27 = (f32[5120]{0:T(1024)S(1)}, f32[5120]{0:T(1024)S(1)}, u32[]{:S(2)}, u32[]{:S(2)}) collective-permute-start(f32[5120]{0:T(1024)S(1)} %constant_dynamic-update-slice_fusion), channel_id=1, source_target_pairs={{0,4},{4,0},{8,12},{12,8},{16,20},{20,16},{24,28},{28,24},{1,5},{5... | collective-permute-start | bytes 61448 | tf_op jit(solution)/shard_map/ppermute | solution.py:237
  304.8 45.9 %segment_flash_bwd.1 = (f32[4,64,2048]{2,1,0:T(8,128)}, f32[4,2048,64]{2,1,0:T(8,128)}, f32[4,2048,64]{2,1,0:T(8,128)}) custom-call(s32[8]{0:T(128)S(1)} %copy-done.21, s32[8]{0:T(128)S(1)} %fusion.99.hi_ref, s32[2048,1]{1,0:T(8,128)S(1)} %copy-done.12, s32[1,2048]{1,0:T(1,128)S(1)} %bitcast.120, bf16[4,2048,64]{2,1,0:T(8,128)(2,1)} %copy.102.q_ref, ...), custom_call_target="tpu_custom_call" | custom-call | flops 5153960960 | bytes 15761408 | tf_op jit(solution)/shard_map/segment_flash_bwd/pallas_call | solution.py:172
  360.9 8.8 %collective-permute-start.28 = (f32[5120]{0:T(1024)S(1)}, f32[5120]{0:T(1024)S(1)}, u32[]{:S(2)}, u32[]{:S(2)}) collective-permute-start(f32[5120]{0:T(1024)S(1)} %add.363), channel_id=1, source_target_pairs={{0,8},{4,12},{8,0},{12,4},{16,24},{20,28},{24,16},{28,20},{1,9},{5... | collective-permute-start | bytes 61448 | tf_op jit(solution)/shard_map/ppermute | solution.py:237
  369.8 3.0 collective-permute-done.13
  374.0 26.1 %collective-permute-done.16 = bf16[640,1024]{1,0:T(8,128)(2,1)S(1)} collective-permute-done((bf16[640,1024]{1,0:T(8,128)(2,1)S(1)}, bf16[640,1024]{1,0:T(8,128)(2,1)S(1)}, u32[]{:S(2)}, u32[]{:S(2)}) %collective-permute-start.16) | collective-permute-done | bytes 1310752 | tf_op jit(solution)/shard_map/ppermute | solution.py:223
  400.8 2.1 fusion.78
  403.2 2.9 copy.105
  406.1 2.3 copy.108
  409.9 2.3 copy.109
  414.4 3.7 add_convert_fusion.3
  419.7 2.5 add_convert_fusion.1
  422.2 2.0 copy.115
  426.2 3.3 bitcast_convert_fusion.2
  430.2 2.5 pad_maximum_fusion.1
  432.8 2.2 bitcast_convert_fusion
  437.5 4.6 fusion.69
  442.0 14.2 %collective-permute-done.19 = bf16[384,1024]{1,0:T(8,128)(2,1)S(1)} collective-permute-done((bf16[384,1024]{1,0:T(8,128)(2,1)S(1)}, bf16[384,1024]{1,0:T(8,128)(2,1)S(1)}, u32[]{:S(2)}, u32[]{:S(2)}) %collective-permute-start.19) | collective-permute-done | bytes 786464 | tf_op jit(solution)/shard_map/ppermute | solution.py:223
  462.7 2.6 copy.116
  468.9 3.6 fusion.39
  472.5 16.8 %collective-permute-done.22 = bf16[640,1024]{1,0:T(8,128)(2,1)} collective-permute-done((bf16[640,1024]{1,0:T(8,128)(2,1)S(1)}, bf16[640,1024]{1,0:T(8,128)(2,1)}, u32[]{:S(2)}, u32[]{:S(2)}) %collective-permute-start.22) | collective-permute-done | bytes 1310752 | tf_op jit(solution)/shard_map/ppermute | solution.py:223
  491.3 3.6 fusion.112
  497.4 3.8 fusion.8
  501.3 7.6 %collective-permute-start.24 = (f32[2560]{0:T(1024)S(1)}, f32[2560]{0:T(1024)S(1)}, u32[]{:S(2)}, u32[]{:S(2)}) collective-permute-start(f32[2560]{0:T(1024)S(1)} %pad_maximum_fusion.11), channel_id=1, source_target_pairs={{0,4},{4,0},{8,12},{12,8},{16,20},{20,16},{24,28},{28,24},{1,5},{5... | collective-permute-start | bytes 30728 | tf_op jit(solution)/shard_map/ppermute | solution.py:237
  508.9 3.3 fusion.113
  512.3 3.1 collective-permute-start.25
  517.0 2.0 collective-permute-start.26
  519.0 4.5 pad_maximum_fusion
  524.7 17.0 %reduce-scatter.9.cloned.1.call-done = bf16[128,1024]{1,0:T(8,128)(2,1)} async-done(((bf16[1024,1024]{1,0:T(8,128)(2,1)}), bf16[128,1024]{1,0:T(8,128)(2,1)}) %reduce-scatter.9.cloned.1.call-update) | async-done | bytes 262160
  (394 shorter events, 114.4 us)
Async XLA Ops:
  7.2 119.4 %copy-start = (bf16[1024,1024]{1,0:T(8,128)(2,1)S(1)}, bf16[1024,1024]{1,0:T(8,128)(2,1)}, u32[]{:S(2)}) copy-start(bf16[1024,1024]{1,0:T(8,128)(2,1)} %param.24) | copy-start | bytes 6291460
  7.2 415.1 %reduce-scatter.7.cloned.1.call-start = ((), (), s32[]{:S(2)}) async-start(), calls=%async_computation.2 | async-start | bytes 4718592
  35.1 13.6 %copy-start.49 = (bf16[256,1024]{1,0:T(8,128)(2,1)S(1)}, bf16[256,1024]{1,0:T(8,128)(2,1)}, u32[]{:S(2)}) copy-start(bf16[256,1024]{1,0:T(8,128)(2,1)} %param.22) | copy-start | bytes 1572868
  50.3 43.7 %collective-permute-start = (bf16[384,1024]{1,0:T(8,128)(2,1)}, bf16[384,1024]{1,0:T(8,128)(2,1)}, u32[]{:S(2)}, u32[]{:S(2)}) collective-permute-start(bf16[384,1024]{1,0:T(8,128)(2,1)} %constant_dynamic-slice_fusion.7), channel_id=1, source_target_pairs={{0,1},{1,0},{2,3},{3,2},{4,5},{5,4},{6,7},{7,6},{8,9},{9,8},{10,11... | collective-permute-start | bytes 2359304 | tf_op jit(solution)/shard_map/ppermute | solution.py:221
  55.4 26.3 %copy-start.50 = (bf16[256,1024]{1,0:T(8,128)(2,1)S(1)}, bf16[256,1024]{1,0:T(8,128)(2,1)}, u32[]{:S(2)}) copy-start(bf16[256,1024]{1,0:T(8,128)(2,1)} %param.22) | copy-start | bytes 1572868
  84.9 33.4 %collective-permute-start.3 = (bf16[640,1024]{1,0:T(8,128)(2,1)}, bf16[640,1024]{1,0:T(8,128)(2,1)}, u32[]{:S(2)}, u32[]{:S(2)}) collective-permute-start(bf16[640,1024]{1,0:T(8,128)(2,1)} %constant_dynamic-slice_fusion.6), channel_id=1, source_target_pairs={{0,1},{1,0},{2,3},{3,2},{4,5},{5,4},{6,7},{7,6},{8,9},{9,8},{10,11... | collective-permute-start | bytes 3932168 | tf_op jit(solution)/shard_map/ppermute | solution.py:221
  91.8 6.8 %copy-start.6 = (f32[4,64,1280]{2,1,0:T(8,128)S(1)}, f32[4,64,1280]{2,1,0:T(8,128)}, u32[]{:S(2)}) copy-start(f32[4,64,1280]{2,1,0:T(8,128)} %copy-done.5) | copy-start | bytes 3932164
  91.8 6.8 %copy-start.14 = (f32[4,64,768]{2,1,0:T(8,128)S(1)}, f32[4,64,768]{2,1,0:T(8,128)}, u32[]{:S(2)}) copy-start(f32[4,64,768]{2,1,0:T(8,128)} %copy-done.13) | copy-start | bytes 2359300
  95.7 20.8 %collective-permute-start.1 = (bf16[384,1024]{1,0:T(8,128)(2,1)S(1)}, bf16[384,1024]{1,0:T(8,128)(2,1)S(1)}, u32[]{:S(2)}, u32[]{:S(2)}) collective-permute-start(bf16[384,1024]{1,0:T(8,128)(2,1)S(1)} %add_convert_fusion.20), channel_id=1, source_target_pairs={{0,2},{1,3},{2,0},{3,1},{4,6},{5,7},{6,4},{7,5},{8,10},{9,11},{10,... | collective-permute-start | bytes 2359304 | tf_op jit(solution)/shard_map/ppermute | solution.py:223
  100.2 16.7 %copy-start.31 = (bf16[2048,1024]{1,0:T(8,128)(2,1)S(1)}, bf16[2048,1024]{1,0:T(8,128)(2,1)}, u32[]{:S(2)}) copy-start(bf16[2048,1024]{1,0:T(8,128)(2,1)} %param.18) | copy-start | bytes 12582916
  103.1 15.1 %copy-start.30 = (bf16[1280,1024]{1,0:T(8,128)(2,1)S(1)}, bf16[1280,1024]{1,0:T(8,128)(2,1)}, u32[]{:S(2)}) copy-start(bf16[1280,1024]{1,0:T(8,128)(2,1)} %copy-done.29) | copy-start | bytes 7864324
  116.8 5.1 collective-permute-start.2
  120.1 31.2 %collective-permute-start.4 = (bf16[640,1024]{1,0:T(8,128)(2,1)S(1)}, bf16[640,1024]{1,0:T(8,128)(2,1)S(1)}, u32[]{:S(2)}, u32[]{:S(2)}) collective-permute-start(bf16[640,1024]{1,0:T(8,128)(2,1)S(1)} %add_convert_fusion.12), channel_id=1, source_target_pairs={{0,2},{1,3},{2,0},{3,1},{4,6},{5,7},{6,4},{7,5},{8,10},{9,11},{10,... | collective-permute-start | bytes 3932168 | tf_op jit(solution)/shard_map/ppermute | solution.py:223
  124.8 38.5 %copy-start.70 = (f32[768]{0:T(1024)}, f32[768]{0:T(1024)S(1)}, u32[]{:S(2)}) copy-start(f32[768]{0:T(1024)S(1)} %get-tuple-element.141) | copy-start | bytes 9220
  126.5 18.7 %copy-start.57 = (bf16[768,1024]{1,0:T(8,128)(2,1)}, bf16[768,1024]{1,0:T(8,128)(2,1)S(1)}, u32[]{:S(2)}) copy-start(bf16[768,1024]{1,0:T(8,128)(2,1)S(1)} %add_convert_fusion.4) | copy-start | bytes 4718596
  126.5 18.7 %copy-start.79 = (bf16[1024,1024]{1,0:T(8,128)(2,1)S(1)}, bf16[1024,1024]{1,0:T(8,128)(2,1)}, u32[]{:S(2)}) copy-start(bf16[1024,1024]{1,0:T(8,128)(2,1)} %param.26) | copy-start | bytes 6291460
  153.0 19.2 %collective-permute-start.5 = (bf16[640,1024]{1,0:T(8,128)(2,1)}, bf16[640,1024]{1,0:T(8,128)(2,1)}, u32[]{:S(2)}, u32[]{:S(2)}) collective-permute-start(bf16[640,1024]{1,0:T(8,128)(2,1)} %add_convert_fusion.11), channel_id=1, source_target_pairs={{0,1},{1,0},{2,3},{3,2},{4,5},{5,4},{6,7},{7,6},{8,9},{9,8},{10,11... | collective-permute-start | bytes 3932168 | tf_op jit(solution)/shard_map/ppermute | solution.py:225
  154.0 15.0 %collective-permute-start.6 = (bf16[384,1024]{1,0:T(8,128)(2,1)}, bf16[384,1024]{1,0:T(8,128)(2,1)}, u32[]{:S(2)}, u32[]{:S(2)}) collective-permute-start(bf16[384,1024]{1,0:T(8,128)(2,1)} %constant_dynamic-slice_fusion.5), channel_id=1, source_target_pairs={{0,1},{1,0},{2,3},{3,2},{4,5},{5,4},{6,7},{7,6},{8,9},{9,8},{10,11... | collective-permute-start | bytes 2359304 | tf_op jit(solution)/shard_map/ppermute | solution.py:221
  154.5 19.6 %copy-start.63 = (f32[1280]{0:T(1024)}, f32[1280]{0:T(1024)S(1)}, u32[]{:S(2)}) copy-start(f32[1280]{0:T(1024)S(1)} %broadcast_multiply_fusion) | copy-start | bytes 15364
  163.9 10.2 %slice-start.4 = ((s8[8388608]{0:T(1024)(128)(4,1)}), s8[4194304]{0:T(1024)(128)(4,1)S(1)}, s32[]{:S(2)}) async-start(s8[8388608]{0:T(1024)(128)(4,1)} %bitcast.129), calls=%async_computation.8 | async-start | bytes 8388608
  163.9 10.2 %slice-start.5 = ((s8[8388608]{0:T(1024)(128)(4,1)}), s8[4194304]{0:T(1024)(128)(4,1)S(1)}, s32[]{:S(2)}) async-start(s8[8388608]{0:T(1024)(128)(4,1)} %bitcast.129), calls=%async_computation.9 | async-start | bytes 8388608
  170.4 43.1 %collective-permute-start.7 = (bf16[384,1024]{1,0:T(8,128)(2,1)S(1)}, bf16[384,1024]{1,0:T(8,128)(2,1)S(1)}, u32[]{:S(2)}, u32[]{:S(2)}) collective-permute-start(bf16[384,1024]{1,0:T(8,128)(2,1)S(1)} %add_convert_fusion.18), channel_id=1, source_target_pairs={{0,2},{1,3},{2,0},{3,1},{4,6},{5,7},{6,4},{7,5},{8,10},{9,11},{10,... | collective-permute-start | bytes 2359304 | tf_op jit(solution)/shard_map/ppermute | solution.py:223
  179.3 15.7 %copy-start.32 = (bf16[2048,1024]{1,0:T(8,128)(2,1)S(1)}, bf16[2048,1024]{1,0:T(8,128)(2,1)}, u32[]{:S(2)}) copy-start(bf16[2048,1024]{1,0:T(8,128)(2,1)} %param.18) | copy-start | bytes 12582916
  179.3 15.7 %copy-start.80 = (bf16[1024,1024]{1,0:T(8,128)(2,1)S(1)}, bf16[1024,1024]{1,0:T(8,128)(2,1)}, u32[]{:S(2)}) copy-start(bf16[1024,1024]{1,0:T(8,128)(2,1)} %param.26) | copy-start | bytes 6291460
  195.0 21.2 %copy-start.85 = (bf16[1280,1024]{1,0:T(8,128)(2,1)}, bf16[1280,1024]{1,0:T(8,128)(2,1)S(1)}, u32[]{:S(2)}) copy-start(bf16[1280,1024]{1,0:T(8,128)(2,1)S(1)} %get-tuple-element.133) | copy-start | bytes 7864324
  195.0 8.7 %copy-start.58 = (bf16[768,1024]{1,0:T(8,128)(2,1)S(1)}, bf16[768,1024]{1,0:T(8,128)(2,1)}, u32[]{:S(2)}) copy-start(bf16[768,1024]{1,0:T(8,128)(2,1)} %copy-done.57) | copy-start | bytes 4718596
  195.0 8.7 %copy-start.88 = (bf16[768,1024]{1,0:T(8,128)(2,1)S(1)}, bf16[768,1024]{1,0:T(8,128)(2,1)}, u32[]{:S(2)}) copy-start(bf16[768,1024]{1,0:T(8,128)(2,1)} %copy-done.87) | copy-start | bytes 4718596
  213.8 7.1 %copy-start.43 = (bf16[384,1024]{1,0:T(8,128)(2,1)}, bf16[384,1024]{1,0:T(8,128)(2,1)S(1)}, u32[]{:S(2)}) copy-start(bf16[384,1024]{1,0:T(8,128)(2,1)S(1)} %add_convert_fusion.17) | copy-start | bytes 2359300
  213.8 24.7 %collective-permute-start.8 = (bf16[384,1024]{1,0:T(8,128)(2,1)S(1)}, bf16[384,1024]{1,0:T(8,128)(2,1)}, u32[]{:S(2)}, u32[]{:S(2)}) collective-permute-start(bf16[384,1024]{1,0:T(8,128)(2,1)S(1)} %add_convert_fusion.17), channel_id=1, source_target_pairs={{0,1},{1,0},{2,3},{3,2},{4,5},{5,4},{6,7},{7,6},{8,9},{9,8},{10,11... | collective-permute-start | bytes 2359304 | tf_op jit(solution)/shard_map/ppermute | solution.py:225
  216.1 13.8 %collective-permute-start.9 = (bf16[640,1024]{1,0:T(8,128)(2,1)}, bf16[640,1024]{1,0:T(8,128)(2,1)S(1)}, u32[]{:S(2)}, u32[]{:S(2)}) collective-permute-start(bf16[640,1024]{1,0:T(8,128)(2,1)} %constant_dynamic-slice_fusion.4), channel_id=1, source_target_pairs={{0,1},{1,0},{2,3},{3,2},{4,5},{5,4},{6,7},{7,6},{8,9},{9,8},{10,11... | collective-permute-start | bytes 3932168 | tf_op jit(solution)/shard_map/ppermute | solution.py:221
  229.9 311.8 %reduce-scatter.9.cloned.1.call-start = ((), (), s32[]{:S(2)}) async-start(), calls=%async_computation.3 | async-start | bytes 2359296
  230.0 36.2 %slice-start.10 = ((s8[8388608]{0:T(1024)(128)(4,1)}), s8[4194304]{0:T(1024)(128)(4,1)S(1)}, s32[]{:S(2)}) async-start(s8[8388608]{0:T(1024)(128)(4,1)} %bitcast.135), calls=%async_computation.14 | async-start | bytes 8388608
  231.8 6.7 %copy-start.44 = (bf16[384,1024]{1,0:T(8,128)(2,1)S(1)}, bf16[384,1024]{1,0:T(8,128)(2,1)}, u32[]{:S(2)}) copy-start(bf16[384,1024]{1,0:T(8,128)(2,1)} %copy-done.43) | copy-start | bytes 2359300
  231.8 34.3 %slice-start.11 = ((s8[8388608]{0:T(1024)(128)(4,1)}), s8[4194304]{0:T(1024)(128)(4,1)S(1)}, s32[]{:S(2)}) async-start(s8[8388608]{0:T(1024)(128)(4,1)} %bitcast.135), calls=%async_computation.15 | async-start | bytes 8388608
  231.8 31.2 %collective-permute-start.10 = (bf16[640,1024]{1,0:T(8,128)(2,1)S(1)}, bf16[640,1024]{1,0:T(8,128)(2,1)S(1)}, u32[]{:S(2)}, u32[]{:S(2)}) collective-permute-start(bf16[640,1024]{1,0:T(8,128)(2,1)S(1)} %add_convert_fusion.10), channel_id=1, source_target_pairs={{0,2},{1,3},{2,0},{3,1},{4,6},{5,7},{6,4},{7,5},{8,10},{9,11},{10,... | collective-permute-start | bytes 3932168 | tf_op jit(solution)/shard_map/ppermute | solution.py:223
  263.6 7.6 %collective-permute-start.11 = (bf16[640,1024]{1,0:T(8,128)(2,1)S(1)}, bf16[640,1024]{1,0:T(8,128)(2,1)S(1)}, u32[]{:S(2)}, u32[]{:S(2)}) collective-permute-start(bf16[640,1024]{1,0:T(8,128)(2,1)S(1)} %add_convert_fusion.9), channel_id=1, source_target_pairs={{0,1},{1,0},{2,3},{3,2},{4,5},{5,4},{6,7},{7,6},{8,9},{9,8},{10,11... | collective-permute-start | bytes 3932168 | tf_op jit(solution)/shard_map/ppermute | solution.py:225
  289.7 13.9 %copy-start.12 = (s32[2048,1]{1,0:T(8,128)S(1)}, s32[2048,1]{1,0:T(8,128)}, u32[]{:S(2)}) copy-start(s32[2048,1]{1,0:T(8,128)} %copy.95.segc_ref) | copy-start | bytes 24580
  289.7 13.9 %copy-start.21 = (s32[8]{0:T(128)S(1)}, s32[8]{0:T(128)}, u32[]{:S(2)}) copy-start(s32[8]{0:T(128)} %fusion.100.lo_ref) | copy-start | bytes 100
  289.7 61.0 %collective-permute-start.12 = (bf16[384,1024]{1,0:T(8,128)(2,1)}, bf16[384,1024]{1,0:T(8,128)(2,1)}, u32[]{:S(2)}, u32[]{:S(2)}) collective-permute-start(bf16[384,1024]{1,0:T(8,128)(2,1)} %constant_dynamic-slice_fusion.3), channel_id=1, source_target_pairs={{0,1},{1,0},{2,3},{3,2},{4,5},{5,4},{6,7},{7,6},{8,9},{9,8},{10,11... | collective-permute-start | bytes 2359304 | tf_op jit(solution)/shard_map/ppermute | solution.py:221
  292.7 60.5 %collective-permute-start.15 = (bf16[640,1024]{1,0:T(8,128)(2,1)}, bf16[640,1024]{1,0:T(8,128)(2,1)}, u32[]{:S(2)}, u32[]{:S(2)}) collective-permute-start(bf16[640,1024]{1,0:T(8,128)(2,1)} %constant_dynamic-slice_fusion.2), channel_id=1, source_target_pairs={{0,1},{1,0},{2,3},{3,2},{4,5},{5,4},{6,7},{7,6},{8,9},{9,8},{10,11... | collective-permute-start | bytes 3932168 | tf_op jit(solution)/shard_map/ppermute | solution.py:221
  292.8 68.1 %collective-permute-start.27 = (f32[5120]{0:T(1024)S(1)}, f32[5120]{0:T(1024)S(1)}, u32[]{:S(2)}, u32[]{:S(2)}) collective-permute-start(f32[5120]{0:T(1024)S(1)} %constant_dynamic-update-slice_fusion), channel_id=1, source_target_pairs={{0,4},{4,0},{8,12},{12,8},{16,20},{20,16},{24,28},{28,24},{1,5},{5... | collective-permute-start | bytes 61448 | tf_op jit(solution)/shard_map/ppermute | solution.py:237
  304.8 45.9 %copy-start.52 = (bf16[768,1024]{1,0:T(8,128)(2,1)S(1)}, bf16[768,1024]{1,0:T(8,128)(2,1)}, u32[]{:S(2)}) copy-start(bf16[768,1024]{1,0:T(8,128)(2,1)} %convolution_convert_fusion.6) | copy-start | bytes 4718596
  304.8 48.3 %copy-start.45 = (bf16[1280,1024]{1,0:T(8,128)(2,1)S(1)}, bf16[1280,1024]{1,0:T(8,128)(2,1)}, u32[]{:S(2)}) copy-start(bf16[1280,1024]{1,0:T(8,128)(2,1)} %convolution_convert_fusion.2) | copy-start | bytes 7864324
  352.3 20.5 %collective-permute-start.13 = (bf16[384,1024]{1,0:T(8,128)(2,1)S(1)}, bf16[384,1024]{1,0:T(8,128)(2,1)S(1)}, u32[]{:S(2)}, u32[]{:S(2)}) collective-permute-start(bf16[384,1024]{1,0:T(8,128)(2,1)S(1)} %add_convert_fusion.16), channel_id=1, source_target_pairs={{0,2},{1,3},{2,0},{3,1},{4,6},{5,7},{6,4},{7,5},{8,10},{9,11},{10,... | collective-permute-start | bytes 2359304 | tf_op jit(solution)/shard_map/ppermute | solution.py:223
  355.0 45.1 %collective-permute-start.16 = (bf16[640,1024]{1,0:T(8,128)(2,1)S(1)}, bf16[640,1024]{1,0:T(8,128)(2,1)S(1)}, u32[]{:S(2)}, u32[]{:S(2)}) collective-permute-start(bf16[640,1024]{1,0:T(8,128)(2,1)S(1)} %add_convert_fusion.8), channel_id=1, source_target_pairs={{0,2},{1,3},{2,0},{3,1},{4,6},{5,7},{6,4},{7,5},{8,10},{9,11},{10,... | collective-permute-start | bytes 3932168 | tf_op jit(solution)/shard_map/ppermute | solution.py:223
  360.9 39.8 %copy-start.3 = (bf16[4,64,1280]{2,1,0:T(8,128)(2,1)S(1)}, bf16[4,64,1280]{2,1,0:T(8,128)(2,1)}, u32[]{:S(2)}) copy-start(bf16[4,64,1280]{2,1,0:T(8,128)(2,1)} %copy-done.2) | copy-start | bytes 1966084
  360.9 39.8 %copy-start.17 = (bf16[4,64,768]{2,1,0:T(8,128)(2,1)S(1)}, bf16[4,64,768]{2,1,0:T(8,128)(2,1)}, u32[]{:S(2)}) copy-start(bf16[4,64,768]{2,1,0:T(8,128)(2,1)} %copy-done.16) | copy-start | bytes 1179652
  360.9 39.8 %copy-start.48 = (bf16[1280,1024]{1,0:T(8,128)(2,1)S(1)}, bf16[1280,1024]{1,0:T(8,128)(2,1)}, u32[]{:S(2)}) copy-start(bf16[1280,1024]{1,0:T(8,128)(2,1)} %copy-done.47) | copy-start | bytes 7864324
  360.9 39.8 %copy-start.56 = (bf16[768,1024]{1,0:T(8,128)(2,1)S(1)}, bf16[768,1024]{1,0:T(8,128)(2,1)}, u32[]{:S(2)}) copy-start(bf16[768,1024]{1,0:T(8,128)(2,1)} %copy-done.55) | copy-start | bytes 4718596
  360.9 41.9 %collective-permute-start.28 = (f32[5120]{0:T(1024)S(1)}, f32[5120]{0:T(1024)S(1)}, u32[]{:S(2)}, u32[]{:S(2)}) collective-permute-start(f32[5120]{0:T(1024)S(1)} %add.363), channel_id=1, source_target_pairs={{0,8},{4,12},{8,0},{12,4},{16,24},{20,28},{24,16},{28,20},{1,9},{5... | collective-permute-start | bytes 61448 | tf_op jit(solution)/shard_map/ppermute | solution.py:237
  374.0 39.0 %collective-permute-start.14 = (bf16[384,1024]{1,0:T(8,128)(2,1)}, bf16[384,1024]{1,0:T(8,128)(2,1)}, u32[]{:S(2)}, u32[]{:S(2)}) collective-permute-start(bf16[384,1024]{1,0:T(8,128)(2,1)} %add_convert_fusion.15), channel_id=1, source_target_pairs={{0,1},{1,0},{2,3},{3,2},{4,5},{5,4},{6,7},{7,6},{8,9},{9,8},{10,11... | collective-permute-start | bytes 2359304 | tf_op jit(solution)/shard_map/ppermute | solution.py:225
  400.6 17.6 %collective-permute-start.17 = (bf16[640,1024]{1,0:T(8,128)(2,1)S(1)}, bf16[640,1024]{1,0:T(8,128)(2,1)}, u32[]{:S(2)}, u32[]{:S(2)}) collective-permute-start(bf16[640,1024]{1,0:T(8,128)(2,1)S(1)} %add_convert_fusion.7), channel_id=1, source_target_pairs={{0,1},{1,0},{2,3},{3,2},{4,5},{5,4},{6,7},{7,6},{8,9},{9,8},{10,11... | collective-permute-start | bytes 3932168 | tf_op jit(solution)/shard_map/ppermute | solution.py:225
  402.8 9.5 %collective-permute-start.29 = (f32[5120]{0:T(1024)S(1)}, f32[5120]{0:T(1024)S(1)}, u32[]{:S(2)}, u32[]{:S(2)}) collective-permute-start(f32[5120]{0:T(1024)S(1)} %add.364), channel_id=1, source_target_pairs={{0,16},{4,20},{8,24},{12,28},{16,0},{20,4},{24,8},{28,12},{1,17},{... | collective-permute-start | bytes 61448 | tf_op jit(solution)/shard_map/ppermute | solution.py:237
  429.6 6.7 %collective-permute-start.18 = (bf16[384,1024]{1,0:T(8,128)(2,1)S(1)}, bf16[384,1024]{1,0:T(8,128)(2,1)S(1)}, u32[]{:S(2)}, u32[]{:S(2)}) collective-permute-start(bf16[384,1024]{1,0:T(8,128)(2,1)S(1)} %constant_dynamic-slice_fusion.1), channel_id=1, source_target_pairs={{0,1},{1,0},{2,3},{3,2},{4,5},{5,4},{6,7},{7,6},{8,9},{9,8},{10,11... | collective-permute-start | bytes 2359304 | tf_op jit(solution)/shard_map/ppermute | solution.py:221
  435.2 22.3 %collective-permute-start.21 = (bf16[640,1024]{1,0:T(8,128)(2,1)S(1)}, bf16[640,1024]{1,0:T(8,128)(2,1)S(1)}, u32[]{:S(2)}, u32[]{:S(2)}) collective-permute-start(bf16[640,1024]{1,0:T(8,128)(2,1)S(1)} %constant_dynamic-slice_fusion), channel_id=1, source_target_pairs={{0,1},{1,0},{2,3},{3,2},{4,5},{5,4},{6,7},{7,6},{8,9},{9,8},{10,11... | collective-permute-start | bytes 3932168 | tf_op jit(solution)/shard_map/ppermute | solution.py:221
  436.7 19.5 %collective-permute-start.19 = (bf16[384,1024]{1,0:T(8,128)(2,1)S(1)}, bf16[384,1024]{1,0:T(8,128)(2,1)S(1)}, u32[]{:S(2)}, u32[]{:S(2)}) collective-permute-start(bf16[384,1024]{1,0:T(8,128)(2,1)S(1)} %add_convert_fusion.14), channel_id=1, source_target_pairs={{0,2},{1,3},{2,0},{3,1},{4,6},{5,7},{6,4},{7,5},{8,10},{9,11},{10,... | collective-permute-start | bytes 2359304 | tf_op jit(solution)/shard_map/ppermute | solution.py:223
  457.4 10.0 %collective-permute-start.20 = (bf16[384,1024]{1,0:T(8,128)(2,1)}, bf16[384,1024]{1,0:T(8,128)(2,1)}, u32[]{:S(2)}, u32[]{:S(2)}) collective-permute-start(bf16[384,1024]{1,0:T(8,128)(2,1)} %add_convert_fusion.13), channel_id=1, source_target_pairs={{0,1},{1,0},{2,3},{3,2},{4,5},{5,4},{6,7},{7,6},{8,9},{9,8},{10,11... | collective-permute-start | bytes 2359304 | tf_op jit(solution)/shard_map/ppermute | solution.py:225
  458.0 31.4 %collective-permute-start.22 = (bf16[640,1024]{1,0:T(8,128)(2,1)S(1)}, bf16[640,1024]{1,0:T(8,128)(2,1)}, u32[]{:S(2)}, u32[]{:S(2)}) collective-permute-start(bf16[640,1024]{1,0:T(8,128)(2,1)S(1)} %add_convert_fusion.6), channel_id=1, source_target_pairs={{0,2},{1,3},{2,0},{3,1},{4,6},{5,7},{6,4},{7,5},{8,10},{9,11},{10,... | collective-permute-start | bytes 3932168 | tf_op jit(solution)/shard_map/ppermute | solution.py:223
  472.5 18.8 %copy-start.71 = (f32[768]{0:T(1024)S(1)}, f32[768]{0:T(1024)}, u32[]{:S(2)}) copy-start(f32[768]{0:T(1024)} %copy-done.70) | copy-start | bytes 9220
  491.2 4.2 collective-permute-start.23
  501.3 11.0 %collective-permute-start.24 = (f32[2560]{0:T(1024)S(1)}, f32[2560]{0:T(1024)S(1)}, u32[]{:S(2)}, u32[]{:S(2)}) collective-permute-start(f32[2560]{0:T(1024)S(1)} %pad_maximum_fusion.11), channel_id=1, source_target_pairs={{0,4},{4,0},{8,12},{12,8},{16,20},{20,16},{24,28},{28,24},{1,5},{5... | collective-permute-start | bytes 30728 | tf_op jit(solution)/shard_map/ppermute | solution.py:237
  512.3 4.7 collective-permute-start.25
  517.0 6.5 %collective-permute-start.26 = (f32[2560]{0:T(1024)S(1)}, f32[2560]{0:T(1024)S(1)}, u32[]{:S(2)}, u32[]{:S(2)}) collective-permute-start(f32[2560]{0:T(1024)S(1)} %add.358), channel_id=1, source_target_pairs={{0,16},{4,20},{8,24},{12,28},{16,0},{20,4},{24,8},{28,12},{1,17},{... | collective-permute-start | bytes 30728 | tf_op jit(solution)/shard_map/ppermute | solution.py:237
  519.0 26.3 %copy-start.1 = (bf16[1024,1024]{1,0:T(8,128)(2,1)S(1)}, bf16[1024,1024]{1,0:T(8,128)(2,1)}, u32[]{:S(2)}) copy-start(bf16[1024,1024]{1,0:T(8,128)(2,1)} %param.24) | copy-start | bytes 6291460
  (70 other events, 195.9 us)
Sparse Core Ops, SparseCore 0:
  230.0 95.3 reduce-scatter.6
  465.4 76.1 reduce-scatter.8

commit v6 on v4

--- a/solution.py
+++ b/solution.py
@@ -330,11 +330,10 @@
     d_pre_low = jnp.concatenate([p["d_pre_low"] for p in pieces_fwd], axis=0)
     grad_b_fc1 = sum(p["b_fc1"] for p in pieces_fwd)
     grad_w_fc2 = jnp.einsum("tf,td->fd", activated, cotangent, preferred_element_type=jnp.float32)
-    grad_w_fc1_t = jnp.einsum("tf,td->fd", d_pre_low, normed_two, preferred_element_type=jnp.float32)
+    grad_w_fc1_t = jnp.einsum(
+        "tf,td->fd", d_pre_low, normed_two, preferred_element_type=jnp.float32
+    )
     mlp_weight_grads = jnp.concatenate([grad_w_fc2, grad_w_fc1_t], axis=0).astype(jnp.bfloat16)
-    mlp_weight_grads, pieces_fwd[-1]["dn_two_partial"] = lax.optimization_barrier(
-        (mlp_weight_grads, pieces_fwd[-1]["dn_two_partial"])
-    )
     summed_mlp = lax.psum_scatter(mlp_weight_grads, "dp", scatter_dimension=1, tiled=True)
     for piece in pieces_fwd:
         d_normed_two_h = mp_allreduce(piece["dn_two_partial"], n_mp)
@@ -375,7 +374,9 @@
     d_values = from_heads(d_v_heads)
     grad_b_qv = jnp.stack([jnp.sum(d_queries, axis=0), jnp.sum(d_values, axis=0)])
     stacked = jnp.stack([d_queries, d_keys, d_values]).astype(jnp.bfloat16)
-    grad_w_qkv_t = jnp.einsum("stc,td->scd", stacked, normed_one, preferred_element_type=jnp.float32)
+    grad_w_qkv_t = jnp.einsum(
+        "stc,td->scd", stacked, normed_one, preferred_element_type=jnp.float32
+    )
     d_normed_one = mp_allreduce(
         jnp.einsum("stc,sdc->td", stacked, w_qkv, preferred_element_type=jnp.float32).astype(
             jnp.bfloat16

time: 595 us -> 587 us (0.987)
  waiting for transfers between devices: 150 us -> 141 us
    ppermute x7, waiting for transfers between devices: 98.8 us -> 90.4 us  [mp_allreduce(): got_far = lax.ppermute(first, 'mp', [(k, k ^ 2) for k in range(4)])]
    unnamed x185 -> x197, local copies, waits for them, and re-layouts: 38.2 us -> 36.8 us
  transfers between devices with their start and end apart: 29 -> 29, of which waited for: 10 -> 8; matrix products, arithmetic and copies ran while one was open for 38% -> 39% of each run, Pallas kernels for 12% -> 12%
where the time goes in v6:
time: 587 us; the launch traced here: 578 us
  waiting for transfers between devices  141 us (24%)
  other arithmetic  127 us (22%)
  matrix products  92.9 us (16%)
  Pallas kernels  83.5 us (14%)
  local copies, waits for them, and re-layouts  73.5 us (13%)
  starting transfers between devices  45.6 us (8%)
  between operations  15.5 us (3%)
    ppermute x7, waiting for transfers between devices, mp_allreduce(): got_far = lax.ppermute(first, 'mp', [(k, k ^ 2) for k in range(4)])  90.4 us
    pallas_call x1, Pallas kernels, flash_backward(): pl.pallas_call(_bwd_kernel, out_shape=(jax.ShapeDtypeStruct((heads, HEAD,...  45.3 us
    unnamed x4, waiting for transfers between devices  42.9 us
    pallas_call x2, Pallas kernels, flash_forward(): pl.pallas_call(_fwd_kernel, out_shape=(jax.ShapeDtypeStruct((heads, HEAD,...  38.2 us
    unnamed x197, local copies, waits for them, and re-layouts  36.8 us
    dot_general x2, matrix products, per_device(): jnp.dot(normed_two_h, w_fc1, preferred_element_type=jnp.float32) + b_fc1  33.9 us
    ppermute x6, starting transfers between devices, dp_allreduce(): lax.ppermute(total, 'dp', [(k, k ^ step) for k in range(n_dp)])  32.8 us
    reduce_sum x6, other arithmetic, normalize(): return centered * lax.rsqrt(spread + 1e-06) * gain + shift  20 us
  transfers between devices with their start and end apart: 29, of which 8 were waited for; matrix products, arithmetic and copies ran while one was open for 39% of the time, Pallas kernels for 12%

profile of v6, /device:TPU:0, one launch (start us, length us, event | category | flops | bytes accessed | tf_op | source)
XLA Modules:
  0.0 578.4 jit_solution(12674977142275959951)
XLA Ops:
  11.6 3.1 convert_reduce_fusion.2
  19.1 2.4 convolution_convert_fusion.4
  22.8 2.8 copy.96.k_ref
  25.5 4.6 fusion.49
  36.9 11.9 %segment_flash_fwd.2 = (bf16[4,64,768]{2,1,0:T(8,128)(2,1)S(1)}, f32[4,64,768]{2,1,0:T(8,128)S(1)}, f32[4,1,768]{2,1,0:T(1,128)S(1)}) custom-call(s32[3]{0:T(128)S(1)} %bitcast.119, s32[3]{0:T(128)S(1)} %bitcast.118, s32[2048,1]{1,0:T(8,128)S(1)} %copy-done.9, s32[1,768]{1,0:T(1,128)S(1)} %reshape.216.segr_ref, bf16[4,64,768]{2,1,0:T(8,128)(2,1)S(1)} %slice.149.qt_ref, ...), custom_call_target="tpu_custom_call" | custom-call | flops 966367616 | bytes 3670016 | tf_op jit(solution)/shard_map/segment_flash_fwd/pallas_call | solution.py:146
  57.6 26.4 %segment_flash_fwd.3 = (bf16[4,64,1280]{2,1,0:T(8,128)(2,1)S(1)}, f32[4,64,1280]{2,1,0:T(8,128)S(1)}, f32[4,1,1280]{2,1,0:T(1,128)S(1)}) custom-call(s32[5]{0:T(128)S(1)} %slice.122.lo_ref, s32[5]{0:T(128)S(1)} %slice.123.hi_ref, s32[2048,1]{1,0:T(8,128)S(1)} %copy-done.10, s32[1,1280]{1,0:T(1,128)S(1)} %reshape.221.segr_ref, ...), custom_call_target="tpu_custom_call" | custom-call | flops 1610612736 | bytes 4718592 | tf_op jit(solution)/shard_map/segment_flash_fwd/pallas_call | solution.py:146
  85.1 2.6 add_convert_fusion.18
  87.7 2.5 collective-permute-start.1
  90.2 2.4 convolution_convert_fusion
  92.6 2.5 constant_dynamic-slice_fusion.5
  95.3 13.5 %collective-permute-done.1 = bf16[384,1024]{1,0:T(8,128)(2,1)} collective-permute-done((bf16[384,1024]{1,0:T(8,128)(2,1)}, bf16[384,1024]{1,0:T(8,128)(2,1)}, u32[]{:S(2)}, u32[]{:S(2)}) %collective-permute-start.1) | collective-permute-done | bytes 786464 | tf_op jit(solution)/shard_map/ppermute | solution.py:223
  108.7 2.6 add_convert_fusion.17
  111.3 6.6 %convert_element_type.234 = f32[2048,1024]{1,0:T(8,128)} convert(bf16[2048,1024]{1,0:T(8,128)(2,1)} %param.17) | non-fusion elementwise | flops 2097152 | bytes 12582912 | tf_op jit(solution)/shard_map/convert_element_type | solution.py:263
  118.0 2.2 add_convert_fusion.12
  123.5 2.4 fusion.96
  127.6 18.6 %multiply_convert_fusion.1 = (bf16[768,1024]{1,0:T(8,128)(2,1)}, f32[768,1024]{1,0:T(8,128)S(1)}, f32[768,1024]{1,0:T(8,128)S(1)}) fusion(f32[1024]{0:T(1024)S(1)} %copy-done.84, bf16[768,1024]{1,0:T(8,128)(2,1)S(1)} %add_convert_fusion.6, bf16[1024,1024]{1,0:T(8,128)(2,1)S(1)} %copy-done), kind=kOutput, calls=%fused_computation.90 | convolution fusion | flops 1662517248 | bytes 11538432 | tf_op jit(solution)/shard_map/dot_general | solution.py:306
  146.3 3.5 fusion.99
  154.7 4.3 convert_element_type.262
  159.0 2.7 copy.100
  163.6 3.3 pad_maximum_fusion.5.o32t_ref
  166.9 3.0 convolution_convert_fusion.6
  169.9 1.9 add_convert_fusion.16
  178.7 15.3 %multiply_convert_fusion = (bf16[1280,1024]{1,0:T(8,128)(2,1)S(1)}, f32[1280,1024]{1,0:T(8,128)S(1)}, f32[1280,1024]{1,0:T(8,128)}) fusion(f32[1024]{0:T(1024)S(1)} %copy-done.84, bf16[1280,1024]{1,0:T(8,128)(2,1)S(1)} %add_convert_fusion.2, bf16[1024,1024]{1,0:T(8,128)(2,1)S(1)} %copy-done), kind=kOutput, calls=%fused_computation.31 | convolution fusion | flops 2770862080 | bytes 17829888 | tf_op jit(solution)/shard_map/dot_general | solution.py:306
  194.0 7.5 %fusion.98 = (f32[1024]{0:T(1024)S(1)}, bf16[1280,1024]{1,0:T(8,128)(2,1)S(1)}) fusion(f32[1280,1024]{1,0:T(8,128)S(1)} %get-tuple-element.127, bf16[1024,1024]{1,0:T(8,128)(2,1)S(1)} %copy-done.81, bf16[2048,1024]{1,0:T(8,128)(2,1)S(1)} %copy-done.30, f32[1280,1024]{1,0:T(8,128)} %get-tuple-element.162, f32[1024]{0:T(1024)S(1)} %copy-done.84), kind=kOutput, calls=%fused_computation.230 | convolution fusion | flops 2705325056 | bytes 17833984 | tf_op jit(solution)/shard_map/td,fd->tf/dot_general | solution.py:319
  201.6 3.2 convolution_convert_fusion.1
  207.5 4.6 fusion.50
  213.0 4.8 fusion.55
  217.8 2.5 pad_maximum_fusion.1
  220.3 6.5 %copy.114 = bf16[2048,1024]{0,1:T(8,128)(2,1)} copy(bf16[2048,1024]{1,0:T(8,128)(2,1)} %pad_maximum_fusion.1) | data formatting | bytes 8388608
  227.0 2.0 add_convert_fusion.10
  229.5 6.2 %convolution_convert_fusion.2 = bf16[1280,1024]{1,0:T(8,128)(2,1)} fusion(bf16[1280,1024]{1,0:T(8,128)(2,1)} %copy-done.85, bf16[1024,1024]{1,0:T(8,128)(2,1)S(1)} %copy-done.82), kind=kOutput, calls=%fused_computation.78 | convolution fusion | flops 2685665280 | bytes 7340032 | tf_op jit(solution)/shard_map/dot_general | solution.py:309
  238.6 21.2 %collective-permute-done.10 = bf16[640,1024]{1,0:T(8,128)(2,1)S(1)} collective-permute-done((bf16[640,1024]{1,0:T(8,128)(2,1)S(1)}, bf16[640,1024]{1,0:T(8,128)(2,1)S(1)}, u32[]{:S(2)}, u32[]{:S(2)}) %collective-permute-start.10) | collective-permute-done | bytes 1310752 | tf_op jit(solution)/shard_map/ppermute | solution.py:223
  260.4 2.5 fusion.37
  263.0 2.0 fusion.91
  269.7 2.4 fusion.7
  272.1 4.2 fusion.9
  276.4 3.3 fusion.90
  289.1 45.3 %segment_flash_bwd.1 = (f32[4,64,2048]{2,1,0:T(8,128)}, f32[4,2048,64]{2,1,0:T(8,128)}, f32[4,2048,64]{2,1,0:T(8,128)}) custom-call(s32[8]{0:T(128)S(1)} %copy-done.19, s32[8]{0:T(128)S(1)} %fusion.80.hi_ref, s32[2048,1]{1,0:T(8,128)S(1)} %copy-done.11, s32[1,2048]{1,0:T(1,128)S(1)} %bitcast.117, bf16[4,2048,64]{2,1,0:T(8,128)(2,1)} %copy.102.q_ref, ...), custom_call_target="tpu_custom_call" | custom-call | flops 5153960960 | bytes 15761408 | tf_op jit(solution)/shard_map/segment_flash_bwd/pallas_call | solution.py:172
  334.3 2.5 convert_bitcast_fusion
  338.9 2.5 bitcast_convert_fusion.1
  343.6 2.0 copy.115
  346.7 5.9 %bitcast_convert_fusion = bf16[2048,1024]{1,0:T(8,128)(2,1)S(1)} fusion(bf16[3,1024,256]{2,1,0:T(8,128)(2,1)} %param.20, bf16[1,2048,256]{2,1,0:T(8,128)(2,1)} %copy.109, bf16[1,2048,256]{2,1,0:T(8,128)(2,1)} %copy.108, bf16[1,2048,256]{2,1,0:T(8,128)(2,1)S(1)} %copy.107), kind=kOutput, calls=%fused_computation.11 | convolution fusion | flops 3226468352 | bytes 8912896 | tf_op jit(solution)/shard_map/stc,sdc->td/dot_general | solution.py:381
  354.9 2.2 copy-done.31
  360.7 16.0 %collective-permute-start.24 = (f32[5120]{0:T(1024)S(1)}, f32[5120]{0:T(1024)S(1)}, u32[]{:S(2)}, u32[]{:S(2)}) collective-permute-start(f32[5120]{0:T(1024)S(1)} %constant_dynamic-update-slice_fusion), channel_id=1, source_target_pairs={{0,4},{4,0},{8,12},{12,8},{16,20},{20,16},{24,28},{28,24},{1,5},{5... | collective-permute-start | bytes 61448 | tf_op jit(solution)/shard_map/ppermute | solution.py:237
  378.5 2.1 collective-permute-start.25
  380.6 4.5 add_convert_fusion.4
  386.8 2.3 add_convert_fusion.13
  391.8 2.0 fusion.65
  393.9 2.7 collective-permute-start.26
  400.7 3.6 add_convert_fusion.5
  404.3 55.7 %collective-permute-done.16 = bf16[640,1024]{1,0:T(8,128)(2,1)} collective-permute-done((bf16[640,1024]{1,0:T(8,128)(2,1)S(1)}, bf16[640,1024]{1,0:T(8,128)(2,1)}, u32[]{:S(2)}, u32[]{:S(2)}) %collective-permute-start.16) | collective-permute-done | bytes 1310752 | tf_op jit(solution)/shard_map/ppermute | solution.py:223
  460.1 3.0 add_convert_fusion.7
  463.1 4.7 add_convert_fusion.3
  468.1 3.7 fusion.58
  472.0 2.6 copy.116
  476.1 3.6 add_convert_fusion.1
  479.7 2.5 pad_maximum_fusion
  482.6 2.6 broadcast_select_fusion.1
  486.0 3.2 fusion.2
  489.3 7.0 %fusion.3 = (f32[1024]{0:T(1024)S(1)}, f32[2048]{0:T(1024)S(1)}, f32[1024]{0:T(1024)S(1)}) fusion(bf16[2048,1024]{1,0:T(8,128)(2,1)S(1)} %copy-done.22, f32[2048]{0:T(1024)S(1)} %copy-done.68, f32[2048]{0:T(1024)S(1)} %copy-done.65, bf16[1024,1024]{1,0:T(8,128)(2,1)S(1)} %get-tuple-element.137, bf16[1024,1024]{1,0:T(8,128)(2,1)S(1)} %get-tuple-element.136, ...), kind=kLoop, calls=%fused_computation.9 | loop fusion | flops 33550336 | bytes 8433664 | tf_op jit(solution)/shard_map/transpose(jvp())/reduce_sum | solution.py:200
  496.3 9.6 %collective-permute-start.21 = (f32[2560]{0:T(1024)S(1)}, f32[2560]{0:T(1024)S(1)}, u32[]{:S(2)}, u32[]{:S(2)}) collective-permute-start(f32[2560]{0:T(1024)S(1)} %pad_maximum_fusion.12), channel_id=1, source_target_pairs={{0,4},{4,0},{8,12},{12,8},{16,20},{20,16},{24,28},{28,24},{1,5},{5... | collective-permute-start | bytes 30728 | tf_op jit(solution)/shard_map/ppermute | solution.py:237
  507.8 42.8 %reduce-scatter.9.cloned.1.call-done = bf16[128,1024]{1,0:T(8,128)(2,1)} async-done(((bf16[1024,1024]{1,0:T(8,128)(2,1)}), bf16[128,1024]{1,0:T(8,128)(2,1)}) %reduce-scatter.9.cloned.1.call-update) | async-done | bytes 262160
  555.3 2.8 collective-permute-done.22
  559.4 10.8 %maximum_add_fusion = f32[2048,1024]{1,0:T(8,128)} fusion(f32[1280,1024]{1,0:T(8,128)} %copy-done.25, f32[768,1024]{1,0:T(8,128)} %copy-done.28, bf16[2048,1024]{1,0:T(8,128)(2,1)} %param.17, f32[2048]{0:T(1024)S(1)} %negate_multiply_fusion.2, f32[2048]{0:T(1024)S(1)} %multiply_multiply_fusion.10, f32[1024]{0:T(1024)S(1)} %copy-done.72, ...), kind=kLoop, calls=%fused_computation.10 | loop fusion | flops 29360128 | bytes 25202688 | tf_op jit(solution)/shard_map/add | solution.py:387
  (352 shorter events, 100.8 us)
Async XLA Ops:
  7.2 120.4 %copy-start = (bf16[1024,1024]{1,0:T(8,128)(2,1)S(1)}, bf16[1024,1024]{1,0:T(8,128)(2,1)}, u32[]{:S(2)}) copy-start(bf16[1024,1024]{1,0:T(8,128)(2,1)} %param.24) | copy-start | bytes 6291460
  7.2 336.4 %reduce-scatter.7.cloned.1.call-start = ((), (), s32[]{:S(2)}) async-start(), calls=%async_computation.2 | async-start | bytes 4718592
  36.9 13.5 %copy-start.49 = (bf16[256,1024]{1,0:T(8,128)(2,1)S(1)}, bf16[256,1024]{1,0:T(8,128)(2,1)}, u32[]{:S(2)}) copy-start(bf16[256,1024]{1,0:T(8,128)(2,1)} %param.22) | copy-start | bytes 1572868
  52.5 32.6 %collective-permute-start = (bf16[384,1024]{1,0:T(8,128)(2,1)}, bf16[384,1024]{1,0:T(8,128)(2,1)}, u32[]{:S(2)}, u32[]{:S(2)}) collective-permute-start(bf16[384,1024]{1,0:T(8,128)(2,1)} %constant_dynamic-slice_fusion.6), channel_id=1, source_target_pairs={{0,1},{1,0},{2,3},{3,2},{4,5},{5,4},{6,7},{7,6},{8,9},{9,8},{10,11... | collective-permute-start | bytes 2359304 | tf_op jit(solution)/shard_map/ppermute | solution.py:221
  57.6 27.5 %copy-start.37 = (bf16[768,1024]{1,0:T(8,128)(2,1)S(1)}, bf16[768,1024]{1,0:T(8,128)(2,1)}, u32[]{:S(2)}) copy-start(bf16[768,1024]{1,0:T(8,128)(2,1)} %copy-done.36) | copy-start | bytes 4718596
  57.6 32.6 %copy-start.50 = (bf16[256,1024]{1,0:T(8,128)(2,1)S(1)}, bf16[256,1024]{1,0:T(8,128)(2,1)}, u32[]{:S(2)}) copy-start(bf16[256,1024]{1,0:T(8,128)(2,1)} %param.22) | copy-start | bytes 1572868
  85.1 5.1 copy-start.2
  87.7 21.0 %collective-permute-start.1 = (bf16[384,1024]{1,0:T(8,128)(2,1)}, bf16[384,1024]{1,0:T(8,128)(2,1)}, u32[]{:S(2)}, u32[]{:S(2)}) collective-permute-start(bf16[384,1024]{1,0:T(8,128)(2,1)} %add_convert_fusion.18), channel_id=1, source_target_pairs={{0,2},{1,3},{2,0},{3,1},{4,6},{5,7},{6,4},{7,5},{8,10},{9,11},{10,... | collective-permute-start | bytes 2359304 | tf_op jit(solution)/shard_map/ppermute | solution.py:223
  95.0 22.9 %collective-permute-start.3 = (bf16[640,1024]{1,0:T(8,128)(2,1)}, bf16[640,1024]{1,0:T(8,128)(2,1)}, u32[]{:S(2)}, u32[]{:S(2)}) collective-permute-start(bf16[640,1024]{1,0:T(8,128)(2,1)} %constant_dynamic-slice_fusion.5), channel_id=1, source_target_pairs={{0,1},{1,0},{2,3},{3,2},{4,5},{5,4},{6,7},{7,6},{8,9},{9,8},{10,11... | collective-permute-start | bytes 3932168 | tf_op jit(solution)/shard_map/ppermute | solution.py:221
  111.3 10.7 %collective-permute-start.2 = (bf16[384,1024]{1,0:T(8,128)(2,1)}, bf16[384,1024]{1,0:T(8,128)(2,1)}, u32[]{:S(2)}, u32[]{:S(2)}) collective-permute-start(bf16[384,1024]{1,0:T(8,128)(2,1)} %add_convert_fusion.17), channel_id=1, source_target_pairs={{0,1},{1,0},{2,3},{3,2},{4,5},{5,4},{6,7},{7,6},{8,9},{9,8},{10,11... | collective-permute-start | bytes 2359304 | tf_op jit(solution)/shard_map/ppermute | solution.py:225
  118.0 5.6 copy-start.73
  120.2 31.4 %collective-permute-start.4 = (bf16[640,1024]{1,0:T(8,128)(2,1)S(1)}, bf16[640,1024]{1,0:T(8,128)(2,1)S(1)}, u32[]{:S(2)}, u32[]{:S(2)}) collective-permute-start(bf16[640,1024]{1,0:T(8,128)(2,1)S(1)} %add_convert_fusion.12), channel_id=1, source_target_pairs={{0,2},{1,3},{2,0},{3,1},{4,6},{5,7},{6,4},{7,5},{8,10},{9,11},{10,... | collective-permute-start | bytes 3932168 | tf_op jit(solution)/shard_map/ppermute | solution.py:223
  127.6 18.7 %copy-start.57 = (bf16[768,1024]{1,0:T(8,128)(2,1)}, bf16[768,1024]{1,0:T(8,128)(2,1)S(1)}, u32[]{:S(2)}) copy-start(bf16[768,1024]{1,0:T(8,128)(2,1)S(1)} %add_convert_fusion.6) | copy-start | bytes 4718596
  127.6 18.7 %copy-start.29 = (bf16[2048,1024]{1,0:T(8,128)(2,1)S(1)}, bf16[2048,1024]{1,0:T(8,128)(2,1)}, u32[]{:S(2)}) copy-start(bf16[2048,1024]{1,0:T(8,128)(2,1)} %param.18) | copy-start | bytes 12582916
  127.6 18.7 %copy-start.80 = (bf16[1024,1024]{1,0:T(8,128)(2,1)S(1)}, bf16[1024,1024]{1,0:T(8,128)(2,1)}, u32[]{:S(2)}) copy-start(bf16[1024,1024]{1,0:T(8,128)(2,1)} %param.26) | copy-start | bytes 6291460
  153.2 20.3 %collective-permute-start.5 = (bf16[640,1024]{1,0:T(8,128)(2,1)}, bf16[640,1024]{1,0:T(8,128)(2,1)}, u32[]{:S(2)}, u32[]{:S(2)}) collective-permute-start(bf16[640,1024]{1,0:T(8,128)(2,1)} %add_convert_fusion.11), channel_id=1, source_target_pairs={{0,1},{1,0},{2,3},{3,2},{4,5},{5,4},{6,7},{7,6},{8,9},{9,8},{10,11... | collective-permute-start | bytes 3932168 | tf_op jit(solution)/shard_map/ppermute | solution.py:225
  154.4 15.5 %collective-permute-start.6 = (bf16[384,1024]{1,0:T(8,128)(2,1)}, bf16[384,1024]{1,0:T(8,128)(2,1)}, u32[]{:S(2)}, u32[]{:S(2)}) collective-permute-start(bf16[384,1024]{1,0:T(8,128)(2,1)} %constant_dynamic-slice_fusion.4), channel_id=1, source_target_pairs={{0,1},{1,0},{2,3},{3,2},{4,5},{5,4},{6,7},{7,6},{8,9},{9,8},{10,11... | collective-permute-start | bytes 2359304 | tf_op jit(solution)/shard_map/ppermute | solution.py:221
  166.9 8.5 %slice-start.2 = ((s8[8388608]{0:T(1024)(128)(4,1)}), s8[4194304]{0:T(1024)(128)(4,1)S(1)}, s32[]{:S(2)}) async-start(s8[8388608]{0:T(1024)(128)(4,1)} %bitcast.124), calls=%async_computation.6 | async-start | bytes 8388608
  166.9 8.5 %slice-start.3 = ((s8[8388608]{0:T(1024)(128)(4,1)}), s8[4194304]{0:T(1024)(128)(4,1)S(1)}, s32[]{:S(2)}) async-start(s8[8388608]{0:T(1024)(128)(4,1)} %bitcast.124), calls=%async_computation.7 | async-start | bytes 8388608
  171.8 40.3 %collective-permute-start.7 = (bf16[384,1024]{1,0:T(8,128)(2,1)S(1)}, bf16[384,1024]{1,0:T(8,128)(2,1)S(1)}, u32[]{:S(2)}, u32[]{:S(2)}) collective-permute-start(bf16[384,1024]{1,0:T(8,128)(2,1)S(1)} %add_convert_fusion.16), channel_id=1, source_target_pairs={{0,2},{1,3},{2,0},{3,1},{4,6},{5,7},{6,4},{7,5},{8,10},{9,11},{10,... | collective-permute-start | bytes 2359304 | tf_op jit(solution)/shard_map/ppermute | solution.py:223
  178.7 15.3 %copy-start.30 = (bf16[2048,1024]{1,0:T(8,128)(2,1)S(1)}, bf16[2048,1024]{1,0:T(8,128)(2,1)}, u32[]{:S(2)}) copy-start(bf16[2048,1024]{1,0:T(8,128)(2,1)} %param.18) | copy-start | bytes 12582916
  194.0 19.0 %copy-start.85 = (bf16[1280,1024]{1,0:T(8,128)(2,1)}, bf16[1280,1024]{1,0:T(8,128)(2,1)S(1)}, u32[]{:S(2)}) copy-start(bf16[1280,1024]{1,0:T(8,128)(2,1)S(1)} %get-tuple-element.126) | copy-start | bytes 7864324
  201.5 6.0 %copy-start.58 = (bf16[768,1024]{1,0:T(8,128)(2,1)S(1)}, bf16[768,1024]{1,0:T(8,128)(2,1)}, u32[]{:S(2)}) copy-start(bf16[768,1024]{1,0:T(8,128)(2,1)} %copy-done.57) | copy-start | bytes 4718596
  201.5 6.0 %copy-start.88 = (bf16[768,1024]{1,0:T(8,128)(2,1)S(1)}, bf16[768,1024]{1,0:T(8,128)(2,1)}, u32[]{:S(2)}) copy-start(bf16[768,1024]{1,0:T(8,128)(2,1)} %copy-done.87) | copy-start | bytes 4718596
  207.5 19.4 %collective-permute-start.9 = (bf16[640,1024]{1,0:T(8,128)(2,1)}, bf16[640,1024]{1,0:T(8,128)(2,1)S(1)}, u32[]{:S(2)}, u32[]{:S(2)}) collective-permute-start(bf16[640,1024]{1,0:T(8,128)(2,1)} %constant_dynamic-slice_fusion.3), channel_id=1, source_target_pairs={{0,1},{1,0},{2,3},{3,2},{4,5},{5,4},{6,7},{7,6},{8,9},{9,8},{10,11... | collective-permute-start | bytes 3932168 | tf_op jit(solution)/shard_map/ppermute | solution.py:221
  212.5 5.3 copy-start.42
  212.5 23.2 %collective-permute-start.8 = (bf16[384,1024]{1,0:T(8,128)(2,1)S(1)}, bf16[384,1024]{1,0:T(8,128)(2,1)}, u32[]{:S(2)}, u32[]{:S(2)}) collective-permute-start(bf16[384,1024]{1,0:T(8,128)(2,1)S(1)} %add_convert_fusion.15), channel_id=1, source_target_pairs={{0,1},{1,0},{2,3},{3,2},{4,5},{5,4},{6,7},{7,6},{8,9},{9,8},{10,11... | collective-permute-start | bytes 2359304 | tf_op jit(solution)/shard_map/ppermute | solution.py:225
  226.9 323.7 %reduce-scatter.9.cloned.1.call-start = ((), (), s32[]{:S(2)}) async-start(), calls=%async_computation.3 | async-start | bytes 2359296
  227.0 36.0 %slice-start.4 = ((s8[8388608]{0:T(1024)(128)(4,1)}), s8[4194304]{0:T(1024)(128)(4,1)S(1)}, s32[]{:S(2)}) async-start(s8[8388608]{0:T(1024)(128)(4,1)} %bitcast.126), calls=%async_computation.8 | async-start | bytes 8388608
  229.0 6.7 %copy-start.43 = (bf16[384,1024]{1,0:T(8,128)(2,1)S(1)}, bf16[384,1024]{1,0:T(8,128)(2,1)}, u32[]{:S(2)}) copy-start(bf16[384,1024]{1,0:T(8,128)(2,1)} %copy-done.42) | copy-start | bytes 2359300
  229.0 34.0 %slice-start.5 = ((s8[8388608]{0:T(1024)(128)(4,1)}), s8[4194304]{0:T(1024)(128)(4,1)S(1)}, s32[]{:S(2)}) async-start(s8[8388608]{0:T(1024)(128)(4,1)} %bitcast.126), calls=%async_computation.9 | async-start | bytes 8388608
  229.0 30.8 %collective-permute-start.10 = (bf16[640,1024]{1,0:T(8,128)(2,1)S(1)}, bf16[640,1024]{1,0:T(8,128)(2,1)S(1)}, u32[]{:S(2)}, u32[]{:S(2)}) collective-permute-start(bf16[640,1024]{1,0:T(8,128)(2,1)S(1)} %add_convert_fusion.10), channel_id=1, source_target_pairs={{0,2},{1,3},{2,0},{3,1},{4,6},{5,7},{6,4},{7,5},{8,10},{9,11},{10,... | collective-permute-start | bytes 3932168 | tf_op jit(solution)/shard_map/ppermute | solution.py:223
  260.4 7.7 %collective-permute-start.11 = (bf16[640,1024]{1,0:T(8,128)(2,1)S(1)}, bf16[640,1024]{1,0:T(8,128)(2,1)S(1)}, u32[]{:S(2)}, u32[]{:S(2)}) collective-permute-start(bf16[640,1024]{1,0:T(8,128)(2,1)S(1)} %add_convert_fusion.9), channel_id=1, source_target_pairs={{0,1},{1,0},{2,3},{3,2},{4,5},{5,4},{6,7},{7,6},{8,9},{9,8},{10,11... | collective-permute-start | bytes 3932168 | tf_op jit(solution)/shard_map/ppermute | solution.py:225
  346.7 5.9 %copy-start.61 = (bf16[1,2048,256]{2,1,0:T(8,128)(2,1)}, bf16[1,2048,256]{2,1,0:T(8,128)(2,1)S(1)}, u32[]{:S(2)}) copy-start(bf16[1,2048,256]{2,1,0:T(8,128)(2,1)S(1)} %copy.107) | copy-start | bytes 3145732
  346.7 8.1 %copy-start.52 = (bf16[768,1024]{1,0:T(8,128)(2,1)S(1)}, bf16[768,1024]{1,0:T(8,128)(2,1)}, u32[]{:S(2)}) copy-start(bf16[768,1024]{1,0:T(8,128)(2,1)} %convolution_convert_fusion.6) | copy-start | bytes 4718596
  352.7 5.1 copy-start.41
  352.7 4.4 copy-start.31
  354.2 26.4 %collective-permute-start.18 = (bf16[1024,1024]{1,0:T(8,128)(2,1)}, bf16[1024,1024]{1,0:T(8,128)(2,1)}, u32[]{:S(2)}, u32[]{:S(2)}) collective-permute-start(bf16[1024,1024]{1,0:T(8,128)(2,1)} %constant_dynamic-slice_fusion), channel_id=1, source_target_pairs={{0,1},{1,0},{2,3},{3,2},{4,5},{5,4},{6,7},{7,6},{8,9},{9,8},{10,11... | collective-permute-start | bytes 6291464 | tf_op jit(solution)/shard_map/ppermute | solution.py:221
  354.9 5.1 collective-permute-start.12
  358.0 31.1 %collective-permute-start.15 = (bf16[640,1024]{1,0:T(8,128)(2,1)S(1)}, bf16[640,1024]{1,0:T(8,128)(2,1)}, u32[]{:S(2)}, u32[]{:S(2)}) collective-permute-start(bf16[640,1024]{1,0:T(8,128)(2,1)S(1)} %constant_dynamic-slice_fusion.1), channel_id=1, source_target_pairs={{0,1},{1,0},{2,3},{3,2},{4,5},{5,4},{6,7},{7,6},{8,9},{9,8},{10,11... | collective-permute-start | bytes 3932168 | tf_op jit(solution)/shard_map/ppermute | solution.py:221
  360.2 26.6 %collective-permute-start.13 = (bf16[384,1024]{1,0:T(8,128)(2,1)S(1)}, bf16[384,1024]{1,0:T(8,128)(2,1)}, u32[]{:S(2)}, u32[]{:S(2)}) collective-permute-start(bf16[384,1024]{1,0:T(8,128)(2,1)S(1)} %add_convert_fusion.14), channel_id=1, source_target_pairs={{0,2},{1,3},{2,0},{3,1},{4,6},{5,7},{6,4},{7,5},{8,10},{9,11},{10,... | collective-permute-start | bytes 2359304 | tf_op jit(solution)/shard_map/ppermute | solution.py:223
  360.7 17.8 %collective-permute-start.24 = (f32[5120]{0:T(1024)S(1)}, f32[5120]{0:T(1024)S(1)}, u32[]{:S(2)}, u32[]{:S(2)}) collective-permute-start(f32[5120]{0:T(1024)S(1)} %constant_dynamic-update-slice_fusion), channel_id=1, source_target_pairs={{0,4},{4,0},{8,12},{12,8},{16,20},{20,16},{24,28},{28,24},{1,5},{5... | collective-permute-start | bytes 61448 | tf_op jit(solution)/shard_map/ppermute | solution.py:237
  378.5 10.6 %copy-start.45 = (bf16[1280,1024]{1,0:T(8,128)(2,1)S(1)}, bf16[1280,1024]{1,0:T(8,128)(2,1)}, u32[]{:S(2)}) copy-start(bf16[1280,1024]{1,0:T(8,128)(2,1)} %convolution_convert_fusion.2) | copy-start | bytes 7864324
  378.5 15.3 %collective-permute-start.25 = (f32[5120]{0:T(1024)S(1)}, f32[5120]{0:T(1024)S(1)}, u32[]{:S(2)}, u32[]{:S(2)}) collective-permute-start(f32[5120]{0:T(1024)S(1)} %add.334), channel_id=1, source_target_pairs={{0,8},{4,12},{8,0},{12,4},{16,24},{20,28},{24,16},{28,20},{1,9},{5... | collective-permute-start | bytes 61448 | tf_op jit(solution)/shard_map/ppermute | solution.py:237
  385.1 6.6 %copy-start.3 = (bf16[4,64,1280]{2,1,0:T(8,128)(2,1)S(1)}, bf16[4,64,1280]{2,1,0:T(8,128)(2,1)}, u32[]{:S(2)}) copy-start(bf16[4,64,1280]{2,1,0:T(8,128)(2,1)} %copy-done.2) | copy-start | bytes 1966084
  385.1 6.6 %copy-start.15 = (bf16[4,64,768]{2,1,0:T(8,128)(2,1)S(1)}, bf16[4,64,768]{2,1,0:T(8,128)(2,1)}, u32[]{:S(2)}) copy-start(bf16[4,64,768]{2,1,0:T(8,128)(2,1)} %copy-done.14) | copy-start | bytes 1179652
  385.1 6.6 %copy-start.48 = (bf16[1280,1024]{1,0:T(8,128)(2,1)S(1)}, bf16[1280,1024]{1,0:T(8,128)(2,1)}, u32[]{:S(2)}) copy-start(bf16[1280,1024]{1,0:T(8,128)(2,1)} %copy-done.47) | copy-start | bytes 7864324
  385.1 6.6 %copy-start.56 = (bf16[768,1024]{1,0:T(8,128)(2,1)S(1)}, bf16[768,1024]{1,0:T(8,128)(2,1)}, u32[]{:S(2)}) copy-start(bf16[768,1024]{1,0:T(8,128)(2,1)} %copy-done.55) | copy-start | bytes 4718596
  385.2 77.9 %collective-permute-start.19 = (bf16[1024,1024]{1,0:T(8,128)(2,1)}, bf16[1024,1024]{1,0:T(8,128)(2,1)}, u32[]{:S(2)}, u32[]{:S(2)}) collective-permute-start(bf16[1024,1024]{1,0:T(8,128)(2,1)} %add_convert_fusion.4), channel_id=1, source_target_pairs={{0,2},{1,3},{2,0},{3,1},{4,6},{5,7},{6,4},{7,5},{8,10},{9,11},{10,... | collective-permute-start | bytes 6291464 | tf_op jit(solution)/shard_map/ppermute | solution.py:223
  389.1 10.1 %collective-permute-start.14 = (bf16[384,1024]{1,0:T(8,128)(2,1)}, bf16[384,1024]{1,0:T(8,128)(2,1)}, u32[]{:S(2)}, u32[]{:S(2)}) collective-permute-start(bf16[384,1024]{1,0:T(8,128)(2,1)} %add_convert_fusion.13), channel_id=1, source_target_pairs={{0,1},{1,0},{2,3},{3,2},{4,5},{5,4},{6,7},{7,6},{8,9},{9,8},{10,11... | collective-permute-start | bytes 2359304 | tf_op jit(solution)/shard_map/ppermute | solution.py:225
  391.0 5.6 copy-start.32
  391.0 69.1 %collective-permute-start.16 = (bf16[640,1024]{1,0:T(8,128)(2,1)S(1)}, bf16[640,1024]{1,0:T(8,128)(2,1)}, u32[]{:S(2)}, u32[]{:S(2)}) collective-permute-start(bf16[640,1024]{1,0:T(8,128)(2,1)S(1)} %add_convert_fusion.8), channel_id=1, source_target_pairs={{0,2},{1,3},{2,0},{3,1},{4,6},{5,7},{6,4},{7,5},{8,10},{9,11},{10,... | collective-permute-start | bytes 3932168 | tf_op jit(solution)/shard_map/ppermute | solution.py:223
  393.8 6.9 %copy-start.75 = (f32[1024]{0:T(1024)S(1)}, f32[1024]{0:T(1024)}, u32[]{:S(2)}) copy-start(f32[1024]{0:T(1024)} %param.27) | copy-start | bytes 12292
  393.9 4.7 collective-permute-start.26
  460.1 8.1 %copy-start.62 = (bf16[1,2048,256]{2,1,0:T(8,128)(2,1)S(1)}, bf16[1,2048,256]{2,1,0:T(8,128)(2,1)}, u32[]{:S(2)}) copy-start(bf16[1,2048,256]{2,1,0:T(8,128)(2,1)} %copy-done.61) | copy-start | bytes 3145732
  463.1 5.1 copy-start.40
  463.1 5.1 copy-start.59
  463.1 5.1 copy-start.60
  463.1 11.6 %collective-permute-start.17 = (bf16[640,1024]{1,0:T(8,128)(2,1)}, bf16[640,1024]{1,0:T(8,128)(2,1)S(1)}, u32[]{:S(2)}, u32[]{:S(2)}) collective-permute-start(bf16[640,1024]{1,0:T(8,128)(2,1)} %add_convert_fusion.7), channel_id=1, source_target_pairs={{0,1},{1,0},{2,3},{3,2},{4,5},{5,4},{6,7},{7,6},{8,9},{9,8},{10,11... | collective-permute-start | bytes 3932168 | tf_op jit(solution)/shard_map/ppermute | solution.py:225
  467.8 14.8 %collective-permute-start.20 = (bf16[1024,1024]{1,0:T(8,128)(2,1)}, bf16[1024,1024]{1,0:T(8,128)(2,1)}, u32[]{:S(2)}, u32[]{:S(2)}) collective-permute-start(bf16[1024,1024]{1,0:T(8,128)(2,1)} %add_convert_fusion.3), channel_id=1, source_target_pairs={{0,1},{1,0},{2,3},{3,2},{4,5},{5,4},{6,7},{7,6},{8,9},{9,8},{10,11... | collective-permute-start | bytes 6291464 | tf_op jit(solution)/shard_map/ppermute | solution.py:225
  496.3 58.0 %collective-permute-start.21 = (f32[2560]{0:T(1024)S(1)}, f32[2560]{0:T(1024)S(1)}, u32[]{:S(2)}, u32[]{:S(2)}) collective-permute-start(f32[2560]{0:T(1024)S(1)} %pad_maximum_fusion.12), channel_id=1, source_target_pairs={{0,4},{4,0},{8,12},{12,8},{16,20},{20,16},{24,28},{28,24},{1,5},{5... | collective-permute-start | bytes 30728 | tf_op jit(solution)/shard_map/ppermute | solution.py:237
  554.3 3.8 collective-permute-start.22
  558.0 12.2 %collective-permute-start.23 = (f32[2560]{0:T(1024)S(1)}, f32[2560]{0:T(1024)S(1)}, u32[]{:S(2)}, u32[]{:S(2)}) collective-permute-start(f32[2560]{0:T(1024)S(1)} %add.329), channel_id=1, source_target_pairs={{0,16},{4,20},{8,24},{12,28},{16,0},{20,4},{24,8},{28,12},{1,17},{... | collective-permute-start | bytes 30728 | tf_op jit(solution)/shard_map/ppermute | solution.py:237
  559.4 12.1 %copy-start.1 = (bf16[1024,1024]{1,0:T(8,128)(2,1)S(1)}, bf16[1024,1024]{1,0:T(8,128)(2,1)}, u32[]{:S(2)}) copy-start(bf16[1024,1024]{1,0:T(8,128)(2,1)} %param.24) | copy-start | bytes 6291460
  (60 other events, 135.4 us)
Sparse Core Ops, SparseCore 0:
  227.0 95.0 reduce-scatter.6
  474.7 75.8 reduce-scatter.8

commit v7 on v6

--- a/solution.py
+++ b/solution.py
@@ -102,8 +102,8 @@
         final = lax.fori_loop(lo_ref[j], hi_ref[j], q_body, tuple((zeros, zeros) for _ in range(HPS)))
         for hh in range(HPS):
             dk, dv = final[hh]
-            dk_ref[hh, pl.ds(c0, TK), :] = dk * scale
-            dv_ref[hh, pl.ds(c0, TK), :] = dv
+            dk_ref[pl.ds(c0, TK), pl.ds(hh * HEAD, HEAD)] = dk * scale
+            dv_ref[pl.ds(c0, TK), pl.ds(hh * HEAD, HEAD)] = dv
         return carry
 
     lax.fori_loop(0, rows // TK, kv_body, 0)
@@ -168,19 +168,20 @@
 def flash_backward(q, k, v, do, o32t, lse, segments, lo, hi):
     heads, rows, _ = q.shape
     plain, flipped, stat, col, row = _head_specs(rows)
+    wide = pl.BlockSpec((rows, HPS * HEAD), lambda h, lo, hi: (0, h))
     flops = int(heads * rows * rows * HEAD * 2 * 4 * 0.6)
     return pl.pallas_call(
         _bwd_kernel,
         out_shape=(
             jax.ShapeDtypeStruct((heads, HEAD, rows), jnp.float32),
-            jax.ShapeDtypeStruct((heads, rows, HEAD), jnp.float32),
-            jax.ShapeDtypeStruct((heads, rows, HEAD), jnp.float32),
+            jax.ShapeDtypeStruct((rows, heads * HEAD), jnp.float32),
+            jax.ShapeDtypeStruct((rows, heads * HEAD), jnp.float32),
         ),
         grid_spec=pltpu.PrefetchScalarGridSpec(
             num_scalar_prefetch=2,
             grid=(heads // HPS,),
             in_specs=[col, row, plain, flipped, plain, flipped, plain, plain, flipped, flipped, stat],
-            out_specs=[flipped, plain, plain],
+            out_specs=[flipped, wide, wide],
             scratch_shapes=[pltpu.VMEM((HPS, 1, rows), jnp.float32)],
         ),
         compiler_params=pltpu.CompilerParams(
@@ -275,9 +276,6 @@
 
     def to_heads(values):
         return values.reshape(values.shape[0], heads_here, HEAD).transpose(1, 0, 2)
-
-    def from_heads(values):
-        return values.transpose(1, 0, 2).reshape(row_count, local_cols)
 
     lo_blocks, hi_blocks = block_ranges(segments, item_lengths[0])
     query_heads = to_heads(queries)
@@ -352,7 +350,9 @@
     grad_b_out = jnp.sum(d_middle, axis=0)
     d_middle_low = jnp.concatenate([p["d_middle_low"] for p in pieces_fwd], axis=0)
     attended = jnp.concatenate([p["attended"] for p in pieces_fwd], axis=0)
-    grad_w_out = jnp.einsum("tc,td->cd", attended, d_middle_low, preferred_element_type=jnp.float32)
+    grad_w_out = jnp.einsum(
+        "tc,td->cd", attended, d_middle_low, preferred_element_type=jnp.float32
+    )
     d_attended = jnp.concatenate([p["d_attended"] for p in pieces_fwd], axis=0)
     out_f32 = jnp.concatenate([p["out32_t"] for p in pieces_fwd], axis=2)
     log_norms = jnp.concatenate([p["lse"] for p in pieces_fwd], axis=2)
@@ -370,13 +370,11 @@
     )
     summed_mlp, d_q_heads = lax.optimization_barrier((summed_mlp, d_q_heads))
     d_queries = d_q_heads.transpose(2, 0, 1).reshape(row_count, local_cols)
-    d_keys = from_heads(d_k_heads)
-    d_values = from_heads(d_v_heads)
+    d_keys = d_k_heads
+    d_values = d_v_heads
     grad_b_qv = jnp.stack([jnp.sum(d_queries, axis=0), jnp.sum(d_values, axis=0)])
     stacked = jnp.stack([d_queries, d_keys, d_values]).astype(jnp.bfloat16)
-    grad_w_qkv_t = jnp.einsum(
-        "stc,td->scd", stacked, normed_one, preferred_element_type=jnp.float32
-    )
+    grad_w_qkv_t = jnp.einsum("stc,td->scd", stacked, normed_one, preferred_element_type=jnp.float32)
     d_normed_one = mp_allreduce(
         jnp.einsum("stc,sdc->td", stacked, w_qkv, preferred_element_type=jnp.float32).astype(
             jnp.bfloat16

time: 587 us -> 598 us (1.019)
  matrix products: 92.9 us -> 106 us
  other arithmetic: 127 us -> 117 us
  starting transfers between devices: 45.6 us -> 52.3 us
    dot_general x2, matrix products: 33.9 us -> 49.9 us  [per_device(): jnp.dot(normed_two_h, w_fc1, preferred_element_type=jnp.float32) + b_fc1]
    ppermute x6, starting transfers between devices: 32.8 us -> 39.6 us  [dp_allreduce(): lax.ppermute(total, 'dp', [(k, k ^ step) for k in range(n_dp)])]
  transfers between devices with their start and end apart: 29 -> 29, of which waited for: 8 -> 9; matrix products, arithmetic and copies ran while one was open for 39% -> 38% of each run, Pallas kernels for 12% -> 12%
where the time goes in v7:
time: 598 us; the launch traced here: 590 us
  waiting for transfers between devices  144 us (24%)
  other arithmetic  117 us (20%)
  matrix products  106 us (18%)
  Pallas kernels  83.2 us (14%)
  local copies, waits for them, and re-layouts  72 us (12%)
  starting transfers between devices  52.3 us (9%)
  between operations  15.6 us (3%)
    ppermute x7, waiting for transfers between devices, mp_allreduce(): got_far = lax.ppermute(first, 'mp', [(k, k ^ 2) for k in range(4)])  93.8 us
    dot_general x2, matrix products, per_device(): jnp.dot(normed_two_h, w_fc1, preferred_element_type=jnp.float32) + b_fc1  49.9 us
    pallas_call x1, Pallas kernels, flash_backward(): pl.pallas_call(_bwd_kernel, out_shape=(jax.ShapeDtypeStruct((heads, HEAD,...  44.9 us
    unnamed x4, waiting for transfers between devices  42.9 us
    ppermute x6, starting transfers between devices, dp_allreduce(): lax.ppermute(total, 'dp', [(k, k ^ step) for k in range(n_dp)])  39.6 us
    unnamed x197, local copies, waits for them, and re-layouts  38.3 us
    pallas_call x2, Pallas kernels, flash_forward(): pl.pallas_call(_fwd_kernel, out_shape=(jax.ShapeDtypeStruct((heads, HEAD,...  38.3 us
    reduce_sum x6, other arithmetic, normalize(): return centered * lax.rsqrt(spread + 1e-06) * gain + shift  20 us
  transfers between devices with their start and end apart: 29, of which 9 were waited for; matrix products, arithmetic and copies ran while one was open for 38% of the time, Pallas kernels for 12%

profile of v7, /device:TPU:0, one launch (start us, length us, event | category | flops | bytes accessed | tf_op | source)
XLA Modules:
  0.0 589.8 jit_solution(17073633297270231124)
XLA Ops:
  11.6 3.1 convert_reduce_fusion.2
  19.1 2.4 convolution_convert_fusion.4
  22.8 2.7 copy.70.k_ref
  25.5 4.6 fusion.49
  36.9 11.9 %segment_flash_fwd.2 = (bf16[4,64,768]{2,1,0:T(8,128)(2,1)S(1)}, f32[4,64,768]{2,1,0:T(8,128)S(1)}, f32[4,1,768]{2,1,0:T(1,128)S(1)}) custom-call(s32[3]{0:T(128)S(1)} %bitcast.117, s32[3]{0:T(128)S(1)} %bitcast.116, s32[2048,1]{1,0:T(8,128)S(1)} %copy-done.9, s32[1,768]{1,0:T(1,128)S(1)} %reshape.213.segr_ref, bf16[4,64,768]{2,1,0:T(8,128)(2,1)S(1)} %slice.149.qt_ref, ...), custom_call_target="tpu_custom_call" | custom-call | flops 966367616 | bytes 3670016 | tf_op jit(solution)/shard_map/segment_flash_fwd/pallas_call | solution.py:146
  57.5 26.4 %segment_flash_fwd.3 = (bf16[4,64,1280]{2,1,0:T(8,128)(2,1)S(1)}, f32[4,64,1280]{2,1,0:T(8,128)S(1)}, f32[4,1,1280]{2,1,0:T(1,128)S(1)}) custom-call(s32[5]{0:T(128)S(1)} %slice.122.lo_ref, s32[5]{0:T(128)S(1)} %slice.123.hi_ref, s32[2048,1]{1,0:T(8,128)S(1)} %copy-done.10, s32[1,1280]{1,0:T(1,128)S(1)} %reshape.218.segr_ref, ...), custom_call_target="tpu_custom_call" | custom-call | flops 1610612736 | bytes 4718592 | tf_op jit(solution)/shard_map/segment_flash_fwd/pallas_call | solution.py:146
  85.1 2.6 add_convert_fusion.18
  87.6 2.5 collective-permute-start.1
  90.1 2.3 convolution_convert_fusion
  92.5 2.5 constant_dynamic-slice_fusion.5
  95.2 13.4 %collective-permute-done.1 = bf16[384,1024]{1,0:T(8,128)(2,1)} collective-permute-done((bf16[384,1024]{1,0:T(8,128)(2,1)}, bf16[384,1024]{1,0:T(8,128)(2,1)}, u32[]{:S(2)}, u32[]{:S(2)}) %collective-permute-start.1) | collective-permute-done | bytes 786464 | tf_op jit(solution)/shard_map/ppermute | solution.py:224
  108.6 2.6 add_convert_fusion.17
  111.3 6.6 %convert_element_type.234 = f32[2048,1024]{1,0:T(8,128)} convert(bf16[2048,1024]{1,0:T(8,128)(2,1)} %param.17) | non-fusion elementwise | flops 2097152 | bytes 12582912 | tf_op jit(solution)/shard_map/convert_element_type | solution.py:264
  117.9 2.2 add_convert_fusion.12
  123.5 2.4 fusion.96
  127.5 18.6 %multiply_convert_fusion.1 = (bf16[768,1024]{1,0:T(8,128)(2,1)}, f32[768,1024]{1,0:T(8,128)S(1)}, f32[768,1024]{1,0:T(8,128)S(1)}) fusion(f32[1024]{0:T(1024)S(1)} %copy-done.82, bf16[768,1024]{1,0:T(8,128)(2,1)S(1)} %add_convert_fusion.6, bf16[1024,1024]{1,0:T(8,128)(2,1)S(1)} %copy-done), kind=kOutput, calls=%fused_computation.88 | convolution fusion | flops 1662517248 | bytes 11538432 | tf_op jit(solution)/shard_map/dot_general | solution.py:304
  146.2 3.5 fusion.99
  149.7 1.8 convolution_convert_fusion.5
  154.7 4.3 convert_element_type.262
  159.0 2.7 copy.74
  163.5 3.3 pad_maximum_fusion.5.o32t_ref
  166.8 3.0 convolution_convert_fusion.6
  169.8 2.9 add_convert_fusion.16
  174.2 1.9 broadcast_select_fusion.7
  179.5 31.2 %multiply_convert_fusion = (bf16[1280,1024]{1,0:T(8,128)(2,1)S(1)}, f32[1280,1024]{1,0:T(8,128)S(1)}, f32[1280,1024]{1,0:T(8,128)S(1)}) fusion(f32[1024]{0:T(1024)S(1)} %copy-done.82, bf16[1280,1024]{1,0:T(8,128)(2,1)S(1)} %add_convert_fusion.2, bf16[1024,1024]{1,0:T(8,128)(2,1)S(1)} %copy-done), kind=kOutput, calls=%fused_computation.31 | convolution fusion | flops 2770862080 | bytes 17829888 | tf_op jit(solution)/shard_map/dot_general | solution.py:304
  210.8 5.9 %fusion.98 = (f32[1024]{0:T(1024)S(1)}, bf16[1280,1024]{1,0:T(8,128)(2,1)}) fusion(f32[1280,1024]{1,0:T(8,128)S(1)} %get-tuple-element.113, bf16[1024,1024]{1,0:T(8,128)(2,1)S(1)} %copy-done.79, bf16[2048,1024]{1,0:T(8,128)(2,1)S(1)} %copy-done.31, f32[1280,1024]{1,0:T(8,128)S(1)} %get-tuple-element.150, f32[1024]{0:T(1024)S(1)} %copy-done.82), kind=kOutput, calls=%fused_computation.229 | convolution fusion | flops 2705325056 | bytes 17833984 | tf_op jit(solution)/shard_map/td,fd->tf/dot_general | solution.py:317
  216.7 5.2 convolution_convert_fusion.1
  221.9 4.6 fusion.50
  227.7 4.8 fusion.55
  232.5 2.4 pad_maximum_fusion.1
  234.9 6.6 %copy.84 = bf16[2048,1024]{0,1:T(8,128)(2,1)} copy(bf16[2048,1024]{1,0:T(8,128)(2,1)} %pad_maximum_fusion.1) | data formatting | bytes 8388608
  244.0 2.4 add_convert_fusion.10
  246.9 4.3 convolution_convert_fusion.2
  253.9 23.3 %collective-permute-done.10 = bf16[640,1024]{1,0:T(8,128)(2,1)S(1)} collective-permute-done((bf16[640,1024]{1,0:T(8,128)(2,1)S(1)}, bf16[640,1024]{1,0:T(8,128)(2,1)S(1)}, u32[]{:S(2)}, u32[]{:S(2)}) %collective-permute-start.10) | collective-permute-done | bytes 1310752 | tf_op jit(solution)/shard_map/ppermute | solution.py:224
  277.8 2.5 fusion.37
  280.3 2.0 fusion.91
  287.1 2.4 fusion.7
  289.5 4.2 fusion.9
  293.7 3.3 fusion.90
  297.4 1.8 copy-done.26
  306.4 44.9 %segment_flash_bwd.1 = (f32[4,64,2048]{2,1,0:T(8,128)}, f32[2048,256]{1,0:T(8,128)}, f32[2048,256]{1,0:T(8,128)}) custom-call(s32[8]{0:T(128)S(1)} %copy-done.19, s32[8]{0:T(128)S(1)} %fusion.80.hi_ref, s32[2048,1]{1,0:T(8,128)S(1)} %copy-done.11, s32[1,2048]{1,0:T(1,128)S(1)} %bitcast.115, bf16[4,2048,64]{2,1,0:T(8,128)(2,1)} %copy.76.q_ref, ...), custom_call_target="tpu_custom_call" | custom-call | flops 5153960960 | bytes 15761408 | tf_op jit(solution)/shard_map/segment_flash_bwd/pallas_call | solution.py:173
  351.4 3.7 fusion.100
  356.1 2.0 copy.85
  360.4 5.5 bitcast_convert_fusion
  365.9 2.0 copy-done.40
  370.5 3.0 convert_reduce_fusion.4
  376.2 2.7 add_convert_fusion.4
  380.6 15.5 %collective-permute-done.13 = bf16[384,1024]{1,0:T(8,128)(2,1)S(1)} collective-permute-done((bf16[384,1024]{1,0:T(8,128)(2,1)S(1)}, bf16[384,1024]{1,0:T(8,128)(2,1)S(1)}, u32[]{:S(2)}, u32[]{:S(2)}) %collective-permute-start.13) | collective-permute-done | bytes 786464 | tf_op jit(solution)/shard_map/ppermute | solution.py:224
  397.6 16.4 %collective-permute-start.24 = (f32[5120]{0:T(1024)S(1)}, f32[5120]{0:T(1024)S(1)}, u32[]{:S(2)}, u32[]{:S(2)}) collective-permute-start(f32[5120]{0:T(1024)S(1)} %constant_dynamic-update-slice_fusion), channel_id=1, source_target_pairs={{0,4},{4,0},{8,12},{12,8},{16,20},{20,16},{24,28},{28,24},{1,5},{5... | collective-permute-start | bytes 61448 | tf_op jit(solution)/shard_map/ppermute | solution.py:238
  415.8 2.0 collective-permute-start.25
  419.5 2.5 collective-permute-start.26
  427.0 41.6 %collective-permute-done.16 = bf16[640,1024]{1,0:T(8,128)(2,1)S(1)} collective-permute-done((bf16[640,1024]{1,0:T(8,128)(2,1)S(1)}, bf16[640,1024]{1,0:T(8,128)(2,1)S(1)}, u32[]{:S(2)}, u32[]{:S(2)}) %collective-permute-start.16) | collective-permute-done | bytes 1310752 | tf_op jit(solution)/shard_map/ppermute | solution.py:224
  469.2 2.4 add_convert_fusion.3
  472.7 3.7 fusion.58
  476.6 2.6 copy.86
  480.7 3.6 add_convert_fusion.1
  484.3 2.5 pad_maximum_fusion
  487.2 2.6 broadcast_select_fusion.1
  490.6 3.2 fusion.2
  493.9 7.0 %fusion.3 = (f32[1024]{0:T(1024)S(1)}, f32[2048]{0:T(1024)S(1)}, f32[1024]{0:T(1024)S(1)}) fusion(bf16[2048,1024]{1,0:T(8,128)(2,1)S(1)} %copy-done.22, f32[2048]{0:T(1024)S(1)} %copy-done.66, f32[2048]{0:T(1024)S(1)} %copy-done.63, bf16[1024,1024]{1,0:T(8,128)(2,1)S(1)} %get-tuple-element.123, bf16[1024,1024]{1,0:T(8,128)(2,1)S(1)} %get-tuple-element.122, ...), kind=kLoop, calls=%fused_computation.9 | loop fusion | flops 33550336 | bytes 8433664 | tf_op jit(solution)/shard_map/transpose(jvp())/reduce_sum | solution.py:201
  500.9 16.4 %collective-permute-start.21 = (f32[2560]{0:T(1024)S(1)}, f32[2560]{0:T(1024)S(1)}, u32[]{:S(2)}, u32[]{:S(2)}) collective-permute-start(f32[2560]{0:T(1024)S(1)} %pad_maximum_fusion.12), channel_id=1, source_target_pairs={{0,4},{4,0},{8,12},{12,8},{16,20},{20,16},{24,28},{28,24},{1,5},{5... | collective-permute-start | bytes 30728 | tf_op jit(solution)/shard_map/ppermute | solution.py:238
  519.1 42.9 %reduce-scatter.9.cloned.1.call-done = bf16[128,1024]{1,0:T(8,128)(2,1)} async-done(((bf16[1024,1024]{1,0:T(8,128)(2,1)}), bf16[128,1024]{1,0:T(8,128)(2,1)}) %reduce-scatter.9.cloned.1.call-update) | async-done | bytes 262160
  566.6 2.8 collective-permute-done.22
  570.7 10.8 %maximum_add_fusion = f32[2048,1024]{1,0:T(8,128)} fusion(f32[1280,1024]{1,0:T(8,128)} %copy-done.26, f32[768,1024]{1,0:T(8,128)} %copy-done.29, bf16[2048,1024]{1,0:T(8,128)(2,1)} %param.17, f32[2048]{0:T(1024)S(1)} %negate_multiply_fusion.2, f32[2048]{0:T(1024)S(1)} %multiply_multiply_fusion.10, f32[1024]{0:T(1024)S(1)} %copy-done.70, ...), kind=kLoop, calls=%fused_computation.10 | loop fusion | flops 29360128 | bytes 25202688 | tf_op jit(solution)/shard_map/add | solution.py:385
  (346 shorter events, 94.9 us)
Async XLA Ops:
  7.2 120.3 %copy-start = (bf16[1024,1024]{1,0:T(8,128)(2,1)S(1)}, bf16[1024,1024]{1,0:T(8,128)(2,1)}, u32[]{:S(2)}) copy-start(bf16[1024,1024]{1,0:T(8,128)(2,1)} %param.24) | copy-start | bytes 6291460
  7.2 348.9 %reduce-scatter.7.cloned.1.call-start = ((), (), s32[]{:S(2)}) async-start(), calls=%async_computation.2 | async-start | bytes 4718592
  11.1 3.7 copy-start.21
  36.8 13.5 %copy-start.46 = (bf16[256,1024]{1,0:T(8,128)(2,1)S(1)}, bf16[256,1024]{1,0:T(8,128)(2,1)}, u32[]{:S(2)}) copy-start(bf16[256,1024]{1,0:T(8,128)(2,1)} %param.22) | copy-start | bytes 1572868
  52.4 32.6 %collective-permute-start = (bf16[384,1024]{1,0:T(8,128)(2,1)}, bf16[384,1024]{1,0:T(8,128)(2,1)}, u32[]{:S(2)}, u32[]{:S(2)}) collective-permute-start(bf16[384,1024]{1,0:T(8,128)(2,1)} %constant_dynamic-slice_fusion.6), channel_id=1, source_target_pairs={{0,1},{1,0},{2,3},{3,2},{4,5},{5,4},{6,7},{7,6},{8,9},{9,8},{10,11... | collective-permute-start | bytes 2359304 | tf_op jit(solution)/shard_map/ppermute | solution.py:222
  57.5 27.5 %copy-start.36 = (bf16[768,1024]{1,0:T(8,128)(2,1)S(1)}, bf16[768,1024]{1,0:T(8,128)(2,1)}, u32[]{:S(2)}) copy-start(bf16[768,1024]{1,0:T(8,128)(2,1)} %copy-done.35) | copy-start | bytes 4718596
  57.5 32.6 %copy-start.47 = (bf16[256,1024]{1,0:T(8,128)(2,1)S(1)}, bf16[256,1024]{1,0:T(8,128)(2,1)}, u32[]{:S(2)}) copy-start(bf16[256,1024]{1,0:T(8,128)(2,1)} %param.22) | copy-start | bytes 1572868
  85.1 5.1 copy-start.2
  87.6 21.0 %collective-permute-start.1 = (bf16[384,1024]{1,0:T(8,128)(2,1)}, bf16[384,1024]{1,0:T(8,128)(2,1)}, u32[]{:S(2)}, u32[]{:S(2)}) collective-permute-start(bf16[384,1024]{1,0:T(8,128)(2,1)} %add_convert_fusion.18), channel_id=1, source_target_pairs={{0,2},{1,3},{2,0},{3,1},{4,6},{5,7},{6,4},{7,5},{8,10},{9,11},{10,... | collective-permute-start | bytes 2359304 | tf_op jit(solution)/shard_map/ppermute | solution.py:224
  95.0 22.9 %collective-permute-start.3 = (bf16[640,1024]{1,0:T(8,128)(2,1)}, bf16[640,1024]{1,0:T(8,128)(2,1)}, u32[]{:S(2)}, u32[]{:S(2)}) collective-permute-start(bf16[640,1024]{1,0:T(8,128)(2,1)} %constant_dynamic-slice_fusion.5), channel_id=1, source_target_pairs={{0,1},{1,0},{2,3},{3,2},{4,5},{5,4},{6,7},{7,6},{8,9},{9,8},{10,11... | collective-permute-start | bytes 3932168 | tf_op jit(solution)/shard_map/ppermute | solution.py:222
  111.2 10.7 %collective-permute-start.2 = (bf16[384,1024]{1,0:T(8,128)(2,1)}, bf16[384,1024]{1,0:T(8,128)(2,1)}, u32[]{:S(2)}, u32[]{:S(2)}) collective-permute-start(bf16[384,1024]{1,0:T(8,128)(2,1)} %add_convert_fusion.17), channel_id=1, source_target_pairs={{0,1},{1,0},{2,3},{3,2},{4,5},{5,4},{6,7},{7,6},{8,9},{9,8},{10,11... | collective-permute-start | bytes 2359304 | tf_op jit(solution)/shard_map/ppermute | solution.py:226
  117.9 5.6 copy-start.71
  120.1 31.4 %collective-permute-start.4 = (bf16[640,1024]{1,0:T(8,128)(2,1)S(1)}, bf16[640,1024]{1,0:T(8,128)(2,1)S(1)}, u32[]{:S(2)}, u32[]{:S(2)}) collective-permute-start(bf16[640,1024]{1,0:T(8,128)(2,1)S(1)} %add_convert_fusion.12), channel_id=1, source_target_pairs={{0,2},{1,3},{2,0},{3,1},{4,6},{5,7},{6,4},{7,5},{8,10},{9,11},{10,... | collective-permute-start | bytes 3932168 | tf_op jit(solution)/shard_map/ppermute | solution.py:224
  127.5 18.7 %copy-start.56 = (bf16[768,1024]{1,0:T(8,128)(2,1)}, bf16[768,1024]{1,0:T(8,128)(2,1)S(1)}, u32[]{:S(2)}) copy-start(bf16[768,1024]{1,0:T(8,128)(2,1)S(1)} %add_convert_fusion.6) | copy-start | bytes 4718596
  127.5 18.7 %copy-start.30 = (bf16[2048,1024]{1,0:T(8,128)(2,1)S(1)}, bf16[2048,1024]{1,0:T(8,128)(2,1)}, u32[]{:S(2)}) copy-start(bf16[2048,1024]{1,0:T(8,128)(2,1)} %param.18) | copy-start | bytes 12582916
  127.5 18.7 %copy-start.78 = (bf16[1024,1024]{1,0:T(8,128)(2,1)S(1)}, bf16[1024,1024]{1,0:T(8,128)(2,1)}, u32[]{:S(2)}) copy-start(bf16[1024,1024]{1,0:T(8,128)(2,1)} %param.26) | copy-start | bytes 6291460
  153.2 21.1 %collective-permute-start.5 = (bf16[640,1024]{1,0:T(8,128)(2,1)}, bf16[640,1024]{1,0:T(8,128)(2,1)}, u32[]{:S(2)}, u32[]{:S(2)}) collective-permute-start(bf16[640,1024]{1,0:T(8,128)(2,1)} %add_convert_fusion.11), channel_id=1, source_target_pairs={{0,1},{1,0},{2,3},{3,2},{4,5},{5,4},{6,7},{7,6},{8,9},{9,8},{10,11... | collective-permute-start | bytes 3932168 | tf_op jit(solution)/shard_map/ppermute | solution.py:226
  154.3 15.4 %collective-permute-start.6 = (bf16[384,1024]{1,0:T(8,128)(2,1)}, bf16[384,1024]{1,0:T(8,128)(2,1)}, u32[]{:S(2)}, u32[]{:S(2)}) collective-permute-start(bf16[384,1024]{1,0:T(8,128)(2,1)} %constant_dynamic-slice_fusion.4), channel_id=1, source_target_pairs={{0,1},{1,0},{2,3},{3,2},{4,5},{5,4},{6,7},{7,6},{8,9},{9,8},{10,11... | collective-permute-start | bytes 2359304 | tf_op jit(solution)/shard_map/ppermute | solution.py:222
  166.8 9.4 %slice-start.2 = ((s8[8388608]{0:T(1024)(128)(4,1)}), s8[4194304]{0:T(1024)(128)(4,1)S(1)}, s32[]{:S(2)}) async-start(s8[8388608]{0:T(1024)(128)(4,1)} %bitcast.122), calls=%async_computation.6 | async-start | bytes 8388608
  166.8 9.4 %slice-start.3 = ((s8[8388608]{0:T(1024)(128)(4,1)}), s8[4194304]{0:T(1024)(128)(4,1)S(1)}, s32[]{:S(2)}) async-start(s8[8388608]{0:T(1024)(128)(4,1)} %bitcast.122), calls=%async_computation.7 | async-start | bytes 8388608
  172.7 68.9 %collective-permute-start.7 = (bf16[384,1024]{1,0:T(8,128)(2,1)}, bf16[384,1024]{1,0:T(8,128)(2,1)}, u32[]{:S(2)}, u32[]{:S(2)}) collective-permute-start(bf16[384,1024]{1,0:T(8,128)(2,1)} %add_convert_fusion.16), channel_id=1, source_target_pairs={{0,2},{1,3},{2,0},{3,1},{4,6},{5,7},{6,4},{7,5},{8,10},{9,11},{10,... | collective-permute-start | bytes 2359304 | tf_op jit(solution)/shard_map/ppermute | solution.py:224
  179.5 31.3 %copy-start.31 = (bf16[2048,1024]{1,0:T(8,128)(2,1)S(1)}, bf16[2048,1024]{1,0:T(8,128)(2,1)}, u32[]{:S(2)}) copy-start(bf16[2048,1024]{1,0:T(8,128)(2,1)} %param.18) | copy-start | bytes 12582916
  210.7 17.0 %copy-start.83 = (bf16[1280,1024]{1,0:T(8,128)(2,1)}, bf16[1280,1024]{1,0:T(8,128)(2,1)S(1)}, u32[]{:S(2)}) copy-start(bf16[1280,1024]{1,0:T(8,128)(2,1)S(1)} %get-tuple-element.112) | copy-start | bytes 7864324
  216.7 5.2 copy-start.57
  216.7 5.2 copy-start.87
  216.7 5.2 copy-start.88
  221.9 4.6 copy-start.43
  227.7 16.3 %collective-permute-start.9 = (bf16[640,1024]{1,0:T(8,128)(2,1)}, bf16[640,1024]{1,0:T(8,128)(2,1)}, u32[]{:S(2)}, u32[]{:S(2)}) collective-permute-start(bf16[640,1024]{1,0:T(8,128)(2,1)} %constant_dynamic-slice_fusion.3), channel_id=1, source_target_pairs={{0,1},{1,0},{2,3},{3,2},{4,5},{5,4},{6,7},{7,6},{8,9},{9,8},{10,11... | collective-permute-start | bytes 3932168 | tf_op jit(solution)/shard_map/ppermute | solution.py:222
  241.5 5.4 copy-start.80
  241.5 320.5 %reduce-scatter.9.cloned.1.call-start = ((), (), s32[]{:S(2)}) async-start(), calls=%async_computation.3 | async-start | bytes 2359296
  241.5 5.4 copy-start.84
  243.4 7.9 %collective-permute-start.8 = (bf16[384,1024]{1,0:T(8,128)(2,1)S(1)}, bf16[384,1024]{1,0:T(8,128)(2,1)S(1)}, u32[]{:S(2)}, u32[]{:S(2)}) collective-permute-start(bf16[384,1024]{1,0:T(8,128)(2,1)S(1)} %add_convert_fusion.15), channel_id=1, source_target_pairs={{0,1},{1,0},{2,3},{3,2},{4,5},{5,4},{6,7},{7,6},{8,9},{9,8},{10,11... | collective-permute-start | bytes 2359304 | tf_op jit(solution)/shard_map/ppermute | solution.py:226
  244.0 36.3 %slice-start.4 = ((s8[8388608]{0:T(1024)(128)(4,1)}), s8[4194304]{0:T(1024)(128)(4,1)S(1)}, s32[]{:S(2)}) async-start(s8[8388608]{0:T(1024)(128)(4,1)} %bitcast.124), calls=%async_computation.8 | async-start | bytes 8388608
  246.4 34.0 %slice-start.5 = ((s8[8388608]{0:T(1024)(128)(4,1)}), s8[4194304]{0:T(1024)(128)(4,1)S(1)}, s32[]{:S(2)}) async-start(s8[8388608]{0:T(1024)(128)(4,1)} %bitcast.124), calls=%async_computation.9 | async-start | bytes 8388608
  246.4 30.8 %collective-permute-start.10 = (bf16[640,1024]{1,0:T(8,128)(2,1)S(1)}, bf16[640,1024]{1,0:T(8,128)(2,1)S(1)}, u32[]{:S(2)}, u32[]{:S(2)}) collective-permute-start(bf16[640,1024]{1,0:T(8,128)(2,1)S(1)} %add_convert_fusion.10), channel_id=1, source_target_pairs={{0,2},{1,3},{2,0},{3,1},{4,6},{5,7},{6,4},{7,5},{8,10},{9,11},{10,... | collective-permute-start | bytes 3932168 | tf_op jit(solution)/shard_map/ppermute | solution.py:224
  277.7 7.7 %collective-permute-start.11 = (bf16[640,1024]{1,0:T(8,128)(2,1)S(1)}, bf16[640,1024]{1,0:T(8,128)(2,1)S(1)}, u32[]{:S(2)}, u32[]{:S(2)}) collective-permute-start(bf16[640,1024]{1,0:T(8,128)(2,1)S(1)} %add_convert_fusion.9), channel_id=1, source_target_pairs={{0,1},{1,0},{2,3},{3,2},{4,5},{5,4},{6,7},{7,6},{8,9},{9,8},{10,11... | collective-permute-start | bytes 3932168 | tf_op jit(solution)/shard_map/ppermute | solution.py:226
  351.4 3.7 copy-start.49
  351.4 6.8 %copy-start.32 = (f32[4,64,2048]{2,1,0:T(8,128)S(1)}, f32[4,64,2048]{2,1,0:T(8,128)}, u32[]{:S(2)}) copy-start(f32[4,64,2048]{2,1,0:T(8,128)} %get-tuple-element.39) | copy-start | bytes 6291460
  369.4 6.8 %collective-permute-start.18 = (bf16[1024,1024]{1,0:T(8,128)(2,1)}, bf16[1024,1024]{1,0:T(8,128)(2,1)}, u32[]{:S(2)}, u32[]{:S(2)}) collective-permute-start(bf16[1024,1024]{1,0:T(8,128)(2,1)} %constant_dynamic-slice_fusion), channel_id=1, source_target_pairs={{0,1},{1,0},{2,3},{3,2},{4,5},{5,4},{6,7},{7,6},{8,9},{9,8},{10,11... | collective-permute-start | bytes 6291464 | tf_op jit(solution)/shard_map/ppermute | solution.py:222
  370.1 5.2 collective-permute-start.12
  370.5 4.8 copy-start.51
  375.1 21.4 %collective-permute-start.15 = (bf16[640,1024]{1,0:T(8,128)(2,1)S(1)}, bf16[640,1024]{1,0:T(8,128)(2,1)S(1)}, u32[]{:S(2)}, u32[]{:S(2)}) collective-permute-start(bf16[640,1024]{1,0:T(8,128)(2,1)S(1)} %constant_dynamic-slice_fusion.1), channel_id=1, source_target_pairs={{0,1},{1,0},{2,3},{3,2},{4,5},{5,4},{6,7},{7,6},{8,9},{9,8},{10,11... | collective-permute-start | bytes 3932168 | tf_op jit(solution)/shard_map/ppermute | solution.py:222
  375.6 20.5 %collective-permute-start.13 = (bf16[384,1024]{1,0:T(8,128)(2,1)S(1)}, bf16[384,1024]{1,0:T(8,128)(2,1)S(1)}, u32[]{:S(2)}, u32[]{:S(2)}) collective-permute-start(bf16[384,1024]{1,0:T(8,128)(2,1)S(1)} %add_convert_fusion.14), channel_id=1, source_target_pairs={{0,2},{1,3},{2,0},{3,1},{4,6},{5,7},{6,4},{7,5},{8,10},{9,11},{10,... | collective-permute-start | bytes 2359304 | tf_op jit(solution)/shard_map/ppermute | solution.py:224
  376.2 20.3 %copy-start.42 = (bf16[1280,1024]{1,0:T(8,128)(2,1)S(1)}, bf16[1280,1024]{1,0:T(8,128)(2,1)}, u32[]{:S(2)}) copy-start(bf16[1280,1024]{1,0:T(8,128)(2,1)} %convolution_convert_fusion.2) | copy-start | bytes 7864324
  379.0 18.7 %copy-start.75 = (f32[1024]{0:T(1024)S(1)}, f32[1024]{0:T(1024)}, u32[]{:S(2)}) copy-start(f32[1024]{0:T(1024)} %get-tuple-element.124) | copy-start | bytes 12292
  379.0 43.1 %copy-start.3 = (bf16[4,64,1280]{2,1,0:T(8,128)(2,1)S(1)}, bf16[4,64,1280]{2,1,0:T(8,128)(2,1)}, u32[]{:S(2)}) copy-start(bf16[4,64,1280]{2,1,0:T(8,128)(2,1)} %copy-done.2) | copy-start | bytes 1966084
  379.0 43.1 %copy-start.15 = (bf16[4,64,768]{2,1,0:T(8,128)(2,1)S(1)}, bf16[4,64,768]{2,1,0:T(8,128)(2,1)}, u32[]{:S(2)}) copy-start(bf16[4,64,768]{2,1,0:T(8,128)(2,1)} %copy-done.14) | copy-start | bytes 1179652
  379.0 43.1 %copy-start.45 = (bf16[1280,1024]{1,0:T(8,128)(2,1)S(1)}, bf16[1280,1024]{1,0:T(8,128)(2,1)}, u32[]{:S(2)}) copy-start(bf16[1280,1024]{1,0:T(8,128)(2,1)} %copy-done.44) | copy-start | bytes 7864324
  379.0 43.1 %copy-start.55 = (bf16[768,1024]{1,0:T(8,128)(2,1)S(1)}, bf16[768,1024]{1,0:T(8,128)(2,1)}, u32[]{:S(2)}) copy-start(bf16[768,1024]{1,0:T(8,128)(2,1)} %copy-done.54) | copy-start | bytes 4718596
  379.0 90.2 %collective-permute-start.19 = (bf16[1024,1024]{1,0:T(8,128)(2,1)S(1)}, bf16[1024,1024]{1,0:T(8,128)(2,1)S(1)}, u32[]{:S(2)}, u32[]{:S(2)}) collective-permute-start(bf16[1024,1024]{1,0:T(8,128)(2,1)S(1)} %add_convert_fusion.4), channel_id=1, source_target_pairs={{0,2},{1,3},{2,0},{3,1},{4,6},{5,7},{6,4},{7,5},{8,10},{9,11},{10,... | collective-permute-start | bytes 6291464 | tf_op jit(solution)/shard_map/ppermute | solution.py:224
  396.4 28.4 %collective-permute-start.14 = (bf16[384,1024]{1,0:T(8,128)(2,1)S(1)}, bf16[384,1024]{1,0:T(8,128)(2,1)S(1)}, u32[]{:S(2)}, u32[]{:S(2)}) collective-permute-start(bf16[384,1024]{1,0:T(8,128)(2,1)S(1)} %add_convert_fusion.13), channel_id=1, source_target_pairs={{0,1},{1,0},{2,3},{3,2},{4,5},{5,4},{6,7},{7,6},{8,9},{9,8},{10,11... | collective-permute-start | bytes 2359304 | tf_op jit(solution)/shard_map/ppermute | solution.py:226
  397.0 71.5 %collective-permute-start.16 = (bf16[640,1024]{1,0:T(8,128)(2,1)S(1)}, bf16[640,1024]{1,0:T(8,128)(2,1)S(1)}, u32[]{:S(2)}, u32[]{:S(2)}) collective-permute-start(bf16[640,1024]{1,0:T(8,128)(2,1)S(1)} %add_convert_fusion.8), channel_id=1, source_target_pairs={{0,2},{1,3},{2,0},{3,1},{4,6},{5,7},{6,4},{7,5},{8,10},{9,11},{10,... | collective-permute-start | bytes 3932168 | tf_op jit(solution)/shard_map/ppermute | solution.py:224
  397.6 18.1 %collective-permute-start.24 = (f32[5120]{0:T(1024)S(1)}, f32[5120]{0:T(1024)S(1)}, u32[]{:S(2)}, u32[]{:S(2)}) collective-permute-start(f32[5120]{0:T(1024)S(1)} %constant_dynamic-update-slice_fusion), channel_id=1, source_target_pairs={{0,4},{4,0},{8,12},{12,8},{16,20},{20,16},{24,28},{28,24},{1,5},{5... | collective-permute-start | bytes 61448 | tf_op jit(solution)/shard_map/ppermute | solution.py:238
  415.8 3.8 collective-permute-start.25
  419.5 4.7 collective-permute-start.26
  469.1 10.1 %collective-permute-start.17 = (bf16[640,1024]{1,0:T(8,128)(2,1)S(1)}, bf16[640,1024]{1,0:T(8,128)(2,1)}, u32[]{:S(2)}, u32[]{:S(2)}) collective-permute-start(bf16[640,1024]{1,0:T(8,128)(2,1)S(1)} %add_convert_fusion.7), channel_id=1, source_target_pairs={{0,1},{1,0},{2,3},{3,2},{4,5},{5,4},{6,7},{7,6},{8,9},{9,8},{10,11... | collective-permute-start | bytes 3932168 | tf_op jit(solution)/shard_map/ppermute | solution.py:226
  471.6 15.7 %collective-permute-start.20 = (bf16[1024,1024]{1,0:T(8,128)(2,1)}, bf16[1024,1024]{1,0:T(8,128)(2,1)}, u32[]{:S(2)}, u32[]{:S(2)}) collective-permute-start(bf16[1024,1024]{1,0:T(8,128)(2,1)} %add_convert_fusion.3), channel_id=1, source_target_pairs={{0,1},{1,0},{2,3},{3,2},{4,5},{5,4},{6,7},{7,6},{8,9},{9,8},{10,11... | collective-permute-start | bytes 6291464 | tf_op jit(solution)/shard_map/ppermute | solution.py:226
  480.7 3.6 copy-start.34
  489.9 4.0 copy-start.27
  489.9 4.0 copy-start.28
  500.9 64.7 %collective-permute-start.21 = (f32[2560]{0:T(1024)S(1)}, f32[2560]{0:T(1024)S(1)}, u32[]{:S(2)}, u32[]{:S(2)}) collective-permute-start(f32[2560]{0:T(1024)S(1)} %pad_maximum_fusion.12), channel_id=1, source_target_pairs={{0,4},{4,0},{8,12},{12,8},{16,20},{20,16},{24,28},{28,24},{1,5},{5... | collective-permute-start | bytes 30728 | tf_op jit(solution)/shard_map/ppermute | solution.py:238
  565.7 3.8 collective-permute-start.22
  569.4 12.1 %collective-permute-start.23 = (f32[2560]{0:T(1024)S(1)}, f32[2560]{0:T(1024)S(1)}, u32[]{:S(2)}, u32[]{:S(2)}) collective-permute-start(f32[2560]{0:T(1024)S(1)} %add.329), channel_id=1, source_target_pairs={{0,16},{4,20},{8,24},{12,28},{16,0},{20,4},{24,8},{28,12},{1,17},{... | collective-permute-start | bytes 30728 | tf_op jit(solution)/shard_map/ppermute | solution.py:238
  570.7 12.1 %copy-start.1 = (bf16[1024,1024]{1,0:T(8,128)(2,1)S(1)}, bf16[1024,1024]{1,0:T(8,128)(2,1)}, u32[]{:S(2)}) copy-start(bf16[1024,1024]{1,0:T(8,128)(2,1)} %param.24) | copy-start | bytes 6291460
  (60 other events, 126.9 us)
Sparse Core Ops, SparseCore 0:
  241.6 95.2 reduce-scatter.6
  479.3 82.6 reduce-scatter.8

commit v8 on v7

--- a/solution.py
+++ b/solution.py
@@ -350,9 +350,7 @@
     grad_b_out = jnp.sum(d_middle, axis=0)
     d_middle_low = jnp.concatenate([p["d_middle_low"] for p in pieces_fwd], axis=0)
     attended = jnp.concatenate([p["attended"] for p in pieces_fwd], axis=0)
-    grad_w_out = jnp.einsum(
-        "tc,td->cd", attended, d_middle_low, preferred_element_type=jnp.float32
-    )
+    grad_w_out = jnp.einsum("tc,td->cd", attended, d_middle_low, preferred_element_type=jnp.float32)
     d_attended = jnp.concatenate([p["d_attended"] for p in pieces_fwd], axis=0)
     out_f32 = jnp.concatenate([p["out32_t"] for p in pieces_fwd], axis=2)
     log_norms = jnp.concatenate([p["lse"] for p in pieces_fwd], axis=2)
@@ -398,10 +396,12 @@
     units = grad_w_fc2.shape[0]
     summed_fc2 = summed_mlp[:units]
     summed_fc1 = summed_mlp[units:].T
-    early = dp_allreduce(
-        jnp.concatenate([grad_ln2_gain, grad_ln2_bias, grad_b_out, grad_b_fc2, grad_b_fc1]), n_dp
-    )
-    late = dp_allreduce(jnp.concatenate([grad_ln1_gain, grad_ln1_bias, grad_b_qv.reshape(-1)]), n_dp)
+    early_parts = [grad_ln2_gain, grad_ln2_bias, grad_b_out, grad_b_fc2, grad_b_fc1]
+    late_parts = [grad_ln1_gain, grad_ln1_bias, grad_b_qv.reshape(-1)]
+    summed_small = dp_allreduce(jnp.concatenate(early_parts + late_parts), n_dp)
+    split_at = sum(part.shape[0] for part in early_parts)
+    early = summed_small[:split_at]
+    late = summed_small[split_at:]
     width = grad_ln1_gain.shape[0]
     pieces = [late[0:width], late[width : 2 * width]] + [
         early[k * width : (k + 1) * width] for k in range(4)

time: 598 us -> 583 us (0.975)
  starting transfers between devices: 52.3 us -> 30.5 us
  waiting for transfers between devices: 144 us -> 161 us
  matrix products: 106 us -> 93.4 us
    ppermute x6 -> x3, starting transfers between devices: 39.6 us -> 18.4 us  [dp_allreduce(): lax.ppermute(total, 'dp', [(k, k ^ step) for k in range(n_dp)])]
    ppermute x7, waiting for transfers between devices: 93.8 us -> 114 us  [mp_allreduce(): got_far = lax.ppermute(first, 'mp', [(k, k ^ 2) for k in range(4)])]
    dot_general x2, matrix products: 49.9 us -> 33.9 us  [per_device(): jnp.dot(normed_two_h, w_fc1, preferred_element_type=jnp.float32) + b_fc1]
  transfers between devices with their start and end apart: 29 -> 26, of which waited for: 9 -> 7; matrix products, arithmetic and copies ran while one was open for 38% -> 39% of each run, Pallas kernels for 12% -> 12%
where the time goes in v8:
time: 583 us; the launch traced here: 575 us
  waiting for transfers between devices  161 us (28%)
  other arithmetic  116 us (20%)
  matrix products  93.4 us (16%)
  Pallas kernels  83.2 us (14%)
  local copies, waits for them, and re-layouts  74.4 us (13%)
  starting transfers between devices  30.5 us (5%)
  between operations  15.6 us (3%)
    ppermute x7, waiting for transfers between devices, mp_allreduce(): got_far = lax.ppermute(first, 'mp', [(k, k ^ 2) for k in range(4)])  114 us
    pallas_call x1, Pallas kernels, flash_backward(): pl.pallas_call(_bwd_kernel, out_shape=(jax.ShapeDtypeStruct((heads, HEAD,...  44.9 us
    unnamed x4, waiting for transfers between devices  44.2 us
    unnamed x197, local copies, waits for them, and re-layouts  39.2 us
    pallas_call x2, Pallas kernels, flash_forward(): pl.pallas_call(_fwd_kernel, out_shape=(jax.ShapeDtypeStruct((heads, HEAD,...  38.3 us
    dot_general x2, matrix products, per_device(): jnp.dot(normed_two_h, w_fc1, preferred_element_type=jnp.float32) + b_fc1  33.9 us
    reduce_sum x6, other arithmetic, normalize(): return centered * lax.rsqrt(spread + 1e-06) * gain + shift  20 us
    ppermute x3, starting transfers between devices, dp_allreduce(): lax.ppermute(total, 'dp', [(k, k ^ step) for k in range(n_dp)])  18.4 us
  transfers between devices with their start and end apart: 26, of which 7 were waited for; matrix products, arithmetic and copies ran while one was open for 39% of the time, Pallas kernels for 12%

profile of v8, /device:TPU:0, one launch (start us, length us, event | category | flops | bytes accessed | tf_op | source)
XLA Modules:
  0.0 575.0 jit_solution(905332234893772297)
XLA Ops:
  11.6 3.1 convert_reduce_fusion.2
  19.1 2.3 convolution_convert_fusion.4
  22.8 2.8 copy.70.k_ref
  25.5 4.6 fusion.49
  36.9 11.9 %segment_flash_fwd.2 = (bf16[4,64,768]{2,1,0:T(8,128)(2,1)S(1)}, f32[4,64,768]{2,1,0:T(8,128)S(1)}, f32[4,1,768]{2,1,0:T(1,128)S(1)}) custom-call(s32[3]{0:T(128)S(1)} %bitcast.117, s32[3]{0:T(128)S(1)} %bitcast.116, s32[2048,1]{1,0:T(8,128)S(1)} %copy-done.9, s32[1,768]{1,0:T(1,128)S(1)} %reshape.213.segr_ref, bf16[4,64,768]{2,1,0:T(8,128)(2,1)S(1)} %slice.159.qt_ref, ...), custom_call_target="tpu_custom_call" | custom-call | flops 966367616 | bytes 3670016 | tf_op jit(solution)/shard_map/segment_flash_fwd/pallas_call | solution.py:146
  57.6 26.4 %segment_flash_fwd.3 = (bf16[4,64,1280]{2,1,0:T(8,128)(2,1)S(1)}, f32[4,64,1280]{2,1,0:T(8,128)S(1)}, f32[4,1,1280]{2,1,0:T(1,128)S(1)}) custom-call(s32[5]{0:T(128)S(1)} %slice.132.lo_ref, s32[5]{0:T(128)S(1)} %slice.133.hi_ref, s32[2048,1]{1,0:T(8,128)S(1)} %copy-done.10, s32[1,1280]{1,0:T(1,128)S(1)} %reshape.218.segr_ref, ...), custom_call_target="tpu_custom_call" | custom-call | flops 1610612736 | bytes 4718592 | tf_op jit(solution)/shard_map/segment_flash_fwd/pallas_call | solution.py:146
  85.1 2.6 add_convert_fusion.18
  87.7 2.5 collective-permute-start.1
  90.2 2.3 convolution_convert_fusion
  92.5 2.5 constant_dynamic-slice_fusion.5
  95.2 13.5 %collective-permute-done.1 = bf16[384,1024]{1,0:T(8,128)(2,1)} collective-permute-done((bf16[384,1024]{1,0:T(8,128)(2,1)}, bf16[384,1024]{1,0:T(8,128)(2,1)}, u32[]{:S(2)}, u32[]{:S(2)}) %collective-permute-start.1) | collective-permute-done | bytes 786464 | tf_op jit(solution)/shard_map/ppermute | solution.py:224
  108.7 2.6 add_convert_fusion.17
  111.3 6.6 %convert_element_type.234 = f32[2048,1024]{1,0:T(8,128)} convert(bf16[2048,1024]{1,0:T(8,128)(2,1)} %param.17) | non-fusion elementwise | flops 2097152 | bytes 12582912 | tf_op jit(solution)/shard_map/convert_element_type | solution.py:264
  117.9 2.2 add_convert_fusion.12
  123.5 2.4 fusion.95
  127.5 18.7 %multiply_convert_fusion.1 = (bf16[768,1024]{1,0:T(8,128)(2,1)}, f32[768,1024]{1,0:T(8,128)S(1)}, f32[768,1024]{1,0:T(8,128)S(1)}) fusion(f32[1024]{0:T(1024)S(1)} %copy-done.81, bf16[768,1024]{1,0:T(8,128)(2,1)S(1)} %add_convert_fusion.6, bf16[1024,1024]{1,0:T(8,128)(2,1)S(1)} %copy-done), kind=kOutput, calls=%fused_computation.88 | convolution fusion | flops 1662517248 | bytes 11538432 | tf_op jit(solution)/shard_map/dot_general | solution.py:304
  146.2 3.5 fusion.98
  149.7 1.8 convolution_convert_fusion.5
  154.7 4.3 convert_element_type.262
  158.9 2.7 copy.74
  163.5 3.3 pad_maximum_fusion.5.o32t_ref
  166.8 3.0 convolution_convert_fusion.6
  169.8 2.9 add_convert_fusion.16
  174.3 1.9 broadcast_select_fusion.7
  179.5 15.3 %multiply_convert_fusion = (bf16[1280,1024]{1,0:T(8,128)(2,1)S(1)}, f32[1280,1024]{1,0:T(8,128)S(1)}, f32[1280,1024]{1,0:T(8,128)}) fusion(f32[1024]{0:T(1024)S(1)} %copy-done.81, bf16[1280,1024]{1,0:T(8,128)(2,1)S(1)} %add_convert_fusion.2, bf16[1024,1024]{1,0:T(8,128)(2,1)S(1)} %copy-done), kind=kOutput, calls=%fused_computation.31 | convolution fusion | flops 2770862080 | bytes 17829888 | tf_op jit(solution)/shard_map/dot_general | solution.py:304
  194.8 9.3 %fusion.97 = (f32[1024]{0:T(1024)S(1)}, bf16[1280,1024]{1,0:T(8,128)(2,1)}) fusion(f32[1280,1024]{1,0:T(8,128)S(1)} %get-tuple-element.113, bf16[1024,1024]{1,0:T(8,128)(2,1)S(1)} %copy-done.78, bf16[2048,1024]{1,0:T(8,128)(2,1)S(1)} %copy-done.31, f32[1280,1024]{1,0:T(8,128)} %get-tuple-element.150, f32[1024]{0:T(1024)S(1)} %copy-done.81), kind=kOutput, calls=%fused_computation.230 | convolution fusion | flops 2705325056 | bytes 17833984 | tf_op jit(solution)/shard_map/td,fd->tf/dot_general | solution.py:317
  204.1 6.5 %fusion.50 = bf16[1024,1024]{1,0:T(8,128)(2,1)S(1)} fusion(bf16[1280,1024]{1,0:T(8,128)(2,1)S(1)} %add_convert_fusion.2, bf16[768,1024]{1,0:T(8,128)(2,1)S(1)} %copy-done.56, bf16[1280,1024]{1,0:T(8,128)(2,1)} %get-tuple-element.121, bf16[768,1024]{1,0:T(8,128)(2,1)S(1)} %copy-done.86), kind=kOutput, calls=%fused_computation.126 | convolution fusion | flops 4312793088 | bytes 10485760 | tf_op jit(solution)/shard_map/tf,td->fd/dot_general | solution.py:331
  210.6 3.2 convolution_convert_fusion.1
  216.4 4.8 fusion.55
  221.2 2.4 pad_maximum_fusion.1
  223.6 6.5 %copy.84 = bf16[2048,1024]{0,1:T(8,128)(2,1)} copy(bf16[2048,1024]{1,0:T(8,128)(2,1)} %pad_maximum_fusion.1) | data formatting | bytes 8388608
  230.2 1.8 add_convert_fusion.15
  232.6 2.4 add_convert_fusion.10
  235.5 4.3 convolution_convert_fusion.2
  242.5 23.4 %collective-permute-done.10 = bf16[640,1024]{1,0:T(8,128)(2,1)S(1)} collective-permute-done((bf16[640,1024]{1,0:T(8,128)(2,1)S(1)}, bf16[640,1024]{1,0:T(8,128)(2,1)S(1)}, u32[]{:S(2)}, u32[]{:S(2)}) %collective-permute-start.10) | collective-permute-done | bytes 1310752 | tf_op jit(solution)/shard_map/ppermute | solution.py:224
  266.5 2.5 fusion.37
  269.0 2.0 fusion.90
  275.8 2.4 fusion.7
  278.1 4.2 fusion.9
  282.4 3.3 fusion.89
  292.0 2.2 constant_dynamic-slice_fusion.2
  294.7 2.5 constant_dynamic-slice_fusion.1
  297.3 44.9 %segment_flash_bwd.1 = (f32[4,64,2048]{2,1,0:T(8,128)}, f32[2048,256]{1,0:T(8,128)}, f32[2048,256]{1,0:T(8,128)}) custom-call(s32[8]{0:T(128)S(1)} %copy-done.19, s32[8]{0:T(128)S(1)} %fusion.80.hi_ref, s32[2048,1]{1,0:T(8,128)S(1)} %copy-done.11, s32[1,2048]{1,0:T(1,128)S(1)} %bitcast.115, bf16[4,2048,64]{2,1,0:T(8,128)(2,1)} %copy.76.q_ref, ...), custom_call_target="tpu_custom_call" | custom-call | flops 5153960960 | bytes 15761408 | tf_op jit(solution)/shard_map/segment_flash_bwd/pallas_call | solution.py:173
  342.2 3.7 fusion.99
  347.0 2.0 copy.85
  351.1 5.5 bitcast_convert_fusion
  356.6 2.0 copy-done.41
  362.9 2.2 add_convert_fusion.8
  367.5 15.4 %collective-permute-done.13 = bf16[384,1024]{1,0:T(8,128)(2,1)S(1)} collective-permute-done((bf16[384,1024]{1,0:T(8,128)(2,1)S(1)}, bf16[384,1024]{1,0:T(8,128)(2,1)S(1)}, u32[]{:S(2)}, u32[]{:S(2)}) %collective-permute-start.13) | collective-permute-done | bytes 786464 | tf_op jit(solution)/shard_map/ppermute | solution.py:224
  383.2 2.7 add_convert_fusion.4
  386.5 24.4 %collective-permute-done.16 = bf16[640,1024]{1,0:T(8,128)(2,1)S(1)} collective-permute-done((bf16[640,1024]{1,0:T(8,128)(2,1)S(1)}, bf16[640,1024]{1,0:T(8,128)(2,1)S(1)}, u32[]{:S(2)}, u32[]{:S(2)}) %collective-permute-start.16) | collective-permute-done | bytes 1310752 | tf_op jit(solution)/shard_map/ppermute | solution.py:224
  417.8 37.6 %collective-permute-done.19 = bf16[1024,1024]{1,0:T(8,128)(2,1)S(1)} collective-permute-done((bf16[1024,1024]{1,0:T(8,128)(2,1)S(1)}, bf16[1024,1024]{1,0:T(8,128)(2,1)S(1)}, u32[]{:S(2)}, u32[]{:S(2)}) %collective-permute-start.19) | collective-permute-done | bytes 2097184 | tf_op jit(solution)/shard_map/ppermute | solution.py:224
  455.4 2.3 add_convert_fusion.3
  457.8 3.7 fusion.58
  461.7 2.6 copy.86
  464.3 4.0 add_convert_fusion.1
  468.3 2.5 pad_maximum_fusion
  471.2 2.6 broadcast_select_fusion.1
  474.6 3.2 fusion.2
  477.9 7.0 %fusion.3 = (f32[1024]{0:T(1024)S(1)}, f32[2048]{0:T(1024)S(1)}, f32[1024]{0:T(1024)S(1)}) fusion(bf16[2048,1024]{1,0:T(8,128)(2,1)S(1)} %copy-done.22, f32[2048]{0:T(1024)S(1)} %copy-done.65, f32[2048]{0:T(1024)S(1)} %copy-done.62, bf16[1024,1024]{1,0:T(8,128)(2,1)S(1)} %get-tuple-element.123, bf16[1024,1024]{1,0:T(8,128)(2,1)S(1)} %get-tuple-element.122, ...), kind=kLoop, calls=%fused_computation.9 | loop fusion | flops 33550336 | bytes 8433664 | tf_op jit(solution)/shard_map/transpose(jvp())/reduce_sum | solution.py:201
  484.9 16.1 %collective-permute-start.21 = (f32[7680]{0:T(1024)S(1)}, f32[7680]{0:T(1024)S(1)}, u32[]{:S(2)}, u32[]{:S(2)}) collective-permute-start(f32[7680]{0:T(1024)S(1)} %constant_dynamic-update-slice_fusion), channel_id=1, source_target_pairs={{0,4},{4,0},{8,12},{12,8},{16,20},{20,16},{24,28},{28,24},{1,5},{5... | collective-permute-start | bytes 92168 | tf_op jit(solution)/shard_map/ppermute | solution.py:238
  502.8 44.1 %reduce-scatter.9.cloned.1.call-done = bf16[128,1024]{1,0:T(8,128)(2,1)} async-done(((bf16[1024,1024]{1,0:T(8,128)(2,1)}), bf16[128,1024]{1,0:T(8,128)(2,1)}) %reduce-scatter.9.cloned.1.call-update) | async-done | bytes 262160
  551.6 3.0 collective-permute-done.22
  555.9 10.8 %maximum_add_fusion = f32[2048,1024]{1,0:T(8,128)} fusion(f32[1280,1024]{1,0:T(8,128)} %copy-done.26, f32[768,1024]{1,0:T(8,128)} %copy-done.29, bf16[2048,1024]{1,0:T(8,128)(2,1)} %param.17, f32[2048]{0:T(1024)S(1)} %negate_multiply_fusion.2, f32[2048]{0:T(1024)S(1)} %multiply_multiply_fusion.10, f32[1024]{0:T(1024)S(1)} %copy-done.69, ...), kind=kLoop, calls=%fused_computation.10 | loop fusion | flops 29360128 | bytes 25202688 | tf_op jit(solution)/shard_map/add | solution.py:383
  (336 shorter events, 87.9 us)
Async XLA Ops:
  7.2 120.3 %copy-start = (bf16[1024,1024]{1,0:T(8,128)(2,1)S(1)}, bf16[1024,1024]{1,0:T(8,128)(2,1)}, u32[]{:S(2)}) copy-start(bf16[1024,1024]{1,0:T(8,128)(2,1)} %param.24) | copy-start | bytes 6291460
  7.2 339.8 %reduce-scatter.7.cloned.1.call-start = ((), (), s32[]{:S(2)}) async-start(), calls=%async_computation.2 | async-start | bytes 4718592
  36.9 13.5 %copy-start.46 = (bf16[256,1024]{1,0:T(8,128)(2,1)S(1)}, bf16[256,1024]{1,0:T(8,128)(2,1)}, u32[]{:S(2)}) copy-start(bf16[256,1024]{1,0:T(8,128)(2,1)} %param.22) | copy-start | bytes 1572868
  52.5 32.6 %collective-permute-start = (bf16[384,1024]{1,0:T(8,128)(2,1)}, bf16[384,1024]{1,0:T(8,128)(2,1)}, u32[]{:S(2)}, u32[]{:S(2)}) collective-permute-start(bf16[384,1024]{1,0:T(8,128)(2,1)} %constant_dynamic-slice_fusion.6), channel_id=1, source_target_pairs={{0,1},{1,0},{2,3},{3,2},{4,5},{5,4},{6,7},{7,6},{8,9},{9,8},{10,11... | collective-permute-start | bytes 2359304 | tf_op jit(solution)/shard_map/ppermute | solution.py:222
  57.6 27.5 %copy-start.37 = (bf16[768,1024]{1,0:T(8,128)(2,1)S(1)}, bf16[768,1024]{1,0:T(8,128)(2,1)}, u32[]{:S(2)}) copy-start(bf16[768,1024]{1,0:T(8,128)(2,1)} %copy-done.36) | copy-start | bytes 4718596
  57.6 32.6 %copy-start.47 = (bf16[256,1024]{1,0:T(8,128)(2,1)S(1)}, bf16[256,1024]{1,0:T(8,128)(2,1)}, u32[]{:S(2)}) copy-start(bf16[256,1024]{1,0:T(8,128)(2,1)} %param.22) | copy-start | bytes 1572868
  85.1 5.1 copy-start.2
  87.7 21.0 %collective-permute-start.1 = (bf16[384,1024]{1,0:T(8,128)(2,1)}, bf16[384,1024]{1,0:T(8,128)(2,1)}, u32[]{:S(2)}, u32[]{:S(2)}) collective-permute-start(bf16[384,1024]{1,0:T(8,128)(2,1)} %add_convert_fusion.18), channel_id=1, source_target_pairs={{0,2},{1,3},{2,0},{3,1},{4,6},{5,7},{6,4},{7,5},{8,10},{9,11},{10,... | collective-permute-start | bytes 2359304 | tf_op jit(solution)/shard_map/ppermute | solution.py:224
  95.0 22.9 %collective-permute-start.3 = (bf16[640,1024]{1,0:T(8,128)(2,1)}, bf16[640,1024]{1,0:T(8,128)(2,1)}, u32[]{:S(2)}, u32[]{:S(2)}) collective-permute-start(bf16[640,1024]{1,0:T(8,128)(2,1)} %constant_dynamic-slice_fusion.5), channel_id=1, source_target_pairs={{0,1},{1,0},{2,3},{3,2},{4,5},{5,4},{6,7},{7,6},{8,9},{9,8},{10,11... | collective-permute-start | bytes 3932168 | tf_op jit(solution)/shard_map/ppermute | solution.py:222
  111.3 10.7 %collective-permute-start.2 = (bf16[384,1024]{1,0:T(8,128)(2,1)}, bf16[384,1024]{1,0:T(8,128)(2,1)}, u32[]{:S(2)}, u32[]{:S(2)}) collective-permute-start(bf16[384,1024]{1,0:T(8,128)(2,1)} %add_convert_fusion.17), channel_id=1, source_target_pairs={{0,1},{1,0},{2,3},{3,2},{4,5},{5,4},{6,7},{7,6},{8,9},{9,8},{10,11... | collective-permute-start | bytes 2359304 | tf_op jit(solution)/shard_map/ppermute | solution.py:226
  117.9 5.6 copy-start.70
  120.2 31.4 %collective-permute-start.4 = (bf16[640,1024]{1,0:T(8,128)(2,1)S(1)}, bf16[640,1024]{1,0:T(8,128)(2,1)S(1)}, u32[]{:S(2)}, u32[]{:S(2)}) collective-permute-start(bf16[640,1024]{1,0:T(8,128)(2,1)S(1)} %add_convert_fusion.12), channel_id=1, source_target_pairs={{0,2},{1,3},{2,0},{3,1},{4,6},{5,7},{6,4},{7,5},{8,10},{9,11},{10,... | collective-permute-start | bytes 3932168 | tf_op jit(solution)/shard_map/ppermute | solution.py:224
  127.5 18.7 %copy-start.55 = (bf16[768,1024]{1,0:T(8,128)(2,1)}, bf16[768,1024]{1,0:T(8,128)(2,1)S(1)}, u32[]{:S(2)}) copy-start(bf16[768,1024]{1,0:T(8,128)(2,1)S(1)} %add_convert_fusion.6) | copy-start | bytes 4718596
  127.5 18.7 %copy-start.30 = (bf16[2048,1024]{1,0:T(8,128)(2,1)S(1)}, bf16[2048,1024]{1,0:T(8,128)(2,1)}, u32[]{:S(2)}) copy-start(bf16[2048,1024]{1,0:T(8,128)(2,1)} %param.18) | copy-start | bytes 12582916
  127.5 18.7 %copy-start.77 = (bf16[1024,1024]{1,0:T(8,128)(2,1)S(1)}, bf16[1024,1024]{1,0:T(8,128)(2,1)}, u32[]{:S(2)}) copy-start(bf16[1024,1024]{1,0:T(8,128)(2,1)} %param.26) | copy-start | bytes 6291460
  153.2 21.1 %collective-permute-start.5 = (bf16[640,1024]{1,0:T(8,128)(2,1)}, bf16[640,1024]{1,0:T(8,128)(2,1)}, u32[]{:S(2)}, u32[]{:S(2)}) collective-permute-start(bf16[640,1024]{1,0:T(8,128)(2,1)} %add_convert_fusion.11), channel_id=1, source_target_pairs={{0,1},{1,0},{2,3},{3,2},{4,5},{5,4},{6,7},{7,6},{8,9},{9,8},{10,11... | collective-permute-start | bytes 3932168 | tf_op jit(solution)/shard_map/ppermute | solution.py:226
  154.3 15.4 %collective-permute-start.6 = (bf16[384,1024]{1,0:T(8,128)(2,1)}, bf16[384,1024]{1,0:T(8,128)(2,1)}, u32[]{:S(2)}, u32[]{:S(2)}) collective-permute-start(bf16[384,1024]{1,0:T(8,128)(2,1)} %constant_dynamic-slice_fusion.4), channel_id=1, source_target_pairs={{0,1},{1,0},{2,3},{3,2},{4,5},{5,4},{6,7},{7,6},{8,9},{9,8},{10,11... | collective-permute-start | bytes 2359304 | tf_op jit(solution)/shard_map/ppermute | solution.py:222
  166.7 9.4 %slice-start.2 = ((s8[8388608]{0:T(1024)(128)(4,1)}), s8[4194304]{0:T(1024)(128)(4,1)S(1)}, s32[]{:S(2)}) async-start(s8[8388608]{0:T(1024)(128)(4,1)} %bitcast.122), calls=%async_computation.6 | async-start | bytes 8388608
  166.8 9.4 %slice-start.3 = ((s8[8388608]{0:T(1024)(128)(4,1)}), s8[4194304]{0:T(1024)(128)(4,1)S(1)}, s32[]{:S(2)}) async-start(s8[8388608]{0:T(1024)(128)(4,1)} %bitcast.122), calls=%async_computation.7 | async-start | bytes 8388608
  172.7 57.6 %collective-permute-start.7 = (bf16[384,1024]{1,0:T(8,128)(2,1)}, bf16[384,1024]{1,0:T(8,128)(2,1)}, u32[]{:S(2)}, u32[]{:S(2)}) collective-permute-start(bf16[384,1024]{1,0:T(8,128)(2,1)} %add_convert_fusion.16), channel_id=1, source_target_pairs={{0,2},{1,3},{2,0},{3,1},{4,6},{5,7},{6,4},{7,5},{8,10},{9,11},{10,... | collective-permute-start | bytes 2359304 | tf_op jit(solution)/shard_map/ppermute | solution.py:224
  179.5 15.3 %copy-start.31 = (bf16[2048,1024]{1,0:T(8,128)(2,1)S(1)}, bf16[2048,1024]{1,0:T(8,128)(2,1)}, u32[]{:S(2)}) copy-start(bf16[2048,1024]{1,0:T(8,128)(2,1)} %param.18) | copy-start | bytes 12582916
  194.8 21.7 %copy-start.82 = (bf16[1280,1024]{1,0:T(8,128)(2,1)}, bf16[1280,1024]{1,0:T(8,128)(2,1)S(1)}, u32[]{:S(2)}) copy-start(bf16[1280,1024]{1,0:T(8,128)(2,1)S(1)} %get-tuple-element.112) | copy-start | bytes 7864324
  194.8 9.3 %copy-start.56 = (bf16[768,1024]{1,0:T(8,128)(2,1)S(1)}, bf16[768,1024]{1,0:T(8,128)(2,1)}, u32[]{:S(2)}) copy-start(bf16[768,1024]{1,0:T(8,128)(2,1)} %copy-done.55) | copy-start | bytes 4718596
  194.8 9.3 %copy-start.86 = (bf16[768,1024]{1,0:T(8,128)(2,1)S(1)}, bf16[768,1024]{1,0:T(8,128)(2,1)}, u32[]{:S(2)}) copy-start(bf16[768,1024]{1,0:T(8,128)(2,1)} %copy-done.85) | copy-start | bytes 4718596
  204.1 6.5 %copy-start.87 = (bf16[1280,1024]{1,0:T(8,128)(2,1)S(1)}, bf16[1280,1024]{1,0:T(8,128)(2,1)}, u32[]{:S(2)}) copy-start(bf16[1280,1024]{1,0:T(8,128)(2,1)} %get-tuple-element.121) | copy-start | bytes 7864324
  216.4 16.2 %collective-permute-start.9 = (bf16[640,1024]{1,0:T(8,128)(2,1)}, bf16[640,1024]{1,0:T(8,128)(2,1)}, u32[]{:S(2)}, u32[]{:S(2)}) collective-permute-start(bf16[640,1024]{1,0:T(8,128)(2,1)} %constant_dynamic-slice_fusion.3), channel_id=1, source_target_pairs={{0,1},{1,0},{2,3},{3,2},{4,5},{5,4},{6,7},{7,6},{8,9},{9,8},{10,11... | collective-permute-start | bytes 3932168 | tf_op jit(solution)/shard_map/ppermute | solution.py:222
  230.2 5.4 copy-start.79
  230.2 316.8 %reduce-scatter.9.cloned.1.call-start = ((), (), s32[]{:S(2)}) async-start(), calls=%async_computation.3 | async-start | bytes 2359296
  230.2 5.3 copy-start.83
  232.1 7.8 %collective-permute-start.8 = (bf16[384,1024]{1,0:T(8,128)(2,1)S(1)}, bf16[384,1024]{1,0:T(8,128)(2,1)S(1)}, u32[]{:S(2)}, u32[]{:S(2)}) collective-permute-start(bf16[384,1024]{1,0:T(8,128)(2,1)S(1)} %add_convert_fusion.15), channel_id=1, source_target_pairs={{0,1},{1,0},{2,3},{3,2},{4,5},{5,4},{6,7},{7,6},{8,9},{9,8},{10,11... | collective-permute-start | bytes 2359304 | tf_op jit(solution)/shard_map/ppermute | solution.py:226
  232.6 36.3 %slice-start.4 = ((s8[8388608]{0:T(1024)(128)(4,1)}), s8[4194304]{0:T(1024)(128)(4,1)S(1)}, s32[]{:S(2)}) async-start(s8[8388608]{0:T(1024)(128)(4,1)} %bitcast.124), calls=%async_computation.8 | async-start | bytes 8388608
  235.0 34.0 %slice-start.5 = ((s8[8388608]{0:T(1024)(128)(4,1)}), s8[4194304]{0:T(1024)(128)(4,1)S(1)}, s32[]{:S(2)}) async-start(s8[8388608]{0:T(1024)(128)(4,1)} %bitcast.124), calls=%async_computation.9 | async-start | bytes 8388608
  235.1 30.8 %collective-permute-start.10 = (bf16[640,1024]{1,0:T(8,128)(2,1)S(1)}, bf16[640,1024]{1,0:T(8,128)(2,1)S(1)}, u32[]{:S(2)}, u32[]{:S(2)}) collective-permute-start(bf16[640,1024]{1,0:T(8,128)(2,1)S(1)} %add_convert_fusion.10), channel_id=1, source_target_pairs={{0,2},{1,3},{2,0},{3,1},{4,6},{5,7},{6,4},{7,5},{8,10},{9,11},{10,... | collective-permute-start | bytes 3932168 | tf_op jit(solution)/shard_map/ppermute | solution.py:224
  266.4 7.7 %collective-permute-start.11 = (bf16[640,1024]{1,0:T(8,128)(2,1)S(1)}, bf16[640,1024]{1,0:T(8,128)(2,1)S(1)}, u32[]{:S(2)}, u32[]{:S(2)}) collective-permute-start(bf16[640,1024]{1,0:T(8,128)(2,1)S(1)} %add_convert_fusion.9), channel_id=1, source_target_pairs={{0,1},{1,0},{2,3},{3,2},{4,5},{5,4},{6,7},{7,6},{8,9},{9,8},{10,11... | collective-permute-start | bytes 3932168 | tf_op jit(solution)/shard_map/ppermute | solution.py:226
  292.0 5.2 copy-start.6
  292.0 5.2 copy-start.11
  294.2 66.3 %collective-permute-start.12 = (bf16[384,1024]{1,0:T(8,128)(2,1)}, bf16[384,1024]{1,0:T(8,128)(2,1)}, u32[]{:S(2)}, u32[]{:S(2)}) collective-permute-start(bf16[384,1024]{1,0:T(8,128)(2,1)} %constant_dynamic-slice_fusion.2), channel_id=1, source_target_pairs={{0,1},{1,0},{2,3},{3,2},{4,5},{5,4},{6,7},{7,6},{8,9},{9,8},{10,11... | collective-permute-start | bytes 2359304 | tf_op jit(solution)/shard_map/ppermute | solution.py:222
  297.2 65.7 %collective-permute-start.15 = (bf16[640,1024]{1,0:T(8,128)(2,1)}, bf16[640,1024]{1,0:T(8,128)(2,1)}, u32[]{:S(2)}, u32[]{:S(2)}) collective-permute-start(bf16[640,1024]{1,0:T(8,128)(2,1)} %constant_dynamic-slice_fusion.1), channel_id=1, source_target_pairs={{0,1},{1,0},{2,3},{3,2},{4,5},{5,4},{6,7},{7,6},{8,9},{9,8},{10,11... | collective-permute-start | bytes 3932168 | tf_op jit(solution)/shard_map/ppermute | solution.py:222
  342.2 6.8 %copy-start.33 = (f32[4,64,2048]{2,1,0:T(8,128)S(1)}, f32[4,64,2048]{2,1,0:T(8,128)}, u32[]{:S(2)}) copy-start(f32[4,64,2048]{2,1,0:T(8,128)} %get-tuple-element.39) | copy-start | bytes 6291460
  360.1 23.1 %collective-permute-start.18 = (bf16[1024,1024]{1,0:T(8,128)(2,1)}, bf16[1024,1024]{1,0:T(8,128)(2,1)}, u32[]{:S(2)}, u32[]{:S(2)}) collective-permute-start(bf16[1024,1024]{1,0:T(8,128)(2,1)} %constant_dynamic-slice_fusion), channel_id=1, source_target_pairs={{0,1},{1,0},{2,3},{3,2},{4,5},{5,4},{6,7},{7,6},{8,9},{9,8},{10,11... | collective-permute-start | bytes 6291464 | tf_op jit(solution)/shard_map/ppermute | solution.py:222
  360.5 6.2 %copy-start.32 = (bf16[2048,1024]{1,0:T(8,128)(2,1)S(1)}, bf16[2048,1024]{1,0:T(8,128)(2,1)}, u32[]{:S(2)}) copy-start(bf16[2048,1024]{1,0:T(8,128)(2,1)} %param.18) | copy-start | bytes 12582916
  362.3 20.5 %collective-permute-start.13 = (bf16[384,1024]{1,0:T(8,128)(2,1)S(1)}, bf16[384,1024]{1,0:T(8,128)(2,1)S(1)}, u32[]{:S(2)}, u32[]{:S(2)}) collective-permute-start(bf16[384,1024]{1,0:T(8,128)(2,1)S(1)} %add_convert_fusion.14), channel_id=1, source_target_pairs={{0,2},{1,3},{2,0},{3,1},{4,6},{5,7},{6,4},{7,5},{8,10},{9,11},{10,... | collective-permute-start | bytes 2359304 | tf_op jit(solution)/shard_map/ppermute | solution.py:224
  365.1 18.1 %copy-start.42 = (bf16[2048,1024]{1,0:T(8,128)(2,1)S(1)}, bf16[2048,1024]{1,0:T(8,128)(2,1)}, u32[]{:S(2)}) copy-start(bf16[2048,1024]{1,0:T(8,128)(2,1)} %copy-done.41) | copy-start | bytes 12582916
  365.1 45.8 %collective-permute-start.16 = (bf16[640,1024]{1,0:T(8,128)(2,1)S(1)}, bf16[640,1024]{1,0:T(8,128)(2,1)S(1)}, u32[]{:S(2)}, u32[]{:S(2)}) collective-permute-start(bf16[640,1024]{1,0:T(8,128)(2,1)S(1)} %add_convert_fusion.8), channel_id=1, source_target_pairs={{0,2},{1,3},{2,0},{3,1},{4,6},{5,7},{6,4},{7,5},{8,10},{9,11},{10,... | collective-permute-start | bytes 3932168 | tf_op jit(solution)/shard_map/ppermute | solution.py:224
  383.1 29.8 %collective-permute-start.14 = (bf16[384,1024]{1,0:T(8,128)(2,1)S(1)}, bf16[384,1024]{1,0:T(8,128)(2,1)S(1)}, u32[]{:S(2)}, u32[]{:S(2)}) collective-permute-start(bf16[384,1024]{1,0:T(8,128)(2,1)S(1)} %add_convert_fusion.13), channel_id=1, source_target_pairs={{0,1},{1,0},{2,3},{3,2},{4,5},{5,4},{6,7},{7,6},{8,9},{9,8},{10,11... | collective-permute-start | bytes 2359304 | tf_op jit(solution)/shard_map/ppermute | solution.py:226
  383.2 28.3 %copy-start.54 = (bf16[768,1024]{1,0:T(8,128)(2,1)S(1)}, bf16[768,1024]{1,0:T(8,128)(2,1)}, u32[]{:S(2)}) copy-start(bf16[768,1024]{1,0:T(8,128)(2,1)} %copy-done.53) | copy-start | bytes 4718596
  385.9 25.6 %copy-start.74 = (f32[1024]{0:T(1024)S(1)}, f32[1024]{0:T(1024)}, u32[]{:S(2)}) copy-start(f32[1024]{0:T(1024)} %get-tuple-element.124) | copy-start | bytes 12292
  385.9 25.7 %copy-start.3 = (bf16[4,64,1280]{2,1,0:T(8,128)(2,1)S(1)}, bf16[4,64,1280]{2,1,0:T(8,128)(2,1)}, u32[]{:S(2)}) copy-start(bf16[4,64,1280]{2,1,0:T(8,128)(2,1)} %copy-done.2) | copy-start | bytes 1966084
  385.9 25.7 %copy-start.15 = (bf16[4,64,768]{2,1,0:T(8,128)(2,1)S(1)}, bf16[4,64,768]{2,1,0:T(8,128)(2,1)}, u32[]{:S(2)}) copy-start(bf16[4,64,768]{2,1,0:T(8,128)(2,1)} %copy-done.14) | copy-start | bytes 1179652
  385.9 25.6 %copy-start.45 = (bf16[1280,1024]{1,0:T(8,128)(2,1)S(1)}, bf16[1280,1024]{1,0:T(8,128)(2,1)}, u32[]{:S(2)}) copy-start(bf16[1280,1024]{1,0:T(8,128)(2,1)} %copy-done.44) | copy-start | bytes 7864324
  386.0 69.5 %collective-permute-start.19 = (bf16[1024,1024]{1,0:T(8,128)(2,1)S(1)}, bf16[1024,1024]{1,0:T(8,128)(2,1)S(1)}, u32[]{:S(2)}, u32[]{:S(2)}) collective-permute-start(bf16[1024,1024]{1,0:T(8,128)(2,1)S(1)} %add_convert_fusion.4), channel_id=1, source_target_pairs={{0,2},{1,3},{2,0},{3,1},{4,6},{5,7},{6,4},{7,5},{8,10},{9,11},{10,... | collective-permute-start | bytes 6291464 | tf_op jit(solution)/shard_map/ppermute | solution.py:224
  411.4 5.1 collective-permute-start.17
  416.5 41.2 %copy-start.60 = (bf16[1,2048,256]{2,1,0:T(8,128)(2,1)S(1)}, bf16[1,2048,256]{2,1,0:T(8,128)(2,1)}, u32[]{:S(2)}) copy-start(bf16[1,2048,256]{2,1,0:T(8,128)(2,1)} %copy-done.59) | copy-start | bytes 3145732
  417.8 40.0 %copy-start.40 = (bf16[2048,1024]{1,0:T(8,128)(2,1)S(1)}, bf16[2048,1024]{1,0:T(8,128)(2,1)}, u32[]{:S(2)}) copy-start(bf16[2048,1024]{1,0:T(8,128)(2,1)} %copy-done.39) | copy-start | bytes 12582916
  417.8 40.0 %copy-start.57 = (bf16[1,2048,256]{2,1,0:T(8,128)(2,1)S(1)}, bf16[1,2048,256]{2,1,0:T(8,128)(2,1)}, u32[]{:S(2)}) copy-start(bf16[1,2048,256]{2,1,0:T(8,128)(2,1)} %convert_bitcast_fusion.1) | copy-start | bytes 3145732
  417.8 40.0 %copy-start.58 = (bf16[1,2048,256]{2,1,0:T(8,128)(2,1)S(1)}, bf16[1,2048,256]{2,1,0:T(8,128)(2,1)}, u32[]{:S(2)}) copy-start(bf16[1,2048,256]{2,1,0:T(8,128)(2,1)} %get-tuple-element.133) | copy-start | bytes 3145732
  457.7 13.4 %collective-permute-start.20 = (bf16[1024,1024]{1,0:T(8,128)(2,1)}, bf16[1024,1024]{1,0:T(8,128)(2,1)}, u32[]{:S(2)}, u32[]{:S(2)}) collective-permute-start(bf16[1024,1024]{1,0:T(8,128)(2,1)} %add_convert_fusion.3), channel_id=1, source_target_pairs={{0,1},{1,0},{2,3},{3,2},{4,5},{5,4},{6,7},{7,6},{8,9},{9,8},{10,11... | collective-permute-start | bytes 6291464 | tf_op jit(solution)/shard_map/ppermute | solution.py:226
  464.3 4.0 copy-start.35
  473.8 4.0 copy-start.27
  473.8 4.0 copy-start.28
  484.9 65.7 %collective-permute-start.21 = (f32[7680]{0:T(1024)S(1)}, f32[7680]{0:T(1024)S(1)}, u32[]{:S(2)}, u32[]{:S(2)}) collective-permute-start(f32[7680]{0:T(1024)S(1)} %constant_dynamic-update-slice_fusion), channel_id=1, source_target_pairs={{0,4},{4,0},{8,12},{12,8},{16,20},{20,16},{24,28},{28,24},{1,5},{5... | collective-permute-start | bytes 92168 | tf_op jit(solution)/shard_map/ppermute | solution.py:238
  550.6 4.0 collective-permute-start.22
  554.6 12.2 %collective-permute-start.23 = (f32[7680]{0:T(1024)S(1)}, f32[7680]{0:T(1024)S(1)}, u32[]{:S(2)}, u32[]{:S(2)}) collective-permute-start(f32[7680]{0:T(1024)S(1)} %add.323), channel_id=1, source_target_pairs={{0,16},{4,20},{8,24},{12,28},{16,0},{20,4},{24,8},{28,12},{1,17},{... | collective-permute-start | bytes 92168 | tf_op jit(solution)/shard_map/ppermute | solution.py:238
  555.9 12.1 %copy-start.1 = (bf16[1024,1024]{1,0:T(8,128)(2,1)S(1)}, bf16[1024,1024]{1,0:T(8,128)(2,1)}, u32[]{:S(2)}) copy-start(bf16[1024,1024]{1,0:T(8,128)(2,1)} %param.24) | copy-start | bytes 6291460
  (56 other events, 115.1 us)
Sparse Core Ops, SparseCore 0:
  230.3 95.2 reduce-scatter.6
  464.4 82.4 reduce-scatter.8

commit v9 on v8

--- a/solution.py
+++ b/solution.py
@@ -13,6 +13,7 @@
 
 
 HPS = 4
+HPS_B = 2
 
 
 def _fwd_kernel(lo_ref, hi_ref, segc_ref, segr_ref, qt_ref, k_ref, vt_ref, ot_ref, o32t_ref, lse_ref):
@@ -66,7 +67,7 @@
 
     def d_body(i, carry):
         r0 = pl.multiple_of(i * TQ, TQ)
-        for hh in range(HPS):
+        for hh in range(HPS_B):
             prod = dot_ref[hh, :, pl.ds(r0, TQ)].astype(jnp.float32) * o32t_ref[hh, :, pl.ds(r0, TQ)]
             dvec_ref[hh, :, pl.ds(r0, TQ)] = jnp.sum(prod, axis=0, keepdims=True)
         return carry
@@ -75,16 +76,16 @@
 
     def kv_body(j, carry):
         c0 = pl.multiple_of(j * TK, TK)
-        ks = [k_ref[hh, pl.ds(c0, TK), :] for hh in range(HPS)]
-        vs = [v_ref[hh, pl.ds(c0, TK), :] for hh in range(HPS)]
-        kts = [kt_ref[hh, :, pl.ds(c0, TK)] for hh in range(HPS)]
+        ks = [k_ref[hh, pl.ds(c0, TK), :] for hh in range(HPS_B)]
+        vs = [v_ref[hh, pl.ds(c0, TK), :] for hh in range(HPS_B)]
+        kts = [kt_ref[hh, :, pl.ds(c0, TK)] for hh in range(HPS_B)]
         sk = segc_ref[pl.ds(c0, TK), :]
 
         def q_body(i, grads):
             r0 = pl.multiple_of(i * TQ, TQ)
             same = sk == segr_ref[:, pl.ds(r0, TQ)]
             new_grads = []
-            for hh in range(HPS):
+            for hh in range(HPS_B):
                 dk, dv = grads[hh]
                 s = jnp.dot(ks[hh], qt_ref[hh, :, pl.ds(r0, TQ)], preferred_element_type=jnp.float32) * scale
                 s = jnp.where(same, s, NEG)
@@ -99,8 +100,8 @@
             return tuple(new_grads)
 
         zeros = jnp.zeros((TK, HEAD), jnp.float32)
-        final = lax.fori_loop(lo_ref[j], hi_ref[j], q_body, tuple((zeros, zeros) for _ in range(HPS)))
-        for hh in range(HPS):
+        final = lax.fori_loop(lo_ref[j], hi_ref[j], q_body, tuple((zeros, zeros) for _ in range(HPS_B)))
+        for hh in range(HPS_B):
             dk, dv = final[hh]
             dk_ref[pl.ds(c0, TK), pl.ds(hh * HEAD, HEAD)] = dk * scale
             dv_ref[pl.ds(c0, TK), pl.ds(hh * HEAD, HEAD)] = dv
@@ -125,9 +126,9 @@
 
 
 def _head_specs(rows):
-    plain = pl.BlockSpec((HPS, rows, HEAD), lambda h, lo, hi: (h, 0, 0))
-    flipped = pl.BlockSpec((HPS, HEAD, rows), lambda h, lo, hi: (h, 0, 0))
-    stat = pl.BlockSpec((HPS, 1, rows), lambda h, lo, hi: (h, 0, 0))
+    plain = pl.BlockSpec((HPS_B, rows, HEAD), lambda h, lo, hi: (h, 0, 0))
+    flipped = pl.BlockSpec((HPS_B, HEAD, rows), lambda h, lo, hi: (h, 0, 0))
+    stat = pl.BlockSpec((HPS_B, 1, rows), lambda h, lo, hi: (h, 0, 0))
     col = pl.BlockSpec((rows, 1), lambda h, lo, hi: (0, 0))
     row = pl.BlockSpec((1, rows), lambda h, lo, hi: (0, 0))
     return plain, flipped, stat, col, row
@@ -168,7 +169,7 @@
 def flash_backward(q, k, v, do, o32t, lse, segments, lo, hi):
     heads, rows, _ = q.shape
     plain, flipped, stat, col, row = _head_specs(rows)
-    wide = pl.BlockSpec((rows, HPS * HEAD), lambda h, lo, hi: (0, h))
+    wide = pl.BlockSpec((rows, HPS_B * HEAD), lambda h, lo, hi: (0, h))
     flops = int(heads * rows * rows * HEAD * 2 * 4 * 0.6)
     return pl.pallas_call(
         _bwd_kernel,
@@ -179,10 +180,10 @@
         ),
         grid_spec=pltpu.PrefetchScalarGridSpec(
             num_scalar_prefetch=2,
-            grid=(heads // HPS,),
+            grid=(heads // HPS_B,),
             in_specs=[col, row, plain, flipped, plain, flipped, plain, plain, flipped, flipped, stat],
             out_specs=[flipped, wide, wide],
-            scratch_shapes=[pltpu.VMEM((HPS, 1, rows), jnp.float32)],
+            scratch_shapes=[pltpu.VMEM((HPS_B, 1, rows), jnp.float32)],
         ),
         compiler_params=pltpu.CompilerParams(
             dimension_semantics=("arbitrary",), vmem_limit_bytes=48 * 1024 * 1024),

time: 583 us -> 585 us (level)
  transfers between devices with their start and end apart: 26 -> 26, of which waited for: 7 -> 7; matrix products, arithmetic and copies ran while one was open for 39% -> 39% of each run, Pallas kernels for 12% -> 13%
where the time goes in v9:
time: 585 us; the launch traced here: 577 us
  waiting for transfers between devices  162 us (28%)
  other arithmetic  116 us (20%)
  matrix products  93.4 us (16%)
  Pallas kernels  84 us (14%)
  local copies, waits for them, and re-layouts  74.4 us (13%)
  starting transfers between devices  31.1 us (5%)
  between operations  15.6 us (3%)
    ppermute x7, waiting for transfers between devices, mp_allreduce(): got_far = lax.ppermute(first, 'mp', [(k, k ^ 2) for k in range(4)])  114 us
    pallas_call x1, Pallas kernels, flash_backward(): pl.pallas_call(_bwd_kernel, out_shape=(jax.ShapeDtypeStruct((heads, HEAD,...  45.8 us
    unnamed x4, waiting for transfers between devices  44.3 us
    unnamed x197, local copies, waits for them, and re-layouts  39.3 us
    pallas_call x2, Pallas kernels, flash_forward(): pl.pallas_call(_fwd_kernel, out_shape=(jax.ShapeDtypeStruct((heads, HEAD,...  38.3 us
    dot_general x2, matrix products, per_device(): jnp.dot(normed_two_h, w_fc1, preferred_element_type=jnp.float32) + b_fc1  33.9 us
    reduce_sum x6, other arithmetic, normalize(): return centered * lax.rsqrt(spread + 1e-06) * gain + shift  20 us
    ppermute x3, starting transfers between devices, dp_allreduce(): lax.ppermute(total, 'dp', [(k, k ^ step) for k in range(n_dp)])  18.9 us
  transfers between devices with their start and end apart: 26, of which 7 were waited for; matrix products, arithmetic and copies ran while one was open for 39% of the time, Pallas kernels for 13%

profile of v9, /device:TPU:0, one launch (start us, length us, event | category | flops | bytes accessed | tf_op | source)
XLA Modules:
  0.0 576.6 jit_solution(5380664761652764637)
XLA Ops:
  11.6 3.1 convert_reduce_fusion.2
  19.1 2.3 convolution_convert_fusion.4
  22.8 2.8 copy.70.k_ref
  25.5 4.6 fusion.49
  36.9 11.9 %segment_flash_fwd.2 = (bf16[4,64,768]{2,1,0:T(8,128)(2,1)S(1)}, f32[4,64,768]{2,1,0:T(8,128)S(1)}, f32[4,1,768]{2,1,0:T(1,128)S(1)}) custom-call(s32[3]{0:T(128)S(1)} %bitcast.117, s32[3]{0:T(128)S(1)} %bitcast.116, s32[2048,1]{1,0:T(8,128)S(1)} %copy-done.9, s32[1,768]{1,0:T(1,128)S(1)} %reshape.213.segr_ref, bf16[4,64,768]{2,1,0:T(8,128)(2,1)S(1)} %slice.159.qt_ref, ...), custom_call_target="tpu_custom_call" | custom-call | flops 966367616 | bytes 3670016 | tf_op jit(solution)/shard_map/segment_flash_fwd/pallas_call | solution.py:147
  57.6 26.4 %segment_flash_fwd.3 = (bf16[4,64,1280]{2,1,0:T(8,128)(2,1)S(1)}, f32[4,64,1280]{2,1,0:T(8,128)S(1)}, f32[4,1,1280]{2,1,0:T(1,128)S(1)}) custom-call(s32[5]{0:T(128)S(1)} %slice.132.lo_ref, s32[5]{0:T(128)S(1)} %slice.133.hi_ref, s32[2048,1]{1,0:T(8,128)S(1)} %copy-done.10, s32[1,1280]{1,0:T(1,128)S(1)} %reshape.218.segr_ref, ...), custom_call_target="tpu_custom_call" | custom-call | flops 1610612736 | bytes 4718592 | tf_op jit(solution)/shard_map/segment_flash_fwd/pallas_call | solution.py:147
  85.1 2.6 add_convert_fusion.18
  87.7 2.5 collective-permute-start.1
  90.2 2.3 convolution_convert_fusion
  92.5 2.5 constant_dynamic-slice_fusion.5
  95.2 13.5 %collective-permute-done.1 = bf16[384,1024]{1,0:T(8,128)(2,1)} collective-permute-done((bf16[384,1024]{1,0:T(8,128)(2,1)}, bf16[384,1024]{1,0:T(8,128)(2,1)}, u32[]{:S(2)}, u32[]{:S(2)}) %collective-permute-start.1) | collective-permute-done | bytes 786464 | tf_op jit(solution)/shard_map/ppermute | solution.py:225
  108.7 2.6 add_convert_fusion.17
  111.3 6.6 %convert_element_type.234 = f32[2048,1024]{1,0:T(8,128)} convert(bf16[2048,1024]{1,0:T(8,128)(2,1)} %param.17) | non-fusion elementwise | flops 2097152 | bytes 12582912 | tf_op jit(solution)/shard_map/convert_element_type | solution.py:265
  117.9 2.2 add_convert_fusion.12
  123.5 2.4 fusion.95
  127.5 18.7 %multiply_convert_fusion.1 = (bf16[768,1024]{1,0:T(8,128)(2,1)}, f32[768,1024]{1,0:T(8,128)S(1)}, f32[768,1024]{1,0:T(8,128)S(1)}) fusion(f32[1024]{0:T(1024)S(1)} %copy-done.81, bf16[768,1024]{1,0:T(8,128)(2,1)S(1)} %add_convert_fusion.6, bf16[1024,1024]{1,0:T(8,128)(2,1)S(1)} %copy-done), kind=kOutput, calls=%fused_computation.88 | convolution fusion | flops 1662517248 | bytes 11538432 | tf_op jit(solution)/shard_map/dot_general | solution.py:305
  146.2 3.5 fusion.98
  149.7 1.8 convolution_convert_fusion.5
  154.7 4.3 convert_element_type.262
  158.9 2.7 copy.74
  163.5 3.3 pad_maximum_fusion.5.o32t_ref
  166.8 3.0 convolution_convert_fusion.6
  169.8 2.9 add_convert_fusion.16
  174.3 1.9 broadcast_select_fusion.7
  179.5 15.3 %multiply_convert_fusion = (bf16[1280,1024]{1,0:T(8,128)(2,1)S(1)}, f32[1280,1024]{1,0:T(8,128)S(1)}, f32[1280,1024]{1,0:T(8,128)}) fusion(f32[1024]{0:T(1024)S(1)} %copy-done.81, bf16[1280,1024]{1,0:T(8,128)(2,1)S(1)} %add_convert_fusion.2, bf16[1024,1024]{1,0:T(8,128)(2,1)S(1)} %copy-done), kind=kOutput, calls=%fused_computation.31 | convolution fusion | flops 2770862080 | bytes 17829888 | tf_op jit(solution)/shard_map/dot_general | solution.py:305
  194.8 9.3 %fusion.97 = (f32[1024]{0:T(1024)S(1)}, bf16[1280,1024]{1,0:T(8,128)(2,1)}) fusion(f32[1280,1024]{1,0:T(8,128)S(1)} %get-tuple-element.113, bf16[1024,1024]{1,0:T(8,128)(2,1)S(1)} %copy-done.78, bf16[2048,1024]{1,0:T(8,128)(2,1)S(1)} %copy-done.31, f32[1280,1024]{1,0:T(8,128)} %get-tuple-element.150, f32[1024]{0:T(1024)S(1)} %copy-done.81), kind=kOutput, calls=%fused_computation.230 | convolution fusion | flops 2705325056 | bytes 17833984 | tf_op jit(solution)/shard_map/td,fd->tf/dot_general | solution.py:318
  204.1 6.5 %fusion.50 = bf16[1024,1024]{1,0:T(8,128)(2,1)S(1)} fusion(bf16[1280,1024]{1,0:T(8,128)(2,1)S(1)} %add_convert_fusion.2, bf16[768,1024]{1,0:T(8,128)(2,1)S(1)} %copy-done.56, bf16[1280,1024]{1,0:T(8,128)(2,1)} %get-tuple-element.121, bf16[768,1024]{1,0:T(8,128)(2,1)S(1)} %copy-done.86), kind=kOutput, calls=%fused_computation.126 | convolution fusion | flops 4312793088 | bytes 10485760 | tf_op jit(solution)/shard_map/tf,td->fd/dot_general | solution.py:332
  210.6 3.2 convolution_convert_fusion.1
  216.4 4.8 fusion.55
  221.2 2.4 pad_maximum_fusion.1
  223.6 6.5 %copy.84 = bf16[2048,1024]{0,1:T(8,128)(2,1)} copy(bf16[2048,1024]{1,0:T(8,128)(2,1)} %pad_maximum_fusion.1) | data formatting | bytes 8388608
  230.2 1.8 add_convert_fusion.15
  232.6 2.4 add_convert_fusion.10
  235.5 4.3 convolution_convert_fusion.2
  242.5 23.4 %collective-permute-done.10 = bf16[640,1024]{1,0:T(8,128)(2,1)S(1)} collective-permute-done((bf16[640,1024]{1,0:T(8,128)(2,1)S(1)}, bf16[640,1024]{1,0:T(8,128)(2,1)S(1)}, u32[]{:S(2)}, u32[]{:S(2)}) %collective-permute-start.10) | collective-permute-done | bytes 1310752 | tf_op jit(solution)/shard_map/ppermute | solution.py:225
  266.5 2.5 fusion.37
  269.0 2.0 fusion.90
  275.8 2.4 fusion.7
  278.1 4.2 fusion.9
  282.4 3.3 fusion.89
  292.0 2.2 constant_dynamic-slice_fusion.2
  294.7 2.5 constant_dynamic-slice_fusion.1
  297.3 45.8 %segment_flash_bwd.1 = (f32[4,64,2048]{2,1,0:T(8,128)}, f32[2048,256]{1,0:T(8,128)}, f32[2048,256]{1,0:T(8,128)}) custom-call(s32[8]{0:T(128)S(1)} %copy-done.19, s32[8]{0:T(128)S(1)} %fusion.80.hi_ref, s32[2048,1]{1,0:T(8,128)S(1)} %copy-done.11, s32[1,2048]{1,0:T(1,128)S(1)} %bitcast.115, bf16[4,2048,64]{2,1,0:T(8,128)(2,1)} %copy.76.q_ref, ...), custom_call_target="tpu_custom_call" | custom-call | flops 5153960960 | bytes 15761408 | tf_op jit(solution)/shard_map/segment_flash_bwd/pallas_call | solution.py:174
  343.0 3.7 fusion.99
  347.8 2.0 copy.85
  352.0 5.5 bitcast_convert_fusion
  357.5 2.0 copy-done.41
  363.7 2.2 add_convert_fusion.8
  368.3 15.3 %collective-permute-done.13 = bf16[384,1024]{1,0:T(8,128)(2,1)S(1)} collective-permute-done((bf16[384,1024]{1,0:T(8,128)(2,1)S(1)}, bf16[384,1024]{1,0:T(8,128)(2,1)S(1)}, u32[]{:S(2)}, u32[]{:S(2)}) %collective-permute-start.13) | collective-permute-done | bytes 786464 | tf_op jit(solution)/shard_map/ppermute | solution.py:225
  384.1 2.7 add_convert_fusion.4
  387.4 24.4 %collective-permute-done.16 = bf16[640,1024]{1,0:T(8,128)(2,1)S(1)} collective-permute-done((bf16[640,1024]{1,0:T(8,128)(2,1)S(1)}, bf16[640,1024]{1,0:T(8,128)(2,1)S(1)}, u32[]{:S(2)}, u32[]{:S(2)}) %collective-permute-start.16) | collective-permute-done | bytes 1310752 | tf_op jit(solution)/shard_map/ppermute | solution.py:225
  418.7 37.6 %collective-permute-done.19 = bf16[1024,1024]{1,0:T(8,128)(2,1)S(1)} collective-permute-done((bf16[1024,1024]{1,0:T(8,128)(2,1)S(1)}, bf16[1024,1024]{1,0:T(8,128)(2,1)S(1)}, u32[]{:S(2)}, u32[]{:S(2)}) %collective-permute-start.19) | collective-permute-done | bytes 2097184 | tf_op jit(solution)/shard_map/ppermute | solution.py:225
  456.3 2.3 add_convert_fusion.3
  458.6 3.7 fusion.58
  462.5 2.6 copy.86
  465.2 4.0 add_convert_fusion.1
  469.2 2.5 pad_maximum_fusion
  472.0 2.6 broadcast_select_fusion.1
  475.5 3.2 fusion.2
  478.7 7.0 %fusion.3 = (f32[1024]{0:T(1024)S(1)}, f32[2048]{0:T(1024)S(1)}, f32[1024]{0:T(1024)S(1)}) fusion(bf16[2048,1024]{1,0:T(8,128)(2,1)S(1)} %copy-done.22, f32[2048]{0:T(1024)S(1)} %copy-done.65, f32[2048]{0:T(1024)S(1)} %copy-done.62, bf16[1024,1024]{1,0:T(8,128)(2,1)S(1)} %get-tuple-element.123, bf16[1024,1024]{1,0:T(8,128)(2,1)S(1)} %get-tuple-element.122, ...), kind=kLoop, calls=%fused_computation.9 | loop fusion | flops 33550336 | bytes 8433664 | tf_op jit(solution)/shard_map/transpose(jvp())/reduce_sum | solution.py:202
  485.7 16.7 %collective-permute-start.21 = (f32[7680]{0:T(1024)S(1)}, f32[7680]{0:T(1024)S(1)}, u32[]{:S(2)}, u32[]{:S(2)}) collective-permute-start(f32[7680]{0:T(1024)S(1)} %constant_dynamic-update-slice_fusion), channel_id=1, source_target_pairs={{0,4},{4,0},{8,12},{12,8},{16,20},{20,16},{24,28},{28,24},{1,5},{5... | collective-permute-start | bytes 92168 | tf_op jit(solution)/shard_map/ppermute | solution.py:239
  504.3 44.2 %reduce-scatter.9.cloned.1.call-done = bf16[128,1024]{1,0:T(8,128)(2,1)} async-done(((bf16[1024,1024]{1,0:T(8,128)(2,1)}), bf16[128,1024]{1,0:T(8,128)(2,1)}) %reduce-scatter.9.cloned.1.call-update) | async-done | bytes 262160
  553.1 3.0 collective-permute-done.22
  557.5 10.8 %maximum_add_fusion = f32[2048,1024]{1,0:T(8,128)} fusion(f32[1280,1024]{1,0:T(8,128)} %copy-done.26, f32[768,1024]{1,0:T(8,128)} %copy-done.29, bf16[2048,1024]{1,0:T(8,128)(2,1)} %param.17, f32[2048]{0:T(1024)S(1)} %negate_multiply_fusion.2, f32[2048]{0:T(1024)S(1)} %multiply_multiply_fusion.10, f32[1024]{0:T(1024)S(1)} %copy-done.69, ...), kind=kLoop, calls=%fused_computation.10 | loop fusion | flops 29360128 | bytes 25202688 | tf_op jit(solution)/shard_map/add | solution.py:384
  (336 shorter events, 87.9 us)
Async XLA Ops:
  7.2 120.3 %copy-start = (bf16[1024,1024]{1,0:T(8,128)(2,1)S(1)}, bf16[1024,1024]{1,0:T(8,128)(2,1)}, u32[]{:S(2)}) copy-start(bf16[1024,1024]{1,0:T(8,128)(2,1)} %param.24) | copy-start | bytes 6291460
  7.2 340.6 %reduce-scatter.7.cloned.1.call-start = ((), (), s32[]{:S(2)}) async-start(), calls=%async_computation.2 | async-start | bytes 4718592
  36.9 13.5 %copy-start.46 = (bf16[256,1024]{1,0:T(8,128)(2,1)S(1)}, bf16[256,1024]{1,0:T(8,128)(2,1)}, u32[]{:S(2)}) copy-start(bf16[256,1024]{1,0:T(8,128)(2,1)} %param.22) | copy-start | bytes 1572868
  52.5 32.6 %collective-permute-start = (bf16[384,1024]{1,0:T(8,128)(2,1)}, bf16[384,1024]{1,0:T(8,128)(2,1)}, u32[]{:S(2)}, u32[]{:S(2)}) collective-permute-start(bf16[384,1024]{1,0:T(8,128)(2,1)} %constant_dynamic-slice_fusion.6), channel_id=1, source_target_pairs={{0,1},{1,0},{2,3},{3,2},{4,5},{5,4},{6,7},{7,6},{8,9},{9,8},{10,11... | collective-permute-start | bytes 2359304 | tf_op jit(solution)/shard_map/ppermute | solution.py:223
  57.6 27.5 %copy-start.37 = (bf16[768,1024]{1,0:T(8,128)(2,1)S(1)}, bf16[768,1024]{1,0:T(8,128)(2,1)}, u32[]{:S(2)}) copy-start(bf16[768,1024]{1,0:T(8,128)(2,1)} %copy-done.36) | copy-start | bytes 4718596
  57.6 32.6 %copy-start.47 = (bf16[256,1024]{1,0:T(8,128)(2,1)S(1)}, bf16[256,1024]{1,0:T(8,128)(2,1)}, u32[]{:S(2)}) copy-start(bf16[256,1024]{1,0:T(8,128)(2,1)} %param.22) | copy-start | bytes 1572868
  85.1 5.1 copy-start.2
  87.7 21.0 %collective-permute-start.1 = (bf16[384,1024]{1,0:T(8,128)(2,1)}, bf16[384,1024]{1,0:T(8,128)(2,1)}, u32[]{:S(2)}, u32[]{:S(2)}) collective-permute-start(bf16[384,1024]{1,0:T(8,128)(2,1)} %add_convert_fusion.18), channel_id=1, source_target_pairs={{0,2},{1,3},{2,0},{3,1},{4,6},{5,7},{6,4},{7,5},{8,10},{9,11},{10,... | collective-permute-start | bytes 2359304 | tf_op jit(solution)/shard_map/ppermute | solution.py:225
  95.0 22.9 %collective-permute-start.3 = (bf16[640,1024]{1,0:T(8,128)(2,1)}, bf16[640,1024]{1,0:T(8,128)(2,1)}, u32[]{:S(2)}, u32[]{:S(2)}) collective-permute-start(bf16[640,1024]{1,0:T(8,128)(2,1)} %constant_dynamic-slice_fusion.5), channel_id=1, source_target_pairs={{0,1},{1,0},{2,3},{3,2},{4,5},{5,4},{6,7},{7,6},{8,9},{9,8},{10,11... | collective-permute-start | bytes 3932168 | tf_op jit(solution)/shard_map/ppermute | solution.py:223
  111.3 10.7 %collective-permute-start.2 = (bf16[384,1024]{1,0:T(8,128)(2,1)}, bf16[384,1024]{1,0:T(8,128)(2,1)}, u32[]{:S(2)}, u32[]{:S(2)}) collective-permute-start(bf16[384,1024]{1,0:T(8,128)(2,1)} %add_convert_fusion.17), channel_id=1, source_target_pairs={{0,1},{1,0},{2,3},{3,2},{4,5},{5,4},{6,7},{7,6},{8,9},{9,8},{10,11... | collective-permute-start | bytes 2359304 | tf_op jit(solution)/shard_map/ppermute | solution.py:227
  117.9 5.6 copy-start.70
  120.2 31.4 %collective-permute-start.4 = (bf16[640,1024]{1,0:T(8,128)(2,1)S(1)}, bf16[640,1024]{1,0:T(8,128)(2,1)S(1)}, u32[]{:S(2)}, u32[]{:S(2)}) collective-permute-start(bf16[640,1024]{1,0:T(8,128)(2,1)S(1)} %add_convert_fusion.12), channel_id=1, source_target_pairs={{0,2},{1,3},{2,0},{3,1},{4,6},{5,7},{6,4},{7,5},{8,10},{9,11},{10,... | collective-permute-start | bytes 3932168 | tf_op jit(solution)/shard_map/ppermute | solution.py:225
  127.5 18.7 %copy-start.55 = (bf16[768,1024]{1,0:T(8,128)(2,1)}, bf16[768,1024]{1,0:T(8,128)(2,1)S(1)}, u32[]{:S(2)}) copy-start(bf16[768,1024]{1,0:T(8,128)(2,1)S(1)} %add_convert_fusion.6) | copy-start | bytes 4718596
  127.5 18.7 %copy-start.30 = (bf16[2048,1024]{1,0:T(8,128)(2,1)S(1)}, bf16[2048,1024]{1,0:T(8,128)(2,1)}, u32[]{:S(2)}) copy-start(bf16[2048,1024]{1,0:T(8,128)(2,1)} %param.18) | copy-start | bytes 12582916
  127.5 18.7 %copy-start.77 = (bf16[1024,1024]{1,0:T(8,128)(2,1)S(1)}, bf16[1024,1024]{1,0:T(8,128)(2,1)}, u32[]{:S(2)}) copy-start(bf16[1024,1024]{1,0:T(8,128)(2,1)} %param.26) | copy-start | bytes 6291460
  153.2 21.1 %collective-permute-start.5 = (bf16[640,1024]{1,0:T(8,128)(2,1)}, bf16[640,1024]{1,0:T(8,128)(2,1)}, u32[]{:S(2)}, u32[]{:S(2)}) collective-permute-start(bf16[640,1024]{1,0:T(8,128)(2,1)} %add_convert_fusion.11), channel_id=1, source_target_pairs={{0,1},{1,0},{2,3},{3,2},{4,5},{5,4},{6,7},{7,6},{8,9},{9,8},{10,11... | collective-permute-start | bytes 3932168 | tf_op jit(solution)/shard_map/ppermute | solution.py:227
  154.3 15.4 %collective-permute-start.6 = (bf16[384,1024]{1,0:T(8,128)(2,1)}, bf16[384,1024]{1,0:T(8,128)(2,1)}, u32[]{:S(2)}, u32[]{:S(2)}) collective-permute-start(bf16[384,1024]{1,0:T(8,128)(2,1)} %constant_dynamic-slice_fusion.4), channel_id=1, source_target_pairs={{0,1},{1,0},{2,3},{3,2},{4,5},{5,4},{6,7},{7,6},{8,9},{9,8},{10,11... | collective-permute-start | bytes 2359304 | tf_op jit(solution)/shard_map/ppermute | solution.py:223
  166.7 9.4 %slice-start.2 = ((s8[8388608]{0:T(1024)(128)(4,1)}), s8[4194304]{0:T(1024)(128)(4,1)S(1)}, s32[]{:S(2)}) async-start(s8[8388608]{0:T(1024)(128)(4,1)} %bitcast.122), calls=%async_computation.6 | async-start | bytes 8388608
  166.8 9.4 %slice-start.3 = ((s8[8388608]{0:T(1024)(128)(4,1)}), s8[4194304]{0:T(1024)(128)(4,1)S(1)}, s32[]{:S(2)}) async-start(s8[8388608]{0:T(1024)(128)(4,1)} %bitcast.122), calls=%async_computation.7 | async-start | bytes 8388608
  172.7 57.6 %collective-permute-start.7 = (bf16[384,1024]{1,0:T(8,128)(2,1)}, bf16[384,1024]{1,0:T(8,128)(2,1)}, u32[]{:S(2)}, u32[]{:S(2)}) collective-permute-start(bf16[384,1024]{1,0:T(8,128)(2,1)} %add_convert_fusion.16), channel_id=1, source_target_pairs={{0,2},{1,3},{2,0},{3,1},{4,6},{5,7},{6,4},{7,5},{8,10},{9,11},{10,... | collective-permute-start | bytes 2359304 | tf_op jit(solution)/shard_map/ppermute | solution.py:225
  179.5 15.3 %copy-start.31 = (bf16[2048,1024]{1,0:T(8,128)(2,1)S(1)}, bf16[2048,1024]{1,0:T(8,128)(2,1)}, u32[]{:S(2)}) copy-start(bf16[2048,1024]{1,0:T(8,128)(2,1)} %param.18) | copy-start | bytes 12582916
  194.8 21.7 %copy-start.82 = (bf16[1280,1024]{1,0:T(8,128)(2,1)}, bf16[1280,1024]{1,0:T(8,128)(2,1)S(1)}, u32[]{:S(2)}) copy-start(bf16[1280,1024]{1,0:T(8,128)(2,1)S(1)} %get-tuple-element.112) | copy-start | bytes 7864324
  194.8 9.3 %copy-start.56 = (bf16[768,1024]{1,0:T(8,128)(2,1)S(1)}, bf16[768,1024]{1,0:T(8,128)(2,1)}, u32[]{:S(2)}) copy-start(bf16[768,1024]{1,0:T(8,128)(2,1)} %copy-done.55) | copy-start | bytes 4718596
  194.8 9.3 %copy-start.86 = (bf16[768,1024]{1,0:T(8,128)(2,1)S(1)}, bf16[768,1024]{1,0:T(8,128)(2,1)}, u32[]{:S(2)}) copy-start(bf16[768,1024]{1,0:T(8,128)(2,1)} %copy-done.85) | copy-start | bytes 4718596
  204.1 6.5 %copy-start.87 = (bf16[1280,1024]{1,0:T(8,128)(2,1)S(1)}, bf16[1280,1024]{1,0:T(8,128)(2,1)}, u32[]{:S(2)}) copy-start(bf16[1280,1024]{1,0:T(8,128)(2,1)} %get-tuple-element.121) | copy-start | bytes 7864324
  216.4 16.2 %collective-permute-start.9 = (bf16[640,1024]{1,0:T(8,128)(2,1)}, bf16[640,1024]{1,0:T(8,128)(2,1)}, u32[]{:S(2)}, u32[]{:S(2)}) collective-permute-start(bf16[640,1024]{1,0:T(8,128)(2,1)} %constant_dynamic-slice_fusion.3), channel_id=1, source_target_pairs={{0,1},{1,0},{2,3},{3,2},{4,5},{5,4},{6,7},{7,6},{8,9},{9,8},{10,11... | collective-permute-start | bytes 3932168 | tf_op jit(solution)/shard_map/ppermute | solution.py:223
  230.2 5.4 copy-start.79
  230.2 318.4 %reduce-scatter.9.cloned.1.call-start = ((), (), s32[]{:S(2)}) async-start(), calls=%async_computation.3 | async-start | bytes 2359296
  230.2 5.3 copy-start.83
  232.1 7.8 %collective-permute-start.8 = (bf16[384,1024]{1,0:T(8,128)(2,1)S(1)}, bf16[384,1024]{1,0:T(8,128)(2,1)S(1)}, u32[]{:S(2)}, u32[]{:S(2)}) collective-permute-start(bf16[384,1024]{1,0:T(8,128)(2,1)S(1)} %add_convert_fusion.15), channel_id=1, source_target_pairs={{0,1},{1,0},{2,3},{3,2},{4,5},{5,4},{6,7},{7,6},{8,9},{9,8},{10,11... | collective-permute-start | bytes 2359304 | tf_op jit(solution)/shard_map/ppermute | solution.py:227
  232.6 36.3 %slice-start.4 = ((s8[8388608]{0:T(1024)(128)(4,1)}), s8[4194304]{0:T(1024)(128)(4,1)S(1)}, s32[]{:S(2)}) async-start(s8[8388608]{0:T(1024)(128)(4,1)} %bitcast.124), calls=%async_computation.8 | async-start | bytes 8388608
  235.0 34.0 %slice-start.5 = ((s8[8388608]{0:T(1024)(128)(4,1)}), s8[4194304]{0:T(1024)(128)(4,1)S(1)}, s32[]{:S(2)}) async-start(s8[8388608]{0:T(1024)(128)(4,1)} %bitcast.124), calls=%async_computation.9 | async-start | bytes 8388608
  235.1 30.8 %collective-permute-start.10 = (bf16[640,1024]{1,0:T(8,128)(2,1)S(1)}, bf16[640,1024]{1,0:T(8,128)(2,1)S(1)}, u32[]{:S(2)}, u32[]{:S(2)}) collective-permute-start(bf16[640,1024]{1,0:T(8,128)(2,1)S(1)} %add_convert_fusion.10), channel_id=1, source_target_pairs={{0,2},{1,3},{2,0},{3,1},{4,6},{5,7},{6,4},{7,5},{8,10},{9,11},{10,... | collective-permute-start | bytes 3932168 | tf_op jit(solution)/shard_map/ppermute | solution.py:225
  266.4 7.7 %collective-permute-start.11 = (bf16[640,1024]{1,0:T(8,128)(2,1)S(1)}, bf16[640,1024]{1,0:T(8,128)(2,1)S(1)}, u32[]{:S(2)}, u32[]{:S(2)}) collective-permute-start(bf16[640,1024]{1,0:T(8,128)(2,1)S(1)} %add_convert_fusion.9), channel_id=1, source_target_pairs={{0,1},{1,0},{2,3},{3,2},{4,5},{5,4},{6,7},{7,6},{8,9},{9,8},{10,11... | collective-permute-start | bytes 3932168 | tf_op jit(solution)/shard_map/ppermute | solution.py:227
  292.0 5.2 copy-start.6
  292.0 5.2 copy-start.11
  294.2 67.2 %collective-permute-start.12 = (bf16[384,1024]{1,0:T(8,128)(2,1)}, bf16[384,1024]{1,0:T(8,128)(2,1)}, u32[]{:S(2)}, u32[]{:S(2)}) collective-permute-start(bf16[384,1024]{1,0:T(8,128)(2,1)} %constant_dynamic-slice_fusion.2), channel_id=1, source_target_pairs={{0,1},{1,0},{2,3},{3,2},{4,5},{5,4},{6,7},{7,6},{8,9},{9,8},{10,11... | collective-permute-start | bytes 2359304 | tf_op jit(solution)/shard_map/ppermute | solution.py:223
  297.2 66.6 %collective-permute-start.15 = (bf16[640,1024]{1,0:T(8,128)(2,1)}, bf16[640,1024]{1,0:T(8,128)(2,1)}, u32[]{:S(2)}, u32[]{:S(2)}) collective-permute-start(bf16[640,1024]{1,0:T(8,128)(2,1)} %constant_dynamic-slice_fusion.1), channel_id=1, source_target_pairs={{0,1},{1,0},{2,3},{3,2},{4,5},{5,4},{6,7},{7,6},{8,9},{9,8},{10,11... | collective-permute-start | bytes 3932168 | tf_op jit(solution)/shard_map/ppermute | solution.py:223
  343.0 6.8 %copy-start.33 = (f32[4,64,2048]{2,1,0:T(8,128)S(1)}, f32[4,64,2048]{2,1,0:T(8,128)}, u32[]{:S(2)}) copy-start(f32[4,64,2048]{2,1,0:T(8,128)} %get-tuple-element.39) | copy-start | bytes 6291460
  361.0 23.1 %collective-permute-start.18 = (bf16[1024,1024]{1,0:T(8,128)(2,1)}, bf16[1024,1024]{1,0:T(8,128)(2,1)}, u32[]{:S(2)}, u32[]{:S(2)}) collective-permute-start(bf16[1024,1024]{1,0:T(8,128)(2,1)} %constant_dynamic-slice_fusion), channel_id=1, source_target_pairs={{0,1},{1,0},{2,3},{3,2},{4,5},{5,4},{6,7},{7,6},{8,9},{9,8},{10,11... | collective-permute-start | bytes 6291464 | tf_op jit(solution)/shard_map/ppermute | solution.py:223
  361.4 6.2 %copy-start.32 = (bf16[2048,1024]{1,0:T(8,128)(2,1)S(1)}, bf16[2048,1024]{1,0:T(8,128)(2,1)}, u32[]{:S(2)}) copy-start(bf16[2048,1024]{1,0:T(8,128)(2,1)} %param.18) | copy-start | bytes 12582916
  363.2 20.5 %collective-permute-start.13 = (bf16[384,1024]{1,0:T(8,128)(2,1)S(1)}, bf16[384,1024]{1,0:T(8,128)(2,1)S(1)}, u32[]{:S(2)}, u32[]{:S(2)}) collective-permute-start(bf16[384,1024]{1,0:T(8,128)(2,1)S(1)} %add_convert_fusion.14), channel_id=1, source_target_pairs={{0,2},{1,3},{2,0},{3,1},{4,6},{5,7},{6,4},{7,5},{8,10},{9,11},{10,... | collective-permute-start | bytes 2359304 | tf_op jit(solution)/shard_map/ppermute | solution.py:225
  366.0 18.1 %copy-start.42 = (bf16[2048,1024]{1,0:T(8,128)(2,1)S(1)}, bf16[2048,1024]{1,0:T(8,128)(2,1)}, u32[]{:S(2)}) copy-start(bf16[2048,1024]{1,0:T(8,128)(2,1)} %copy-done.41) | copy-start | bytes 12582916
  366.0 45.8 %collective-permute-start.16 = (bf16[640,1024]{1,0:T(8,128)(2,1)S(1)}, bf16[640,1024]{1,0:T(8,128)(2,1)S(1)}, u32[]{:S(2)}, u32[]{:S(2)}) collective-permute-start(bf16[640,1024]{1,0:T(8,128)(2,1)S(1)} %add_convert_fusion.8), channel_id=1, source_target_pairs={{0,2},{1,3},{2,0},{3,1},{4,6},{5,7},{6,4},{7,5},{8,10},{9,11},{10,... | collective-permute-start | bytes 3932168 | tf_op jit(solution)/shard_map/ppermute | solution.py:225
  384.0 29.8 %collective-permute-start.14 = (bf16[384,1024]{1,0:T(8,128)(2,1)S(1)}, bf16[384,1024]{1,0:T(8,128)(2,1)S(1)}, u32[]{:S(2)}, u32[]{:S(2)}) collective-permute-start(bf16[384,1024]{1,0:T(8,128)(2,1)S(1)} %add_convert_fusion.13), channel_id=1, source_target_pairs={{0,1},{1,0},{2,3},{3,2},{4,5},{5,4},{6,7},{7,6},{8,9},{9,8},{10,11... | collective-permute-start | bytes 2359304 | tf_op jit(solution)/shard_map/ppermute | solution.py:227
  384.1 28.3 %copy-start.54 = (bf16[768,1024]{1,0:T(8,128)(2,1)S(1)}, bf16[768,1024]{1,0:T(8,128)(2,1)}, u32[]{:S(2)}) copy-start(bf16[768,1024]{1,0:T(8,128)(2,1)} %copy-done.53) | copy-start | bytes 4718596
  386.8 25.6 %copy-start.74 = (f32[1024]{0:T(1024)S(1)}, f32[1024]{0:T(1024)}, u32[]{:S(2)}) copy-start(f32[1024]{0:T(1024)} %get-tuple-element.124) | copy-start | bytes 12292
  386.8 25.7 %copy-start.3 = (bf16[4,64,1280]{2,1,0:T(8,128)(2,1)S(1)}, bf16[4,64,1280]{2,1,0:T(8,128)(2,1)}, u32[]{:S(2)}) copy-start(bf16[4,64,1280]{2,1,0:T(8,128)(2,1)} %copy-done.2) | copy-start | bytes 1966084
  386.8 25.7 %copy-start.15 = (bf16[4,64,768]{2,1,0:T(8,128)(2,1)S(1)}, bf16[4,64,768]{2,1,0:T(8,128)(2,1)}, u32[]{:S(2)}) copy-start(bf16[4,64,768]{2,1,0:T(8,128)(2,1)} %copy-done.14) | copy-start | bytes 1179652
  386.8 25.6 %copy-start.45 = (bf16[1280,1024]{1,0:T(8,128)(2,1)S(1)}, bf16[1280,1024]{1,0:T(8,128)(2,1)}, u32[]{:S(2)}) copy-start(bf16[1280,1024]{1,0:T(8,128)(2,1)} %copy-done.44) | copy-start | bytes 7864324
  386.8 69.5 %collective-permute-start.19 = (bf16[1024,1024]{1,0:T(8,128)(2,1)S(1)}, bf16[1024,1024]{1,0:T(8,128)(2,1)S(1)}, u32[]{:S(2)}, u32[]{:S(2)}) collective-permute-start(bf16[1024,1024]{1,0:T(8,128)(2,1)S(1)} %add_convert_fusion.4), channel_id=1, source_target_pairs={{0,2},{1,3},{2,0},{3,1},{4,6},{5,7},{6,4},{7,5},{8,10},{9,11},{10,... | collective-permute-start | bytes 6291464 | tf_op jit(solution)/shard_map/ppermute | solution.py:225
  412.3 5.1 collective-permute-start.17
  417.4 41.2 %copy-start.60 = (bf16[1,2048,256]{2,1,0:T(8,128)(2,1)S(1)}, bf16[1,2048,256]{2,1,0:T(8,128)(2,1)}, u32[]{:S(2)}) copy-start(bf16[1,2048,256]{2,1,0:T(8,128)(2,1)} %copy-done.59) | copy-start | bytes 3145732
  418.6 40.0 %copy-start.40 = (bf16[2048,1024]{1,0:T(8,128)(2,1)S(1)}, bf16[2048,1024]{1,0:T(8,128)(2,1)}, u32[]{:S(2)}) copy-start(bf16[2048,1024]{1,0:T(8,128)(2,1)} %copy-done.39) | copy-start | bytes 12582916
  418.7 40.0 %copy-start.57 = (bf16[1,2048,256]{2,1,0:T(8,128)(2,1)S(1)}, bf16[1,2048,256]{2,1,0:T(8,128)(2,1)}, u32[]{:S(2)}) copy-start(bf16[1,2048,256]{2,1,0:T(8,128)(2,1)} %convert_bitcast_fusion.1) | copy-start | bytes 3145732
  418.7 40.0 %copy-start.58 = (bf16[1,2048,256]{2,1,0:T(8,128)(2,1)S(1)}, bf16[1,2048,256]{2,1,0:T(8,128)(2,1)}, u32[]{:S(2)}) copy-start(bf16[1,2048,256]{2,1,0:T(8,128)(2,1)} %get-tuple-element.133) | copy-start | bytes 3145732
  458.6 13.4 %collective-permute-start.20 = (bf16[1024,1024]{1,0:T(8,128)(2,1)}, bf16[1024,1024]{1,0:T(8,128)(2,1)}, u32[]{:S(2)}, u32[]{:S(2)}) collective-permute-start(bf16[1024,1024]{1,0:T(8,128)(2,1)} %add_convert_fusion.3), channel_id=1, source_target_pairs={{0,1},{1,0},{2,3},{3,2},{4,5},{5,4},{6,7},{7,6},{8,9},{9,8},{10,11... | collective-permute-start | bytes 6291464 | tf_op jit(solution)/shard_map/ppermute | solution.py:227
  465.2 4.0 copy-start.35
  474.7 4.0 copy-start.27
  474.7 4.0 copy-start.28
  485.7 66.4 %collective-permute-start.21 = (f32[7680]{0:T(1024)S(1)}, f32[7680]{0:T(1024)S(1)}, u32[]{:S(2)}, u32[]{:S(2)}) collective-permute-start(f32[7680]{0:T(1024)S(1)} %constant_dynamic-update-slice_fusion), channel_id=1, source_target_pairs={{0,4},{4,0},{8,12},{12,8},{16,20},{20,16},{24,28},{28,24},{1,5},{5... | collective-permute-start | bytes 92168 | tf_op jit(solution)/shard_map/ppermute | solution.py:239
  552.2 4.0 collective-permute-start.22
  556.2 12.2 %collective-permute-start.23 = (f32[7680]{0:T(1024)S(1)}, f32[7680]{0:T(1024)S(1)}, u32[]{:S(2)}, u32[]{:S(2)}) collective-permute-start(f32[7680]{0:T(1024)S(1)} %add.323), channel_id=1, source_target_pairs={{0,16},{4,20},{8,24},{12,28},{16,0},{20,4},{24,8},{28,12},{1,17},{... | collective-permute-start | bytes 92168 | tf_op jit(solution)/shard_map/ppermute | solution.py:239
  557.5 12.1 %copy-start.1 = (bf16[1024,1024]{1,0:T(8,128)(2,1)S(1)}, bf16[1024,1024]{1,0:T(8,128)(2,1)}, u32[]{:S(2)}) copy-start(bf16[1024,1024]{1,0:T(8,128)(2,1)} %param.24) | copy-start | bytes 6291460
  (56 other events, 115.1 us)
Sparse Core Ops, SparseCore 0:
  230.3 95.2 reduce-scatter.6
  465.3 83.1 reduce-scatter.8
